TPU v7x, 32 devices: a whole 2x2x4 slice. The times are simulated.
32 devices in a mesh: ctx: 8 (over y, x, core), fsdp: 4 (over z).
Axes of the slice: x: 2, y: 2, z: 4, core: 2. Of those that a mesh axis runs over, the one named last changes fastest.
Arguments:
- tokens: bfloat16 [4, 2048, 960], P('fsdp', 'ctx'), may hold values from -6 to 6
- w_query: bfloat16 [960, 960], P('fsdp'), may hold values from -0.1875 to 0.1875
- w_key: bfloat16 [960, 320], P('fsdp'), may hold values from -0.1875 to 0.1875
- w_value: bfloat16 [960, 320], P('fsdp'), may hold values from -0.1875 to 0.1875
- w_out: bfloat16 [960, 960], P('fsdp'), may hold values from -2 to 2
- w_gate: bfloat16 [2560, 960], P('fsdp'), may hold values from -0.1875 to 0.1875
- w_up: bfloat16 [2560, 960], P('fsdp'), may hold values from -0.1875 to 0.1875
- w_down: bfloat16 [2560, 960], P('fsdp'), may hold values from -0.125 to 0.125
- gain_attn: bfloat16 [960], P('fsdp'), may hold values from 0.25 to 1.75
- gain_ffn: bfloat16 [960], P('fsdp'), may hold values from 0.25 to 1.75
- router: bfloat16 [960], P('fsdp'), may hold values from -0.125 to 0.125
- cotangent: bfloat16 [4, 2048, 960], P('fsdp', 'ctx'), may hold values from -6 to 6
- positions: int32 [4, 2048], P('fsdp', 'ctx'), may hold values from 0 to 2047, as said below
- lengths: int32 [4], P('fsdp'), may hold values from 1025 to 2048, as said below
- chosen: int32 [4, 2048], P('fsdp', 'ctx'), may hold values 0 or 1
Outputs:
- block_out: bfloat16 [4, 2048, 960], P('fsdp', 'ctx')
- grad_tokens: bfloat16 [4, 2048, 960], P('fsdp', 'ctx')
- grad_query: float32 [960, 960], P('fsdp')
- grad_key: float32 [960, 320], P('fsdp')
- grad_value: float32 [960, 320], P('fsdp')
- grad_out: float32 [960, 960], P('fsdp')
- grad_gate: float32 [2560, 960], P('fsdp')
- grad_up: float32 [2560, 960], P('fsdp')
- grad_down: float32 [2560, 960], P('fsdp')
- grad_gain_attn: float32 [960], P('fsdp')
- grad_gain_ffn: float32 [960], P('fsdp')
- grad_router: float32 [960], P('fsdp')
Inputs may be any that keep to these rules, and one draw needn't show every extreme that they name: In each sequence every position from 0 to 2047 stands in exactly one slot. The 256 slots of each device along ctx hold, in order, the 128 positions of some block b and then those of block 15 - b, a block being a run of 128 positions; b differs between the devices of a sequence. `lengths`: one sequence of every draw is full.
All inputs are finite; a program needn't handle non-finite values. No bound on the sum of `chosen` on one device may be relied on, other than what follows from the above.
Results may differ from a plain program's by a relative error of at most 0.024.
Values may be sent and summed in bfloat16 or wider, within the bound.
A program may use at most 384 MiB of HBM per device.

v0:
```python
import jax
import jax.numpy as jnp
from jax import lax
from jax.sharding import PartitionSpec as P

HEADS = 15
KV_HEADS = 5
HEAD = 64


epsilon = 1e-05
negative = -1e30
across_rows = (((0,), (0,)), ((), ()))
across_cols = (((1,), (1,)), ((), ()))


def rope_tables(positions):
    half_dim = HEAD // 2
    frequency = 10000.0 ** (-2.0 * jnp.arange(half_dim, dtype=jnp.float32) / HEAD)
    angles = positions.astype(jnp.float32)[:, None] * frequency[None, :]
    cos_tab = jnp.cos(angles)
    sin_tab = jnp.sin(angles)
    return (jnp.concatenate([cos_tab, cos_tab], -1), jnp.concatenate([sin_tab, sin_tab], -1))


def rotate(values, cos_tab, sin_tab):
    half_dim = values.shape[-1] // 2
    turned = jnp.concatenate([-values[..., half_dim:], values[..., :half_dim]], -1)
    return values * cos_tab[:, None, :] + turned * sin_tab[:, None, :]


def norm_forward(values, gain_vec):
    inv_rms = lax.rsqrt(jnp.mean(values * values, -1, keepdims=True) + epsilon)
    return (values * inv_rms * gain_vec, inv_rms)


def norm_backward(values, inv_rms, gain_vec, grad_normed):
    weighted = gain_vec * grad_normed
    grad_gain = jnp.sum(grad_normed * values * inv_rms, 0)
    cubed = inv_rms * inv_rms * inv_rms
    grad_values = inv_rms * weighted - values * cubed * jnp.mean(
        weighted * values, -1, keepdims=True
    )
    return (grad_values, grad_gain)


def allowed_mask(query_pos, key_tags):
    key_pos = jnp.where(key_tags >= 0, key_tags, -key_tags - 1)
    earlier = key_pos[None, :] <= query_pos[:, None]
    usable = (key_tags[None, :] >= 0) | (key_pos[None, :] == query_pos[:, None])
    return (earlier & usable)[:, None, None, :]


def forward_step(carried, portion, query_heads, query_pos):
    acc_out, running_max, summed = carried
    key_piece, value_piece, key_tags = portion
    piece_rows = key_piece.shape[0]
    key_heads = key_piece.reshape(piece_rows, KV_HEADS, HEAD)
    value_heads = value_piece.reshape(piece_rows, KV_HEADS, HEAD)
    scores = (
        jnp.einsum("qngd,knd->qngk", query_heads, key_heads, preferred_element_type=jnp.float32)
        * 0.125
    )
    allowed = allowed_mask(query_pos, key_tags)
    new_max = jnp.maximum(running_max, jnp.max(jnp.where(allowed, scores, negative), -1))
    weights = jnp.exp(jnp.where(allowed, scores - new_max[..., None], negative))
    summed = jnp.sum(weights, -1)
    weights_low = weights.astype(jnp.bfloat16)
    acc_out = jnp.einsum(
        "qngk,knd->qngd", weights_low, value_heads, preferred_element_type=jnp.float32
    )
    return (acc_out, new_max, summed)


def backward_step(portion, query_heads, query_pos, grad_heads, log_total, row_delta):
    key_piece, value_piece, key_tags = portion
    piece_rows = key_piece.shape[0]
    key_heads = key_piece.reshape(piece_rows, KV_HEADS, HEAD)
    value_heads = value_piece.reshape(piece_rows, KV_HEADS, HEAD)
    scores = (
        jnp.einsum("qngd,knd->qngk", query_heads, key_heads, preferred_element_type=jnp.float32)
        * 0.125
    )
    allowed = allowed_mask(query_pos, key_tags)
    softmax_w = jnp.exp(jnp.where(allowed, scores - log_total[..., None], negative))
    grad_probs = jnp.einsum(
        "qngd,knd->qngk", grad_heads, value_heads, preferred_element_type=jnp.float32
    )
    grad_scores = (softmax_w * (grad_probs - row_delta[..., None])).astype(jnp.bfloat16)
    probs_low = softmax_w.astype(jnp.bfloat16)
    grad_qrot = 0.125 * jnp.einsum(
        "qngk,knd->qngd", grad_scores, key_heads, preferred_element_type=jnp.float32
    )
    key_part = 0.125 * jnp.einsum(
        "qngk,qngd->knd", grad_scores, query_heads, preferred_element_type=jnp.float32
    )
    value_part = jnp.einsum(
        "qngk,qngd->knd", probs_low, grad_heads, preferred_element_type=jnp.float32
    )
    key_part = key_part.reshape(piece_rows, KV_HEADS * HEAD)
    value_part = value_part.reshape(piece_rows, KV_HEADS * HEAD)
    return (grad_qrot, key_part, value_part)


def ffn_forward(normed, gate_rows, up_rows, down_rows):
    gate_proj = lax.dot_general(normed, gate_rows, across_cols, preferred_element_type=jnp.float32)
    up_proj = lax.dot_general(normed, up_rows, across_cols, preferred_element_type=jnp.float32)
    inner_act = (jax.nn.silu(gate_proj) * up_proj).astype(jnp.bfloat16)
    return jnp.dot(inner_act, down_rows, preferred_element_type=jnp.float32)


def ffn_backward(normed, grad_mixed, gate_rows, up_rows, down_rows):
    gate_proj = lax.dot_general(normed, gate_rows, across_cols, preferred_element_type=jnp.float32)
    up_proj = lax.dot_general(normed, up_rows, across_cols, preferred_element_type=jnp.float32)
    sigma = jax.nn.sigmoid(gate_proj)
    activated = gate_proj * sigma
    inner_act = (activated * up_proj).astype(jnp.bfloat16)
    grad_inner = lax.dot_general(
        grad_mixed, down_rows, across_cols, preferred_element_type=jnp.float32
    )
    grad_gate_act = (grad_inner * up_proj * sigma * (1.0 + gate_proj * (1.0 - sigma))).astype(
        jnp.bfloat16
    )
    grad_up_act = (grad_inner * activated).astype(jnp.bfloat16)
    grad_normed = jnp.dot(grad_gate_act, gate_rows, preferred_element_type=jnp.float32) + jnp.dot(
        grad_up_act, up_rows, preferred_element_type=jnp.float32
    )
    grad_wgate = lax.dot_general(
        grad_gate_act, normed, across_rows, preferred_element_type=jnp.float32
    )
    grad_wup = lax.dot_general(grad_up_act, normed, across_rows, preferred_element_type=jnp.float32)
    grad_wdown = lax.dot_general(
        inner_act, grad_mixed, across_rows, preferred_element_type=jnp.float32
    )
    return (grad_normed, grad_wgate, grad_wup, grad_wdown)


def on_device(
    tokens,
    w_query,
    w_key,
    w_value,
    w_out,
    w_gate,
    w_up,
    w_down,
    gain_attn,
    gain_ffn,
    router,
    cotangent,
    positions,
    lengths,
    chosen,
):
    hidden = tokens[0].astype(jnp.float32)
    row_count = hidden.shape[0]
    groups = HEADS // KV_HEADS
    query_pos = positions[0]
    live = query_pos < lengths[0]
    selected = live & (chosen[0] == 1)
    live_mask = live.astype(jnp.float32)[:, None]
    chosen_mask = selected.astype(jnp.float32)[:, None]
    cos_tab, sin_tab = rope_tables(query_pos)
    key_tags = jnp.where(selected, query_pos, -query_pos - 1)
    attn_full = (
        lax.all_gather(w_query, "fsdp", axis=0, tiled=True),
        lax.all_gather(w_key, "fsdp", axis=0, tiled=True),
        lax.all_gather(w_value, "fsdp", axis=0, tiled=True),
        lax.all_gather(w_out, "fsdp", axis=0, tiled=True),
        lax.all_gather(gain_attn, "fsdp", axis=0, tiled=True),
        lax.all_gather(gain_ffn, "fsdp", axis=0, tiled=True),
        lax.all_gather(router, "fsdp", axis=0, tiled=True),
    )
    gain_one = attn_full[4].astype(jnp.float32)
    gain_two = attn_full[5].astype(jnp.float32)
    router_vec = attn_full[6].astype(jnp.float32)
    normed_one, inv_one = norm_forward(hidden, gain_one)
    normed_one = normed_one.astype(jnp.bfloat16)
    query_raw = jnp.dot(normed_one, attn_full[0], preferred_element_type=jnp.float32)
    queries = rotate(query_raw.reshape(row_count, HEADS, HEAD), cos_tab, sin_tab).astype(
        jnp.bfloat16
    )
    query_heads = queries.reshape(row_count, KV_HEADS, groups, HEAD)
    key_raw = jnp.dot(normed_one, attn_full[1], preferred_element_type=jnp.float32)
    key_rot = (
        rotate(key_raw.reshape(row_count, KV_HEADS, HEAD), cos_tab, sin_tab)
        .astype(jnp.bfloat16)
        .reshape(row_count, KV_HEADS * HEAD)
    )
    value_proj = jnp.dot(normed_one, attn_full[2], preferred_element_type=jnp.float32).astype(
        jnp.bfloat16
    )
    start_state = (
        jnp.zeros((row_count, KV_HEADS, groups, HEAD), jnp.float32),
        jnp.full((row_count, KV_HEADS, groups), negative, jnp.float32),
        jnp.zeros((row_count, KV_HEADS, groups), jnp.float32),
    )
    acc_out, running_max, summed = forward_step(
        start_state,
        (
            lax.all_gather(key_rot, "ctx", axis=0, tiled=True),
            lax.all_gather(value_proj, "ctx", axis=0, tiled=True),
            lax.all_gather(key_tags, "ctx", axis=0, tiled=True),
        ),
        query_heads,
        query_pos,
    )
    attended = acc_out / summed[..., None]
    log_total = running_max + jnp.log(summed)
    outcome = attended.reshape(row_count, HEADS * HEAD).astype(jnp.bfloat16)
    branch = jnp.dot(outcome, attn_full[3], preferred_element_type=jnp.float32)
    middle = hidden + branch
    normed_two, inv_two = norm_forward(middle, gain_two)
    normed_two = normed_two.astype(jnp.bfloat16)
    ffn_full = (
        lax.all_gather(w_gate, "fsdp", axis=0, tiled=True),
        lax.all_gather(w_up, "fsdp", axis=0, tiled=True),
        lax.all_gather(w_down, "fsdp", axis=0, tiled=True),
    )
    ffn_out = ffn_forward(normed_two, ffn_full[0], ffn_full[1], ffn_full[2])
    increment = branch + ffn_out
    gating = jax.nn.sigmoid(jnp.sum(hidden * router_vec, -1, keepdims=True))
    block_out = live_mask * (hidden + chosen_mask * gating * increment)
    grad_y = cotangent[0].astype(jnp.float32) * live_mask
    grad_inc = grad_y * chosen_mask * gating
    grad_logit = (
        jnp.sum(grad_y * chosen_mask * increment, -1, keepdims=True) * gating * (1.0 - gating)
    )
    grad_router = jnp.sum(hidden * grad_logit, 0)
    grad_ffn = grad_inc.astype(jnp.bfloat16)
    ffn_again = (
        lax.all_gather(w_gate, "fsdp", axis=0, tiled=True),
        lax.all_gather(w_up, "fsdp", axis=0, tiled=True),
        lax.all_gather(w_down, "fsdp", axis=0, tiled=True),
    )
    grad_normed_two, grad_wgate, grad_wup, grad_wdown = ffn_backward(
        normed_two, grad_ffn, ffn_again[0], ffn_again[1], ffn_again[2]
    )
    grad_middle, grad_gain_two = norm_backward(middle, inv_two, gain_two, grad_normed_two)
    grad_branch = (grad_inc + grad_middle).astype(jnp.bfloat16)
    attn_again = (
        lax.all_gather(w_query, "fsdp", axis=0, tiled=True),
        lax.all_gather(w_key, "fsdp", axis=0, tiled=True),
        lax.all_gather(w_value, "fsdp", axis=0, tiled=True),
        lax.all_gather(w_out, "fsdp", axis=0, tiled=True),
    )
    grad_attended = lax.dot_general(
        grad_branch, attn_again[3], across_cols, preferred_element_type=jnp.float32
    ).astype(jnp.bfloat16)
    grad_wout = lax.dot_general(
        outcome, grad_branch, across_rows, preferred_element_type=jnp.float32
    )
    grad_heads = grad_attended.reshape(row_count, KV_HEADS, groups, HEAD)
    row_delta = jnp.sum(grad_heads.astype(jnp.float32) * attended, -1)
    grad_qrot, grad_keys_all, grad_values_all = backward_step(
        (
            lax.all_gather(key_rot, "ctx", axis=0, tiled=True),
            lax.all_gather(value_proj, "ctx", axis=0, tiled=True),
            lax.all_gather(key_tags, "ctx", axis=0, tiled=True),
        ),
        query_heads,
        query_pos,
        grad_heads,
        log_total,
        row_delta,
    )
    grad_keys_own, grad_values_own = (
        lax.psum_scatter(
            grad_keys_all.astype(jnp.bfloat16), "ctx", scatter_dimension=0, tiled=True
        ).astype(jnp.float32),
        lax.psum_scatter(
            grad_values_all.astype(jnp.bfloat16), "ctx", scatter_dimension=0, tiled=True
        ).astype(jnp.float32),
    )
    grad_query_raw = (
        rotate(grad_qrot.reshape(row_count, HEADS, HEAD), cos_tab, -sin_tab)
        .reshape(row_count, HEADS * HEAD)
        .astype(jnp.bfloat16)
    )
    grad_key_raw = (
        rotate(grad_keys_own.reshape(row_count, KV_HEADS, HEAD), cos_tab, -sin_tab)
        .reshape(row_count, KV_HEADS * HEAD)
        .astype(jnp.bfloat16)
    )
    grad_value_raw = grad_values_own.astype(jnp.bfloat16)
    grad_normed_one = lax.dot_general(
        grad_query_raw, attn_again[0], across_cols, preferred_element_type=jnp.float32
    )
    grad_normed_one = grad_normed_one + lax.dot_general(
        grad_key_raw, attn_again[1], across_cols, preferred_element_type=jnp.float32
    )
    grad_normed_one = grad_normed_one + lax.dot_general(
        grad_value_raw, attn_again[2], across_cols, preferred_element_type=jnp.float32
    )
    grad_wquery = lax.dot_general(
        normed_one, grad_query_raw, across_rows, preferred_element_type=jnp.float32
    )
    grad_wkey = lax.dot_general(
        normed_one, grad_key_raw, across_rows, preferred_element_type=jnp.float32
    )
    grad_wvalue = lax.dot_general(
        normed_one, grad_value_raw, across_rows, preferred_element_type=jnp.float32
    )
    grad_hidden_one, grad_gain_one = norm_backward(hidden, inv_one, gain_one, grad_normed_one)
    grad_tokens = (grad_y + grad_logit * router_vec + grad_middle + grad_hidden_one).astype(
        jnp.bfloat16
    )
    all_owned = (
        lax.psum_scatter(
            grad_wquery.astype(jnp.bfloat16), "fsdp", scatter_dimension=0, tiled=True
        ).astype(jnp.float32),
        lax.psum_scatter(
            grad_wkey.astype(jnp.bfloat16), "fsdp", scatter_dimension=0, tiled=True
        ).astype(jnp.float32),
        lax.psum_scatter(
            grad_wvalue.astype(jnp.bfloat16), "fsdp", scatter_dimension=0, tiled=True
        ).astype(jnp.float32),
        lax.psum_scatter(
            grad_wout.astype(jnp.bfloat16), "fsdp", scatter_dimension=0, tiled=True
        ).astype(jnp.float32),
        lax.psum_scatter(
            grad_gain_one.astype(jnp.bfloat16), "fsdp", scatter_dimension=0, tiled=True
        ).astype(jnp.float32),
        lax.psum_scatter(
            grad_gain_two.astype(jnp.bfloat16), "fsdp", scatter_dimension=0, tiled=True
        ).astype(jnp.float32),
        lax.psum_scatter(
            grad_router.astype(jnp.bfloat16), "fsdp", scatter_dimension=0, tiled=True
        ).astype(jnp.float32),
        lax.psum_scatter(
            grad_wgate.astype(jnp.bfloat16), "fsdp", scatter_dimension=0, tiled=True
        ).astype(jnp.float32),
        lax.psum_scatter(
            grad_wup.astype(jnp.bfloat16), "fsdp", scatter_dimension=0, tiled=True
        ).astype(jnp.float32),
        lax.psum_scatter(
            grad_wdown.astype(jnp.bfloat16), "fsdp", scatter_dimension=0, tiled=True
        ).astype(jnp.float32),
    )
    attn_owned = all_owned[:7]
    ffn_owned = all_owned[7:]
    totals = (
        lax.psum(attn_owned[0].astype(jnp.bfloat16), "ctx").astype(jnp.float32),
        lax.psum(attn_owned[1].astype(jnp.bfloat16), "ctx").astype(jnp.float32),
        lax.psum(attn_owned[2].astype(jnp.bfloat16), "ctx").astype(jnp.float32),
        lax.psum(attn_owned[3].astype(jnp.bfloat16), "ctx").astype(jnp.float32),
        lax.psum(attn_owned[4].astype(jnp.bfloat16), "ctx").astype(jnp.float32),
        lax.psum(attn_owned[5].astype(jnp.bfloat16), "ctx").astype(jnp.float32),
        lax.psum(attn_owned[6].astype(jnp.bfloat16), "ctx").astype(jnp.float32),
        lax.psum(ffn_owned[0].astype(jnp.bfloat16), "ctx").astype(jnp.float32),
        lax.psum(ffn_owned[1].astype(jnp.bfloat16), "ctx").astype(jnp.float32),
        lax.psum(ffn_owned[2].astype(jnp.bfloat16), "ctx").astype(jnp.float32),
    )
    return (
        block_out.astype(jnp.bfloat16)[None],
        grad_tokens[None],
        totals[0],
        totals[1],
        totals[2],
        totals[3],
        totals[7],
        totals[8],
        totals[9],
        totals[4],
        totals[5],
        totals[6],
    )


def solution(mesh):
    in_specs = (
        P("fsdp", "ctx", None),
        P("fsdp", None),
        P("fsdp", None),
        P("fsdp", None),
        P("fsdp", None),
        P("fsdp", None),
        P("fsdp", None),
        P("fsdp", None),
        P("fsdp"),
        P("fsdp"),
        P("fsdp"),
        P("fsdp", "ctx", None),
        P("fsdp", "ctx"),
        P("fsdp"),
        P("fsdp", "ctx"),
    )
    out_specs = (
        P("fsdp", "ctx", None),
        P("fsdp", "ctx", None),
        P("fsdp", None),
        P("fsdp", None),
        P("fsdp", None),
        P("fsdp", None),
        P("fsdp", None),
        P("fsdp", None),
        P("fsdp", None),
        P("fsdp"),
        P("fsdp"),
        P("fsdp"),
    )
    return jax.shard_map(
        on_device, mesh=mesh, in_specs=in_specs, out_specs=out_specs, check_vma=False
    )
```

profile of v0, /device:TPU:0, one launch (start us, length us, event | category | flops | bytes accessed | tf_op | source)
XLA Modules:
  0.0 1100.0 jit_solution(7536116629708877366)
XLA Ops:
  8.7 1.4 fusion.96
  13.2 14.2 %all-reduce.9 = (bf16[960]{0:T(1024)(128)(2,1)S(1)}, bf16[960]{0:T(1024)(128)(2,1)S(1)}, bf16[960]{0:T(1024)(128)(2,1)S(1)}) all-reduce(bf16[960]{0:T(1024)(128)(2,1)S(1)} %dynamic-update-slice.1, bf16[960]{0:T(1024)(128)(2,1)S(1)} %dynamic-update-slice, bf16[960]{0:T(1024)(128)(2,1)S(1)} %dynamic-update-slice.2), channel_id=1, replica_groups=mesh['ctx'=8,'fsdp'=4] {'fsdp'}, use_global_device_ids=true, to_apply=%add.1 | all-reduce | flops 2880 | bytes 11520
  27.5 25.4 %all-gather.2 = bf16[4,240,320]{1,2,0:T(8,128)(2,1)S(1)} all-gather(bf16[1,240,320]{1,2,0:T(8,128)(2,1)} %bitcast.281), channel_id=1, replica_groups=mesh['ctx'=8,'fsdp'=4] {'fsdp'}, dimensions={0}, use_global_device_ids=true | all-gather | bytes 768000 | tf_op jit(solution)/shard_map/all_gather | solution.py:167
  57.6 20.1 %all-gather = bf16[4,240,320]{1,2,0:T(8,128)(2,1)S(1)} all-gather(bf16[1,240,320]{1,2,0:T(8,128)(2,1)S(1)} %bitcast.282), channel_id=1, replica_groups=mesh['ctx'=8,'fsdp'=4] {'fsdp'}, dimensions={0}, use_global_device_ids=true | all-gather | bytes 768000 | tf_op jit(solution)/shard_map/all_gather | solution.py:168
  78.8 1.1 convolution_convert_fusion.8
  83.2 9.3 all-gather.1
  92.6 1.5 or_and_fusion
  94.1 3.8 copy.41
  98.0 2.4 fusion.69
  100.7 14.2 %fusion.2 = (f32[256,5,3]{0,2,1:T(4,128)S(1)}, f32[5,2048,256,3]{2,1,3,0:T(8,128)}) fusion(pred[256,2048]{0,1:T(8,128)(4,1)S(1)} %or_and_fusion, bf16[2048,5,64,1]{0,2,3,1:T(8,128)(2,1)} %bitcast.263, bf16[256,5,3,64]{0,3,2,1:T(8,128)(2,1)S(1)} %bitcast.265), kind=kOutput, calls=%fused_computation.6 | convolution fusion | flops 1030222080 | bytes 33799168 | tf_op jit(solution)/shard_map/qngd,knd->qngk/dot_general | solution.py:61
  115.0 13.9 %fusion.8 = f32[256,5,3]{0,2,1:T(4,128)S(1)} fusion(f32[5,2048,256,3]{2,1,3,0:T(8,128)} %get-tuple-element.65, f32[256,5,3]{0,2,1:T(4,128)S(1)} %broadcast_maximum_fusion, pred[256,2048]{0,1:T(8,128)(4,1)S(1)} %or_and_fusion), kind=kLoop, calls=%fused_computation.12 | loop fusion | flops 31453440 | bytes 32012288 | tf_op jit(solution)/shard_map/reduce_sum | solution.py:67
  128.9 15.8 %fusion.97 = (bf16[256,5,3,64]{0,3,2,1:T(8,128)(2,1)S(1)}, f32[256,5,3,64]{0,3,2,1:T(8,128)}) fusion(f32[256,5,3]{0,2,1:T(4,128)S(1)} %fusion.8, bf16[2048,5,64,1]{0,2,3,1:T(8,128)(2,1)} %bitcast.292, f32[5,2048,256,3]{2,1,3,0:T(8,128)} %get-tuple-element.65, f32[256,5,3]{0,2,1:T(4,128)S(1)} %broadcast_maximum_fusion, pred[256,2048]{0,1:T(8,128)(4,1)S(1)} %or_and_fusion), kind=kOutput, calls=%fused_computation.148 | convolution fusion | flops 1038581760 | bytes 34797568 | tf_op jit(solution)/shard_map/qngk,knd->qngd/dot_general | solution.py:69
  144.7 26.7 %all-gather.17.cloned.1.call-done = bf16[960,960]{1,0:T(8,128)(2,1)} async-done(((bf16[240,960]{1,0:T(8,128)(2,1)}), bf16[960,960]{1,0:T(8,128)(2,1)}) %all-gather.17.cloned.1.call-update) | async-done | bytes 1843216 | tf_op jit(solution)/shard_map/all_gather | solution.py:169
  171.4 2.5 multiply_reduce_fusion.3
  175.3 89.0 %all-gather.19.cloned.1.call-done = bf16[2560,960]{0,1:T(8,128)(2,1)} async-done(((bf16[640,960]{0,1:T(8,128)(2,1)}), bf16[2560,960]{0,1:T(8,128)(2,1)}) %all-gather.19.cloned.1.call-update) | async-done | bytes 4915216 | tf_op jit(solution)/shard_map/all_gather | solution.py:216
  264.3 5.4 fusion.98
  269.8 87.1 %all-gather.21.cloned.1.call-done = bf16[2560,960]{0,1:T(8,128)(2,1)} async-done(((bf16[640,960]{0,1:T(8,128)(2,1)}), bf16[2560,960]{0,1:T(8,128)(2,1)}) %all-gather.21.cloned.1.call-update) | async-done | bytes 4915216 | tf_op jit(solution)/shard_map/all_gather | solution.py:217
  356.8 7.0 multiply_convert_fusion.2
  363.8 85.7 %all-gather.23.cloned.1.call-done = bf16[2560,960]{0,1:T(8,128)(2,1)} async-done(((bf16[640,960]{0,1:T(8,128)(2,1)}), bf16[2560,960]{0,1:T(8,128)(2,1)}) %all-gather.23.cloned.1.call-update) | async-done | bytes 4915216 | tf_op jit(solution)/shard_map/all_gather | solution.py:218
  449.5 5.4 fusion.62
  454.9 5.0 multiply_convert_fusion
  460.0 1.5 fusion.99
  461.5 2.3 multiply_reduce_fusion
  468.1 15.2 %fusion.19 = bf16[5,64,2048]{2,1,0:T(8,128)(2,1)} fusion(bf16[256,5,3,64]{0,3,2,1:T(8,128)(2,1)} %bitcast.279, f32[5,2048,256,3]{2,1,3,0:T(8,128)} %get-tuple-element.65, f32[256,5,3]{0,2,1:T(4,128)} %log_add_fusion, pred[256,2048]{0,1:T(8,128)(4,1)S(1)} %or_and_fusion), kind=kOutput, calls=%fused_computation.23 | convolution fusion | flops 1038745600 | bytes 33799168 | tf_op jit(solution)/shard_map/qngk,qngd->knd/dot_general | solution.py:97
  483.4 21.7 %fusion.1 = bf16[256,5,3,2048]{0,3,2,1:T(8,128)(2,1)} fusion(f32[5,2048,256,3]{2,1,3,0:T(8,128)} %get-tuple-element.65, bf16[2048,5,64,1]{0,2,3,1:T(8,128)(2,1)} %bitcast.293, bf16[256,5,3,64]{0,3,2,1:T(8,128)(2,1)} %bitcast.280, f32[256,5,3]{0,2,1:T(4,128)} %multiply_reduce_fusion.1, f32[256,5,3]{0,2,1:T(4,128)} %log_add_fusion, ...), kind=kOutput, calls=%fused_computation.2 | convolution fusion | flops 1053818880 | bytes 49543168 | tf_op jit(solution)/shard_map/qngd,knd->qngk/dot_general | solution.py:86
  505.1 11.5 %fusion.23 = bf16[5,64,2048]{2,1,0:T(8,128)(2,1)} fusion(bf16[256,5,3,64]{0,3,2,1:T(8,128)(2,1)S(1)} %bitcast.266, bf16[256,5,3,2048]{0,3,2,1:T(8,128)(2,1)} %fusion.1), kind=kOutput, calls=%fused_computation.25 | convolution fusion | flops 1007943680 | bytes 17530880 | tf_op jit(solution)/shard_map/qngk,qngd->knd/dot_general | solution.py:94
  516.6 2.4 reduce-scatter.22.cloned.1.call-done
  519.0 2.2 convolution_convert_fusion.5
  521.2 2.2 copy.56
  523.6 36.5 %reduce-scatter.20.cloned.1.call-done = bf16[256,320]{0,1:T(8,128)(2,1)} async-done(((bf16[2048,320]{0,1:T(8,128)(2,1)}), bf16[256,320]{0,1:T(8,128)(2,1)}) %reduce-scatter.20.cloned.1.call-update) | async-done | bytes 163856 | tf_op jit(solution)/shard_map/reduce_scatter | solution.py:268
  563.0 1.3 convolution_convert_fusion.6
  564.3 2.2 copy.54
  566.8 5.1 convolution_convert_fusion
  571.8 7.9 copy.62
  579.8 4.9 convolution_convert_fusion.1
  584.7 7.9 copy.60
  592.7 5.0 convolution_convert_fusion.2
  597.7 7.9 copy.58
  606.8 2.0 convolution_convert_fusion.3
  608.8 8.5 broadcast_multiply_fusion.1
  618.7 2.0 convolution_convert_fusion.4
  620.8 1.7 copy.57
  622.5 1.7 copy.55
  624.2 81.4 %reduce-scatter.36.cloned.1.call-done = bf16[640,960]{1,0:T(8,128)(2,1)} async-done(((bf16[2560,960]{1,0:T(8,128)(2,1)}), bf16[640,960]{1,0:T(8,128)(2,1)}) %reduce-scatter.36.cloned.1.call-update) | async-done | bytes 1228816
  705.6 2.4 copy.63
  708.0 94.2 %reduce-scatter.34.cloned.1.call-done = bf16[640,960]{1,0:T(8,128)(2,1)} async-done(((bf16[2560,960]{1,0:T(8,128)(2,1)}), bf16[640,960]{1,0:T(8,128)(2,1)}) %reduce-scatter.34.cloned.1.call-update) | async-done | bytes 1228816
  802.2 2.4 copy.61
  804.6 94.1 %reduce-scatter.32.cloned.1.call-done = bf16[640,960]{1,0:T(8,128)(2,1)} async-done(((bf16[2560,960]{1,0:T(8,128)(2,1)}), bf16[640,960]{1,0:T(8,128)(2,1)}) %reduce-scatter.32.cloned.1.call-update) | async-done | bytes 1228816
  898.7 2.4 copy.59
  901.1 42.5 %reduce-scatter.26.cloned.1.call-done = bf16[240,960]{1,0:T(8,128)(2,1)} async-done(((bf16[960,960]{1,0:T(8,128)(2,1)}), bf16[240,960]{1,0:T(8,128)(2,1)}) %reduce-scatter.26.cloned.1.call-update) | async-done | bytes 460816 | tf_op jit(solution)/shard_map/reduce_scatter | solution.py:318
  943.6 43.5 %reduce-scatter.24.cloned.1.call-done = bf16[240,960]{1,0:T(8,128)(2,1)} async-done(((bf16[960,960]{1,0:T(8,128)(2,1)}), bf16[240,960]{1,0:T(8,128)(2,1)}) %reduce-scatter.24.cloned.1.call-update) | async-done | bytes 460816 | tf_op jit(solution)/shard_map/reduce_scatter | solution.py:309
  987.7 1.3 fusion.64
  989.1 2.3 fusion.100
  992.5 1.6 fusion.49
  994.1 10.2 all-reduce.8
  1004.5 12.6 %all-reduce.6 = (bf16[240]{0:T(256)(128)(2,1)S(1)}, bf16[240]{0:T(256)(128)(2,1)S(1)}, bf16[240]{0:T(256)(128)(2,1)S(1)}) all-reduce(bf16[240]{0:T(256)(128)(2,1)S(1)} %dynamic-slice.4, bf16[240]{0:T(256)(128)(2,1)S(1)} %dynamic-slice.6, bf16[240]{0:T(256)(128)(2,1)S(1)} %dynamic-slice.8), channel_id=1, replica_groups=mesh['ctx'=8,'fsdp'=4] {'ctx'}, use_global_device_ids=true, to_apply=%region_27.28 | all-reduce | flops 720 | bytes 2880 | tf_op jit(solution)/shard_map/psum | solution.py:347
  1018.9 3.0 fusion.74
  1021.9 59.8 %all-reduce.12.cloned.1.call-done = (bf16[240,960]{1,0:T(8,128)(2,1)}, bf16[240,320]{0,1:T(8,128)(2,1)}, bf16[240,320]{0,1:T(8,128)(2,1)}, bf16[240,960]{1,0:T(8...) async-done(((bf16[240,960]{1,0:T(8,128)(2,1)}, bf16[240,320]{0,1:T(8,128)(2,1)}, bf16[240,320]{0,1:T(8,128)(2,1)}, ...) | async-done | bytes 4915216 | tf_op jit(solution)/shard_map/psum | solution.py:343
  1081.7 1.8 convert_element_type.273
  1083.5 1.7 convert_element_type.275
  1085.2 2.1 convert_element_type.271
  1088.3 1.6 convert_element_type.279
  1089.9 1.6 convert_element_type.281
  1091.7 1.6 convert_element_type.283
  (213 shorter events, 28.5 us)
Async XLA Ops:
  7.2 47.7 %copy-start = (bf16[1,256,960]{1,2,0:T(8,128)(2,1)S(1)}, bf16[1,256,960]{1,2,0:T(8,128)(2,1)}, u32[]{:S(2)}) copy-start(bf16[1,256,960]{1,2,0:T(8,128)(2,1)} %param.15) | copy-start | bytes 1474564
  7.2 86.9 %all-gather.15.cloned.1.call-start = ((), (), s32[]{:S(2)}) async-start(), calls=%async_computation.11 | async-start | bytes 2457600 | tf_op jit(solution)/shard_map/all_gather | solution.py:166
  7.9 92.8 %all-gather.13.cloned.1.call-start = ((), (), s32[]{:S(2)}) async-start(), calls=%async_computation.10 | async-start | bytes 1474560 | tf_op jit(solution)/shard_map/all_gather | solution.py:201
  27.5 29.2 %copy-start.28 = (f32[960]{0:T(1024)}, f32[960]{0:T(1024)S(1)}, u32[]{:S(2)}) copy-start(f32[960]{0:T(1024)S(1)} %convert_element_type.230) | copy-start | bytes 11524
  53.4 4.1 copy-start.27
  54.0 24.2 %copy-start.5 = (bf16[960,320]{0,1:T(8,128)(2,1)}, bf16[960,320]{0,1:T(8,128)(2,1)S(1)}, u32[]{:S(2)}) copy-start(bf16[960,320]{0,1:T(8,128)(2,1)S(1)} %reshape.343) | copy-start | bytes 1843204
  54.9 22.8 %copy-start.19 = (f32[256,64]{0,1:T(8,128)}, f32[256,64]{0,1:T(8,128)S(1)}, u32[]{:S(2)}) copy-start(f32[256,64]{0,1:T(8,128)S(1)} %get-tuple-element.78) | copy-start | bytes 196612
  56.3 41.7 %copy-start.34 = (f32[256]{0:T(256)}, f32[256]{0:T(256)S(1)}, u32[]{:S(2)}) copy-start(f32[256]{0:T(256)S(1)} %get-tuple-element.58) | copy-start | bytes 3076
  57.5 71.4 %all-gather.11.cloned.1.call-start = ((), (), s32[]{:S(2)}) async-start(), calls=%async_computation.9 | async-start | bytes 1474560 | tf_op jit(solution)/shard_map/all_gather | solution.py:202
  78.8 3.7 copy-start.7
  78.8 4.4 copy-start.53
  78.8 4.4 copy-start.33
  80.0 91.5 %all-gather.17.cloned.1.call-start = ((), (), s32[]{:S(2)}) async-start(), calls=%async_computation.12 | async-start | bytes 2457600 | tf_op jit(solution)/shard_map/all_gather | solution.py:169
  80.5 183.8 %all-gather.19.cloned.1.call-start = ((), (), s32[]{:S(2)}) async-start(), calls=%async_computation.13 | async-start | bytes 6144000 | tf_op jit(solution)/shard_map/all_gather | solution.py:216
  81.1 275.7 %all-gather.21.cloned.1.call-start = ((), (), s32[]{:S(2)}) async-start(), calls=%async_computation.14 | async-start | bytes 6144000 | tf_op jit(solution)/shard_map/all_gather | solution.py:217
  81.7 367.7 %all-gather.23.cloned.1.call-start = ((), (), s32[]{:S(2)}) async-start(), calls=%async_computation.15 | async-start | bytes 6144000 | tf_op jit(solution)/shard_map/all_gather | solution.py:218
  82.5 436.6 %reduce-scatter.22.cloned.1.call-start = ((), (), s32[]{:S(2)}) async-start(), calls=%async_computation.17 | async-start | bytes 1474560 | tf_op jit(solution)/shard_map/reduce_scatter | solution.py:271
  83.2 9.4 copy-start.43
  83.2 366.2 %copy-start.30 = (f32[256]{0:T(256)}, f32[256]{0:T(256)S(1)}, u32[]{:S(2)}) copy-start(f32[256]{0:T(256)S(1)} %get-tuple-element.37) | copy-start | bytes 3076
  98.0 2.5 copy-start.20
  144.7 30.4 %copy-start.21 = (bf16[256,5,3,64]{0,3,2,1:T(8,128)(2,1)}, bf16[256,5,3,64]{0,3,2,1:T(8,128)(2,1)S(1)}, u32[]{:S(2)}) copy-start(bf16[256,5,3,64]{0,3,2,1:T(8,128)(2,1)S(1)} %get-tuple-element.66) | copy-start | bytes 1474564
  174.5 89.9 %copy-start.36 = (f32[256]{0:T(256)}, f32[256]{0:T(256)S(1)}, u32[]{:S(2)}) copy-start(f32[256]{0:T(256)S(1)} %get-tuple-element.60) | copy-start | bytes 3076
  269.7 179.7 %copy-start.1 = (bf16[1,256,960]{1,2,0:T(8,128)(2,1)S(1)}, bf16[1,256,960]{1,2,0:T(8,128)(2,1)}, u32[]{:S(2)}) copy-start(bf16[1,256,960]{1,2,0:T(8,128)(2,1)} %param.26) | copy-start | bytes 1474564
  449.4 5.4 copy-start.45
  449.4 5.4 copy-start.9
  449.4 5.4 copy-start.51
  449.5 10.5 slice-start
  449.5 12.0 %slice-start.2 = ((s8[4915200]{0:T(1024)(128)(4,1)}), s8[4194304]{0:T(1024)(128)(4,1)S(1)}, s32[]{:S(2)}) async-start(s8[4915200]{0:T(1024)(128)(4,1)} %bitcast.290), calls=%async_computation.28 | async-start | bytes 8388608
  454.8 6.6 copy-start.47
  454.9 5.1 slice-start.1
  454.9 6.6 slice-start.3
  461.5 2.9 copy-start.31
  461.5 2.9 copy-start.39
  463.8 2.6 copy-start.3
  463.8 1.9 copy-start.52
  465.7 1.6 copy-start.18
  483.3 76.8 %reduce-scatter.20.cloned.1.call-start = ((), (), s32[]{:S(2)}) async-start(), calls=%async_computation.16 | async-start | bytes 1474560 | tf_op jit(solution)/shard_map/reduce_scatter | solution.py:268
  505.1 14.0 %copy-start.35 = (f32[256]{0:T(256)S(1)}, f32[256]{0:T(256)}, u32[]{:S(2)}) copy-start(f32[256]{0:T(256)} %copy-done.34) | copy-start | bytes 3076
  516.6 45.4 %copy-start.17 = (f32[256,64]{0,1:T(8,128)S(1)}, f32[256,64]{0,1:T(8,128)}, u32[]{:S(2)}) copy-start(f32[256,64]{0,1:T(8,128)} %get-tuple-element.79) | copy-start | bytes 196612
  516.6 104.2 %reduce-scatter.30.cloned.1.call-start = ((), (), s32[]{:S(2)}) async-start(), calls=%async_computation.21 | async-start | bytes 921600
  523.5 99.0 %reduce-scatter.28.cloned.1.call-start = ((), (), s32[]{:S(2)}) async-start(), calls=%async_computation.20 | async-start | bytes 921600
  561.9 4.8 copy-start.32
  566.5 139.0 %reduce-scatter.36.cloned.1.call-start = ((), (), s32[]{:S(2)}) async-start(), calls=%async_computation.24 | async-start | bytes 6553600
  579.7 222.5 %reduce-scatter.34.cloned.1.call-start = ((), (), s32[]{:S(2)}) async-start(), calls=%async_computation.23 | async-start | bytes 6553600
  592.6 306.0 %reduce-scatter.32.cloned.1.call-start = ((), (), s32[]{:S(2)}) async-start(), calls=%async_computation.22 | async-start | bytes 6553600
  605.6 338.0 %reduce-scatter.26.cloned.1.call-start = ((), (), s32[]{:S(2)}) async-start(), calls=%async_computation.19 | async-start | bytes 2457600 | tf_op jit(solution)/shard_map/reduce_scatter | solution.py:318
  608.8 378.3 %reduce-scatter.24.cloned.1.call-start = ((), (), s32[]{:S(2)}) async-start(), calls=%async_computation.18 | async-start | bytes 2457600 | tf_op jit(solution)/shard_map/reduce_scatter | solution.py:309
  620.7 461.0 %all-reduce.12.cloned.1.call-start = ((), (), s32[]{:S(2)}) async-start(), calls=%async_computation.25 | async-start | bytes 9994240 | tf_op jit(solution)/shard_map/psum | solution.py:343
  987.0 2.0 copy-start.44
  989.1 2.3 copy-start.6
  991.4 2.7 copy-start.49
  991.4 2.7 copy-start.50
  991.4 27.4 %copy-start.2 = (bf16[1,256,960]{1,2,0:T(8,128)(2,1)S(1)}, bf16[1,256,960]{1,2,0:T(8,128)(2,1)}, u32[]{:S(2)}) copy-start(bf16[1,256,960]{1,2,0:T(8,128)(2,1)} %param.26) | copy-start | bytes 1474564
  991.4 27.4 %copy-start.4 = (f32[256,960]{0,1:T(8,128)S(1)}, f32[256,960]{0,1:T(8,128)}, u32[]{:S(2)}) copy-start(f32[256,960]{0,1:T(8,128)} %copy-done.3) | copy-start | bytes 2949124
  991.5 27.4 %copy-start.29 = (f32[960]{0:T(1024)S(1)}, f32[960]{0:T(1024)}, u32[]{:S(2)}) copy-start(f32[960]{0:T(1024)} %copy-done.28) | copy-start | bytes 11524
  991.5 27.4 %copy-start.38 = (f32[256]{0:T(256)S(1)}, f32[256]{0:T(256)}, u32[]{:S(2)}) copy-start(f32[256]{0:T(256)} %copy-done.36) | copy-start | bytes 3076
  991.5 27.4 %copy-start.40 = (f32[256]{0:T(256)S(1)}, f32[256]{0:T(256)}, u32[]{:S(2)}) copy-start(f32[256]{0:T(256)} %get-tuple-element.59) | copy-start | bytes 3076
  991.5 27.4 %copy-start.42 = (f32[256]{0:T(256)S(1)}, f32[256]{0:T(256)}, u32[]{:S(2)}) copy-start(f32[256]{0:T(256)} %copy-done.41) | copy-start | bytes 3076
  991.5 27.4 %copy-start.46 = (f32[256]{0:T(256)S(1)}, f32[256]{0:T(256)}, u32[]{:S(2)}) copy-start(f32[256]{0:T(256)} %get-tuple-element.57) | copy-start | bytes 3076
  991.5 27.4 %copy-start.48 = (f32[256]{0:T(256)S(1)}, f32[256]{0:T(256)}, u32[]{:S(2)}) copy-start(f32[256]{0:T(256)} %copy-done.47) | copy-start | bytes 3076
  1081.7 5.5 copy-start.23
  1081.7 6.6 copy-start.16
  1087.3 2.7 copy-start.15
  1089.9 1.8 copy-start.14
  (11 other events, 12.4 us)
Sparse Core Ops, SparseCore 0:
  9.6 64.5 all-gather.14
  76.6 22.6 all-gather.12
  101.8 24.6 all-gather.10
  127.9 43.4 all-gather.16
  172.8 91.4 all-gather.18
  265.8 91.0 all-gather.20
  358.4 91.0 all-gather.22
  483.5 35.5 reduce-scatter.21
  522.9 37.1 reduce-scatter.19
  562.2 23.0 reduce-scatter.29
  588.2 22.2 reduce-scatter.27
  612.7 92.8 reduce-scatter.35
  707.9 94.2 reduce-scatter.33
  804.4 94.2 reduce-scatter.31
  901.4 42.0 reduce-scatter.25
  946.3 40.6 reduce-scatter.23
  991.7 89.9 all-reduce.11
where the time goes:
time: 1110 us; the launch traced here: 1100 us
  waiting for transfers between devices  746 us (67%)
  matrix products  147 us (13%)
  blocking collectives  91.9 us (8%)
  local copies, waits for them, and re-layouts  54 us (5%)
  other arithmetic  42.8 us (4%)
  between operations  17 us (2%)
    unnamed x22, waiting for transfers between devices  273 us
    all_gather x1, waiting for transfers between devices, on_device(): lax.all_gather(w_gate, 'fsdp', axis=0, tiled=True)  89 us
    all_gather x1, waiting for transfers between devices, on_device(): lax.all_gather(w_up, 'fsdp', axis=0, tiled=True)  87.1 us
    all_gather x1, waiting for transfers between devices, on_device(): lax.all_gather(w_down, 'fsdp', axis=0, tiled=True)  85.7 us
    psum x1, waiting for transfers between devices, on_device(): lax.psum(attn_owned[0].astype(jnp.bfloat16), 'ctx').astype(jnp.float32)  59.8 us
    unnamed x138, local copies, waits for them, and re-layouts  48.3 us
    reduce_scatter x1, waiting for transfers between devices, on_device(): lax.psum_scatter(grad_wquery.astype(jnp.bfloat16), 'fsdp', scatter_dimens...  43.5 us
    reduce_scatter x1, waiting for transfers between devices, on_device(): lax.psum_scatter(grad_wout.astype(jnp.bfloat16), 'fsdp', scatter_dimensio...  42.5 us
  transfers between devices with their start and end apart: 17, of which 12 were waited for; matrix products, arithmetic and copies ran while one was open for 18% of the time, Pallas kernels for 0%

commit v1 on v0

v1 whole, which is shorter than its diff:
```python
import jax
import jax.numpy as jnp
from jax import lax
from jax.sharding import PartitionSpec as P

HEADS = 15
KV_HEADS = 5
HEAD = 64


epsilon = 1e-05
negative = -1e30
across_rows = (((0,), (0,)), ((), ()))
across_cols = (((1,), (1,)), ((), ()))


def rope_tables(positions):
    half_dim = HEAD // 2
    frequency = 10000.0 ** (-2.0 * jnp.arange(half_dim, dtype=jnp.float32) / HEAD)
    angles = positions.astype(jnp.float32)[:, None] * frequency[None, :]
    cos_tab = jnp.cos(angles)
    sin_tab = jnp.sin(angles)
    return (jnp.concatenate([cos_tab, cos_tab], -1), jnp.concatenate([sin_tab, sin_tab], -1))


def rotate(values, cos_tab, sin_tab):
    half_dim = values.shape[-1] // 2
    turned = jnp.concatenate([-values[..., half_dim:], values[..., :half_dim]], -1)
    return values * cos_tab[:, None, :] + turned * sin_tab[:, None, :]


def norm_forward(values, gain_vec):
    inv_rms = lax.rsqrt(jnp.mean(values * values, -1, keepdims=True) + epsilon)
    return (values * inv_rms * gain_vec, inv_rms)


def norm_backward(values, inv_rms, gain_vec, grad_normed):
    weighted = gain_vec * grad_normed
    grad_gain = jnp.sum(grad_normed * values * inv_rms, 0)
    cubed = inv_rms * inv_rms * inv_rms
    grad_values = inv_rms * weighted - values * cubed * jnp.mean(
        weighted * values, -1, keepdims=True
    )
    return (grad_values, grad_gain)


def allowed_mask(query_pos, key_tags):
    key_pos = jnp.where(key_tags >= 0, key_tags, -key_tags - 1)
    earlier = key_pos[None, :] <= query_pos[:, None]
    usable = (key_tags[None, :] >= 0) | (key_pos[None, :] == query_pos[:, None])
    return (earlier & usable)[:, None, None, :]


def forward_step(carried, portion, query_heads, query_pos):
    acc_out, running_max, summed = carried
    key_piece, value_piece, key_tags = portion
    piece_rows = key_piece.shape[0]
    key_heads = key_piece.reshape(piece_rows, KV_HEADS, HEAD)
    value_heads = value_piece.reshape(piece_rows, KV_HEADS, HEAD)
    scores = (
        jnp.einsum("qngd,knd->qngk", query_heads, key_heads, preferred_element_type=jnp.float32)
        * 0.125
    )
    allowed = allowed_mask(query_pos, key_tags)
    new_max = jnp.maximum(running_max, jnp.max(jnp.where(allowed, scores, negative), -1))
    weights = jnp.exp(jnp.where(allowed, scores - new_max[..., None], negative))
    summed = jnp.sum(weights, -1)
    weights_low = weights.astype(jnp.bfloat16)
    acc_out = jnp.einsum(
        "qngk,knd->qngd", weights_low, value_heads, preferred_element_type=jnp.float32
    )
    return (acc_out, new_max, summed)


def backward_step(portion, query_heads, query_pos, grad_heads, log_total, row_delta):
    key_piece, value_piece, key_tags = portion
    piece_rows = key_piece.shape[0]
    key_heads = key_piece.reshape(piece_rows, KV_HEADS, HEAD)
    value_heads = value_piece.reshape(piece_rows, KV_HEADS, HEAD)
    scores = (
        jnp.einsum("qngd,knd->qngk", query_heads, key_heads, preferred_element_type=jnp.float32)
        * 0.125
    )
    allowed = allowed_mask(query_pos, key_tags)
    softmax_w = jnp.exp(jnp.where(allowed, scores - log_total[..., None], negative))
    grad_probs = jnp.einsum(
        "qngd,knd->qngk", grad_heads, value_heads, preferred_element_type=jnp.float32
    )
    grad_scores = (softmax_w * (grad_probs - row_delta[..., None])).astype(jnp.bfloat16)
    probs_low = softmax_w.astype(jnp.bfloat16)
    grad_qrot = 0.125 * jnp.einsum(
        "qngk,knd->qngd", grad_scores, key_heads, preferred_element_type=jnp.float32
    )
    key_part = 0.125 * jnp.einsum(
        "qngk,qngd->knd", grad_scores, query_heads, preferred_element_type=jnp.float32
    )
    value_part = jnp.einsum(
        "qngk,qngd->knd", probs_low, grad_heads, preferred_element_type=jnp.float32
    )
    key_part = key_part.reshape(piece_rows, KV_HEADS * HEAD)
    value_part = value_part.reshape(piece_rows, KV_HEADS * HEAD)
    return (grad_qrot, key_part, value_part)


def ffn_both(normed, grad_mixed, gate_rows, up_rows, down_rows):
    gate_proj = lax.dot_general(normed, gate_rows, across_cols, preferred_element_type=jnp.float32)
    up_proj = lax.dot_general(normed, up_rows, across_cols, preferred_element_type=jnp.float32)
    sigma = jax.nn.sigmoid(gate_proj)
    activated = gate_proj * sigma
    inner_act = (activated * up_proj).astype(jnp.bfloat16)
    grad_inner = lax.dot_general(
        grad_mixed, down_rows, across_cols, preferred_element_type=jnp.float32
    )
    grad_gate_act = (grad_inner * up_proj * sigma * (1.0 + gate_proj * (1.0 - sigma))).astype(
        jnp.bfloat16
    )
    grad_up_act = (grad_inner * activated).astype(jnp.bfloat16)
    grad_normed = jnp.dot(grad_gate_act, gate_rows, preferred_element_type=jnp.float32) + jnp.dot(
        grad_up_act, up_rows, preferred_element_type=jnp.float32
    )
    return (inner_act, grad_gate_act, grad_up_act, grad_normed.astype(jnp.bfloat16))


def on_device(
    tokens,
    w_query,
    w_key,
    w_value,
    w_out,
    w_gate,
    w_up,
    w_down,
    gain_attn,
    gain_ffn,
    router,
    cotangent,
    positions,
    lengths,
    chosen,
):
    hidden = tokens[0].astype(jnp.float32)
    row_count, width = hidden.shape
    groups = HEADS // KV_HEADS
    qdim = HEADS * HEAD
    kdim = KV_HEADS * HEAD
    query_pos = positions[0]
    live = query_pos < lengths[0]
    selected = live & (chosen[0] == 1)
    live_mask = live.astype(jnp.float32)[:, None]
    chosen_mask = selected.astype(jnp.float32)[:, None]
    cos_tab, sin_tab = rope_tables(query_pos)
    key_tags = jnp.where(selected, query_pos, -query_pos - 1)
    tags_all = lax.all_gather(key_tags, "ctx", axis=0, tiled=True)
    vectors = lax.all_gather(jnp.stack([gain_attn, gain_ffn, router]), "fsdp", axis=1, tiled=True)
    gain_one = vectors[0].astype(jnp.float32)
    gain_two = vectors[1].astype(jnp.float32)
    router_vec = vectors[2].astype(jnp.float32)
    w_qkv = lax.all_gather(
        jnp.concatenate([w_query, w_key, w_value], 1), "fsdp", axis=0, tiled=True
    )
    w_out_full = lax.all_gather(w_out, "fsdp", axis=0, tiled=True)
    gating = jax.nn.sigmoid(jnp.sum(hidden * router_vec, -1, keepdims=True))
    grad_y = cotangent[0].astype(jnp.float32) * live_mask
    grad_inc = grad_y * chosen_mask * gating
    grad_ffn = grad_inc.astype(jnp.bfloat16)
    grad_ffn_all = lax.all_gather(grad_ffn, "fsdp", axis=0, tiled=True)

    normed_one, inv_one = norm_forward(hidden, gain_one)
    normed_one = normed_one.astype(jnp.bfloat16)
    qkv_raw = jnp.dot(normed_one, w_qkv, preferred_element_type=jnp.float32)
    rotated = rotate(
        qkv_raw[:, : qdim + kdim].reshape(row_count, HEADS + KV_HEADS, HEAD), cos_tab, sin_tab
    ).astype(jnp.bfloat16)
    query_heads = rotated[:, :HEADS].reshape(row_count, KV_HEADS, groups, HEAD)
    key_rot = rotated[:, HEADS:].reshape(row_count, kdim)
    value_proj = qkv_raw[:, qdim + kdim :].astype(jnp.bfloat16)
    kv_all = lax.all_gather(
        jnp.concatenate([key_rot, value_proj], 1), "ctx", axis=0, tiled=True
    )
    portion = (kv_all[:, :kdim], kv_all[:, kdim:], tags_all)
    start_state = (None, jnp.full((row_count, KV_HEADS, groups), negative, jnp.float32), None)
    acc_out, running_max, summed = forward_step(start_state, portion, query_heads, query_pos)
    attended = acc_out / summed[..., None]
    log_total = running_max + jnp.log(summed)
    outcome = attended.reshape(row_count, qdim).astype(jnp.bfloat16)
    branch = jnp.dot(outcome, w_out_full, preferred_element_type=jnp.float32)
    middle = hidden + branch
    normed_two, inv_two = norm_forward(middle, gain_two)
    normed_two = normed_two.astype(jnp.bfloat16)
    normed_all = lax.all_gather(normed_two, "fsdp", axis=0, tiled=True)
    inner_act, grad_gate_act, grad_up_act, grad_normed_part = ffn_both(
        normed_all, grad_ffn_all, w_gate, w_up, w_down
    )
    grad_normed_two = lax.psum_scatter(
        grad_normed_part, "fsdp", scatter_dimension=0, tiled=True
    ).astype(jnp.float32)
    ffn_part = jnp.dot(inner_act, w_down, preferred_element_type=jnp.float32).astype(jnp.bfloat16)
    grad_wgate = lax.dot_general(
        grad_gate_act, normed_all, across_rows, preferred_element_type=jnp.float32
    )
    grad_wup = lax.dot_general(
        grad_up_act, normed_all, across_rows, preferred_element_type=jnp.float32
    )
    grad_wdown = lax.dot_general(
        inner_act, grad_ffn_all, across_rows, preferred_element_type=jnp.float32
    )
    low = jnp.bfloat16
    totals = tuple(
        lax.psum(grad.astype(low), "ctx") for grad in (grad_wgate, grad_wup, grad_wdown)
    )
    grad_middle, grad_gain_two = norm_backward(middle, inv_two, gain_two, grad_normed_two)
    ffn_part, grad_middle = lax.optimization_barrier((ffn_part, grad_middle))
    ffn_out = lax.psum_scatter(ffn_part, "fsdp", scatter_dimension=0, tiled=True).astype(
        jnp.float32
    )
    grad_branch = (grad_inc + grad_middle).astype(jnp.bfloat16)
    grad_attended = lax.dot_general(
        grad_branch, w_out_full, across_cols, preferred_element_type=jnp.float32
    ).astype(jnp.bfloat16)
    grad_wout = lax.dot_general(
        outcome, grad_branch, across_rows, preferred_element_type=jnp.float32
    )
    grad_heads = grad_attended.reshape(row_count, KV_HEADS, groups, HEAD)
    row_delta = jnp.sum(grad_heads.astype(jnp.float32) * attended, -1)
    grad_qrot, grad_keys_all, grad_values_all = backward_step(
        portion, query_heads, query_pos, grad_heads, log_total, row_delta
    )
    grad_kv = lax.psum_scatter(
        jnp.concatenate([grad_keys_all, grad_values_all], 1).astype(jnp.bfloat16),
        "ctx",
        scatter_dimension=0,
        tiled=True,
    ).astype(jnp.float32)
    increment = branch + ffn_out
    block_out = live_mask * (hidden + chosen_mask * gating * increment)
    grad_logit = (
        jnp.sum(grad_y * chosen_mask * increment, -1, keepdims=True) * gating * (1.0 - gating)
    )
    grad_router = jnp.sum(hidden * grad_logit, 0)
    grad_rotated = jnp.concatenate(
        [
            grad_qrot.reshape(row_count, HEADS, HEAD),
            grad_kv[:, :kdim].reshape(row_count, KV_HEADS, HEAD),
        ],
        1,
    )
    grad_qkv = jnp.concatenate(
        [
            rotate(grad_rotated, cos_tab, -sin_tab).reshape(row_count, qdim + kdim),
            grad_kv[:, kdim:],
        ],
        1,
    ).astype(jnp.bfloat16)
    grad_normed_one = lax.dot_general(
        grad_qkv, w_qkv, across_cols, preferred_element_type=jnp.float32
    )
    grad_wqkv = lax.dot_general(
        normed_one, grad_qkv, across_rows, preferred_element_type=jnp.float32
    )
    grad_hidden_one, grad_gain_one = norm_backward(hidden, inv_one, gain_one, grad_normed_one)
    grad_tokens = (grad_y + grad_logit * router_vec + grad_middle + grad_hidden_one).astype(
        jnp.bfloat16
    )
    own_out = lax.psum_scatter(grad_wout.astype(low), "fsdp", scatter_dimension=0, tiled=True)
    own_qkv = lax.psum_scatter(grad_wqkv.astype(low), "fsdp", scatter_dimension=0, tiled=True)
    own_out, own_qkv, *totals = lax.optimization_barrier((own_out, own_qkv, *totals))
    total_gate, total_up, total_down = (total.astype(jnp.float32) for total in totals)
    total_out = lax.psum(own_out, "ctx").astype(jnp.float32)
    total_qkv = lax.psum(own_qkv, "ctx").astype(jnp.float32)
    small = lax.psum(
        jnp.stack([grad_gain_one, grad_gain_two, grad_router]), ("ctx", "fsdp")
    )
    mine = lax.dynamic_slice_in_dim(
        small, lax.axis_index("fsdp") * gain_attn.shape[0], gain_attn.shape[0], 1
    )
    return (
        block_out.astype(jnp.bfloat16)[None],
        grad_tokens[None],
        total_qkv[:, :qdim],
        total_qkv[:, qdim : qdim + kdim],
        total_qkv[:, qdim + kdim :],
        total_out,
        total_gate,
        total_up,
        total_down,
        mine[0],
        mine[1],
        mine[2],
    )


def solution(mesh):
    in_specs = (
        P("fsdp", "ctx", None),
        P("fsdp", None),
        P("fsdp", None),
        P("fsdp", None),
        P("fsdp", None),
        P("fsdp", None),
        P("fsdp", None),
        P("fsdp", None),
        P("fsdp"),
        P("fsdp"),
        P("fsdp"),
        P("fsdp", "ctx", None),
        P("fsdp", "ctx"),
        P("fsdp"),
        P("fsdp", "ctx"),
    )
    out_specs = (
        P("fsdp", "ctx", None),
        P("fsdp", "ctx", None),
        P("fsdp", None),
        P("fsdp", None),
        P("fsdp", None),
        P("fsdp", None),
        P("fsdp", None),
        P("fsdp", None),
        P("fsdp", None),
        P("fsdp"),
        P("fsdp"),
        P("fsdp"),
    )
    return jax.shard_map(
        on_device, mesh=mesh, in_specs=in_specs, out_specs=out_specs, check_vma=False
    )
```

time: 1110 us -> 707 us (0.64)
  waiting for transfers between devices: 746 us -> 436 us
  local copies, waits for them, and re-layouts: 54 us -> 14.8 us
  blocking collectives: 91.9 us -> 63.2 us
  matrix products: 147 us -> 135 us
    unnamed x22 -> x12, waiting for transfers between devices: 273 us -> 0.86 us
    all_gather x7 -> x5, waiting for transfers between devices: 289 us -> 147 us  [the longest x1 52.2 us: on_device(): lax.all_gather(jnp.concatenate([w_query, w_key, w_value], 1), 'fsdp', axi...]
    reduce_scatter x4 -> x5, waiting for transfers between devices: 125 us -> 203 us  [the longest x1 62.8 us: on_device(): lax.psum_scatter(grad_wqkv.astype(low), 'fsdp', scatter_dimension=0, tile...]
    unnamed x138 -> x81, local copies, waits for them, and re-layouts: 48.3 us -> 6.73 us
    all_gather x3 -> x2, blocking collectives: 54.9 us -> 23.1 us  [the longest x1 13.6 us: on_device(): lax.all_gather(jnp.stack([gain_attn, gain_ffn, router]), 'fsdp', axis=1,...]
    psum x1, blocking collectives: 12.6 us -> 40.1 us  [on_device(): lax.psum(jnp.stack([grad_gain_one, grad_gain_two, grad_router]), ('ctx',...]
    psum x1 -> x2, waiting for transfers between devices: 59.8 us -> 85.1 us  [the longest x1 53.9 us: on_device(): total_qkv = lax.psum(own_qkv, 'ctx').astype(jnp.float32)]
    unnamed x2 -> x0, blocking collectives: 24.4 us -> none
  transfers between devices with their start and end apart: 17 -> 12, of which waited for: 12 -> 12; matrix products, arithmetic and copies ran while one was open for 18% -> 14% of each run, Pallas kernels for 0% -> 0%
where the time goes in v1:
time: 707 us; the launch traced here: 703 us
  waiting for transfers between devices  436 us (62%)
  matrix products  135 us (19%)
  blocking collectives  63.2 us (9%)
  other arithmetic  37.1 us (5%)
  between operations  15.8 us (2%)
  local copies, waits for them, and re-layouts  14.8 us (2%)
    reduce_scatter x1, waiting for transfers between devices, on_device(): lax.psum_scatter(grad_wqkv.astype(low), 'fsdp', scatter_dimension=0, tile...  62.8 us
    psum x1, waiting for transfers between devices, on_device(): total_qkv = lax.psum(own_qkv, 'ctx').astype(jnp.float32)  53.9 us
    all_gather x1, waiting for transfers between devices, on_device(): lax.all_gather(jnp.concatenate([w_query, w_key, w_value], 1), 'fsdp', axi...  52.2 us
    reduce_scatter x1, waiting for transfers between devices, on_device(): lax.psum_scatter(grad_wout.astype(low), 'fsdp', scatter_dimension=0, tile...  44.4 us
    reduce_scatter x1, waiting for transfers between devices, on_device(): lax.psum_scatter(ffn_part, 'fsdp', scatter_dimension=0, tiled=True)  41.4 us
    all_gather x1, waiting for transfers between devices, on_device(): normed_all = lax.all_gather(normed_two, 'fsdp', axis=0, tiled=True)  40.8 us
    psum x1, blocking collectives, on_device(): lax.psum(jnp.stack([grad_gain_one, grad_gain_two, grad_router]), ('ctx',...  40.1 us
    all_gather x1, waiting for transfers between devices, on_device(): grad_ffn_all = lax.all_gather(grad_ffn, 'fsdp', axis=0, tiled=True)  35.6 us
  transfers between devices with their start and end apart: 12, of which 12 were waited for; matrix products, arithmetic and copies ran while one was open for 14% of the time, Pallas kernels for 0%

profile of v1, /device:TPU:0, one launch (start us, length us, event | category | flops | bytes accessed | tf_op | source)
XLA Modules:
  0.0 703.0 jit_solution(11269909907838957307)
XLA Ops:
  7.3 1.2 copy.53
  8.5 1.1 copy.54
  9.6 2.0 concatenate.33
  11.7 13.6 %all-gather = bf16[4,240,3]{1,2,0:T(4,128)(2,1)S(1)} all-gather(bf16[1,240,3]{1,2,0:T(4,128)(2,1)S(1)} %maximum_bitcast_fusion), channel_id=1, replica_groups=mesh['ctx'=8,'fsdp'=4] {'fsdp'}, dimensions={0}, use_global_device_ids=true | all-gather | bytes 7200 | tf_op jit(solution)/shard_map/all_gather | solution.py:154
  25.7 0.6 fusion.74
  26.5 52.2 %all-gather.8.cloned.1.call-done = bf16[960,1600]{1,0:T(8,128)(2,1)} async-done(((bf16[240,1600]{1,0:T(8,128)(2,1)}), bf16[960,1600]{1,0:T(8,128)(2,1)}) %all-gather.8.cloned.1.call-update) | async-done | bytes 3072016 | tf_op jit(solution)/shard_map/all_gather | solution.py:158
  78.7 3.5 fusion.72
  82.8 0.7 pad_maximum_fusion.5
  83.6 0.7 all-gather.12.cloned.1.call-update
  85.1 9.4 %all-gather.1 = s32[8,1,256]{2,1,0:T(1,128)S(1)} all-gather(s32[1,1,256]{2,1,0:T(1,128)S(1)} %bitcast.217), channel_id=1, replica_groups=mesh['ctx'=8,'fsdp'=4] {'ctx'}, dimensions={0}, use_global_device_ids=true | all-gather | bytes 9216 | tf_op jit(solution)/shard_map/all_gather | solution.py:153
  94.5 1.5 or_and_fusion
  96.1 16.7 %all-gather.10.cloned.1.call-done = bf16[2048,640]{0,1:T(8,128)(2,1)} async-done(((bf16[256,640]{0,1:T(8,128)(2,1)}), bf16[2048,640]{0,1:T(8,128)(2,1)}) %all-gather.10.cloned.1.call-update) | async-done | bytes 2621456 | tf_op jit(solution)/shard_map/all_gather | solution.py:177
  112.8 1.9 fusion.85
  114.7 13.0 %fusion.2 = (f32[256,5,3]{0,2,1:T(4,128)S(1)}, f32[5,2048,256,3]{2,1,3,0:T(8,128)}) fusion(pred[256,2048]{0,1:T(8,128)(4,1)S(1)} %or_and_fusion, bf16[2048,5,64,1]{0,2,3,1:T(8,128)(2,1)S(1)} %bitcast.177, bf16[256,5,3,64]{0,3,2,1:T(8,128)(2,1)S(1)} %bitcast.184), kind=kOutput, calls=%fused_computation.6 | convolution fusion | flops 1030222080 | bytes 33799168 | tf_op jit(solution)/shard_map/qngd,knd->qngk/dot_general | solution.py:61
  127.8 13.9 %fusion.8 = f32[256,5,3]{0,2,1:T(4,128)S(1)} fusion(f32[5,2048,256,3]{2,1,3,0:T(8,128)} %get-tuple-element.122, f32[256,5,3]{0,2,1:T(4,128)S(1)} %broadcast_maximum_fusion, pred[256,2048]{0,1:T(8,128)(4,1)S(1)} %or_and_fusion), kind=kLoop, calls=%fused_computation.12 | loop fusion | flops 31453440 | bytes 32012288 | tf_op jit(solution)/shard_map/reduce_sum | solution.py:67
  141.6 14.9 %fusion.89 = (bf16[256,5,3,64]{0,3,2,1:T(8,128)(2,1)}, f32[256,5,3,64]{0,3,2,1:T(8,128)}) fusion(f32[256,5,3]{0,2,1:T(4,128)S(1)} %fusion.8, bf16[2048,5,64,1]{0,2,3,1:T(8,128)(2,1)S(1)} %bitcast.188, f32[5,2048,256,3]{2,1,3,0:T(8,128)} %get-tuple-element.122, f32[256,5,3]{0,2,1:T(4,128)S(1)} %broadcast_maximum_fusion, pred[256,2048]{0,1:T(8,128)(4,1)S(1)} %or_and_fusion), kind=kOutput, calls=%fused_computation.150 | convolution fusion | flops 1038581760 | bytes 34797568 | tf_op jit(solution)/shard_map/qngk,knd->qngd/dot_general | solution.py:69
  156.6 1.3 all-gather.12.cloned.1.call-done
  157.9 2.7 fusion.39
  160.6 1.0 multiply_convert_fusion.3
  161.7 2.0 fusion.58
  163.9 40.8 %all-gather.14.cloned.1.call-done = bf16[1024,960]{0,1:T(8,128)(2,1)} async-done(((bf16[256,960]{0,1:T(8,128)(2,1)}), bf16[1024,960]{0,1:T(8,128)(2,1)}) %all-gather.14.cloned.1.call-update) | async-done | bytes 1966096 | tf_op jit(solution)/shard_map/all_gather | solution.py:190
  204.8 5.4 fusion.91
  210.1 3.3 fusion.90
  213.5 35.6 %all-gather.16.cloned.1.call-done = bf16[1024,960]{0,1:T(8,128)(2,1)} async-done(((bf16[256,960]{0,1:T(8,128)(2,1)}), bf16[1024,960]{0,1:T(8,128)(2,1)}) %all-gather.16.cloned.1.call-update) | async-done | bytes 1966096 | tf_op jit(solution)/shard_map/all_gather | solution.py:166
  249.1 6.9 multiply_convert_fusion
  256.0 1.7 fusion.92
  258.2 3.0 add_convert_fusion
  261.3 4.3 convolution_convert_fusion.2
  265.6 35.6 %reduce-scatter.6.cloned.1.call-done = bf16[256,960]{0,1:T(8,128)(2,1)} async-done(((bf16[1024,960]{0,1:T(8,128)(2,1)}), bf16[256,960]{0,1:T(8,128)(2,1)}) %reduce-scatter.6.cloned.1.call-update) | async-done | bytes 491536 | tf_op jit(solution)/shard_map/reduce_scatter | solution.py:194
  301.2 1.6 fusion.38
  303.4 41.4 %reduce-scatter.8.cloned.1.call-done = bf16[256,960]{0,1:T(8,128)(2,1)} async-done(((bf16[1024,960]{0,1:T(8,128)(2,1)}), bf16[256,960]{0,1:T(8,128)(2,1)}) %reduce-scatter.8.cloned.1.call-update) | async-done | bytes 491536 | tf_op jit(solution)/shard_map/reduce_scatter | solution.py:213
  344.8 2.5 fusion.60
  347.4 0.7 convolution_convert_fusion.6
  348.1 0.6 copy-done.17
  348.9 15.0 %fusion.19 = bf16[5,64,2048]{2,1,0:T(8,128)(2,1)} fusion(bf16[256,5,3,64]{0,3,2,1:T(8,128)(2,1)S(1)} %bitcast.196, f32[5,2048,256,3]{2,1,3,0:T(8,128)} %get-tuple-element.122, f32[256,5,3]{0,2,1:T(4,128)S(1)} %log_add_fusion, pred[256,2048]{0,1:T(8,128)(4,1)S(1)} %or_and_fusion), kind=kOutput, calls=%fused_computation.31 | convolution fusion | flops 1038745600 | bytes 33799168 | tf_op jit(solution)/shard_map/qngk,qngd->knd/dot_general | solution.py:97
  363.9 21.4 %fusion.1 = bf16[256,5,3,2048]{0,3,2,1:T(8,128)(2,1)} fusion(f32[5,2048,256,3]{2,1,3,0:T(8,128)} %get-tuple-element.122, bf16[2048,5,64,1]{0,2,3,1:T(8,128)(2,1)} %bitcast.189, bf16[256,5,3,64]{0,3,2,1:T(8,128)(2,1)S(1)} %bitcast.197, f32[256,5,3]{0,2,1:T(4,128)S(1)} %multiply_reduce_fusion, f32[256,5,3]{0,2,1:T(4,128)S(1)} %log_add_fusion, ...), kind=kOutput, calls=%fused_computation.2 | convolution fusion | flops 1053818880 | bytes 49543168 | tf_op jit(solution)/shard_map/qngd,knd->qngk/dot_general | solution.py:86
  385.3 10.3 %fusion.23 = bf16[5,64,2048]{2,1,0:T(8,128)(2,1)S(1)} fusion(bf16[256,5,3,64]{0,3,2,1:T(8,128)(2,1)S(1)} %bitcast.185, bf16[256,5,3,2048]{0,3,2,1:T(8,128)(2,1)} %fusion.1), kind=kOutput, calls=%fused_computation.33 | convolution fusion | flops 1007943680 | bytes 17530880 | tf_op jit(solution)/shard_map/qngk,qngd->knd/dot_general | solution.py:94
  395.6 3.1 pad_maximum_fusion
  399.0 4.8 convolution_convert_fusion.3
  403.8 2.7 convolution_convert_fusion.4
  406.6 2.7 convolution_convert_fusion.5
  409.4 1.0 copy-done.12
  410.4 3.0 convolution_convert_fusion.1
  413.5 9.0 %convolution_multiply_fusion = f32[5,64,256,3]{2,1,3,0:T(8,128)} fusion(bf16[2048,5,64,1]{0,2,3,1:T(8,128)(2,1)S(1)} %bitcast.178, bf16[256,5,3,2048]{0,3,2,1:T(8,128)(2,1)} %fusion.1), kind=kOutput, calls=%fused_computation.51 | convolution fusion | flops 1006878720 | bytes 18022400 | tf_op jit(solution)/shard_map/qngk,knd->qngd/dot_general | solution.py:91
  422.5 19.0 %reduce-scatter.10.cloned.1.call-done = bf16[256,640]{0,1:T(8,128)(2,1)} async-done(((bf16[2048,640]{0,1:T(8,128)(2,1)}), bf16[256,640]{0,1:T(8,128)(2,1)}) %reduce-scatter.10.cloned.1.call-update) | async-done | bytes 327696 | tf_op jit(solution)/shard_map/reduce_scatter | solution.py:228
  441.5 1.0 fusion.87
  442.6 1.3 fusion.66
  444.3 2.8 convolution_convert_fusion
  447.1 4.0 fusion.51
  451.1 40.1 %psum.47 = f32[3,960]{1,0:T(4,128)S(1)} all-reduce(f32[3,960]{1,0:T(4,128)S(1)} %pad_maximum_fusion.8), channel_id=1, replica_groups=mesh['ctx'=8,'fsdp'=4] {'ctx','fsdp'}, use_global_device_ids=true, to_apply=%region_22.23 | all-reduce | flops 2880 | bytes 23040 | tf_op jit(solution)/shard_map/psum | solution.py:270
  491.2 31.2 %all-reduce.7.cloned.1.call-done = (bf16[640,960]{0,1:T(8,128)(2,1)}, bf16[640,960]{0,1:T(8,128)(2,1)}, bf16[640,960]{0,1:T(8,128)(2,1)}) async-done(((bf16[640,960]{0,1:T(8,128)(2,1)}, bf16[640,960]{0,1:T(8,128)(2,1)}, bf16[640,960]{0,1:T(8,128)(2,1)}), (bf16[640,960]{0,1:T(8,128)(2,1)}, bf16[640,960]{0,1:T(8,128)(2,1)}, bf16[640,960]{0,1:T(8,128)(2,1)})) %all-reduce.7.cloned.1.call-update) | async-done | bytes 3686416 | tf_op jit(solution)/shard_map/psum | solution.py:209
  522.4 44.4 %reduce-scatter.12.cloned.1.call-done = bf16[240,960]{1,0:T(8,128)(2,1)} async-done(((bf16[960,960]{1,0:T(8,128)(2,1)}), bf16[240,960]{1,0:T(8,128)(2,1)}) %reduce-scatter.12.cloned.1.call-update) | async-done | bytes 460816 | tf_op jit(solution)/shard_map/reduce_scatter | solution.py:264
  566.8 62.8 %reduce-scatter.14.cloned.1.call-done = bf16[240,1600]{1,0:T(8,128)(2,1)} async-done(((bf16[960,1600]{1,0:T(8,128)(2,1)}), bf16[240,1600]{1,0:T(8,128)(2,1)}) %reduce-scatter.14.cloned.1.call-update) | async-done | bytes 768016 | tf_op jit(solution)/shard_map/reduce_scatter | solution.py:265
  629.6 0.7 fusion.88
  630.2 1.2 fusion.70
  631.5 1.6 convert_element_type.172
  633.2 1.6 convert_element_type.173
  635.0 1.6 convert_element_type.174
  636.6 53.9 %all-reduce.5.cloned.1.call-done = (bf16[240,1600]{1,0:T(8,128)(2,1)}, bf16[240,960]{1,0:T(8,128)(2,1)}) async-done(((bf16[240,1600]{1,0:T(8,128)(2,1)}, bf16[240,960]{1,0:T(8,128)(2,1)}), (bf16[240,1600]{1,0:T(8,128)(2,1)}, bf16[240,960]{1,0:T(8,128)(2,1)})) %all-reduce.5.cloned.1.call-update) | async-done | bytes 1228816 | tf_op jit(solution)/shard_map/psum | solution.py:269
  690.5 1.3 fusion.86
  691.9 1.1 slice.104
  692.9 1.1 convert_element_type.171
  694.0 0.9 copy.60
  694.9 0.9 copy.59
  (133 shorter events, 4.4 us)
Async XLA Ops:
  7.2 241.9 %copy-start = (bf16[640,960]{0,1:T(8,128)(2,1)S(1)}, bf16[640,960]{0,1:T(8,128)(2,1)}, u32[]{:S(2)}) copy-start(bf16[640,960]{0,1:T(8,128)(2,1)} %param.22) | copy-start | bytes 3686404
  7.2 4.4 copy-start.31
  7.2 4.4 copy-start.32
  7.2 4.4 copy-start.33
  7.2 4.4 copy-start.23
  7.2 19.1 %copy-start.2 = (bf16[1,256,960]{1,2,0:T(8,128)(2,1)S(1)}, bf16[1,256,960]{1,2,0:T(8,128)(2,1)}, u32[]{:S(2)}) copy-start(bf16[1,256,960]{1,2,0:T(8,128)(2,1)} %param.15) | copy-start | bytes 1474564
  7.2 71.4 %all-gather.8.cloned.1.call-start = ((), (), s32[]{:S(2)}) async-start(), calls=%async_computation.5 | async-start | bytes 3993600 | tf_op jit(solution)/shard_map/all_gather | solution.py:158
  11.5 101.3 %all-gather.10.cloned.1.call-start = ((), (), s32[]{:S(2)}) async-start(), calls=%async_computation.6 | async-start | bytes 2949120 | tf_op jit(solution)/shard_map/all_gather | solution.py:177
  25.7 56.8 %copy-start.19 = (f32[256,64]{0,1:T(8,128)}, f32[256,64]{0,1:T(8,128)S(1)}, u32[]{:S(2)}) copy-start(f32[256,64]{0,1:T(8,128)S(1)} %pad_maximum_fusion.6) | copy-start | bytes 196612
  82.5 2.5 copy-start.30
  83.6 74.3 %all-gather.12.cloned.1.call-start = ((), (), s32[]{:S(2)}) async-start(), calls=%async_computation.7 | async-start | bytes 2457600 | tf_op jit(solution)/shard_map/all_gather | solution.py:161
  84.3 120.4 %all-gather.14.cloned.1.call-start = ((), (), s32[]{:S(2)}) async-start(), calls=%async_computation.8 | async-start | bytes 2457600 | tf_op jit(solution)/shard_map/all_gather | solution.py:190
  96.1 18.7 %copy-start.6 = (bf16[256,15,64]{0,2,1:T(8,128)(2,1)}, bf16[256,15,64]{0,2,1:T(8,128)(2,1)S(1)}, u32[]{:S(2)}) copy-start(bf16[256,15,64]{0,2,1:T(8,128)(2,1)S(1)} %slice.96) | copy-start | bytes 1474564
  114.7 13.1 %copy-start.3 = (bf16[2048,320]{0,1:T(8,128)(2,1)}, bf16[2048,320]{0,1:T(8,128)(2,1)S(1)}, u32[]{:S(2)}) copy-start(bf16[2048,320]{0,1:T(8,128)(2,1)S(1)} %get-tuple-element.93) | copy-start | bytes 3932164
  114.7 26.9 %copy-start.13 = (bf16[2048,320]{0,1:T(8,128)(2,1)}, bf16[2048,320]{0,1:T(8,128)(2,1)S(1)}, u32[]{:S(2)}) copy-start(bf16[2048,320]{0,1:T(8,128)(2,1)S(1)} %get-tuple-element.94) | copy-start | bytes 3932164
  161.6 87.4 %all-gather.16.cloned.1.call-start = ((), (), s32[]{:S(2)}) async-start(), calls=%async_computation.9 | async-start | bytes 2457600 | tf_op jit(solution)/shard_map/all_gather | solution.py:166
  163.7 137.5 %reduce-scatter.6.cloned.1.call-start = ((), (), s32[]{:S(2)}) async-start(), calls=%async_computation.10 | async-start | bytes 2457600 | tf_op jit(solution)/shard_map/reduce_scatter | solution.py:194
  204.8 5.4 copy-start.25
  204.8 5.4 copy-start.27
  249.1 6.9 copy-start.28
  256.0 1.7 copy-start.34
  256.0 1.8 copy-start.36
  256.0 2.2 copy-start.29
  261.2 83.6 %reduce-scatter.8.cloned.1.call-start = ((), (), s32[]{:S(2)}) async-start(), calls=%async_computation.11 | async-start | bytes 2457600 | tf_op jit(solution)/shard_map/reduce_scatter | solution.py:213
  301.2 1.6 copy-start.10
  303.1 138.3 %reduce-scatter.10.cloned.1.call-start = ((), (), s32[]{:S(2)}) async-start(), calls=%async_computation.12 | async-start | bytes 2949120 | tf_op jit(solution)/shard_map/reduce_scatter | solution.py:228
  344.8 2.6 copy-start.24
  347.3 0.8 copy-start.11
  347.4 1.4 copy-start.17
  363.9 21.4 %copy-start.7 = (bf16[256,15,64]{0,2,1:T(8,128)(2,1)S(1)}, bf16[256,15,64]{0,2,1:T(8,128)(2,1)}, u32[]{:S(2)}) copy-start(bf16[256,15,64]{0,2,1:T(8,128)(2,1)} %copy-done.6) | copy-start | bytes 1474564
  398.7 5.1 copy-start.37
  398.7 123.7 %all-reduce.7.cloned.1.call-start = ((), (), s32[]{:S(2)}) async-start(), calls=%async_computation.16 | async-start | bytes 7372800 | tf_op jit(solution)/shard_map/psum | solution.py:209
  399.0 4.8 copy-start.26
  403.8 2.7 copy-start.35
  409.3 1.1 copy-start.12
  409.3 4.1 copy-start.4
  409.3 157.4 %reduce-scatter.12.cloned.1.call-start = ((), (), s32[]{:S(2)}) async-start(), calls=%async_computation.13 | async-start | bytes 2457600 | tf_op jit(solution)/shard_map/reduce_scatter | solution.py:264
  413.4 216.1 %reduce-scatter.14.cloned.1.call-start = ((), (), s32[]{:S(2)}) async-start(), calls=%async_computation.14 | async-start | bytes 3993600 | tf_op jit(solution)/shard_map/reduce_scatter | solution.py:265
  422.5 21.4 %copy-start.5 = (f32[5,64,256,3]{2,1,3,0:T(8,128)S(1)}, f32[5,64,256,3]{2,1,3,0:T(8,128)}, u32[]{:S(2)}) copy-start(f32[5,64,256,3]{2,1,3,0:T(8,128)} %convolution_multiply_fusion) | copy-start | bytes 2949124
  422.5 21.4 %copy-start.20 = (f32[256,64]{0,1:T(8,128)S(1)}, f32[256,64]{0,1:T(8,128)}, u32[]{:S(2)}) copy-start(f32[256,64]{0,1:T(8,128)} %copy-done.19) | copy-start | bytes 196612
  441.5 2.4 copy-start.22
  447.0 243.5 %all-reduce.5.cloned.1.call-start = ((), (), s32[]{:S(2)}) async-start(), calls=%async_computation.15 | async-start | bytes 2580480 | tf_op jit(solution)/shard_map/psum | solution.py:269
  447.1 183.1 %copy-start.8 = (bf16[1,256,960]{1,2,0:T(8,128)(2,1)S(1)}, bf16[1,256,960]{1,2,0:T(8,128)(2,1)}, u32[]{:S(2)}) copy-start(bf16[1,256,960]{1,2,0:T(8,128)(2,1)} %param.26) | copy-start | bytes 1474564
  451.1 179.2 %copy-start.18 = (f32[256,960]{0,1:T(8,128)S(1)}, f32[256,960]{0,1:T(8,128)}, u32[]{:S(2)}) copy-start(f32[256,960]{0,1:T(8,128)} %get-tuple-element.126) | copy-start | bytes 2949124
  629.6 1.9 copy-start.16
  631.5 1.8 copy-start.15
  633.2 1.8 copy-start.14
  690.5 1.3 copy-start.9
  690.5 2.4 copy-start.21
  690.5 5.2 copy-start.1
Sparse Core Ops, SparseCore 0:
  11.7 66.9 all-gather.7
  83.7 29.0 all-gather.9
  114.4 43.4 all-gather.11
  161.8 42.9 all-gather.13
  206.7 42.2 all-gather.15
  261.4 39.7 reduce-scatter.5
  304.1 40.6 reduce-scatter.7
  398.8 42.5 reduce-scatter.9
  445.7 76.6 all-reduce.6
  525.1 41.5 reduce-scatter.11
  569.1 60.4 reduce-scatter.13
  632.7 57.7 all-reduce.4

commit v2 on v1

--- a/solution.py
+++ b/solution.py
@@ -1,6 +1,10 @@
+import functools
+
 import jax
 import jax.numpy as jnp
 from jax import lax
+from jax.experimental import pallas as pl
+from jax.experimental.pallas import tpu as pltpu
 from jax.sharding import PartitionSpec as P
 
 HEADS = 15
@@ -102,6 +106,13 @@
     return (grad_qrot, key_part, value_part)
 
 
+def padded_to(values, row_dim):
+    pads = [(0, 0)] * values.ndim
+    pads[row_dim] = (0, -values.shape[row_dim] % 128)
+    pads[-1] = (0, -values.shape[-1] % 128)
+    return jnp.pad(values, pads)
+
+
 def ffn_both(normed, grad_mixed, gate_rows, up_rows, down_rows):
     gate_proj = lax.dot_general(normed, gate_rows, across_cols, preferred_element_type=jnp.float32)
     up_proj = lax.dot_general(normed, up_rows, across_cols, preferred_element_type=jnp.float32)
@@ -119,6 +130,338 @@
         grad_up_act, up_rows, preferred_element_type=jnp.float32
     )
     return (inner_act, grad_gate_act, grad_up_act, grad_normed.astype(jnp.bfloat16))
+
+
+CHIPS = 4
+SPAN = 2 * CHIPS
+VMEM_BYTES = 60 * 1024 * 1024
+MESH = pl.DeviceIdType.MESH
+
+
+def plane_of():
+    me = lax.axis_index("ctx")
+    core = lax.rem(me, 2)
+    chip = me // 2
+    return me, core, chip, me + 1 - 2 * core
+
+
+def chip_at(chip, core, step):
+    return 2 * lax.rem(chip + step + CHIPS, CHIPS) + core
+
+
+def greet(devices):
+    barrier = pltpu.get_barrier_semaphore()
+    for device in devices:
+        pl.semaphore_signal(barrier, inc=1, device_id=device, device_id_type=MESH)
+    pl.semaphore_wait(barrier, len(devices))
+
+
+def send(src, dst, send_sem, recv_sem, device):
+    copy = pltpu.make_async_remote_copy(
+        src_ref=src,
+        dst_ref=dst,
+        send_sem=send_sem,
+        recv_sem=recv_sem,
+        device_id=device,
+        device_id_type=MESH,
+    )
+    copy.start()
+    return copy
+
+
+def comm_params(number):
+    return pltpu.CompilerParams(
+        collective_id=number, has_side_effects=True, vmem_limit_bytes=VMEM_BYTES
+    )
+
+
+def comm_cost(moved):
+    return pl.CostEstimate(flops=0, bytes_accessed=moved * 30, transcendentals=0)
+
+
+def in_vmem(count):
+    return [pl.BlockSpec(memory_space=pltpu.VMEM)] * count
+
+
+def gather_rows_kernel(depth, own_ref, out_ref, z_sems, p_sems, f_sems):
+    me, core, chip, partner = plane_of()
+    layer = lax.axis_index("fsdp")
+    layers = [lax.rem(layer + d, depth) for d in range(1, depth)]
+    peers = [chip_at(chip, core, j) for j in range(1, CHIPS)]
+    greet([(me, other) for other in layers] + [(peer, layer) for peer in peers + [partner]])
+    first = [
+        send(own_ref.at[me], out_ref.at[layer, me], z_sems.at[0, d], z_sems.at[1, d], (me, other))
+        for d, other in enumerate(layers)
+    ]
+    for piece in range(SPAN):
+        out_ref[layer, piece] = own_ref[piece]
+    spread = []
+    for d, copy in enumerate(first):
+        copy.wait_recv()
+        source = lax.rem(layer + depth - d - 1, depth)
+        for j, peer in enumerate(peers):
+            block = out_ref.at[source, me]
+            spread.append(
+                send(block, block, p_sems.at[0, d, j], p_sems.at[1, d, j], (peer, layer))
+            )
+        block = out_ref.at[source, me]
+        first[d] = (
+            copy,
+            send(block, block, f_sems.at[0, d, 3], f_sems.at[1, d, 3], (partner, layer)),
+        )
+    passed = []
+    for d in range(depth - 1):
+        source = lax.rem(layer + depth - d - 1, depth)
+        for j in range(CHIPS - 1):
+            spread[d * (CHIPS - 1) + j].wait_recv()
+            block = out_ref.at[source, chip_at(chip, core, -j - 1)]
+            passed.append(
+                send(block, block, f_sems.at[0, d, j], f_sems.at[1, d, j], (partner, layer))
+            )
+    for copy, handed in first:
+        copy.wait_send()
+        handed.wait()
+    for copy in spread:
+        copy.wait_send()
+    for copy in passed:
+        copy.wait()
+
+
+def gather_rows(own, depth):
+    if lax.axis_size("ctx") != SPAN:
+        return lax.all_gather(own, "fsdp", axis=0)
+    rows, columns = own.shape
+    piece = rows // SPAN
+    return pl.pallas_call(
+        functools.partial(gather_rows_kernel, depth),
+        out_shape=jax.ShapeDtypeStruct((depth, SPAN, piece, columns), own.dtype),
+        in_specs=in_vmem(1),
+        out_specs=in_vmem(1)[0],
+        scratch_shapes=[
+            pltpu.SemaphoreType.DMA((2, depth - 1)),
+            pltpu.SemaphoreType.DMA((2, depth - 1, CHIPS - 1)),
+            pltpu.SemaphoreType.DMA((2, depth - 1, CHIPS)),
+        ],
+        compiler_params=comm_params(1),
+        cost_estimate=comm_cost(own.size * 2 * depth),
+    )(own.reshape(SPAN, piece, columns)).reshape(depth, rows, columns)
+
+
+def gather_plane_kernel(kv_ref, tag_ref, kv_out, tag_out, p_sems, f_sems):
+    me, core, chip, partner = plane_of()
+    layer = lax.axis_index("fsdp")
+    peers = [chip_at(chip, core, j) for j in range(1, CHIPS)]
+    greet([(peer, layer) for peer in peers + [partner]])
+    pairs = ((kv_ref, kv_out), (tag_ref, tag_out))
+    spread, passed = [], []
+    for j, peer in enumerate(peers):
+        for a, (own, out) in enumerate(pairs):
+            spread.append(
+                send(own, out.at[me], p_sems.at[0, a, j], p_sems.at[1, a, j], (peer, layer))
+            )
+    for a, (own, out) in enumerate(pairs):
+        passed.append(
+            send(own, out.at[me], f_sems.at[0, a, 3], f_sems.at[1, a, 3], (partner, layer))
+        )
+    kv_out[me] = kv_ref[...]
+    tag_out[me] = tag_ref[...]
+    for j in range(CHIPS - 1):
+        for a, (own, out) in enumerate(pairs):
+            spread[2 * j + a].wait_recv()
+            block = out.at[chip_at(chip, core, -j - 1)]
+            passed.append(
+                send(block, block, f_sems.at[0, a, j], f_sems.at[1, a, j], (partner, layer))
+            )
+    for copy in spread:
+        copy.wait_send()
+    for copy in passed:
+        copy.wait()
+
+
+def gather_plane(kv, tags):
+    if lax.axis_size("ctx") != SPAN:
+        return tuple(lax.all_gather(part, "ctx", axis=0, tiled=True) for part in (kv, tags))
+    rows, columns = kv.shape
+    kv_all, tags_all = pl.pallas_call(
+        gather_plane_kernel,
+        out_shape=(
+            jax.ShapeDtypeStruct((SPAN, rows, columns), kv.dtype),
+            jax.ShapeDtypeStruct((SPAN, 1, rows), tags.dtype),
+        ),
+        in_specs=in_vmem(2),
+        out_specs=tuple(in_vmem(2)),
+        scratch_shapes=[
+            pltpu.SemaphoreType.DMA((2, 2, CHIPS - 1)),
+            pltpu.SemaphoreType.DMA((2, 2, CHIPS)),
+        ],
+        compiler_params=comm_params(2),
+        cost_estimate=comm_cost(kv.size * 2 * SPAN),
+    )(kv, tags[None])
+    return kv_all.reshape(SPAN * rows, columns), tags_all.reshape(SPAN * rows)
+
+
+def added(*parts):
+    total = parts[0].astype(jnp.float32)
+    for part in parts[1:]:
+        total = total + part.astype(jnp.float32)
+    return total
+
+
+def reduce_plane(x_ref, axis, halves, sums, arrived, h_sems, p_sems, layer):
+    me, core, chip, partner = plane_of()
+    slabs = x_ref.shape[1 - axis]
+
+    def piece_of(index):
+        return x_ref.at[index] if axis == 0 else x_ref.at[:, index]
+
+    handed, spread = [], []
+    for j in range(CHIPS):
+        slot = (j + 1) % CHIPS
+        handed.append(
+            send(
+                piece_of(chip_at(chip, 1 - core, slot)),
+                halves.at[slot],
+                h_sems.at[0, slot],
+                h_sems.at[1, slot],
+                (partner, layer),
+            )
+        )
+    for j in range(CHIPS):
+        slot = (j + 1) % CHIPS
+        handed[j].wait_recv()
+        mine = chip_at(chip, core, slot)
+
+        def add_half(slab, carry, slot=slot, mine=mine):
+            sums[slot, slab] = added(piece_of(mine)[slab], halves[slot, slab]).astype(sums.dtype)
+            return carry
+
+        lax.fori_loop(0, slabs, add_half, 0)
+        if slot:
+            spread.append(
+                send(
+                    sums.at[slot],
+                    arrived.at[slot - 1],
+                    p_sems.at[0, slot - 1],
+                    p_sems.at[1, slot - 1],
+                    (mine, layer),
+                )
+            )
+    for copy in spread:
+        copy.wait_recv()
+    return handed + spread
+
+
+def reduce_plane_kernel(x_ref, out_ref, halves, sums, arrived, h_sems, p_sems):
+    me, core, chip, partner = plane_of()
+    layer = lax.axis_index("fsdp")
+    greet([(chip_at(chip, core, j), layer) for j in range(1, CHIPS)] + [(partner, layer)])
+    copies = reduce_plane(x_ref, 0, halves, sums, arrived, h_sems, p_sems, layer)
+
+    def add_slab(slab, carry):
+        out_ref[slab] = added(
+            sums[0, slab], arrived[0, slab], arrived[1, slab], arrived[2, slab]
+        )
+        return carry
+
+    lax.fori_loop(0, x_ref.shape[1], add_slab, 0)
+    for copy in copies:
+        copy.wait_send()
+
+
+def plane_scratch(block, dtype):
+    return [
+        pltpu.VMEM((CHIPS, *block), dtype),
+        pltpu.VMEM((CHIPS, *block), dtype),
+        pltpu.VMEM((CHIPS - 1, *block), dtype),
+        pltpu.SemaphoreType.DMA((2, CHIPS)),
+        pltpu.SemaphoreType.DMA((2, CHIPS - 1)),
+    ]
+
+
+def scatter_plane(values):
+    if lax.axis_size("ctx") != SPAN:
+        own = lax.psum_scatter(values, "ctx", scatter_dimension=0, tiled=True)
+        return own.astype(jnp.float32)
+    rows, columns = values.shape
+    slabs = 8
+    block = (slabs, rows // SPAN // slabs, columns)
+    return pl.pallas_call(
+        reduce_plane_kernel,
+        out_shape=jax.ShapeDtypeStruct(block, jnp.float32),
+        in_specs=in_vmem(1),
+        out_specs=in_vmem(1)[0],
+        scratch_shapes=plane_scratch(block, values.dtype),
+        compiler_params=comm_params(3),
+        cost_estimate=comm_cost(values.size * 2),
+    )(values.reshape(SPAN, *block)).reshape(rows // SPAN, columns)
+
+
+def reduce_rows_kernel(
+    depth, x_ref, out_ref, halves, sums, arrived, across, h_sems, p_sems, z_sems, g_sems, f_sems
+):
+    me, core, chip, partner = plane_of()
+    layer = lax.axis_index("fsdp")
+    layers = [lax.rem(layer + d, depth) for d in range(1, depth)]
+    peers = [chip_at(chip, core, j) for j in range(1, CHIPS)]
+    greet([(me, other) for other in layers] + [(peer, layer) for peer in peers + [partner]])
+    copies = reduce_plane(x_ref, 1, halves, sums, arrived, h_sems, p_sems, layer)
+    for d in list(range(1, depth)) + [0]:
+        target = lax.rem(layer + d, depth)
+        across[0, d] = added(
+            sums[0, target], arrived[0, target], arrived[1, target], arrived[2, target]
+        ).astype(across.dtype)
+        if d:
+            copies.append(
+                send(
+                    across.at[0, d],
+                    across.at[1, d],
+                    z_sems.at[0, d - 1],
+                    z_sems.at[1, d - 1],
+                    (me, target),
+                )
+            )
+    for copy in copies[-(depth - 1) :]:
+        copy.wait_recv()
+    parts = [across[0, 0]] + [across[1, d] for d in range(1, depth)]
+    out_ref[me] = added(*parts).astype(out_ref.dtype)
+    spread, passed = [], []
+    mine = out_ref.at[me]
+    for j, peer in enumerate(peers):
+        spread.append(send(mine, mine, g_sems.at[0, j], g_sems.at[1, j], (peer, layer)))
+    passed.append(send(mine, mine, f_sems.at[0, 3], f_sems.at[1, 3], (partner, layer)))
+    for j in range(CHIPS - 1):
+        spread[j].wait_recv()
+        block = out_ref.at[chip_at(chip, core, -j - 1)]
+        passed.append(send(block, block, f_sems.at[0, j], f_sems.at[1, j], (partner, layer)))
+    for copy in copies + spread:
+        copy.wait_send()
+    for copy in passed:
+        copy.wait()
+
+
+def reduce_rows(values, depth, number):
+    if lax.axis_size("ctx") != SPAN:
+        return lax.psum(lax.psum_scatter(values, "fsdp", scatter_dimension=0), "ctx")
+    _, rows, columns = values.shape
+    piece = rows // SPAN
+    block = (depth, piece, columns)
+    pieces = values.reshape(depth, SPAN, piece, columns)
+    return pl.pallas_call(
+        functools.partial(reduce_rows_kernel, depth),
+        out_shape=jax.ShapeDtypeStruct((SPAN, piece, columns), values.dtype),
+        in_specs=in_vmem(1),
+        out_specs=in_vmem(1)[0],
+        scratch_shapes=plane_scratch(block, values.dtype)[:3]
+        + [pltpu.VMEM((2, depth, piece, columns), values.dtype)]
+        + plane_scratch(block, values.dtype)[3:]
+        + [
+            pltpu.SemaphoreType.DMA((2, depth - 1)),
+            pltpu.SemaphoreType.DMA((2, CHIPS - 1)),
+            pltpu.SemaphoreType.DMA((2, CHIPS)),
+        ],
+        compiler_params=comm_params(number),
+        cost_estimate=comm_cost(values.size * 2),
+    )(pieces).reshape(rows, columns)
 
 
 def on_device(
@@ -150,15 +493,15 @@
     chosen_mask = selected.astype(jnp.float32)[:, None]
     cos_tab, sin_tab = rope_tables(query_pos)
     key_tags = jnp.where(selected, query_pos, -query_pos - 1)
-    tags_all = lax.all_gather(key_tags, "ctx", axis=0, tiled=True)
-    vectors = lax.all_gather(jnp.stack([gain_attn, gain_ffn, router]), "fsdp", axis=1, tiled=True)
-    gain_one = vectors[0].astype(jnp.float32)
-    gain_two = vectors[1].astype(jnp.float32)
-    router_vec = vectors[2].astype(jnp.float32)
-    w_qkv = lax.all_gather(
-        jnp.concatenate([w_query, w_key, w_value], 1), "fsdp", axis=0, tiled=True
-    )
+    depth = lax.axis_size("fsdp")
+    own_rows = w_query.shape[0]
     w_out_full = lax.all_gather(w_out, "fsdp", axis=0, tiled=True)
+    vectors = jnp.stack([gain_attn, gain_ffn, router], 1)
+    own_attn = padded_to(jnp.concatenate([w_query, w_key, w_value, vectors], 1), 0)
+    gathered = gather_rows(own_attn, depth)[:, :own_rows]
+    w_qkv = gathered[..., : qdim + 2 * kdim].reshape(width, qdim + 2 * kdim)
+    vectors = gathered[..., qdim + 2 * kdim : qdim + 2 * kdim + 3].reshape(width, 3)
+    gain_one, gain_two, router_vec = vectors.T.astype(jnp.float32)
     gating = jax.nn.sigmoid(jnp.sum(hidden * router_vec, -1, keepdims=True))
     grad_y = cotangent[0].astype(jnp.float32) * live_mask
     grad_inc = grad_y * chosen_mask * gating
@@ -174,14 +517,15 @@
     query_heads = rotated[:, :HEADS].reshape(row_count, KV_HEADS, groups, HEAD)
     key_rot = rotated[:, HEADS:].reshape(row_count, kdim)
     value_proj = qkv_raw[:, qdim + kdim :].astype(jnp.bfloat16)
-    kv_all = lax.all_gather(
-        jnp.concatenate([key_rot, value_proj], 1), "ctx", axis=0, tiled=True
-    )
+    kv_all, tags_all = gather_plane(jnp.concatenate([key_rot, value_proj], 1), key_tags)
     portion = (kv_all[:, :kdim], kv_all[:, kdim:], tags_all)
     start_state = (None, jnp.full((row_count, KV_HEADS, groups), negative, jnp.float32), None)
     acc_out, running_max, summed = forward_step(start_state, portion, query_heads, query_pos)
     attended = acc_out / summed[..., None]
     log_total = running_max + jnp.log(summed)
+    attended, grad_ffn_all, w_out_full = lax.optimization_barrier(
+        (attended, grad_ffn_all, w_out_full)
+    )
     outcome = attended.reshape(row_count, qdim).astype(jnp.bfloat16)
     branch = jnp.dot(outcome, w_out_full, preferred_element_type=jnp.float32)
     middle = hidden + branch
@@ -205,14 +549,14 @@
         inner_act, grad_ffn_all, across_rows, preferred_element_type=jnp.float32
     )
     low = jnp.bfloat16
-    totals = tuple(
-        lax.psum(grad.astype(low), "ctx") for grad in (grad_wgate, grad_wup, grad_wdown)
-    )
-    grad_middle, grad_gain_two = norm_backward(middle, inv_two, gain_two, grad_normed_two)
-    ffn_part, grad_middle = lax.optimization_barrier((ffn_part, grad_middle))
+    grad_normed_two, ffn_part, *grads = lax.optimization_barrier(
+        (grad_normed_two, ffn_part, *(g.astype(low) for g in (grad_wgate, grad_wup, grad_wdown)))
+    )
     ffn_out = lax.psum_scatter(ffn_part, "fsdp", scatter_dimension=0, tiled=True).astype(
         jnp.float32
     )
+    totals = tuple(lax.psum(grad, "ctx") for grad in grads)
+    grad_middle, grad_gain_two = norm_backward(middle, inv_two, gain_two, grad_normed_two)
     grad_branch = (grad_inc + grad_middle).astype(jnp.bfloat16)
     grad_attended = lax.dot_general(
         grad_branch, w_out_full, across_cols, preferred_element_type=jnp.float32
@@ -225,12 +569,9 @@
     grad_qrot, grad_keys_all, grad_values_all = backward_step(
         portion, query_heads, query_pos, grad_heads, log_total, row_delta
     )
-    grad_kv = lax.psum_scatter(
-        jnp.concatenate([grad_keys_all, grad_values_all], 1).astype(jnp.bfloat16),
-        "ctx",
-        scatter_dimension=0,
-        tiled=True,
-    ).astype(jnp.float32)
+    grad_kv = scatter_plane(
+        jnp.concatenate([grad_keys_all, grad_values_all], 1).astype(jnp.bfloat16)
+    )
     increment = branch + ffn_out
     block_out = live_mask * (hidden + chosen_mask * gating * increment)
     grad_logit = (
@@ -261,24 +602,20 @@
     grad_tokens = (grad_y + grad_logit * router_vec + grad_middle + grad_hidden_one).astype(
         jnp.bfloat16
     )
-    own_out = lax.psum_scatter(grad_wout.astype(low), "fsdp", scatter_dimension=0, tiled=True)
-    own_qkv = lax.psum_scatter(grad_wqkv.astype(low), "fsdp", scatter_dimension=0, tiled=True)
-    own_out, own_qkv, *totals = lax.optimization_barrier((own_out, own_qkv, *totals))
+    vectors = jnp.stack([grad_gain_one, grad_gain_two, grad_router], 1)
+    grads = jnp.concatenate([grad_wqkv.astype(low), grad_wout.astype(low), vectors.astype(low)], 1)
+    grads = grads.reshape(depth, own_rows, grads.shape[-1])
+    owned = reduce_rows(padded_to(grads, 1), depth, 4)[:own_rows].astype(jnp.float32)
     total_gate, total_up, total_down = (total.astype(jnp.float32) for total in totals)
-    total_out = lax.psum(own_out, "ctx").astype(jnp.float32)
-    total_qkv = lax.psum(own_qkv, "ctx").astype(jnp.float32)
-    small = lax.psum(
-        jnp.stack([grad_gain_one, grad_gain_two, grad_router]), ("ctx", "fsdp")
-    )
-    mine = lax.dynamic_slice_in_dim(
-        small, lax.axis_index("fsdp") * gain_attn.shape[0], gain_attn.shape[0], 1
-    )
+    ends = (0, qdim, qdim + kdim, qdim + 2 * kdim, qdim + 2 * kdim + width)
+    total_q, total_k, total_v, total_out = (owned[:, a:b] for a, b in zip(ends, ends[1:]))
+    mine = owned[:, ends[-1] : ends[-1] + 3].T
     return (
         block_out.astype(jnp.bfloat16)[None],
         grad_tokens[None],
-        total_qkv[:, :qdim],
-        total_qkv[:, qdim : qdim + kdim],
-        total_qkv[:, qdim + kdim :],
+        total_q,
+        total_k,
+        total_v,
         total_out,
         total_gate,
         total_up,

time: 707 us -> 597 us (0.84)
  waiting for transfers between devices: 436 us -> 185 us
  Pallas kernels: 0 us -> 141 us
  blocking collectives: 63.2 us -> 0 us
  local copies, waits for them, and re-layouts: 14.8 us -> 72.9 us
  other arithmetic: 37.1 us -> 45.3 us
    pallas_call x0 -> x4, Pallas kernels: none -> 141 us  [the longest x1 64.7 us: reduce_rows(): pl.pallas_call(functools.partial(reduce_rows_kernel, depth), out_shape=ja...]
    reduce_scatter x3 -> x0, waiting for transfers between devices: 126 us -> none  [the longest x1 62.8 us: on_device(): lax.psum_scatter(grad_wqkv.astype(low), 'fsdp', scatter_dimension=0, tile...]
    all_gather x2 -> x0, waiting for transfers between devices: 68.9 us -> none  [the longest x1 52.2 us: on_device(): lax.all_gather(jnp.concatenate([w_query, w_key, w_value], 1), 'fsdp', axi...]
    psum x1 -> x0, blocking collectives: 40.1 us -> none  [on_device(): lax.psum(jnp.stack([grad_gain_one, grad_gain_two, grad_router]), ('ctx',...]
    all_gather x1, waiting for transfers between devices: 35.6 us -> 0.02 us  [on_device(): grad_ffn_all = lax.all_gather(grad_ffn, 'fsdp', axis=0, tiled=True)]
    all_gather x2 -> x0, blocking collectives: 23.1 us -> none  [the longest x1 13.6 us: on_device(): lax.all_gather(jnp.stack([gain_attn, gain_ffn, router]), 'fsdp', axis=1,...]
    concatenate x1 -> x4, local copies, waits for them, and re-layouts: 1.96 us -> 22.4 us  [the longest x2 11.9 us: on_device(): jnp.concatenate([grad_keys_all, grad_values_all], 1).astype(jnp.bfloat16)]
    reduce_scatter x1, waiting for transfers between devices: 35.6 us -> 24.1 us  [on_device(): lax.psum_scatter(grad_normed_part, 'fsdp', scatter_dimension=0, tiled=True)]
  transfers between devices with their start and end apart: 12 -> 6, of which waited for: 12 -> 4; matrix products, arithmetic and copies ran while one was open for 14% -> 17% of each run, Pallas kernels for 0% -> 9%
where the time goes in v2:
time: 597 us; the launch traced here: 589 us
  waiting for transfers between devices  185 us (31%)
  Pallas kernels  141 us (24%)
  matrix products  128 us (21%)
  local copies, waits for them, and re-layouts  72.9 us (12%)
  other arithmetic  45.3 us (8%)
  between operations  15.7 us (3%)
    psum x1, waiting for transfers between devices, on_device(): totals = tuple((lax.psum(grad, 'ctx') for grad in grads))  77.3 us
    pallas_call x1, Pallas kernels, reduce_rows(): pl.pallas_call(functools.partial(reduce_rows_kernel, depth), out_shape=ja...  64.7 us
    all_gather x1, waiting for transfers between devices, on_device(): normed_all = lax.all_gather(normed_two, 'fsdp', axis=0, tiled=True)  44.6 us
    reduce_scatter x1, waiting for transfers between devices, on_device(): lax.psum_scatter(ffn_part, 'fsdp', scatter_dimension=0, tiled=True)  37.5 us
    pallas_call x1, Pallas kernels, gather_rows(): pl.pallas_call(functools.partial(gather_rows_kernel, depth), out_shape=ja...  32.3 us
    reduce_scatter x1, waiting for transfers between devices, on_device(): lax.psum_scatter(grad_normed_part, 'fsdp', scatter_dimension=0, tiled=True)  24.1 us
    pallas_call x1, Pallas kernels, scatter_plane(): pl.pallas_call(reduce_plane_kernel, out_shape=jax.ShapeDtypeStruct(block,...  22 us
    pallas_call x1, Pallas kernels, gather_plane(): pl.pallas_call(gather_plane_kernel, out_shape=(jax.ShapeDtypeStruct((SPAN...  21.9 us
  transfers between devices with their start and end apart: 6, of which 4 were waited for; matrix products, arithmetic and copies ran while one was open for 17% of the time, Pallas kernels for 9%

profile of v2, /device:TPU:0, one launch (start us, length us, event | category | flops | bytes accessed | tf_op | source)
XLA Modules:
  0.0 588.6 jit_solution(1847159801379000101)
XLA Ops:
  8.0 1.1 copy.68
  9.0 1.1 copy.69
  12.4 1.3 concatenate.42
  13.7 1.0 pad.8
  14.7 32.3 %shard_map.238 = bf16[4,8,32,1664]{3,2,1,0:T(8,128)(2,1)} custom-call(bf16[8,32,1664]{2,1,0:T(8,128)(2,1)} %bitcast.235), custom_call_target="tpu_custom_call" | custom-call | bytes 102236160 | tf_op jit(solution)/shard_map/pallas_call | solution.py:235
  47.0 1.2 slice_convert_fusion.2
  51.1 0.9 fusion.67
  52.1 2.2 slice.98
  54.3 1.6 fusion.79
  60.0 21.9 %shard_map.239 = (bf16[8,256,640]{2,1,0:T(8,128)(2,1)}, s32[8,1,256]{2,1,0:T(1,128)}) custom-call(bf16[256,640]{1,0:T(8,128)(2,1)} %pad_maximum_fusion.5.kv_ref, s32[1,256]{1,0:T(1,128)} %and_select_fusion.tag_ref), custom_call_target="tpu_custom_call" | custom-call | bytes 78643200 | tf_op jit(solution)/shard_map/pallas_call | solution.py:285
  82.0 1.3 add_select_fusion
  83.3 1.3 broadcast_compare_fusion
  84.5 1.9 slice.106
  86.4 4.4 fusion.95
  90.8 1.8 copy.77
  92.7 2.5 or_and_fusion
  95.1 13.6 %fusion.2 = (f32[256,5,3]{0,2,1:T(4,128)S(1)}, f32[5,2048,256,3]{2,1,3,0:T(8,128)}) fusion(pred[256,2048]{0,1:T(8,128)(4,1)S(1)} %or_and_fusion, bf16[2048,5,64,1]{0,2,3,1:T(8,128)(2,1)S(1)} %bitcast.225, bf16[256,5,3,64]{0,3,2,1:T(8,128)(2,1)} %bitcast.232), kind=kOutput, calls=%fused_computation.6 | convolution fusion | flops 1030222080 | bytes 33799168 | tf_op jit(solution)/shard_map/qngd,knd->qngk/dot_general | solution.py:65
  108.8 13.7 %fusion.8 = f32[256,5,3]{0,2,1:T(4,128)S(1)} fusion(f32[5,2048,256,3]{2,1,3,0:T(8,128)} %get-tuple-element.113, f32[256,5,3]{0,2,1:T(4,128)S(1)} %broadcast_maximum_fusion, pred[256,2048]{0,1:T(8,128)(4,1)S(1)} %or_and_fusion), kind=kLoop, calls=%fused_computation.12 | loop fusion | flops 31453440 | bytes 32012288 | tf_op jit(solution)/shard_map/reduce_sum | solution.py:71
  122.5 2.6 copy.76
  125.1 14.1 %fusion.71 = f32[256,5,3,64]{0,3,2,1:T(8,128)S(1)} fusion(bf16[2048,5,64,1]{0,2,3,1:T(8,128)(2,1)} %bitcast.247, f32[5,2048,256,3]{2,1,3,0:T(8,128)} %get-tuple-element.113, f32[256,5,3]{0,2,1:T(4,128)S(1)} %broadcast_maximum_fusion, pred[256,2048]{0,1:T(8,128)(4,1)S(1)} %or_and_fusion, f32[256,5,3]{0,2,1:T(4,128)S(1)} %fusion.8), kind=kOutput, calls=%fused_computation.99 | convolution fusion | flops 1038336000 | bytes 34306048 | tf_op jit(solution)/shard_map/qngk,knd->qngd/dot_general | solution.py:73
  140.1 2.7 multiply_reduce_fusion.3
  142.8 1.0 multiply_convert_fusion.3
  144.1 5.2 fusion.100
  149.2 44.6 %all-gather.8.cloned.1.call-done = bf16[1024,960]{0,1:T(8,128)(2,1)} async-done(((bf16[256,960]{0,1:T(8,128)(2,1)}), bf16[1024,960]{0,1:T(8,128)(2,1)}) %all-gather.8.cloned.1.call-update) | async-done | bytes 1966096 | tf_op jit(solution)/shard_map/all_gather | solution.py:534
  193.8 3.9 fusion.101
  197.8 3.9 multiply_convert_fusion
  201.7 1.7 fusion.102
  203.4 3.0 add_convert_fusion
  207.7 4.3 convolution_convert_fusion.2
  212.1 4.8 convolution_convert_fusion.3
  216.8 2.7 convolution_convert_fusion.5
  219.6 2.7 convolution_convert_fusion.4
  222.3 24.1 %reduce-scatter.3.cloned.1.call-done = bf16[256,960]{0,1:T(8,128)(2,1)} async-done(((bf16[1024,960]{0,1:T(8,128)(2,1)}), bf16[256,960]{0,1:T(8,128)(2,1)}) %reduce-scatter.3.cloned.1.call-update) | async-done | bytes 491536 | tf_op jit(solution)/shard_map/reduce_scatter | solution.py:538
  246.4 1.1 convert_element_type.172
  248.3 77.3 %all-reduce.5.cloned.1.call-done = (bf16[640,960]{0,1:T(8,128)(2,1)}, bf16[640,960]{0,1:T(8,128)(2,1)}, bf16[640,960]{0,1:T(8,128)(2,1)}) async-done(((bf16[640,960]{0,1:T(8,128)(2,1)}, bf16[640,960]{0,1:T(8,128)(2,1)}, bf16[640,960]{0,1:T(8,128)(2,1)}), (bf16[640,960]{0,1:T(8,128)(2,1)}, bf16[640,960]{0,1:T(8,128)(2,1)}, bf16[640,960]{0,1:T(8,128)(2,1)})) %all-reduce.5.cloned.1.call-update) | async-done | bytes 3686416 | tf_op jit(solution)/shard_map/psum | solution.py:558
  325.6 3.0 convert_element_type.190
  328.6 1.6 convert_element_type.191
  330.3 1.6 convert_element_type.192
  331.9 37.5 %reduce-scatter.5.cloned.1.call-done = bf16[256,960]{0,1:T(8,128)(2,1)} async-done(((bf16[1024,960]{0,1:T(8,128)(2,1)}), bf16[256,960]{0,1:T(8,128)(2,1)}) %reduce-scatter.5.cloned.1.call-update) | async-done | bytes 491536 | tf_op jit(solution)/shard_map/reduce_scatter | solution.py:555
  369.4 2.6 multiply_reduce_fusion
  372.5 1.1 copy-done.44
  375.3 15.0 %fusion.26 = bf16[2048,5,64]{0,2,1:T(8,128)(2,1)} fusion(bf16[256,5,3,64]{0,3,2,1:T(8,128)(2,1)} %bitcast.251, f32[5,2048,256,3]{2,1,3,0:T(8,128)} %get-tuple-element.113, f32[256,5,3]{0,2,1:T(4,128)S(1)} %log_add_fusion, pred[256,2048]{0,1:T(8,128)(4,1)S(1)} %or_and_fusion), kind=kOutput, calls=%fused_computation.32 | convolution fusion | flops 1038745600 | bytes 33799168 | tf_op jit(solution)/shard_map/qngk,qngd->knd/dot_general | solution.py:101
  390.3 5.5 copy.83
  395.8 5.9 concatenate.48
  401.7 21.4 %fusion.1 = bf16[256,5,3,2048]{0,3,2,1:T(8,128)(2,1)} fusion(f32[5,2048,256,3]{2,1,3,0:T(8,128)} %get-tuple-element.113, bf16[2048,5,64,1]{0,2,3,1:T(8,128)(2,1)} %bitcast.248, bf16[256,5,3,64]{0,3,2,1:T(8,128)(2,1)S(1)} %bitcast.252, f32[256,5,3]{0,2,1:T(4,128)S(1)} %multiply_reduce_fusion.1, f32[256,5,3]{0,2,1:T(4,128)S(1)} %log_add_fusion, ...), kind=kOutput, calls=%fused_computation.2 | convolution fusion | flops 1053818880 | bytes 49543168 | tf_op jit(solution)/shard_map/qngd,knd->qngk/dot_general | solution.py:90
  423.1 11.4 %fusion.25 = bf16[2048,5,64]{0,2,1:T(8,128)(2,1)} fusion(bf16[256,5,3,64]{0,3,2,1:T(8,128)(2,1)S(1)} %bitcast.233, bf16[256,5,3,2048]{0,3,2,1:T(8,128)(2,1)} %fusion.1), kind=kOutput, calls=%fused_computation.31 | convolution fusion | flops 1007943680 | bytes 17530880 | tf_op jit(solution)/shard_map/qngk,qngd->knd/dot_general | solution.py:98
  434.5 5.5 copy.81
  439.9 6.0 %concatenate.47 = bf16[8,8,32,320]{3,2,1,0:T(8,128)(2,1)} reshape(bf16[2048,5,64]{2,1,0:T(8,128)(2,1)} %copy.81) | data formatting | bytes 2621440 | tf_op jit(solution)/shard_map/concatenate | solution.py:573
  446.0 4.4 pad_maximum_fusion.x_ref
  450.4 22.0 %shard_map.240 = f32[8,32,640]{2,1,0:T(8,128)} custom-call(bf16[8,8,32,640]{3,2,1,0:T(8,128)(2,1)} %pad_maximum_fusion.x_ref), custom_call_target="tpu_custom_call" | custom-call | bytes 78643200 | tf_op jit(solution)/shard_map/pallas_call | solution.py:388
  472.4 1.1 slice.112
  473.5 1.8 slice.107
  475.3 8.5 %convolution_multiply_fusion = f32[5,64,256,3]{2,1,3,0:T(8,128)S(1)} fusion(bf16[2048,5,64,1]{0,2,3,1:T(8,128)(2,1)} %bitcast.226, bf16[256,5,3,2048]{0,3,2,1:T(8,128)(2,1)} %fusion.1), kind=kOutput, calls=%fused_computation.44 | convolution fusion | flops 1006878720 | bytes 18022400 | tf_op jit(solution)/shard_map/qngk,knd->qngd/dot_general | solution.py:95
  483.9 2.0 convolution_convert_fusion.1
  486.0 1.1 copy.101
  488.0 2.8 convolution_convert_fusion
  490.8 2.1 fusion.58
  493.4 9.2 %concatenate.53 = bf16[960,2563]{1,0:T(8,128)(2,1)} concatenate(bf16[960,1600]{1,0:T(8,128)(2,1)} %convolution_convert_fusion, bf16[960,960]{1,0:T(8,128)(2,1)} %convolution_convert_fusion.1, bf16[960,1]{1,0:T(8,128)(2,1)S(1)} %stack.32, bf16[960,1]{1,0:T(8,128)(2,1)S(1)} %stack.33, bf16[960,1]{1,0:T(8,128)(2,1)S(1)} %stack.34), dimensions={1} | concatenate | bytes 9841920 | tf_op jit(solution)/shard_map/concatenate | solution.py:606
  502.5 5.3 pad.9
  507.8 64.7 %shard_map.241 = bf16[8,32,2688]{2,1,0:T(8,128)(2,1)} custom-call(bf16[4,8,32,2688]{3,2,1,0:T(8,128)(2,1)} %bitcast.221), custom_call_target="tpu_custom_call" | custom-call | bytes 165150720 | tf_op jit(solution)/shard_map/pallas_call | solution.py:449
  572.6 1.5 slice_convert_fusion
  574.0 1.6 fusion.96
  575.8 0.9 copy.89
  578.5 3.0 fusion.87
  (163 shorter events, 18.3 us)
Async XLA Ops:
  7.2 190.6 %copy-start = (bf16[640,960]{0,1:T(8,128)(2,1)S(1)}, bf16[640,960]{0,1:T(8,128)(2,1)}, u32[]{:S(2)}) copy-start(bf16[640,960]{0,1:T(8,128)(2,1)} %param.21) | copy-start | bytes 3686404
  7.2 132.0 %all-gather.6.cloned.1.call-start = ((), (), s32[]{:S(2)}) async-start(), calls=%async_computation.3 | async-start | bytes 2457600 | tf_op jit(solution)/shard_map/all_gather | solution.py:498
  7.9 131.3 %all-gather.4.cloned.1.call-start = ((), (), s32[]{:S(2)}) async-start(), calls=%async_computation.2 | async-start | bytes 2457600 | tf_op jit(solution)/shard_map/all_gather | solution.py:509
  14.7 34.3 %copy-start.43 = (s32[1,256]{1,0:T(1,128)S(1)}, s32[1,256]{1,0:T(1,128)}, u32[]{:S(2)}) copy-start(s32[1,256]{1,0:T(1,128)} %param.29) | copy-start | bytes 3076
  14.7 35.0 %copy-start.2 = (bf16[1,256,960]{1,2,0:T(8,128)(2,1)S(1)}, bf16[1,256,960]{1,2,0:T(8,128)(2,1)}, u32[]{:S(2)}) copy-start(bf16[1,256,960]{1,2,0:T(8,128)(2,1)} %param.15) | copy-start | bytes 1474564
  14.7 35.2 %copy-start.40 = (s32[1,256]{1,0:T(1,128)S(1)}, s32[1,256]{1,0:T(1,128)}, u32[]{:S(2)}) copy-start(s32[1,256]{1,0:T(1,128)} %param.27) | copy-start | bytes 3076
  47.0 4.1 copy-start.5
  49.6 4.6 copy-start.30
  49.6 4.6 copy-start.27
  50.5 0.6 copy-start.38
  50.5 3.8 copy-start.34
  50.5 0.6 copy-start.32
  50.5 0.6 copy-start.36
  52.0 141.8 %all-gather.8.cloned.1.call-start = ((), (), s32[]{:S(2)}) async-start(), calls=%async_computation.4 | async-start | bytes 2457600 | tf_op jit(solution)/shard_map/all_gather | solution.py:534
  54.3 1.7 copy-start.11
  57.3 1.2 copy-start.20
  57.6 0.8 copy-start.13
  92.6 16.1 %copy-start.4 = (bf16[2048,320]{0,1:T(8,128)(2,1)}, bf16[2048,320]{0,1:T(8,128)(2,1)S(1)}, u32[]{:S(2)}) copy-start(bf16[2048,320]{0,1:T(8,128)(2,1)S(1)} %copy.77) | copy-start | bytes 3932164
  108.7 13.8 %copy-start.25 = (f32[256,5,3]{0,2,1:T(4,128)}, f32[256,5,3]{0,2,1:T(4,128)S(1)}, u32[]{:S(2)}) copy-start(f32[256,5,3]{0,2,1:T(4,128)S(1)} %get-tuple-element.112) | copy-start | bytes 46084
  139.1 0.9 copy-start.9
  140.1 2.7 copy-start.14
  140.1 2.7 copy-start.29
  143.8 102.6 %reduce-scatter.3.cloned.1.call-start = ((), (), s32[]{:S(2)}) async-start(), calls=%async_computation.5 | async-start | bytes 2457600 | tf_op jit(solution)/shard_map/reduce_scatter | solution.py:538
  193.8 3.9 copy-start.45
  193.8 3.9 copy-start.51
  197.8 3.9 copy-start.47
  201.7 1.7 copy-start.49
  201.7 1.7 copy-start.52
  206.4 1.3 copy-start.48
  206.5 119.1 %all-reduce.5.cloned.1.call-start = ((), (), s32[]{:S(2)}) async-start(), calls=%async_computation.7 | async-start | bytes 7372800 | tf_op jit(solution)/shard_map/psum | solution.py:558
  212.0 4.8 copy-start.46
  212.1 4.8 copy-start.50
  216.8 2.7 copy-start.53
  247.5 124.5 %copy-start.3 = (f32[256,960]{0,1:T(8,128)}, f32[256,960]{0,1:T(8,128)S(1)}, u32[]{:S(2)}) copy-start(f32[256,960]{0,1:T(8,128)S(1)} %convert_element_type.172) | copy-start | bytes 2949124
  247.5 0.8 copy-start.26
  247.5 121.8 %reduce-scatter.5.cloned.1.call-start = ((), (), s32[]{:S(2)}) async-start(), calls=%async_computation.6 | async-start | bytes 2457600 | tf_op jit(solution)/shard_map/reduce_scatter | solution.py:555
  325.6 3.0 copy-start.19
  328.6 1.8 copy-start.18
  330.2 39.2 %copy-start.33 = (f32[256]{0:T(256)S(1)}, f32[256]{0:T(256)}, u32[]{:S(2)}) copy-start(f32[256]{0:T(256)} %copy-done.32) | copy-start | bytes 3076
  330.2 39.2 %copy-start.37 = (f32[256]{0:T(256)S(1)}, f32[256]{0:T(256)}, u32[]{:S(2)}) copy-start(f32[256]{0:T(256)} %copy-done.36) | copy-start | bytes 3076
  330.2 39.2 %copy-start.42 = (f32[256]{0:T(256)S(1)}, f32[256]{0:T(256)}, u32[]{:S(2)}) copy-start(f32[256]{0:T(256)} %get-tuple-element.117) | copy-start | bytes 3076
  369.4 2.6 copy-start.6
  369.4 2.6 copy-start.39
  372.0 1.5 copy-start.44
  373.5 0.8 copy-start.16
  373.5 1.6 copy-start.10
  374.4 0.8 copy-start.22
  395.8 5.9 copy-start.23
  401.7 21.4 %copy-start.8 = (bf16[256,15,64]{0,2,1:T(8,128)(2,1)S(1)}, bf16[256,15,64]{0,2,1:T(8,128)(2,1)}, u32[]{:S(2)}) copy-start(bf16[256,15,64]{0,2,1:T(8,128)(2,1)} %slice.106) | copy-start | bytes 1474564
  475.3 8.5 %copy-start.15 = (bf16[256,5,3,64]{0,3,2,1:T(8,128)(2,1)S(1)}, bf16[256,5,3,64]{0,3,2,1:T(8,128)(2,1)}, u32[]{:S(2)}) copy-start(bf16[256,5,3,64]{0,3,2,1:T(8,128)(2,1)} %copy-done.14) | copy-start | bytes 1474564
  475.3 8.5 %copy-start.17 = (bf16[256,960]{0,1:T(8,128)(2,1)S(1)}, bf16[256,960]{0,1:T(8,128)(2,1)}, u32[]{:S(2)}) copy-start(bf16[256,960]{0,1:T(8,128)(2,1)} %copy-done.16) | copy-start | bytes 1474564
  485.9 1.5 copy-start.21
  485.9 1.5 copy-start.24
  487.3 0.7 copy-start.28
  487.3 0.7 copy-start.35
  488.0 2.8 copy-start.12
  575.6 2.8 copy-start.7
  575.6 2.8 copy-start.31
  575.6 2.8 copy-start.41
  578.5 3.0 copy-start.1
Sparse Core Ops, SparseCore 0:
  9.6 54.4 all-gather.5
  66.2 43.0 all-gather.3
  143.9 49.8 all-gather.7
  206.6 39.7 reduce-scatter.2
  250.5 75.0 all-reduce.4
  327.8 41.5 reduce-scatter.4

commit v3 on v2

--- a/solution.py
+++ b/solution.py
@@ -22,15 +22,23 @@
     half_dim = HEAD // 2
     frequency = 10000.0 ** (-2.0 * jnp.arange(half_dim, dtype=jnp.float32) / HEAD)
     angles = positions.astype(jnp.float32)[:, None] * frequency[None, :]
-    cos_tab = jnp.cos(angles)
-    sin_tab = jnp.sin(angles)
-    return (jnp.concatenate([cos_tab, cos_tab], -1), jnp.concatenate([sin_tab, sin_tab], -1))
+    return (jnp.cos(angles), jnp.sin(angles))
 
 
 def rotate(values, cos_tab, sin_tab):
-    half_dim = values.shape[-1] // 2
-    turned = jnp.concatenate([-values[..., half_dim:], values[..., :half_dim]], -1)
-    return values * cos_tab[:, None, :] + turned * sin_tab[:, None, :]
+    slots, width = values.shape
+    low, high = jnp.split(values.reshape(slots, width // HEAD, HEAD), 2, -1)
+    cos_tab, sin_tab = cos_tab[:, None], sin_tab[:, None]
+    turned = [low * cos_tab - high * sin_tab, high * cos_tab + low * sin_tab]
+    return jnp.concatenate(turned, -1).reshape(slots, width)
+
+
+def rotate_columns(values, cos_tab, sin_tab):
+    width, slots = values.shape
+    low, high = jnp.split(values.reshape(width // HEAD, HEAD, slots), 2, 1)
+    cos_tab, sin_tab = cos_tab.T[None], sin_tab.T[None]
+    turned = [low * cos_tab - high * sin_tab, high * cos_tab + low * sin_tab]
+    return jnp.concatenate(turned, 1).reshape(width, slots)
 
 
 def norm_forward(values, gain_vec):
@@ -48,69 +56,14 @@
     return (grad_values, grad_gain)
 
 
-def allowed_mask(query_pos, key_tags):
-    key_pos = jnp.where(key_tags >= 0, key_tags, -key_tags - 1)
-    earlier = key_pos[None, :] <= query_pos[:, None]
-    usable = (key_tags[None, :] >= 0) | (key_pos[None, :] == query_pos[:, None])
-    return (earlier & usable)[:, None, None, :]
-
-
-def forward_step(carried, portion, query_heads, query_pos):
-    acc_out, running_max, summed = carried
-    key_piece, value_piece, key_tags = portion
-    piece_rows = key_piece.shape[0]
-    key_heads = key_piece.reshape(piece_rows, KV_HEADS, HEAD)
-    value_heads = value_piece.reshape(piece_rows, KV_HEADS, HEAD)
-    scores = (
-        jnp.einsum("qngd,knd->qngk", query_heads, key_heads, preferred_element_type=jnp.float32)
-        * 0.125
-    )
-    allowed = allowed_mask(query_pos, key_tags)
-    new_max = jnp.maximum(running_max, jnp.max(jnp.where(allowed, scores, negative), -1))
-    weights = jnp.exp(jnp.where(allowed, scores - new_max[..., None], negative))
-    summed = jnp.sum(weights, -1)
-    weights_low = weights.astype(jnp.bfloat16)
-    acc_out = jnp.einsum(
-        "qngk,knd->qngd", weights_low, value_heads, preferred_element_type=jnp.float32
-    )
-    return (acc_out, new_max, summed)
-
-
-def backward_step(portion, query_heads, query_pos, grad_heads, log_total, row_delta):
-    key_piece, value_piece, key_tags = portion
-    piece_rows = key_piece.shape[0]
-    key_heads = key_piece.reshape(piece_rows, KV_HEADS, HEAD)
-    value_heads = value_piece.reshape(piece_rows, KV_HEADS, HEAD)
-    scores = (
-        jnp.einsum("qngd,knd->qngk", query_heads, key_heads, preferred_element_type=jnp.float32)
-        * 0.125
-    )
-    allowed = allowed_mask(query_pos, key_tags)
-    softmax_w = jnp.exp(jnp.where(allowed, scores - log_total[..., None], negative))
-    grad_probs = jnp.einsum(
-        "qngd,knd->qngk", grad_heads, value_heads, preferred_element_type=jnp.float32
-    )
-    grad_scores = (softmax_w * (grad_probs - row_delta[..., None])).astype(jnp.bfloat16)
-    probs_low = softmax_w.astype(jnp.bfloat16)
-    grad_qrot = 0.125 * jnp.einsum(
-        "qngk,knd->qngd", grad_scores, key_heads, preferred_element_type=jnp.float32
-    )
-    key_part = 0.125 * jnp.einsum(
-        "qngk,qngd->knd", grad_scores, query_heads, preferred_element_type=jnp.float32
-    )
-    value_part = jnp.einsum(
-        "qngk,qngd->knd", probs_low, grad_heads, preferred_element_type=jnp.float32
-    )
-    key_part = key_part.reshape(piece_rows, KV_HEADS * HEAD)
-    value_part = value_part.reshape(piece_rows, KV_HEADS * HEAD)
-    return (grad_qrot, key_part, value_part)
-
-
 def padded_to(values, row_dim):
     pads = [(0, 0)] * values.ndim
     pads[row_dim] = (0, -values.shape[row_dim] % 128)
-    pads[-1] = (0, -values.shape[-1] % 128)
     return jnp.pad(values, pads)
+
+
+def padded_rows_of(values, rows):
+    return jnp.pad(values, ((0, 0), (0, rows - values.shape[1]), (0, 0)))
 
 
 def ffn_both(normed, grad_mixed, gate_rows, up_rows, down_rows):
@@ -307,65 +260,48 @@
     return total
 
 
-def reduce_plane(x_ref, axis, halves, sums, arrived, h_sems, p_sems, layer):
+def reduce_plane(arrays, h_sems, p_sems):
     me, core, chip, partner = plane_of()
-    slabs = x_ref.shape[1 - axis]
-
-    def piece_of(index):
-        return x_ref.at[index] if axis == 0 else x_ref.at[:, index]
-
+    layer = lax.axis_index("fsdp")
     handed, spread = [], []
-    for j in range(CHIPS):
-        slot = (j + 1) % CHIPS
-        handed.append(
-            send(
-                piece_of(chip_at(chip, 1 - core, slot)),
-                halves.at[slot],
-                h_sems.at[0, slot],
-                h_sems.at[1, slot],
-                (partner, layer),
-            )
-        )
-    for j in range(CHIPS):
-        slot = (j + 1) % CHIPS
-        handed[j].wait_recv()
-        mine = chip_at(chip, core, slot)
-
-        def add_half(slab, carry, slot=slot, mine=mine):
-            sums[slot, slab] = added(piece_of(mine)[slab], halves[slot, slab]).astype(sums.dtype)
-            return carry
-
-        lax.fori_loop(0, slabs, add_half, 0)
-        if slot:
-            spread.append(
+    for a, (piece_of, halves, sums, arrived) in enumerate(arrays):
+        for j in range(CHIPS):
+            slot = (j + 1) % CHIPS
+            handed.append(
                 send(
-                    sums.at[slot],
-                    arrived.at[slot - 1],
-                    p_sems.at[0, slot - 1],
-                    p_sems.at[1, slot - 1],
-                    (mine, layer),
+                    piece_of(chip_at(chip, 1 - core, slot)),
+                    halves.at[slot],
+                    h_sems.at[0, a, slot],
+                    h_sems.at[1, a, slot],
+                    (partner, layer),
                 )
             )
-    for copy in spread:
-        copy.wait_recv()
-    return handed + spread
-
-
-def reduce_plane_kernel(x_ref, out_ref, halves, sums, arrived, h_sems, p_sems):
-    me, core, chip, partner = plane_of()
-    layer = lax.axis_index("fsdp")
-    greet([(chip_at(chip, core, j), layer) for j in range(1, CHIPS)] + [(partner, layer)])
-    copies = reduce_plane(x_ref, 0, halves, sums, arrived, h_sems, p_sems, layer)
-
-    def add_slab(slab, carry):
-        out_ref[slab] = added(
-            sums[0, slab], arrived[0, slab], arrived[1, slab], arrived[2, slab]
-        )
-        return carry
-
-    lax.fori_loop(0, x_ref.shape[1], add_slab, 0)
-    for copy in copies:
-        copy.wait_send()
+    for a, (piece_of, halves, sums, arrived) in enumerate(arrays):
+        for j in range(CHIPS):
+            slot = (j + 1) % CHIPS
+            handed[a * CHIPS + j].wait_recv()
+            mine = chip_at(chip, core, slot)
+
+            def add_half(slab, carry, piece=piece_of(mine), halves=halves, sums=sums, slot=slot):
+                sums[slot, slab] = added(piece[slab], halves[slot, slab]).astype(sums.dtype)
+                return carry
+
+            lax.fori_loop(0, sums.shape[1], add_half, 0)
+            if slot:
+                spread.append(
+                    send(
+                        sums.at[slot],
+                        arrived.at[slot - 1],
+                        p_sems.at[0, a, slot - 1],
+                        p_sems.at[1, a, slot - 1],
+                        (mine, layer),
+                    )
+                )
+    return handed, spread
+
+
+def plane_total(sums, arrived, slab):
+    return added(sums[0, slab], *(arrived[j, slab] for j in range(CHIPS - 1)))
 
 
 def plane_scratch(block, dtype):
@@ -373,9 +309,25 @@
         pltpu.VMEM((CHIPS, *block), dtype),
         pltpu.VMEM((CHIPS, *block), dtype),
         pltpu.VMEM((CHIPS - 1, *block), dtype),
-        pltpu.SemaphoreType.DMA((2, CHIPS)),
-        pltpu.SemaphoreType.DMA((2, CHIPS - 1)),
     ]
+
+
+def scatter_plane_kernel(x_ref, out_ref, halves, sums, arrived, h_sems, p_sems):
+    me, core, chip, partner = plane_of()
+    layer = lax.axis_index("fsdp")
+    greet([(chip_at(chip, core, j), layer) for j in range(1, CHIPS)] + [(partner, layer)])
+    arrays = [(lambda piece: x_ref.at[piece], halves, sums, arrived)]
+    handed, spread = reduce_plane(arrays, h_sems, p_sems)
+    for copy in spread:
+        copy.wait_recv()
+
+    def add_slab(slab, carry):
+        out_ref[slab] = plane_total(sums, arrived, slab)
+        return carry
+
+    lax.fori_loop(0, x_ref.shape[1], add_slab, 0)
+    for copy in handed + spread:
+        copy.wait_send()
 
 
 def scatter_plane(values):
@@ -386,82 +338,293 @@
     slabs = 8
     block = (slabs, rows // SPAN // slabs, columns)
     return pl.pallas_call(
-        reduce_plane_kernel,
+        scatter_plane_kernel,
         out_shape=jax.ShapeDtypeStruct(block, jnp.float32),
         in_specs=in_vmem(1),
         out_specs=in_vmem(1)[0],
-        scratch_shapes=plane_scratch(block, values.dtype),
+        scratch_shapes=plane_scratch(block, values.dtype)
+        + [pltpu.SemaphoreType.DMA((2, 1, CHIPS)), pltpu.SemaphoreType.DMA((2, 1, CHIPS - 1))],
         compiler_params=comm_params(3),
         cost_estimate=comm_cost(values.size * 2),
     )(values.reshape(SPAN, *block)).reshape(rows // SPAN, columns)
 
 
-def reduce_rows_kernel(
-    depth, x_ref, out_ref, halves, sums, arrived, across, h_sems, p_sems, z_sems, g_sems, f_sems
-):
+def reduce_rows_kernel(depth, count, *refs):
+    inputs, outs, scratch = refs[:count], refs[count : 2 * count], refs[2 * count : 6 * count]
+    h_sems, p_sems, z_sems, g_sems, f_sems = refs[6 * count :]
     me, core, chip, partner = plane_of()
     layer = lax.axis_index("fsdp")
     layers = [lax.rem(layer + d, depth) for d in range(1, depth)]
     peers = [chip_at(chip, core, j) for j in range(1, CHIPS)]
     greet([(me, other) for other in layers] + [(peer, layer) for peer in peers + [partner]])
-    copies = reduce_plane(x_ref, 1, halves, sums, arrived, h_sems, p_sems, layer)
-    for d in list(range(1, depth)) + [0]:
-        target = lax.rem(layer + d, depth)
-        across[0, d] = added(
-            sums[0, target], arrived[0, target], arrived[1, target], arrived[2, target]
-        ).astype(across.dtype)
-        if d:
-            copies.append(
-                send(
-                    across.at[0, d],
-                    across.at[1, d],
-                    z_sems.at[0, d - 1],
-                    z_sems.at[1, d - 1],
-                    (me, target),
+    arrays, across = [], []
+    for a, x_ref in enumerate(inputs):
+        halves, sums, arrived, layers_ref = scratch[4 * a : 4 * a + 4]
+        arrays.append((lambda piece, x_ref=x_ref: x_ref.at[:, piece], halves, sums, arrived))
+        across.append(layers_ref)
+    handed, spread = reduce_plane(arrays, h_sems, p_sems)
+    moved = []
+    for a, (_, _, sums, arrived) in enumerate(arrays):
+        for copy in spread[a * (CHIPS - 1) : (a + 1) * (CHIPS - 1)]:
+            copy.wait_recv()
+        for d in list(range(1, depth)) + [0]:
+            target = lax.rem(layer + d, depth)
+            across[a][0, d] = plane_total(sums, arrived, target).astype(across[a].dtype)
+            if d:
+                moved.append(
+                    send(
+                        across[a].at[0, d],
+                        across[a].at[1, d],
+                        z_sems.at[0, a, d - 1],
+                        z_sems.at[1, a, d - 1],
+                        (me, target),
+                    )
                 )
+    given, passed = [], []
+    for a, out_ref in enumerate(outs):
+        for copy in moved[a * (depth - 1) : (a + 1) * (depth - 1)]:
+            copy.wait_recv()
+        parts = [across[a][0, 0]] + [across[a][1, d] for d in range(1, depth)]
+        out_ref[me] = added(*parts).astype(out_ref.dtype)
+        mine = out_ref.at[me]
+        for j, peer in enumerate(peers):
+            given.append(send(mine, mine, g_sems.at[0, a, j], g_sems.at[1, a, j], (peer, layer)))
+        passed.append(send(mine, mine, f_sems.at[0, a, 3], f_sems.at[1, a, 3], (partner, layer)))
+    for a, out_ref in enumerate(outs):
+        for j in range(CHIPS - 1):
+            given[a * (CHIPS - 1) + j].wait_recv()
+            block = out_ref.at[chip_at(chip, core, -j - 1)]
+            passed.append(
+                send(block, block, f_sems.at[0, a, j], f_sems.at[1, a, j], (partner, layer))
             )
-    for copy in copies[-(depth - 1) :]:
-        copy.wait_recv()
-    parts = [across[0, 0]] + [across[1, d] for d in range(1, depth)]
-    out_ref[me] = added(*parts).astype(out_ref.dtype)
-    spread, passed = [], []
-    mine = out_ref.at[me]
-    for j, peer in enumerate(peers):
-        spread.append(send(mine, mine, g_sems.at[0, j], g_sems.at[1, j], (peer, layer)))
-    passed.append(send(mine, mine, f_sems.at[0, 3], f_sems.at[1, 3], (partner, layer)))
-    for j in range(CHIPS - 1):
-        spread[j].wait_recv()
-        block = out_ref.at[chip_at(chip, core, -j - 1)]
-        passed.append(send(block, block, f_sems.at[0, j], f_sems.at[1, j], (partner, layer)))
-    for copy in copies + spread:
+    for copy in handed + spread + moved + given:
         copy.wait_send()
     for copy in passed:
         copy.wait()
 
 
-def reduce_rows(values, depth, number):
+def reduce_rows(arrays, number):
     if lax.axis_size("ctx") != SPAN:
-        return lax.psum(lax.psum_scatter(values, "fsdp", scatter_dimension=0), "ctx")
-    _, rows, columns = values.shape
-    piece = rows // SPAN
-    block = (depth, piece, columns)
-    pieces = values.reshape(depth, SPAN, piece, columns)
-    return pl.pallas_call(
-        functools.partial(reduce_rows_kernel, depth),
-        out_shape=jax.ShapeDtypeStruct((SPAN, piece, columns), values.dtype),
-        in_specs=in_vmem(1),
-        out_specs=in_vmem(1)[0],
-        scratch_shapes=plane_scratch(block, values.dtype)[:3]
-        + [pltpu.VMEM((2, depth, piece, columns), values.dtype)]
-        + plane_scratch(block, values.dtype)[3:]
+        return [lax.psum(lax.psum_scatter(v, "fsdp", scatter_dimension=0), "ctx") for v in arrays]
+    depth, count = arrays[0].shape[0], len(arrays)
+    pieces, outs, scratch = [], [], []
+    for values in arrays:
+        _, rows, columns = values.shape
+        piece = (rows // SPAN, columns)
+        pieces.append(values.reshape(depth, SPAN, *piece))
+        outs.append(jax.ShapeDtypeStruct((SPAN, *piece), values.dtype))
+        scratch += plane_scratch((depth, *piece), values.dtype)
+        scratch.append(pltpu.VMEM((2, depth, *piece), values.dtype))
+    owned = pl.pallas_call(
+        functools.partial(reduce_rows_kernel, depth, count),
+        out_shape=tuple(outs),
+        in_specs=in_vmem(count),
+        out_specs=tuple(in_vmem(count)),
+        scratch_shapes=scratch
         + [
-            pltpu.SemaphoreType.DMA((2, depth - 1)),
-            pltpu.SemaphoreType.DMA((2, CHIPS - 1)),
-            pltpu.SemaphoreType.DMA((2, CHIPS)),
+            pltpu.SemaphoreType.DMA((2, count, CHIPS)),
+            pltpu.SemaphoreType.DMA((2, count, CHIPS - 1)),
+            pltpu.SemaphoreType.DMA((2, count, depth - 1)),
+            pltpu.SemaphoreType.DMA((2, count, CHIPS - 1)),
+            pltpu.SemaphoreType.DMA((2, count, CHIPS)),
         ],
         compiler_params=comm_params(number),
-        cost_estimate=comm_cost(values.size * 2),
-    )(pieces).reshape(rows, columns)
+        cost_estimate=comm_cost(sum(values.size for values in arrays) * 2),
+    )(*pieces)
+    return [own.reshape(values.shape[1:]) for own, values in zip(owned, arrays)]
+
+
+BLOCK = 128
+LANES = (HEADS // KV_HEADS) * BLOCK
+
+
+def dot(left, right, dims=(1, 0)):
+    return lax.dot_general(
+        left, right, (((dims[0],), (dims[1],)), ((), ())), preferred_element_type=jnp.float32
+    )
+
+
+def of_group(ref, group, at):
+    first = group * (HEADS // KV_HEADS)
+    heads = range(first, first + HEADS // KV_HEADS)
+    return jnp.concatenate([ref[head * HEAD : (head + 1) * HEAD, at] for head in heads], 1)
+
+
+def of_rows(ref, group, at):
+    first = group * (HEADS // KV_HEADS)
+    heads = range(first, first + HEADS // KV_HEADS)
+    return jnp.concatenate([ref[head : head + 1, at] for head in heads], 1)
+
+
+def columns_of(group, part):
+    start = (part * KV_HEADS + group) * HEAD
+    return slice(start, start + HEAD)
+
+
+def mask_bias(tags, query_pos):
+    key_pos = jnp.where(tags >= 0, tags, -tags - 1)
+    allowed = (key_pos <= query_pos) & ((tags >= 0) | (key_pos == query_pos))
+    bias = jnp.where(allowed, 0.0, negative)
+    return jnp.concatenate([bias] * (HEADS // KV_HEADS), 1)
+
+
+def attend_kernel(
+    first_ref, q_ref, kv_ref, pos_ref, tag_ref, out_ref, log_ref, max_ref, sum_ref, acc_ref, kept
+):
+    blocks = kv_ref.shape[0] // BLOCK
+    keep = kept.shape[0] == blocks
+
+    def scores(group, at, rows, bias):
+        keys = kv_ref[rows, columns_of(group, 0)]
+        return dot(keys, of_group(q_ref, group, at)) + bias
+
+    def query_block(qb, carry):
+        at = pl.ds(pl.multiple_of(qb * BLOCK, BLOCK), BLOCK)
+        max_ref[...] = jnp.full(max_ref.shape, negative, jnp.float32)
+        sum_ref[...] = jnp.zeros(sum_ref.shape, jnp.float32)
+        acc_ref[...] = jnp.zeros(acc_ref.shape, jnp.float32)
+        limit = first_ref[blocks + qb]
+
+        def find(kb, carry):
+            @pl.when(first_ref[kb] <= limit)
+            def _():
+                rows = pl.ds(pl.multiple_of(kb * BLOCK, BLOCK), BLOCK)
+                bias = mask_bias(tag_ref[rows, :], pos_ref[:, at])
+                for group in range(KV_HEADS):
+                    found = scores(group, at, rows, bias)
+                    if keep:
+                        kept[kb, group] = found
+                    tops = jnp.max(found.reshape(BLOCK // 8, 8, LANES), 0)
+                    max_ref[group] = jnp.maximum(max_ref[group], tops)
+
+            return carry
+
+        lax.fori_loop(0, blocks, find, 0)
+        for group in range(KV_HEADS):
+            top = jnp.max(max_ref[group], 0, keepdims=True)
+            max_ref[group] = jnp.broadcast_to(top, max_ref.shape[1:])
+
+        def gather(kb, carry):
+            @pl.when(first_ref[kb] <= limit)
+            def _():
+                rows = pl.ds(pl.multiple_of(kb * BLOCK, BLOCK), BLOCK)
+                bias = None if keep else mask_bias(tag_ref[rows, :], pos_ref[:, at])
+                for group in range(KV_HEADS):
+                    found = kept[kb, group] if keep else scores(group, at, rows, bias)
+                    weights = jnp.exp(found - max_ref[group, :1])
+                    sum_ref[group] += jnp.sum(weights.reshape(BLOCK // 8, 8, LANES), 0)
+                    values = kv_ref[rows, columns_of(group, 1)]
+                    acc_ref[group] += dot(values, weights.astype(jnp.bfloat16), (0, 0))
+
+            return carry
+
+        lax.fori_loop(0, blocks, gather, 0)
+        for group in range(KV_HEADS):
+            total = jnp.sum(sum_ref[group], 0, keepdims=True)
+            attended = acc_ref[group] / total
+            logs = max_ref[group, :1] + jnp.log(total)
+            for j in range(HEADS // KV_HEADS):
+                head = group * (HEADS // KV_HEADS) + j
+                own = slice(j * BLOCK, (j + 1) * BLOCK)
+                out_ref[head * HEAD : (head + 1) * HEAD, at] = attended[:, own]
+                log_ref[head : head + 1, at] = logs[:, own]
+        return carry
+
+    lax.fori_loop(0, q_ref.shape[1] // BLOCK, query_block, 0)
+
+
+def kernel_params():
+    return pltpu.CompilerParams(vmem_limit_bytes=VMEM_BYTES)
+
+
+def attend(firsts, queries, kv, query_pos, key_tags):
+    blocks = kv.shape[0] // BLOCK
+    slots = queries.shape[1]
+    kept = blocks if blocks <= 16 else 1
+    groups = (KV_HEADS, 8, LANES)
+    work = 4 * kv.shape[0] * slots * HEADS * HEAD
+    return pl.pallas_call(
+        attend_kernel,
+        out_shape=(
+            jax.ShapeDtypeStruct(queries.shape, jnp.float32),
+            jax.ShapeDtypeStruct((HEADS + 1, slots), jnp.float32),
+        ),
+        in_specs=[pl.BlockSpec(memory_space=pltpu.SMEM)] + in_vmem(4),
+        out_specs=tuple(in_vmem(2)),
+        scratch_shapes=[
+            pltpu.VMEM(groups, jnp.float32),
+            pltpu.VMEM(groups, jnp.float32),
+            pltpu.VMEM((KV_HEADS, HEAD, LANES), jnp.float32),
+            pltpu.VMEM((kept, KV_HEADS, BLOCK, LANES), jnp.float32),
+        ],
+        compiler_params=kernel_params(),
+        cost_estimate=pl.CostEstimate(
+            flops=work * 8, bytes_accessed=kv.size * 2, transcendentals=work // 256
+        ),
+    )(firsts, queries, kv, query_pos[None], key_tags[:, None])
+
+
+def attend_back_kernel(
+    first_ref, q_ref, kv_ref, pos_ref, tag_ref, grad_ref, log_ref, delta_ref, dq_ref, dkv_ref, acc
+):
+    blocks = kv_ref.shape[0] // BLOCK
+    dq_ref[...] = jnp.zeros(dq_ref.shape, dq_ref.dtype)
+
+    def key_block(kb, carry):
+        rows = pl.ds(pl.multiple_of(kb * BLOCK, BLOCK), BLOCK)
+        acc[...] = jnp.zeros(acc.shape, jnp.float32)
+
+        def query_block(qb, carry):
+            @pl.when(first_ref[kb] <= first_ref[blocks + qb])
+            def _():
+                at = pl.ds(pl.multiple_of(qb * BLOCK, BLOCK), BLOCK)
+                bias = mask_bias(tag_ref[rows, :], pos_ref[:, at])
+                for group in range(KV_HEADS):
+                    keys = kv_ref[rows, columns_of(group, 0)]
+                    values = kv_ref[rows, columns_of(group, 1)]
+                    queries = of_group(q_ref, group, at)
+                    grads = of_group(grad_ref, group, at)
+                    found = dot(keys, queries) + bias
+                    probs = jnp.exp(found - of_rows(log_ref, group, at))
+                    grad_probs = dot(values, grads)
+                    grad_scores = probs * (grad_probs - of_rows(delta_ref, group, at))
+                    grad_scores = grad_scores.astype(jnp.bfloat16)
+                    acc[group] += dot(grad_scores, queries, (1, 1))
+                    acc[KV_HEADS + group] += dot(probs.astype(jnp.bfloat16), grads, (1, 1))
+                    grad_q = 0.125 * dot(keys, grad_scores, (0, 0))
+                    for j in range(HEADS // KV_HEADS):
+                        head = group * (HEADS // KV_HEADS) + j
+                        own = slice(head * HEAD, (head + 1) * HEAD)
+                        dq_ref[own, at] += grad_q[:, j * BLOCK : (j + 1) * BLOCK]
+
+            return carry
+
+        lax.fori_loop(0, q_ref.shape[1] // BLOCK, query_block, 0)
+        dkv_ref[rows, :] = jnp.concatenate(
+            [acc[index] for index in range(2 * KV_HEADS)], 1
+        ).astype(dkv_ref.dtype)
+        return carry
+
+    lax.fori_loop(0, blocks, key_block, 0)
+
+
+def attend_back(firsts, queries, kv, query_pos, key_tags, grads, log_total, row_delta):
+    slots = queries.shape[1]
+    work = 10 * kv.shape[0] * slots * HEADS * HEAD
+    return pl.pallas_call(
+        attend_back_kernel,
+        out_shape=(
+            jax.ShapeDtypeStruct(queries.shape, jnp.float32),
+            jax.ShapeDtypeStruct(kv.shape, jnp.bfloat16),
+        ),
+        in_specs=[pl.BlockSpec(memory_space=pltpu.SMEM)] + in_vmem(7),
+        out_specs=tuple(in_vmem(2)),
+        scratch_shapes=[pltpu.VMEM((2 * KV_HEADS, BLOCK, HEAD), jnp.float32)],
+        compiler_params=kernel_params(),
+        cost_estimate=pl.CostEstimate(
+            flops=work * 6, bytes_accessed=kv.size * 4, transcendentals=work // 640
+        ),
+    )(firsts, queries, kv, query_pos[None], key_tags[:, None], grads, log_total, row_delta)
 
 
 def on_device(
@@ -483,7 +646,6 @@
 ):
     hidden = tokens[0].astype(jnp.float32)
     row_count, width = hidden.shape
-    groups = HEADS // KV_HEADS
     qdim = HEADS * HEAD
     kdim = KV_HEADS * HEAD
     query_pos = positions[0]
@@ -510,24 +672,23 @@
 
     normed_one, inv_one = norm_forward(hidden, gain_one)
     normed_one = normed_one.astype(jnp.bfloat16)
-    qkv_raw = jnp.dot(normed_one, w_qkv, preferred_element_type=jnp.float32)
-    rotated = rotate(
-        qkv_raw[:, : qdim + kdim].reshape(row_count, HEADS + KV_HEADS, HEAD), cos_tab, sin_tab
-    ).astype(jnp.bfloat16)
-    query_heads = rotated[:, :HEADS].reshape(row_count, KV_HEADS, groups, HEAD)
-    key_rot = rotated[:, HEADS:].reshape(row_count, kdim)
-    value_proj = qkv_raw[:, qdim + kdim :].astype(jnp.bfloat16)
-    kv_all, tags_all = gather_plane(jnp.concatenate([key_rot, value_proj], 1), key_tags)
-    portion = (kv_all[:, :kdim], kv_all[:, kdim:], tags_all)
-    start_state = (None, jnp.full((row_count, KV_HEADS, groups), negative, jnp.float32), None)
-    acc_out, running_max, summed = forward_step(start_state, portion, query_heads, query_pos)
-    attended = acc_out / summed[..., None]
-    log_total = running_max + jnp.log(summed)
+    w_kv = w_qkv[:, qdim:]
+    w_query = w_qkv[:, :qdim]
+    query_raw = dot(w_query, normed_one, (0, 1))
+    queries = rotate_columns(query_raw, cos_tab, sin_tab).astype(jnp.bfloat16) * 0.125
+    kv_raw = dot(normed_one, w_kv)
+    kv_own = jnp.concatenate([rotate(kv_raw[:, :kdim], cos_tab, sin_tab), kv_raw[:, kdim:]], 1)
+    kv_all, tags_all = gather_plane(kv_own.astype(jnp.bfloat16), key_tags)
+    first_tags = tags_all[::BLOCK]
+    firsts = jnp.concatenate(
+        [jnp.where(first_tags >= 0, first_tags, -first_tags - 1), query_pos[BLOCK - 1 :: BLOCK]]
+    )
+    attended, log_total = attend(firsts, queries, kv_all, query_pos, tags_all)
     attended, grad_ffn_all, w_out_full = lax.optimization_barrier(
         (attended, grad_ffn_all, w_out_full)
     )
-    outcome = attended.reshape(row_count, qdim).astype(jnp.bfloat16)
-    branch = jnp.dot(outcome, w_out_full, preferred_element_type=jnp.float32)
+    outcome = attended.astype(jnp.bfloat16)
+    branch = dot(outcome, w_out_full, (0, 0))
     middle = hidden + branch
     normed_two, inv_two = norm_forward(middle, gain_two)
     normed_two = normed_two.astype(jnp.bfloat16)
@@ -558,58 +719,49 @@
     totals = tuple(lax.psum(grad, "ctx") for grad in grads)
     grad_middle, grad_gain_two = norm_backward(middle, inv_two, gain_two, grad_normed_two)
     grad_branch = (grad_inc + grad_middle).astype(jnp.bfloat16)
-    grad_attended = lax.dot_general(
-        grad_branch, w_out_full, across_cols, preferred_element_type=jnp.float32
-    ).astype(jnp.bfloat16)
-    grad_wout = lax.dot_general(
-        outcome, grad_branch, across_rows, preferred_element_type=jnp.float32
-    )
-    grad_heads = grad_attended.reshape(row_count, KV_HEADS, groups, HEAD)
-    row_delta = jnp.sum(grad_heads.astype(jnp.float32) * attended, -1)
-    grad_qrot, grad_keys_all, grad_values_all = backward_step(
-        portion, query_heads, query_pos, grad_heads, log_total, row_delta
-    )
-    grad_kv = scatter_plane(
-        jnp.concatenate([grad_keys_all, grad_values_all], 1).astype(jnp.bfloat16)
-    )
+    grad_attended = dot(w_out_full, grad_branch, (1, 1)).astype(jnp.bfloat16)
+    grad_wout = dot(outcome, grad_branch)
+    row_delta = jnp.sum(
+        (grad_attended.astype(jnp.float32) * attended).reshape(HEADS, HEAD, row_count), 1
+    )
+    row_delta = jnp.pad(row_delta, ((0, 1), (0, 0)))
+    grad_qrot, grad_kv_all = attend_back(
+        firsts, queries, kv_all, query_pos, tags_all, grad_attended, log_total, row_delta
+    )
+    grad_kv = scatter_plane(grad_kv_all)
+    grad_kv, ffn_out = lax.optimization_barrier((grad_kv, ffn_out))
     increment = branch + ffn_out
     block_out = live_mask * (hidden + chosen_mask * gating * increment)
     grad_logit = (
         jnp.sum(grad_y * chosen_mask * increment, -1, keepdims=True) * gating * (1.0 - gating)
     )
     grad_router = jnp.sum(hidden * grad_logit, 0)
-    grad_rotated = jnp.concatenate(
-        [
-            grad_qrot.reshape(row_count, HEADS, HEAD),
-            grad_kv[:, :kdim].reshape(row_count, KV_HEADS, HEAD),
-        ],
-        1,
-    )
-    grad_qkv = jnp.concatenate(
-        [
-            rotate(grad_rotated, cos_tab, -sin_tab).reshape(row_count, qdim + kdim),
-            grad_kv[:, kdim:],
-        ],
-        1,
+    grad_query_raw = rotate_columns(grad_qrot, cos_tab, -sin_tab).astype(jnp.bfloat16)
+    grad_kv_raw = jnp.concatenate(
+        [rotate(grad_kv[:, :kdim], cos_tab, -sin_tab), grad_kv[:, kdim:]], 1
     ).astype(jnp.bfloat16)
-    grad_normed_one = lax.dot_general(
-        grad_qkv, w_qkv, across_cols, preferred_element_type=jnp.float32
-    )
-    grad_wqkv = lax.dot_general(
-        normed_one, grad_qkv, across_rows, preferred_element_type=jnp.float32
-    )
+    grad_normed_one = dot(grad_query_raw, w_query, (0, 1)) + dot(grad_kv_raw, w_kv, (1, 1))
+    spread_one = padded_to(normed_one.reshape(row_count, depth, own_rows), -1)
+    spread_one = spread_one.reshape(row_count, -1)
+    padded_rows = spread_one.shape[1] // depth
+    grad_wq = dot(spread_one, grad_query_raw, (0, 1)).astype(low)
+    grad_wkv = dot(spread_one, grad_kv_raw, (0, 0)).astype(low)
     grad_hidden_one, grad_gain_one = norm_backward(hidden, inv_one, gain_one, grad_normed_one)
     grad_tokens = (grad_y + grad_logit * router_vec + grad_middle + grad_hidden_one).astype(
         jnp.bfloat16
     )
-    vectors = jnp.stack([grad_gain_one, grad_gain_two, grad_router], 1)
-    grads = jnp.concatenate([grad_wqkv.astype(low), grad_wout.astype(low), vectors.astype(low)], 1)
-    grads = grads.reshape(depth, own_rows, grads.shape[-1])
-    owned = reduce_rows(padded_to(grads, 1), depth, 4)[:own_rows].astype(jnp.float32)
+    vectors = jnp.stack([grad_gain_one, grad_gain_two, grad_router]).reshape(3, depth, own_rows)
+    vectors = jnp.pad(vectors.transpose(1, 0, 2).reshape(depth, -1), ((0, 0), (0, -3 * own_rows % 1024)))
+    vectors = jnp.pad(vectors.reshape(depth, -1, 1, 128), ((0, 0), (0, 0), (0, 7), (0, 0)))
+    layered = [grad.reshape(depth, padded_rows, -1) for grad in (grad_wq, grad_wkv)]
+    layered.append(padded_rows_of(grad_wout.astype(low).reshape(depth, own_rows, -1), padded_rows))
+    layered.append(vectors.reshape(depth, -1, 128))
+    owned = reduce_rows(layered, 4)
+    *owned, totals = lax.optimization_barrier((*owned, totals))
+    total_q, total_kv, total_out = (own[:own_rows].astype(jnp.float32) for own in owned[:3])
+    total_k, total_v = total_kv[:, :kdim], total_kv[:, kdim:]
+    mine = owned[3].reshape(-1, 8, 128)[:, 0].reshape(-1)[: 3 * own_rows].reshape(3, own_rows)
     total_gate, total_up, total_down = (total.astype(jnp.float32) for total in totals)
-    ends = (0, qdim, qdim + kdim, qdim + 2 * kdim, qdim + 2 * kdim + width)
-    total_q, total_k, total_v, total_out = (owned[:, a:b] for a, b in zip(ends, ends[1:]))
-    mine = owned[:, ends[-1] : ends[-1] + 3].T
     return (
         block_out.astype(jnp.bfloat16)[None],
         grad_tokens[None],

time: 597 us -> 401 us (0.67); the launches traced: 589 us -> 399 us
  waiting for transfers between devices: 185 us -> 68.8 us
  matrix products: 128 us -> 53 us
  Pallas kernels: 141 us -> 198 us
  local copies, waits for them, and re-layouts: 72.9 us -> 38 us
  other arithmetic: 45.3 us -> 25 us
    psum x1, waiting for transfers between devices: 77.3 us -> 0.02 us  [on_device(): totals = tuple((lax.psum(grad, 'ctx') for grad in grads))]
    dot_general x12 -> x9, matrix products: 95.8 us -> 20.2 us  [dot(): lax.dot_general(left, right, (((dims[0],), (dims[1],)), ((), ())), prefer...]
    pallas_call x2 -> x4, Pallas kernels: 86.7 us -> 144 us  [the longest x1 69.2 us: reduce_rows(): pl.pallas_call(functools.partial(reduce_rows_kernel, depth, count), out_s...]
    reduce_scatter x1, waiting for transfers between devices: 37.5 us -> 0.01 us  [on_device(): lax.psum_scatter(ffn_part, 'fsdp', scatter_dimension=0, tiled=True)]
    concatenate x3 -> x0, local copies, waits for them, and re-layouts: 21.1 us -> none  [the longest x2 11.9 us: on_device(): jnp.concatenate([grad_keys_all, grad_values_all], 1).astype(jnp.bfloat16)]
    reduce_sum x3, other arithmetic: 14.1 us -> 1.44 us  [the longest x1 1.14 us: on_device(): jnp.sum(grad_y * chosen_mask * increment, -1, keepdims=True) * gating]
    slice x10 -> x8, local copies, waits for them, and re-layouts: 14.3 us -> 3.89 us  [the longest x1 1.08 us: on_device(): grad_kv[:, :kdim]]
    unnamed x115 -> x78, local copies, waits for them, and re-layouts: 11.1 us -> 12.5 us
  transfers between devices with their start and end apart: 6 -> 6, of which waited for: 4 -> 3; matrix products, arithmetic and copies ran while one was open for 17% -> 21% of each run, Pallas kernels for 9% -> 50%
where the time goes in v3:
time: 401 us; the launch traced here: 399 us
  Pallas kernels  198 us (49%)
  waiting for transfers between devices  68.8 us (17%)
  matrix products  53 us (13%)
  local copies, waits for them, and re-layouts  38 us (9%)
  other arithmetic  25 us (6%)
  between operations  15.4 us (4%)
    pallas_call x1, Pallas kernels, reduce_rows(): pl.pallas_call(functools.partial(reduce_rows_kernel, depth, count), out_s...  69.2 us
    all_gather x1, waiting for transfers between devices, on_device(): normed_all = lax.all_gather(normed_two, 'fsdp', axis=0, tiled=True)  43.3 us
    pallas_call x1, Pallas kernels, gather_rows(): pl.pallas_call(functools.partial(gather_rows_kernel, depth), out_shape=ja...  32.3 us
    pallas_call x1, Pallas kernels, scatter_plane(): pl.pallas_call(scatter_plane_kernel, out_shape=jax.ShapeDtypeStruct(block...  30 us
    pallas_call x1, Pallas kernels, attend_back(): pl.pallas_call(attend_back_kernel, out_shape=(jax.ShapeDtypeStruct(querie...  29.6 us
    reduce_scatter x1, waiting for transfers between devices, on_device(): lax.psum_scatter(grad_normed_part, 'fsdp', scatter_dimension=0, tiled=True)  23.5 us
    pallas_call x1, Pallas kernels, gather_plane(): pl.pallas_call(gather_plane_kernel, out_shape=(jax.ShapeDtypeStruct((SPAN...  22 us
    dot_general x9, matrix products, dot(): lax.dot_general(left, right, (((dims[0],), (dims[1],)), ((), ())), prefer...  20.2 us
  transfers between devices with their start and end apart: 6, of which 3 were waited for; matrix products, arithmetic and copies ran while one was open for 21% of the time, Pallas kernels for 50%

profile of v3, /device:TPU:0, one launch (start us, length us, event | category | flops | bytes accessed | tf_op | source)
XLA Modules:
  0.0 399.3 jit_solution(11994760371002220776)
XLA Ops:
  8.0 1.1 copy.47
  9.1 1.1 copy.48
  10.1 0.8 stack.28
  10.9 0.8 stack.29
  11.6 0.8 stack.30
  12.4 1.3 concatenate.30
  13.7 1.0 pad.24
  14.7 32.3 %shard_map.238 = bf16[4,8,32,1603]{3,2,1,0:T(8,128)(2,1)} custom-call(bf16[8,32,1603]{2,1,0:T(8,128)(2,1)} %bitcast.154), custom_call_target="tpu_custom_call" | custom-call | bytes 98488320 | tf_op jit(solution)/shard_map/pallas_call | solution.py:188
  47.0 1.2 slice_convert_fusion.5
  49.9 0.9 fusion.9
  50.9 2.1 slice.89
  53.1 1.0 fusion.2
  54.9 3.0 slice.93
  58.5 0.9 pad_maximum_fusion.kv_ref
  59.9 22.0 %shard_map.239 = (bf16[8,256,640]{2,1,0:T(8,128)(2,1)}, s32[8,1,256]{2,1,0:T(1,128)}) custom-call(bf16[256,640]{1,0:T(8,128)(2,1)} %pad_maximum_fusion.kv_ref, s32[1,256]{1,0:T(1,128)} %and_select_fusion.tag_ref), custom_call_target="tpu_custom_call" | custom-call | bytes 78643200 | tf_op jit(solution)/shard_map/pallas_call | solution.py:238
  81.9 0.8 slice.74
  82.7 2.0 copy.56.tag_ref
  84.7 3.8 copy.63
  89.4 2.3 fusion.32
  91.9 0.9 maximum_multiply_fusion
  92.7 15.4 %shard_map.240 = (f32[960,256]{1,0:T(8,128)}, f32[16,256]{1,0:T(8,128)}) custom-call(s32[18]{0:T(128)} %pad_add_fusion.first_ref, bf16[960,256]{1,0:T(8,128)(2,1)} %bitcast.167, bf16[2048,640]{1,0:T(8,128)(2,1)} %bitcast.189, s32[1,256]{1,0:T(1,128)} %pos_ref.3, s32[2048,1]{1,0:T(8,128)} %copy.56.tag_ref), custom_call_target="tpu_custom_call" | custom-call | flops 16106127360 | bytes 2621440 | tf_op jit(solution)/shard_map/pallas_call | solution.py:546
  108.1 1.2 all-gather.4.cloned.1.call-done
  109.4 2.8 multiply_reduce_fusion.2
  112.2 1.0 multiply_convert_fusion.4
  113.4 5.3 %fusion.50 = f32[1024,640]{1,0:T(8,128)} fusion(bf16[1024,960]{0,1:T(8,128)(2,1)} %all-gather.4.cloned.1.call-done, bf16[640,960]{0,1:T(8,128)(2,1)} %param.22), kind=kOutput, calls=%fused_computation.122 | convolution fusion | flops 1258291200 | bytes 5816320 | tf_op jit(solution)/shard_map/dot_general | solution.py:75
  118.7 43.3 %all-gather.8.cloned.1.call-done = bf16[1024,960]{0,1:T(8,128)(2,1)} async-done(((bf16[256,960]{0,1:T(8,128)(2,1)}), bf16[1024,960]{0,1:T(8,128)(2,1)}) %all-gather.8.cloned.1.call-update) | async-done | bytes 1966096 | tf_op jit(solution)/shard_map/all_gather | solution.py:695
  162.0 3.9 fusion.51
  165.9 3.9 multiply_convert_fusion
  169.8 1.7 fusion.52
  171.5 3.0 add_convert_fusion
  175.1 0.9 pad.26
  176.0 4.7 %convolution_convert_fusion.2 = bf16[1024,960]{0,1:T(8,128)(2,1)} fusion(bf16[1024,640]{1,0:T(8,128)(2,1)} %get-tuple-element.80, bf16[640,960]{0,1:T(8,128)(2,1)} %param.22), kind=kOutput, calls=%fused_computation.8 | convolution fusion | flops 1259274240 | bytes 4505600 | tf_op jit(solution)/shard_map/dot_general | solution.py:702
  180.7 4.8 %convolution_convert_fusion.4 = bf16[640,960]{0,1:T(8,128)(2,1)} fusion(bf16[1024,960]{0,1:T(8,128)(2,1)} %all-gather.4.cloned.1.call-done, bf16[1024,640]{1,0:T(8,128)(2,1)} %get-tuple-element.80), kind=kOutput, calls=%fused_computation.10 | convolution fusion | flops 1258905600 | bytes 4505600 | tf_op jit(solution)/shard_map/dot_general | solution.py:709
  185.5 2.7 convolution_convert_fusion.5
  188.2 2.8 convolution_convert_fusion.6
  191.0 23.5 %reduce-scatter.3.cloned.1.call-done = bf16[256,960]{0,1:T(8,128)(2,1)} async-done(((bf16[1024,960]{0,1:T(8,128)(2,1)}), bf16[256,960]{0,1:T(8,128)(2,1)}) %reduce-scatter.3.cloned.1.call-update) | async-done | bytes 491536 | tf_op jit(solution)/shard_map/reduce_scatter | solution.py:699
  214.5 1.1 convert_element_type.193
  218.3 1.5 convert_multiply_fusion.2
  220.4 29.6 %shard_map.241 = (f32[960,256]{1,0:T(8,128)}, bf16[2048,640]{1,0:T(8,128)(2,1)}) custom-call(s32[18]{0:T(128)} %pad_add_fusion.first_ref, bf16[960,256]{1,0:T(8,128)(2,1)} %bitcast.168, bf16[2048,640]{1,0:T(8,128)(2,1)} %bitcast.190, s32[1,256]{1,0:T(1,128)} %pos_ref.3, s32[2048,1]{1,0:T(8,128)} %copy.56.tag_ref, ...), custom_call_target="tpu_custom_call" | custom-call | flops 30198988800 | bytes 5242880 | tf_op jit(solution)/shard_map/pallas_call | solution.py:614
  250.0 1.4 multiply_subtract_fusion.1
  251.4 0.8 maximum_convert_fusion
  252.2 2.0 convolution_convert_fusion
  254.2 1.0 copy-done.10
  255.4 2.0 convolution_convert_fusion.1
  257.4 30.0 %shard_map.242 = f32[8,32,640]{2,1,0:T(8,128)} custom-call(bf16[8,8,32,640]{3,2,1,0:T(8,128)(2,1)} %bitcast.155), custom_call_target="tpu_custom_call" | custom-call | bytes 78643200 | tf_op jit(solution)/shard_map/pallas_call | solution.py:340
  287.5 3.2 pad.27
  290.6 3.9 copy.60
  294.5 3.3 fusion.46
  297.8 2.1 convert_element_type.202
  299.9 1.1 copy.58
  301.0 1.1 slice.94
  302.1 1.0 slice.113
  303.2 1.1 fusion.11
  304.3 3.6 fusion.27
  308.9 1.7 convolution_convert_fusion.3
  310.6 69.2 %shard_map.243 = (bf16[8,32,960]{2,1,0:T(8,128)(2,1)}, bf16[8,32,640]{2,1,0:T(8,128)(2,1)}, bf16[8,32,960]{2,1,0:T(8,128)(2,1)}, f32[8,8,128]{2,1,0:T(8,128)}) custom-call(bf16[4,8,32,960]{3,2,1,0:T(8,128)(2,1)} %bitcast.144, bf16[4,8,32,640]{3,2,1,0:T(8,128)(2,1)} %bitcast.150, bf16[4,8,32,960]{3,2,1,0:T(8,128)(2,1)} %bitcast.143, f32[4,8,8,128]{3,2,1,0:T(8,128)} %pad.29.refs_3_), custom_call_target="tpu_custom_call" | custom-call | bytes 159252480 | tf_op jit(solution)/shard_map/pallas_call | solution.py:418
  379.9 3.0 convert_element_type.216
  382.9 1.6 convert_element_type.217
  384.7 1.6 convert_element_type.218
  386.6 0.9 fusion.48
  387.5 1.1 slice_convert_fusion
  388.5 1.1 slice_convert_fusion.1
  389.6 0.8 slice.99
  391.0 1.5 fusion.38
  (133 shorter events, 11.4 us)
Async XLA Ops:
  7.2 158.7 %copy-start = (bf16[640,960]{0,1:T(8,128)(2,1)S(1)}, bf16[640,960]{0,1:T(8,128)(2,1)}, u32[]{:S(2)}) copy-start(bf16[640,960]{0,1:T(8,128)(2,1)} %param.21) | copy-start | bytes 3686404
  7.2 100.9 %all-gather.6.cloned.1.call-start = ((), (), s32[]{:S(2)}) async-start(), calls=%async_computation.3 | async-start | bytes 2457600 | tf_op jit(solution)/shard_map/all_gather | solution.py:660
  7.9 101.4 %all-gather.4.cloned.1.call-start = ((), (), s32[]{:S(2)}) async-start(), calls=%async_computation.2 | async-start | bytes 2457600 | tf_op jit(solution)/shard_map/all_gather | solution.py:671
  14.7 34.3 %copy-start.26 = (s32[1,256]{1,0:T(1,128)S(1)}, s32[1,256]{1,0:T(1,128)}, u32[]{:S(2)}) copy-start(s32[1,256]{1,0:T(1,128)} %param.29) | copy-start | bytes 3076
  14.7 34.4 %copy-start.22 = (s32[1,256]{1,0:T(1,128)S(1)}, s32[1,256]{1,0:T(1,128)}, u32[]{:S(2)}) copy-start(s32[1,256]{1,0:T(1,128)} %pos_ref.3) | copy-start | bytes 3076
  14.7 34.4 %copy-start.2 = (bf16[1,256,960]{1,2,0:T(8,128)(2,1)S(1)}, bf16[1,256,960]{1,2,0:T(8,128)(2,1)}, u32[]{:S(2)}) copy-start(bf16[1,256,960]{1,2,0:T(8,128)(2,1)} %param.15) | copy-start | bytes 1474564
  47.0 2.9 copy-start.9
  50.9 111.1 %all-gather.8.cloned.1.call-start = ((), (), s32[]{:S(2)}) async-start(), calls=%async_computation.4 | async-start | bytes 2457600 | tf_op jit(solution)/shard_map/all_gather | solution.py:695
  53.1 1.6 copy-start.7
  113.2 101.3 %reduce-scatter.3.cloned.1.call-start = ((), (), s32[]{:S(2)}) async-start(), calls=%async_computation.5 | async-start | bytes 2457600 | tf_op jit(solution)/shard_map/reduce_scatter | solution.py:699
  162.0 3.9 copy-start.28
  162.0 3.9 copy-start.34
  165.9 3.9 copy-start.30
  169.8 1.7 copy-start.32
  169.8 1.7 copy-start.35
  174.6 123.3 %reduce-scatter.5.cloned.1.call-start = ((), (), s32[]{:S(2)}) async-start(), calls=%async_computation.6 | async-start | bytes 2457600 | tf_op jit(solution)/shard_map/reduce_scatter | solution.py:716
  180.7 4.8 %copy-start.29 = (bf16[1024,960]{0,1:T(8,128)(2,1)S(1)}, bf16[1024,960]{0,1:T(8,128)(2,1)}, u32[]{:S(2)}) copy-start(bf16[1024,960]{0,1:T(8,128)(2,1)} %all-gather.8.cloned.1.call-done) | copy-start | bytes 5898244
  180.7 4.8 %copy-start.36 = (bf16[1024,640]{1,0:T(8,128)(2,1)S(1)}, bf16[1024,640]{1,0:T(8,128)(2,1)}, u32[]{:S(2)}) copy-start(bf16[1024,640]{1,0:T(8,128)(2,1)} %copy-done.35) | copy-start | bytes 3932164
  185.5 2.7 copy-start.33
  215.6 1.0 copy-start.3
  216.1 163.8 %all-reduce.9.cloned.1.call-start = ((), (), s32[]{:S(2)}) async-start(), calls=%async_computation.7 | async-start | bytes 7372800 | tf_op jit(solution)/shard_map/psum | solution.py:719
  216.4 1.2 copy-start.5
  216.4 1.8 copy-start.8
  218.3 1.5 copy-start.11
  250.0 2.3 copy-start.6
  250.0 2.3 copy-start.12
  254.2 1.0 copy-start.10
  254.2 1.2 copy-start.15
  294.5 5.4 %copy-start.14 = (f32[8,32,640]{2,1,0:T(8,128)S(1)}, f32[8,32,640]{2,1,0:T(8,128)}, u32[]{:S(2)}) copy-start(f32[8,32,640]{2,1,0:T(8,128)} %shard_map.242) | copy-start | bytes 1966084
  301.0 2.2 copy-start.13
  303.1 1.2 copy-start.31
  304.3 3.7 copy-start.24
  379.9 3.0 copy-start.17
  382.9 1.8 copy-start.16
  384.7 1.6 copy-start.21
  386.4 1.0 copy-start.20
  386.4 2.1 copy-start.19
  386.5 4.5 %copy-start.27 = (f32[256]{0:T(256)S(1)}, f32[256]{0:T(256)}, u32[]{:S(2)}) copy-start(f32[256]{0:T(256)} %get-tuple-element.69) | copy-start | bytes 3076
  386.5 4.5 %copy-start.4 = (f32[256,960]{0,1:T(8,128)S(1)}, f32[256,960]{0,1:T(8,128)}, u32[]{:S(2)}) copy-start(f32[256,960]{0,1:T(8,128)} %copy-done.3) | copy-start | bytes 2949124
  386.5 4.5 %copy-start.18 = (f32[256,960]{0,1:T(8,128)S(1)}, f32[256,960]{0,1:T(8,128)}, u32[]{:S(2)}) copy-start(f32[256,960]{0,1:T(8,128)} %get-tuple-element.116) | copy-start | bytes 2949124
  386.5 4.5 %copy-start.23 = (f32[256]{0:T(256)S(1)}, f32[256]{0:T(256)}, u32[]{:S(2)}) copy-start(f32[256]{0:T(256)} %get-tuple-element.108) | copy-start | bytes 3076
  386.6 4.5 %copy-start.25 = (f32[256]{0:T(256)S(1)}, f32[256]{0:T(256)}, u32[]{:S(2)}) copy-start(f32[256]{0:T(256)} %copy-done.24) | copy-start | bytes 3076
  391.0 1.5 copy-start.1
Sparse Core Ops, SparseCore 0:
  9.6 54.4 all-gather.5
  66.2 43.0 all-gather.3
  113.3 48.6 all-gather.7
  174.7 39.7 reduce-scatter.2
  217.2 40.6 reduce-scatter.4
  261.5 103.9 all-reduce.8

commit v4 on v3

--- a/solution.py
+++ b/solution.py
@@ -60,10 +60,6 @@
     pads = [(0, 0)] * values.ndim
     pads[row_dim] = (0, -values.shape[row_dim] % 128)
     return jnp.pad(values, pads)
-
-
-def padded_rows_of(values, rows):
-    return jnp.pad(values, ((0, 0), (0, rows - values.shape[1]), (0, 0)))
 
 
 def ffn_both(normed, grad_mixed, gate_rows, up_rows, down_rows):
@@ -82,7 +78,9 @@
     grad_normed = jnp.dot(grad_gate_act, gate_rows, preferred_element_type=jnp.float32) + jnp.dot(
         grad_up_act, up_rows, preferred_element_type=jnp.float32
     )
-    return (inner_act, grad_gate_act, grad_up_act, grad_normed.astype(jnp.bfloat16))
+    row_dot = jnp.sum(inner_act.astype(jnp.float32) * grad_inner, -1, keepdims=True)
+    grad_normed = jnp.concatenate([grad_normed, row_dot], 1).astype(jnp.bfloat16)
+    return (inner_act, grad_gate_act, grad_up_act, grad_normed)
 
 
 CHIPS = 4
@@ -136,68 +134,84 @@
     return [pl.BlockSpec(memory_space=pltpu.VMEM)] * count
 
 
-def gather_rows_kernel(depth, own_ref, out_ref, z_sems, p_sems, f_sems):
+def gather_rows_kernel(depth, count, *refs):
+    owns, outs = refs[:count], refs[count : 2 * count]
+    z_sems, p_sems, f_sems = refs[2 * count :]
     me, core, chip, partner = plane_of()
     layer = lax.axis_index("fsdp")
     layers = [lax.rem(layer + d, depth) for d in range(1, depth)]
     peers = [chip_at(chip, core, j) for j in range(1, CHIPS)]
     greet([(me, other) for other in layers] + [(peer, layer) for peer in peers + [partner]])
-    first = [
-        send(own_ref.at[me], out_ref.at[layer, me], z_sems.at[0, d], z_sems.at[1, d], (me, other))
-        for d, other in enumerate(layers)
-    ]
-    for piece in range(SPAN):
-        out_ref[layer, piece] = own_ref[piece]
-    spread = []
-    for d, copy in enumerate(first):
-        copy.wait_recv()
-        source = lax.rem(layer + depth - d - 1, depth)
-        for j, peer in enumerate(peers):
-            block = out_ref.at[source, me]
-            spread.append(
-                send(block, block, p_sems.at[0, d, j], p_sems.at[1, d, j], (peer, layer))
+    first, spread, passed = [], [], []
+    for a, (own, out) in enumerate(zip(owns, outs)):
+        for d, other in enumerate(layers):
+            first.append(
+                send(
+                    own.at[me],
+                    out.at[layer, me],
+                    z_sems.at[0, a, d],
+                    z_sems.at[1, a, d],
+                    (me, other),
+                )
             )
-        block = out_ref.at[source, me]
-        first[d] = (
-            copy,
-            send(block, block, f_sems.at[0, d, 3], f_sems.at[1, d, 3], (partner, layer)),
-        )
-    passed = []
-    for d in range(depth - 1):
-        source = lax.rem(layer + depth - d - 1, depth)
-        for j in range(CHIPS - 1):
-            spread[d * (CHIPS - 1) + j].wait_recv()
-            block = out_ref.at[source, chip_at(chip, core, -j - 1)]
+    for own, out in zip(owns, outs):
+        for piece in range(SPAN):
+            out[layer, piece] = own[piece]
+    for a, out in enumerate(outs):
+        for d in range(depth - 1):
+            first[a * (depth - 1) + d].wait_recv()
+            block = out.at[lax.rem(layer + depth - d - 1, depth), me]
+            for j, peer in enumerate(peers):
+                spread.append(
+                    send(block, block, p_sems.at[0, a, d, j], p_sems.at[1, a, d, j], (peer, layer))
+                )
             passed.append(
-                send(block, block, f_sems.at[0, d, j], f_sems.at[1, d, j], (partner, layer))
+                send(block, block, f_sems.at[0, a, d, 3], f_sems.at[1, a, d, 3], (partner, layer))
             )
-    for copy, handed in first:
-        copy.wait_send()
-        handed.wait()
-    for copy in spread:
+    arrivals = iter(spread)
+    for a, out in enumerate(outs):
+        for d in range(depth - 1):
+            source = lax.rem(layer + depth - d - 1, depth)
+            for j in range(CHIPS - 1):
+                next(arrivals).wait_recv()
+                block = out.at[source, chip_at(chip, core, -j - 1)]
+                passed.append(
+                    send(
+                        block,
+                        block,
+                        f_sems.at[0, a, d, j],
+                        f_sems.at[1, a, d, j],
+                        (partner, layer),
+                    )
+                )
+    for copy in first + spread:
         copy.wait_send()
     for copy in passed:
         copy.wait()
 
 
-def gather_rows(own, depth):
+def gather_rows(arrays, depth):
     if lax.axis_size("ctx") != SPAN:
-        return lax.all_gather(own, "fsdp", axis=0)
-    rows, columns = own.shape
-    piece = rows // SPAN
-    return pl.pallas_call(
-        functools.partial(gather_rows_kernel, depth),
-        out_shape=jax.ShapeDtypeStruct((depth, SPAN, piece, columns), own.dtype),
-        in_specs=in_vmem(1),
-        out_specs=in_vmem(1)[0],
+        return [lax.all_gather(own, "fsdp", axis=0) for own in arrays]
+    count, pieces, outs = len(arrays), [], []
+    for own in arrays:
+        piece = (own.shape[0] // SPAN, own.shape[1])
+        pieces.append(own.reshape(SPAN, *piece))
+        outs.append(jax.ShapeDtypeStruct((depth, SPAN, *piece), own.dtype))
+    whole = pl.pallas_call(
+        functools.partial(gather_rows_kernel, depth, count),
+        out_shape=tuple(outs),
+        in_specs=in_vmem(count),
+        out_specs=tuple(in_vmem(count)),
         scratch_shapes=[
-            pltpu.SemaphoreType.DMA((2, depth - 1)),
-            pltpu.SemaphoreType.DMA((2, depth - 1, CHIPS - 1)),
-            pltpu.SemaphoreType.DMA((2, depth - 1, CHIPS)),
+            pltpu.SemaphoreType.DMA((2, count, depth - 1)),
+            pltpu.SemaphoreType.DMA((2, count, depth - 1, CHIPS - 1)),
+            pltpu.SemaphoreType.DMA((2, count, depth - 1, CHIPS)),
         ],
         compiler_params=comm_params(1),
-        cost_estimate=comm_cost(own.size * 2 * depth),
-    )(own.reshape(SPAN, piece, columns)).reshape(depth, rows, columns)
+        cost_estimate=comm_cost(sum(own.size for own in arrays) * 2 * depth),
+    )(*pieces)
+    return [full.reshape(depth, *own.shape) for full, own in zip(whole, arrays)]
 
 
 def gather_plane_kernel(kv_ref, tag_ref, kv_out, tag_out, p_sems, f_sems):
@@ -462,6 +476,7 @@
 
 
 def mask_bias(tags, query_pos):
+    tags = jnp.broadcast_to(tags, (BLOCK, BLOCK)).T
     key_pos = jnp.where(tags >= 0, tags, -tags - 1)
     allowed = (key_pos <= query_pos) & ((tags >= 0) | (key_pos == query_pos))
     bias = jnp.where(allowed, 0.0, negative)
@@ -489,7 +504,7 @@
             @pl.when(first_ref[kb] <= limit)
             def _():
                 rows = pl.ds(pl.multiple_of(kb * BLOCK, BLOCK), BLOCK)
-                bias = mask_bias(tag_ref[rows, :], pos_ref[:, at])
+                bias = mask_bias(tag_ref[kb], pos_ref[:, at])
                 for group in range(KV_HEADS):
                     found = scores(group, at, rows, bias)
                     if keep:
@@ -508,7 +523,7 @@
             @pl.when(first_ref[kb] <= limit)
             def _():
                 rows = pl.ds(pl.multiple_of(kb * BLOCK, BLOCK), BLOCK)
-                bias = None if keep else mask_bias(tag_ref[rows, :], pos_ref[:, at])
+                bias = None if keep else mask_bias(tag_ref[kb], pos_ref[:, at])
                 for group in range(KV_HEADS):
                     found = kept[kb, group] if keep else scores(group, at, rows, bias)
                     weights = jnp.exp(found - max_ref[group, :1])
@@ -561,13 +576,14 @@
         cost_estimate=pl.CostEstimate(
             flops=work * 8, bytes_accessed=kv.size * 2, transcendentals=work // 256
         ),
-    )(firsts, queries, kv, query_pos[None], key_tags[:, None])
+    )(firsts, queries, kv, query_pos[None], key_tags.reshape(-1, 1, BLOCK))
 
 
 def attend_back_kernel(
-    first_ref, q_ref, kv_ref, pos_ref, tag_ref, grad_ref, log_ref, delta_ref, dq_ref, dkv_ref, acc
+    first_ref, q_ref, kv_ref, pos_ref, tag_ref, grad_ref, log_ref, delta_ref, *refs
 ):
     blocks = kv_ref.shape[0] // BLOCK
+    cos_ref, sin_ref, out_ref, dkv_ref, acc, dq_ref = refs
     dq_ref[...] = jnp.zeros(dq_ref.shape, dq_ref.dtype)
 
     def key_block(kb, carry):
@@ -578,7 +594,7 @@
             @pl.when(first_ref[kb] <= first_ref[blocks + qb])
             def _():
                 at = pl.ds(pl.multiple_of(qb * BLOCK, BLOCK), BLOCK)
-                bias = mask_bias(tag_ref[rows, :], pos_ref[:, at])
+                bias = mask_bias(tag_ref[kb], pos_ref[:, at])
                 for group in range(KV_HEADS):
                     keys = kv_ref[rows, columns_of(group, 0)]
                     values = kv_ref[rows, columns_of(group, 1)]
@@ -606,25 +622,45 @@
         return carry
 
     lax.fori_loop(0, blocks, key_block, 0)
-
-
-def attend_back(firsts, queries, kv, query_pos, key_tags, grads, log_total, row_delta):
+    half_dim = HEAD // 2
+
+    def finish(qb, carry):
+        at = pl.ds(pl.multiple_of(qb * BLOCK, BLOCK), BLOCK)
+        cos_tab, sin_tab = cos_ref[:, at], sin_ref[:, at]
+        for head in range(0, HEADS, 2):
+            pair = []
+            for start in range(head * HEAD, min(head + 2, HEADS) * HEAD, HEAD):
+                low = dq_ref[start : start + half_dim, at]
+                high = dq_ref[start + half_dim : start + HEAD, at]
+                pair += [low * cos_tab + high * sin_tab, high * cos_tab - low * sin_tab]
+            turned = jnp.concatenate(pair, 0).T
+            own = slice(head * HEAD, head * HEAD + turned.shape[1])
+            out_ref[at, own] = turned.astype(out_ref.dtype)
+        return carry
+
+    lax.fori_loop(0, q_ref.shape[1] // BLOCK, finish, 0)
+
+
+def attend_back(firsts, queries, kv, query_pos, key_tags, grads, log_total, row_delta, tables):
     slots = queries.shape[1]
     work = 10 * kv.shape[0] * slots * HEADS * HEAD
     return pl.pallas_call(
         attend_back_kernel,
         out_shape=(
-            jax.ShapeDtypeStruct(queries.shape, jnp.float32),
+            jax.ShapeDtypeStruct(queries.shape[::-1], jnp.bfloat16),
             jax.ShapeDtypeStruct(kv.shape, jnp.bfloat16),
         ),
-        in_specs=[pl.BlockSpec(memory_space=pltpu.SMEM)] + in_vmem(7),
+        in_specs=[pl.BlockSpec(memory_space=pltpu.SMEM)] + in_vmem(9),
         out_specs=tuple(in_vmem(2)),
-        scratch_shapes=[pltpu.VMEM((2 * KV_HEADS, BLOCK, HEAD), jnp.float32)],
+        scratch_shapes=[
+            pltpu.VMEM((2 * KV_HEADS, BLOCK, HEAD), jnp.float32),
+            pltpu.VMEM(queries.shape, jnp.float32),
+        ],
         compiler_params=kernel_params(),
         cost_estimate=pl.CostEstimate(
             flops=work * 6, bytes_accessed=kv.size * 4, transcendentals=work // 640
         ),
-    )(firsts, queries, kv, query_pos[None], key_tags[:, None], grads, log_total, row_delta)
+    )(firsts, queries, kv, query_pos[None], key_tags.reshape(-1, 1, BLOCK), grads, log_total, row_delta, *tables)
 
 
 def on_device(
@@ -659,10 +695,10 @@
     own_rows = w_query.shape[0]
     w_out_full = lax.all_gather(w_out, "fsdp", axis=0, tiled=True)
     vectors = jnp.stack([gain_attn, gain_ffn, router], 1)
-    own_attn = padded_to(jnp.concatenate([w_query, w_key, w_value, vectors], 1), 0)
-    gathered = gather_rows(own_attn, depth)[:, :own_rows]
-    w_qkv = gathered[..., : qdim + 2 * kdim].reshape(width, qdim + 2 * kdim)
-    vectors = gathered[..., qdim + 2 * kdim : qdim + 2 * kdim + 3].reshape(width, 3)
+    own_attn = [w_query, jnp.concatenate([w_key, w_value, vectors], 1)]
+    gathered = gather_rows([padded_to(own, 0) for own in own_attn], depth)
+    w_query, gathered = (full[:, :own_rows].reshape(width, -1) for full in gathered)
+    w_kv, vectors = gathered[:, : 2 * kdim], gathered[:, 2 * kdim :]
     gain_one, gain_two, router_vec = vectors.T.astype(jnp.float32)
     gating = jax.nn.sigmoid(jnp.sum(hidden * router_vec, -1, keepdims=True))
     grad_y = cotangent[0].astype(jnp.float32) * live_mask
@@ -672,8 +708,6 @@
 
     normed_one, inv_one = norm_forward(hidden, gain_one)
     normed_one = normed_one.astype(jnp.bfloat16)
-    w_kv = w_qkv[:, qdim:]
-    w_query = w_qkv[:, :qdim]
     query_raw = dot(w_query, normed_one, (0, 1))
     queries = rotate_columns(query_raw, cos_tab, sin_tab).astype(jnp.bfloat16) * 0.125
     kv_raw = dot(normed_one, w_kv)
@@ -713,38 +747,39 @@
     grad_normed_two, ffn_part, *grads = lax.optimization_barrier(
         (grad_normed_two, ffn_part, *(g.astype(low) for g in (grad_wgate, grad_wup, grad_wdown)))
     )
-    ffn_out = lax.psum_scatter(ffn_part, "fsdp", scatter_dimension=0, tiled=True).astype(
-        jnp.float32
-    )
+    grad_normed_two, row_dot = grad_normed_two[:, :width], grad_normed_two[:, width:]
     totals = tuple(lax.psum(grad, "ctx") for grad in grads)
     grad_middle, grad_gain_two = norm_backward(middle, inv_two, gain_two, grad_normed_two)
     grad_branch = (grad_inc + grad_middle).astype(jnp.bfloat16)
     grad_attended = dot(w_out_full, grad_branch, (1, 1)).astype(jnp.bfloat16)
-    grad_wout = dot(outcome, grad_branch)
+    spread_out = padded_to(outcome.reshape(depth, own_rows, row_count), 1)
+    grad_wout = dot(spread_out.reshape(-1, row_count), grad_branch).astype(low)
     row_delta = jnp.sum(
         (grad_attended.astype(jnp.float32) * attended).reshape(HEADS, HEAD, row_count), 1
     )
     row_delta = jnp.pad(row_delta, ((0, 1), (0, 0)))
-    grad_qrot, grad_kv_all = attend_back(
-        firsts, queries, kv_all, query_pos, tags_all, grad_attended, log_total, row_delta
+    grad_query_raw, grad_kv_all = attend_back(
+        firsts,
+        queries,
+        kv_all,
+        query_pos,
+        tags_all,
+        grad_attended,
+        log_total,
+        row_delta,
+        (cos_tab.T, sin_tab.T),
     )
     grad_kv = scatter_plane(grad_kv_all)
-    grad_kv, ffn_out = lax.optimization_barrier((grad_kv, ffn_out))
-    increment = branch + ffn_out
-    block_out = live_mask * (hidden + chosen_mask * gating * increment)
-    grad_logit = (
-        jnp.sum(grad_y * chosen_mask * increment, -1, keepdims=True) * gating * (1.0 - gating)
-    )
+    grad_logit = (jnp.sum(grad_inc * branch, -1, keepdims=True) + row_dot) * (1.0 - gating)
     grad_router = jnp.sum(hidden * grad_logit, 0)
-    grad_query_raw = rotate_columns(grad_qrot, cos_tab, -sin_tab).astype(jnp.bfloat16)
     grad_kv_raw = jnp.concatenate(
         [rotate(grad_kv[:, :kdim], cos_tab, -sin_tab), grad_kv[:, kdim:]], 1
     ).astype(jnp.bfloat16)
-    grad_normed_one = dot(grad_query_raw, w_query, (0, 1)) + dot(grad_kv_raw, w_kv, (1, 1))
+    grad_normed_one = dot(grad_query_raw, w_query, (1, 1)) + dot(grad_kv_raw, w_kv, (1, 1))
     spread_one = padded_to(normed_one.reshape(row_count, depth, own_rows), -1)
     spread_one = spread_one.reshape(row_count, -1)
     padded_rows = spread_one.shape[1] // depth
-    grad_wq = dot(spread_one, grad_query_raw, (0, 1)).astype(low)
+    grad_wq = dot(spread_one, grad_query_raw, (0, 0)).astype(low)
     grad_wkv = dot(spread_one, grad_kv_raw, (0, 0)).astype(low)
     grad_hidden_one, grad_gain_one = norm_backward(hidden, inv_one, gain_one, grad_normed_one)
     grad_tokens = (grad_y + grad_logit * router_vec + grad_middle + grad_hidden_one).astype(
@@ -753,11 +788,13 @@
     vectors = jnp.stack([grad_gain_one, grad_gain_two, grad_router]).reshape(3, depth, own_rows)
     vectors = jnp.pad(vectors.transpose(1, 0, 2).reshape(depth, -1), ((0, 0), (0, -3 * own_rows % 1024)))
     vectors = jnp.pad(vectors.reshape(depth, -1, 1, 128), ((0, 0), (0, 0), (0, 7), (0, 0)))
-    layered = [grad.reshape(depth, padded_rows, -1) for grad in (grad_wq, grad_wkv)]
-    layered.append(padded_rows_of(grad_wout.astype(low).reshape(depth, own_rows, -1), padded_rows))
+    layered = [grad.reshape(depth, padded_rows, -1) for grad in (grad_wq, grad_wkv, grad_wout)]
     layered.append(vectors.reshape(depth, -1, 128))
     owned = reduce_rows(layered, 4)
-    *owned, totals = lax.optimization_barrier((*owned, totals))
+    ffn_out = lax.psum_scatter(ffn_part, "fsdp", scatter_dimension=0, tiled=True)
+    *owned, totals, ffn_out = lax.optimization_barrier((*owned, totals, ffn_out))
+    increment = branch + ffn_out.astype(jnp.float32)
+    block_out = live_mask * (hidden + chosen_mask * gating * increment)
     total_q, total_kv, total_out = (own[:own_rows].astype(jnp.float32) for own in owned[:3])
     total_k, total_v = total_kv[:, :kdim], total_kv[:, kdim:]
     mine = owned[3].reshape(-1, 8, 128)[:, 0].reshape(-1)[: 3 * own_rows].reshape(3, own_rows)

time: 401 us -> 388 us (0.968)
  Pallas kernels: 198 us -> 189 us
  matrix products: 53 us -> 45.7 us
    pallas_call x1, Pallas kernels: 69.2 us -> 60.7 us  [reduce_rows(): pl.pallas_call(functools.partial(reduce_rows_kernel, depth, count), out_s...]
    unnamed x78 -> x120, local copies, waits for them, and re-layouts: 12.5 us -> 5.7 us
  transfers between devices with their start and end apart: 6 -> 6, of which waited for: 3 -> 3; matrix products, arithmetic and copies ran while one was open for 21% -> 19% of each run, Pallas kernels for 50% -> 49%
where the time goes in v4:
time: 388 us; the launch traced here: 386 us
  Pallas kernels  189 us (49%)
  waiting for transfers between devices  71.4 us (18%)
  matrix products  45.7 us (12%)
  local copies, waits for them, and re-layouts  38.6 us (10%)
  other arithmetic  25.4 us (7%)
  between operations  15.7 us (4%)
    pallas_call x1, Pallas kernels, reduce_rows(): pl.pallas_call(functools.partial(reduce_rows_kernel, depth, count), out_s...  60.7 us
    all_gather x1, waiting for transfers between devices, on_device(): normed_all = lax.all_gather(normed_two, 'fsdp', axis=0, tiled=True)  44.2 us
    pallas_call x1, Pallas kernels, gather_rows(): pl.pallas_call(functools.partial(gather_rows_kernel, depth, count), out_s...  34.9 us
    pallas_call x1, Pallas kernels, attend_back(): pl.pallas_call(attend_back_kernel, out_shape=(jax.ShapeDtypeStruct(querie...  28.9 us
    pallas_call x1, Pallas kernels, scatter_plane(): pl.pallas_call(scatter_plane_kernel, out_shape=jax.ShapeDtypeStruct(block...  27.1 us
    reduce_scatter x1, waiting for transfers between devices, on_device(): lax.psum_scatter(grad_normed_part, 'fsdp', scatter_dimension=0, tiled=True)  25.5 us
    pallas_call x1, Pallas kernels, gather_plane(): pl.pallas_call(gather_plane_kernel, out_shape=(jax.ShapeDtypeStruct((SPAN...  22.1 us
    dot_general x9, matrix products, dot(): lax.dot_general(left, right, (((dims[0],), (dims[1],)), ((), ())), prefer...  18.5 us
  transfers between devices with their start and end apart: 6, of which 3 were waited for; matrix products, arithmetic and copies ran while one was open for 19% of the time, Pallas kernels for 49%

profile of v4, /device:TPU:0, one launch (start us, length us, event | category | flops | bytes accessed | tf_op | source)
XLA Modules:
  0.0 386.2 jit_solution(5334334529203673088)
XLA Ops:
  7.2 0.7 all-gather.6.cloned.1.call-update
  10.0 1.9 concatenate.31
  12.0 0.8 pad.29.clone
  12.8 0.8 pad.28
  13.7 34.9 %shard_map.238 = (bf16[4,8,32,960]{3,2,1,0:T(8,128)(2,1)}, bf16[4,8,32,643]{3,2,1,0:T(8,128)(2,1)}) custom-call(bf16[8,32,960]{2,1,0:T(8,128)(2,1)} %bitcast.158, bf16[8,32,643]{2,1,0:T(8,128)(2,1)} %bitcast.166), custom_call_target="tpu_custom_call" | custom-call | bytes 98488320 | tf_op jit(solution)/shard_map/pallas_call | solution.py:201
  48.6 1.6 slice.93
  50.1 1.1 copy-done.12
  53.1 0.9 fusion.9
  54.1 2.0 fusion.1
  56.6 0.8 fusion.39
  57.6 0.9 pad_maximum_fusion.1.kv_ref
  59.0 22.1 %shard_map.239 = (bf16[8,256,640]{2,1,0:T(8,128)(2,1)}, s32[8,1,256]{2,1,0:T(1,128)}) custom-call(bf16[256,640]{1,0:T(8,128)(2,1)} %pad_maximum_fusion.1.kv_ref, s32[1,256]{1,0:T(1,128)} %and_select_fusion.tag_ref), custom_call_target="tpu_custom_call" | custom-call | bytes 78643200 | tf_op jit(solution)/shard_map/pallas_call | solution.py:252
  81.1 0.8 slice.77
  81.9 3.0 slice.98
  84.9 3.8 copy.36
  89.6 2.4 fusion.32
  92.1 0.9 maximum_multiply_fusion
  93.0 15.2 %shard_map.240 = (f32[960,256]{1,0:T(8,128)}, f32[16,256]{1,0:T(8,128)}) custom-call(s32[18]{0:T(128)} %pad_add_fusion.first_ref, bf16[960,256]{1,0:T(8,128)(2,1)} %bitcast.173, bf16[2048,640]{1,0:T(8,128)(2,1)} %bitcast.197, s32[1,256]{1,0:T(1,128)} %pos_ref.3, s32[16,1,128]{2,1,0:T(1,128)} %bitcast.200), custom_call_target="tpu_custom_call" | custom-call | flops 16106127360 | bytes 2621440 | tf_op jit(solution)/shard_map/pallas_call | solution.py:561
  108.2 0.9 all-gather.4.cloned.1.call-done
  109.1 1.2 convert_element_type.174
  110.4 2.7 multiply_reduce_fusion.3
  113.1 1.0 multiply_convert_fusion.3
  114.3 44.2 %all-gather.8.cloned.1.call-done = bf16[1024,960]{0,1:T(8,128)(2,1)} async-done(((bf16[256,960]{0,1:T(8,128)(2,1)}), bf16[1024,960]{0,1:T(8,128)(2,1)}) %all-gather.8.cloned.1.call-update) | async-done | bytes 1966096 | tf_op jit(solution)/shard_map/all_gather | solution.py:729
  158.5 3.6 fusion.46
  162.2 1.6 fusion.47
  163.8 3.8 multiply_reduce_fusion
  167.6 1.7 fusion.49
  169.7 1.7 add_convert_fusion
  171.5 1.4 pad_maximum_fusion
  173.0 4.3 %convolution_convert_fusion.2 = bf16[1024,960]{0,1:T(8,128)(2,1)} fusion(bf16[640,960]{0,1:T(8,128)(2,1)S(1)} %copy-done, bf16[1024,640]{0,1:T(8,128)(2,1)} %get-tuple-element.83), kind=kOutput, calls=%fused_computation.10 | convolution fusion | flops 1259274240 | bytes 4505600 | tf_op jit(solution)/shard_map/dot_general | solution.py:736
  177.3 4.9 %convolution_convert_fusion.4 = bf16[640,960]{0,1:T(8,128)(2,1)} fusion(bf16[1024,640]{0,1:T(8,128)(2,1)} %get-tuple-element.83, bf16[1024,960]{0,1:T(8,128)(2,1)} %all-gather.4.cloned.1.call-done), kind=kOutput, calls=%fused_computation.12 | convolution fusion | flops 1258905600 | bytes 4505600 | tf_op jit(solution)/shard_map/dot_general | solution.py:743
  182.2 2.7 convolution_convert_fusion.5
  184.9 2.9 convolution_convert_fusion.6
  187.8 25.5 %reduce-scatter.3.cloned.1.call-done = bf16[256,961]{0,1:T(8,128)(2,1)} async-done(((bf16[1024,961]{0,1:T(8,128)(2,1)}), bf16[256,961]{0,1:T(8,128)(2,1)}) %reduce-scatter.3.cloned.1.call-update) | async-done | bytes 492048 | tf_op jit(solution)/shard_map/reduce_scatter | solution.py:733
  213.3 1.1 convert_element_type.183
  215.0 0.8 pad.30
  216.4 1.9 pad.32
  218.2 1.1 multiply_reduce_fusion.1
  219.8 0.7 copy-done.9
  221.2 1.8 convert_multiply_fusion.2
  223.0 1.3 reduce_sum.104
  224.9 28.9 %shard_map.241 = (bf16[256,960]{1,0:T(8,128)(2,1)}, bf16[2048,640]{1,0:T(8,128)(2,1)}) custom-call(s32[18]{0:T(128)} %pad_add_fusion.first_ref, bf16[960,256]{1,0:T(8,128)(2,1)} %bitcast.174, bf16[2048,640]{1,0:T(8,128)(2,1)} %bitcast.198, s32[1,256]{1,0:T(1,128)} %pos_ref.3, s32[16,1,128]{2,1,0:T(1,128)} %bitcast.201, ...), custom_call_target="tpu_custom_call" | custom-call | flops 30198988800 | bytes 5242880 | tf_op jit(solution)/shard_map/pallas_call | solution.py:647
  253.7 27.1 %shard_map.242 = f32[8,32,640]{2,1,0:T(8,128)} custom-call(bf16[8,8,32,640]{3,2,1,0:T(8,128)(2,1)} %bitcast.155), custom_call_target="tpu_custom_call" | custom-call | bytes 78643200 | tf_op jit(solution)/shard_map/pallas_call | solution.py:354
  280.8 1.8 slice.99
  282.6 1.1 slice.100
  283.8 1.2 copy.46
  285.0 0.8 copy.47
  285.9 0.8 add_multiply_fusion
  286.7 2.4 fusion.48
  289.2 1.6 fusion.28
  291.9 2.0 convolution_convert_fusion
  293.9 4.0 %copy.40 = bf16[1024,960]{1,0:T(8,128)(2,1)} copy(bf16[1024,960]{0,1:T(8,128)(2,1)} %convolution_convert_fusion) | data formatting | bytes 3932160 | tf_op jit(solution)/shard_map/convert_element_type | solution.py:756
  297.8 2.0 convolution_convert_fusion.1
  299.9 3.9 %copy.37 = bf16[1024,960]{1,0:T(8,128)(2,1)} copy(bf16[1024,960]{0,1:T(8,128)(2,1)} %convolution_convert_fusion.1) | data formatting | bytes 3932160 | tf_op jit(solution)/shard_map/convert_element_type | solution.py:782
  303.8 1.7 convolution_convert_fusion.3
  305.4 60.7 %shard_map.243 = (bf16[8,32,960]{2,1,0:T(8,128)(2,1)}, bf16[8,32,640]{2,1,0:T(8,128)(2,1)}, bf16[8,32,960]{2,1,0:T(8,128)(2,1)}, f32[8,8,128]{2,1,0:T(8,128)}) custom-call(bf16[4,8,32,960]{3,2,1,0:T(8,128)(2,1)} %bitcast.150, bf16[4,8,32,640]{3,2,1,0:T(8,128)(2,1)} %bitcast.151, bf16[4,8,32,960]{3,2,1,0:T(8,128)(2,1)} %bitcast.149, f32[4,8,8,128]{3,2,1,0:T(8,128)} %pad.34.refs_3_), custom_call_target="tpu_custom_call" | custom-call | bytes 159252480 | tf_op jit(solution)/shard_map/pallas_call | solution.py:432
  366.2 3.0 convert_element_type.200
  369.2 1.6 convert_element_type.201
  371.0 1.6 convert_element_type.202
  372.9 0.9 fusion.42
  373.8 1.1 slice_convert_fusion
  374.9 1.1 slice_convert_fusion.1
  375.9 0.8 slice.104
  377.4 1.9 fusion.38
  (175 shorter events, 11.5 us)
Async XLA Ops:
  7.2 156.6 %copy-start = (bf16[640,960]{0,1:T(8,128)(2,1)S(1)}, bf16[640,960]{0,1:T(8,128)(2,1)}, u32[]{:S(2)}) copy-start(bf16[640,960]{0,1:T(8,128)(2,1)} %param.22) | copy-start | bytes 3686404
  7.2 5.6 %copy-start.20 = (bf16[240,960]{1,0:T(8,128)(2,1)S(1)}, bf16[240,960]{1,0:T(8,128)(2,1)}, u32[]{:S(2)}) copy-start(bf16[240,960]{1,0:T(8,128)(2,1)} %param.16) | copy-start | bytes 1382404
  7.2 101.0 %all-gather.6.cloned.1.call-start = ((), (), s32[]{:S(2)}) async-start(), calls=%async_computation.3 | async-start | bytes 2457600 | tf_op jit(solution)/shard_map/all_gather | solution.py:696
  7.9 101.2 %all-gather.4.cloned.1.call-start = ((), (), s32[]{:S(2)}) async-start(), calls=%async_computation.2 | async-start | bytes 2457600 | tf_op jit(solution)/shard_map/all_gather | solution.py:707
  48.5 3.6 copy-start.48
  48.5 3.7 copy-start.2
  48.5 3.9 %copy-start.44 = (s32[1,256]{1,0:T(1,128)S(1)}, s32[1,256]{1,0:T(1,128)}, u32[]{:S(2)}) copy-start(s32[1,256]{1,0:T(1,128)} %pos_ref.3) | copy-start | bytes 3076
  48.6 4.5 %copy-start.5 = (bf16[1,256,960]{1,2,0:T(8,128)(2,1)S(1)}, bf16[1,256,960]{1,2,0:T(8,128)(2,1)}, u32[]{:S(2)}) copy-start(bf16[1,256,960]{1,2,0:T(8,128)(2,1)} %param.26) | copy-start | bytes 1474564
  50.1 1.1 copy-start.12
  52.2 4.0 %copy-start.30 = (f32[1,960]{1,0:T(1,128)}, f32[1,960]{1,0:T(1,128)S(1)}, u32[]{:S(2)}) copy-start(f32[1,960]{1,0:T(1,128)S(1)} %get-tuple-element.99) | copy-start | bytes 11524
  52.2 37.4 %copy-start.36 = (f32[1,960]{1,0:T(1,128)}, f32[1,960]{1,0:T(1,128)S(1)}, u32[]{:S(2)}) copy-start(f32[1,960]{1,0:T(1,128)S(1)} %get-tuple-element.98) | copy-start | bytes 11524
  52.2 167.1 %copy-start.28 = (f32[1,960]{1,0:T(1,128)}, f32[1,960]{1,0:T(1,128)S(1)}, u32[]{:S(2)}) copy-start(f32[1,960]{1,0:T(1,128)S(1)} %get-tuple-element.96) | copy-start | bytes 11524
  53.1 161.7 %copy-start.38 = (f32[256]{0:T(256)}, f32[256]{0:T(256)S(1)}, u32[]{:S(2)}) copy-start(f32[256]{0:T(256)S(1)} %get-tuple-element.109) | copy-start | bytes 3076
  53.1 166.3 %copy-start.34 = (f32[256]{0:T(256)}, f32[256]{0:T(256)S(1)}, u32[]{:S(2)}) copy-start(f32[256]{0:T(256)S(1)} %get-tuple-element.112) | copy-start | bytes 3076
  54.0 104.5 %all-gather.8.cloned.1.call-start = ((), (), s32[]{:S(2)}) async-start(), calls=%async_computation.4 | async-start | bytes 2457600 | tf_op jit(solution)/shard_map/all_gather | solution.py:729
  89.6 2.6 copy-start.26
  89.6 2.5 copy-start.27
  110.4 2.7 copy-start.14
  113.1 106.3 %copy-start.32 = (f32[256]{0:T(256)}, f32[256]{0:T(256)S(1)}, u32[]{:S(2)}) copy-start(f32[256]{0:T(256)S(1)} %get-tuple-element.111) | copy-start | bytes 3076
  113.1 106.3 %copy-start.40 = (f32[256]{0:T(256)}, f32[256]{0:T(256)S(1)}, u32[]{:S(2)}) copy-start(f32[256]{0:T(256)S(1)} %get-tuple-element.110) | copy-start | bytes 3076
  114.1 99.2 %reduce-scatter.3.cloned.1.call-start = ((), (), s32[]{:S(2)}) async-start(), calls=%async_computation.5 | async-start | bytes 2478080 | tf_op jit(solution)/shard_map/reduce_scatter | solution.py:733
  158.5 3.6 copy-start.50
  158.5 3.6 copy-start.52
  162.2 1.6 copy-start.49
  167.6 1.7 copy-start.54
  167.6 1.7 copy-start.56
  167.6 2.2 copy-start.53
  172.9 193.2 %all-reduce.10.cloned.1.call-start = ((), (), s32[]{:S(2)}) async-start(), calls=%async_computation.7 | async-start | bytes 7372800 | tf_op jit(solution)/shard_map/psum | solution.py:751
  177.3 4.9 %copy-start.51 = (bf16[1024,960]{0,1:T(8,128)(2,1)S(1)}, bf16[1024,960]{0,1:T(8,128)(2,1)}, u32[]{:S(2)}) copy-start(bf16[1024,960]{0,1:T(8,128)(2,1)} %all-gather.8.cloned.1.call-done) | copy-start | bytes 5898244
  177.3 4.9 %copy-start.57 = (bf16[1024,640]{0,1:T(8,128)(2,1)S(1)}, bf16[1024,640]{0,1:T(8,128)(2,1)}, u32[]{:S(2)}) copy-start(bf16[1024,640]{0,1:T(8,128)(2,1)} %copy-done.56) | copy-start | bytes 3932164
  182.2 2.8 copy-start.55
  214.4 71.5 %copy-start.3 = (f32[256,961]{0,1:T(8,128)}, f32[256,961]{0,1:T(8,128)S(1)}, u32[]{:S(2)}) copy-start(f32[256,961]{0,1:T(8,128)S(1)} %convert_element_type.183) | copy-start | bytes 2952196
  214.4 151.8 %reduce-scatter.5.cloned.1.call-start = ((), (), s32[]{:S(2)}) async-start(), calls=%async_computation.6 | async-start | bytes 2457600 | tf_op jit(solution)/shard_map/reduce_scatter | solution.py:794
  219.3 1.2 copy-start.9
  219.3 1.9 copy-start.15
  219.3 3.6 copy-start.42
  221.2 1.8 copy-start.7
  253.7 32.0 %copy-start.25 = (f32[256,32]{0,1:T(8,128)S(1)}, f32[256,32]{0,1:T(8,128)}, u32[]{:S(2)}) copy-start(f32[256,32]{0,1:T(8,128)} %get-tuple-element.103) | copy-start | bytes 98308
  280.8 5.1 %copy-start.45 = (f32[256]{0:T(256)S(1)}, f32[256]{0:T(256)}, u32[]{:S(2)}) copy-start(f32[256]{0:T(256)} %get-tuple-element.72) | copy-start | bytes 3076
  285.8 3.3 copy-start.13
  285.8 3.3 copy-start.19
  285.8 3.3 copy-start.37
  285.8 3.3 copy-start.39
  289.2 2.7 copy-start.8
  289.2 2.7 copy-start.10
  293.9 4.0 %copy-start.6 = (bf16[256,4,256]{0,2,1:T(8,128)(2,1)S(1)}, bf16[256,4,256]{0,2,1:T(8,128)(2,1)}, u32[]{:S(2)}) copy-start(bf16[256,4,256]{0,2,1:T(8,128)(2,1)} %pad.30) | copy-start | bytes 1572868
  293.9 4.0 %copy-start.11 = (bf16[256,960]{1,0:T(8,128)(2,1)S(1)}, bf16[256,960]{1,0:T(8,128)(2,1)}, u32[]{:S(2)}) copy-start(bf16[256,960]{1,0:T(8,128)(2,1)} %get-tuple-element.50) | copy-start | bytes 1474564
  366.2 3.0 copy-start.17
  369.2 1.8 copy-start.16
  371.0 1.6 copy-start.24
  372.8 1.1 copy-start.23
  372.8 2.1 copy-start.22
  372.8 4.5 %copy-start.4 = (f32[256,961]{0,1:T(8,128)S(1)}, f32[256,961]{0,1:T(8,128)}, u32[]{:S(2)}) copy-start(f32[256,961]{0,1:T(8,128)} %copy-done.3) | copy-start | bytes 2952196
  372.8 4.5 %copy-start.18 = (f32[256,960]{0,1:T(8,128)S(1)}, f32[256,960]{0,1:T(8,128)}, u32[]{:S(2)}) copy-start(f32[256,960]{0,1:T(8,128)} %get-tuple-element.118) | copy-start | bytes 2949124
  372.9 4.5 %copy-start.21 = (bf16[256,960]{0,1:T(8,128)(2,1)S(1)}, bf16[256,960]{0,1:T(8,128)(2,1)}, u32[]{:S(2)}) copy-start(bf16[256,960]{0,1:T(8,128)(2,1)} %reduce-scatter.5.cloned.1.call-done) | copy-start | bytes 1474564
  372.9 4.5 %copy-start.29 = (f32[1,960]{1,0:T(1,128)S(1)}, f32[1,960]{1,0:T(1,128)}, u32[]{:S(2)}) copy-start(f32[1,960]{1,0:T(1,128)} %copy-done.28) | copy-start | bytes 11524
  372.9 4.5 %copy-start.31 = (f32[1,960]{1,0:T(1,128)S(1)}, f32[1,960]{1,0:T(1,128)}, u32[]{:S(2)}) copy-start(f32[1,960]{1,0:T(1,128)} %copy-done.30) | copy-start | bytes 11524
  372.9 4.5 %copy-start.33 = (f32[256]{0:T(256)S(1)}, f32[256]{0:T(256)}, u32[]{:S(2)}) copy-start(f32[256]{0:T(256)} %copy-done.32) | copy-start | bytes 3076
  372.9 4.5 %copy-start.35 = (f32[256]{0:T(256)S(1)}, f32[256]{0:T(256)}, u32[]{:S(2)}) copy-start(f32[256]{0:T(256)} %copy-done.34) | copy-start | bytes 3076
  372.9 4.5 %copy-start.41 = (f32[256]{0:T(256)S(1)}, f32[256]{0:T(256)}, u32[]{:S(2)}) copy-start(f32[256]{0:T(256)} %copy-done.40) | copy-start | bytes 3076
  372.9 4.5 %copy-start.43 = (f32[256]{0:T(256)S(1)}, f32[256]{0:T(256)}, u32[]{:S(2)}) copy-start(f32[256]{0:T(256)} %copy-done.42) | copy-start | bytes 3076
  372.9 4.5 %copy-start.46 = (f32[256]{0:T(256)S(1)}, f32[256]{0:T(256)}, u32[]{:S(2)}) copy-start(f32[256]{0:T(256)} %get-tuple-element.108) | copy-start | bytes 3076
  372.9 4.5 %copy-start.47 = (f32[256]{0:T(256)S(1)}, f32[256]{0:T(256)}, u32[]{:S(2)}) copy-start(f32[256]{0:T(256)} %get-tuple-element.119) | copy-start | bytes 3076
  377.3 2.0 copy-start.1
Sparse Core Ops, SparseCore 0:
  9.6 54.0 all-gather.5
  65.8 43.2 all-gather.3
  114.2 44.2 all-gather.7
  173.1 40.1 reduce-scatter.2
  216.8 84.6 all-reduce.9
  304.3 52.8 reduce-scatter.4

commit v5 on v4

--- a/solution.py
+++ b/solution.py
@@ -633,6 +633,8 @@
                 low = dq_ref[start : start + half_dim, at]
                 high = dq_ref[start + half_dim : start + HEAD, at]
                 pair += [low * cos_tab + high * sin_tab, high * cos_tab - low * sin_tab]
+            if len(pair) == 2:
+                pair += [jnp.zeros_like(part) for part in pair]
             turned = jnp.concatenate(pair, 0).T
             own = slice(head * HEAD, head * HEAD + turned.shape[1])
             out_ref[at, own] = turned.astype(out_ref.dtype)
@@ -647,7 +649,7 @@
     return pl.pallas_call(
         attend_back_kernel,
         out_shape=(
-            jax.ShapeDtypeStruct(queries.shape[::-1], jnp.bfloat16),
+            jax.ShapeDtypeStruct((slots, -(-HEADS // 2) * 2 * HEAD), jnp.bfloat16),
             jax.ShapeDtypeStruct(kv.shape, jnp.bfloat16),
         ),
         in_specs=[pl.BlockSpec(memory_space=pltpu.SMEM)] + in_vmem(9),
@@ -695,9 +697,11 @@
     own_rows = w_query.shape[0]
     w_out_full = lax.all_gather(w_out, "fsdp", axis=0, tiled=True)
     vectors = jnp.stack([gain_attn, gain_ffn, router], 1)
-    own_attn = [w_query, jnp.concatenate([w_key, w_value, vectors], 1)]
+    own_attn = [padded_to(w_query, 1), jnp.concatenate([w_key, w_value, vectors], 1)]
     gathered = gather_rows([padded_to(own, 0) for own in own_attn], depth)
-    w_query, gathered = (full[:, :own_rows].reshape(width, -1) for full in gathered)
+    padded_rows = gathered[0].shape[1]
+    w_query = gathered[0].reshape(depth * padded_rows, -1)
+    gathered = gathered[1][:, :own_rows].reshape(width, -1)
     w_kv, vectors = gathered[:, : 2 * kdim], gathered[:, 2 * kdim :]
     gain_one, gain_two, router_vec = vectors.T.astype(jnp.float32)
     gating = jax.nn.sigmoid(jnp.sum(hidden * router_vec, -1, keepdims=True))
@@ -708,7 +712,9 @@
 
     normed_one, inv_one = norm_forward(hidden, gain_one)
     normed_one = normed_one.astype(jnp.bfloat16)
-    query_raw = dot(w_query, normed_one, (0, 1))
+    spread_one = padded_to(normed_one.reshape(row_count, depth, own_rows), -1)
+    spread_one = spread_one.reshape(row_count, -1)
+    query_raw = dot(w_query, spread_one, (0, 1))[:qdim]
     queries = rotate_columns(query_raw, cos_tab, sin_tab).astype(jnp.bfloat16) * 0.125
     kv_raw = dot(normed_one, w_kv)
     kv_own = jnp.concatenate([rotate(kv_raw[:, :kdim], cos_tab, sin_tab), kv_raw[:, kdim:]], 1)
@@ -753,7 +759,7 @@
     grad_branch = (grad_inc + grad_middle).astype(jnp.bfloat16)
     grad_attended = dot(w_out_full, grad_branch, (1, 1)).astype(jnp.bfloat16)
     spread_out = padded_to(outcome.reshape(depth, own_rows, row_count), 1)
-    grad_wout = dot(spread_out.reshape(-1, row_count), grad_branch).astype(low)
+    grad_wout = dot(spread_out.reshape(-1, row_count), padded_to(grad_branch, 1)).astype(low)
     row_delta = jnp.sum(
         (grad_attended.astype(jnp.float32) * attended).reshape(HEADS, HEAD, row_count), 1
     )
@@ -775,10 +781,9 @@
     grad_kv_raw = jnp.concatenate(
         [rotate(grad_kv[:, :kdim], cos_tab, -sin_tab), grad_kv[:, kdim:]], 1
     ).astype(jnp.bfloat16)
-    grad_normed_one = dot(grad_query_raw, w_query, (1, 1)) + dot(grad_kv_raw, w_kv, (1, 1))
-    spread_one = padded_to(normed_one.reshape(row_count, depth, own_rows), -1)
-    spread_one = spread_one.reshape(row_count, -1)
-    padded_rows = spread_one.shape[1] // depth
+    grad_normed_one = dot(grad_query_raw, w_query, (1, 1)).reshape(row_count, depth, -1)
+    grad_normed_one = grad_normed_one[..., :own_rows].reshape(row_count, width)
+    grad_normed_one = grad_normed_one + dot(grad_kv_raw, w_kv, (1, 1))
     grad_wq = dot(spread_one, grad_query_raw, (0, 0)).astype(low)
     grad_wkv = dot(spread_one, grad_kv_raw, (0, 0)).astype(low)
     grad_hidden_one, grad_gain_one = norm_backward(hidden, inv_one, gain_one, grad_normed_one)
@@ -796,6 +801,7 @@
     increment = branch + ffn_out.astype(jnp.float32)
     block_out = live_mask * (hidden + chosen_mask * gating * increment)
     total_q, total_kv, total_out = (own[:own_rows].astype(jnp.float32) for own in owned[:3])
+    total_q, total_out = total_q[:, :qdim], total_out[:, :width]
     total_k, total_v = total_kv[:, :kdim], total_kv[:, kdim:]
     mine = owned[3].reshape(-1, 8, 128)[:, 0].reshape(-1)[: 3 * own_rows].reshape(3, own_rows)
     total_gate, total_up, total_down = (total.astype(jnp.float32) for total in totals)

time: 388 us -> 380 us (0.979)
  local copies, waits for them, and re-layouts: 38.6 us -> 23.1 us
  waiting for transfers between devices: 71.4 us -> 76.1 us
    convert_element_type x2 -> x0, local copies, waits for them, and re-layouts: 7.86 us -> none  [the longest x1 3.98 us: on_device(): grad_wout = dot(spread_out.reshape(-1, row_count), grad_branch).astype(low)]
    all_gather x1, waiting for transfers between devices: 0.93 us -> 7.45 us  [on_device(): grad_ffn_all = lax.all_gather(grad_ffn, 'fsdp', axis=0, tiled=True)]
  transfers between devices with their start and end apart: 6 -> 6, of which waited for: 3 -> 3; matrix products, arithmetic and copies ran while one was open for 19% -> 16% of each run, Pallas kernels for 49% -> 50%
where the time goes in v5:
time: 380 us; the launch traced here: 379 us
  Pallas kernels  191 us (50%)
  waiting for transfers between devices  76.1 us (20%)
  matrix products  46.9 us (12%)
  other arithmetic  25.6 us (7%)
  local copies, waits for them, and re-layouts  23.1 us (6%)
  between operations  15.7 us (4%)
    pallas_call x1, Pallas kernels, reduce_rows(): pl.pallas_call(functools.partial(reduce_rows_kernel, depth, count), out_s...  62.9 us
    all_gather x1, waiting for transfers between devices, on_device(): normed_all = lax.all_gather(normed_two, 'fsdp', axis=0, tiled=True)  42.2 us
    pallas_call x1, Pallas kernels, gather_rows(): pl.pallas_call(functools.partial(gather_rows_kernel, depth, count), out_s...  34.7 us
    pallas_call x1, Pallas kernels, attend_back(): pl.pallas_call(attend_back_kernel, out_shape=(jax.ShapeDtypeStruct((slots...  28.8 us
    pallas_call x1, Pallas kernels, scatter_plane(): pl.pallas_call(scatter_plane_kernel, out_shape=jax.ShapeDtypeStruct(block...  27.4 us
    reduce_scatter x1, waiting for transfers between devices, on_device(): lax.psum_scatter(grad_normed_part, 'fsdp', scatter_dimension=0, tiled=True)  25.6 us
    pallas_call x1, Pallas kernels, gather_plane(): pl.pallas_call(gather_plane_kernel, out_shape=(jax.ShapeDtypeStruct((SPAN...  22.1 us
    dot_general x9, matrix products, dot(): lax.dot_general(left, right, (((dims[0],), (dims[1],)), ((), ())), prefer...  19.9 us
  transfers between devices with their start and end apart: 6, of which 3 were waited for; matrix products, arithmetic and copies ran while one was open for 16% of the time, Pallas kernels for 50%

profile of v5, /device:TPU:0, one launch (start us, length us, event | category | flops | bytes accessed | tf_op | source)
XLA Modules:
  0.0 379.1 jit_solution(5947647616464595299)
XLA Ops:
  7.2 0.7 all-gather.6.cloned.1.call-update
  8.0 0.7 stack.21
  8.6 0.7 stack.22
  9.3 0.7 stack.23
  10.0 1.9 concatenate.31
  12.0 0.8 pad.38.clone
  12.8 0.8 pad.62
  13.7 34.7 %shard_map.238 = (bf16[4,8,32,1024]{3,2,1,0:T(8,128)(2,1)}, bf16[4,8,32,643]{3,2,1,0:T(8,128)(2,1)}) custom-call(bf16[8,32,1024]{2,1,0:T(8,128)(2,1)} %bitcast.152, bf16[8,32,643]{2,1,0:T(8,128)(2,1)} %bitcast.158), custom_call_target="tpu_custom_call" | custom-call | bytes 102420480 | tf_op jit(solution)/shard_map/pallas_call | solution.py:201
  48.4 1.6 slice.111
  50.0 1.1 copy-done.11
  52.9 0.9 fusion.13
  54.0 2.0 fusion.5
  56.4 0.8 fusion.38
  58.0 0.8 pad_maximum_fusion.1.kv_ref
  58.9 22.1 %shard_map.239 = (bf16[8,256,640]{2,1,0:T(8,128)(2,1)}, s32[8,1,256]{2,1,0:T(1,128)}) custom-call(bf16[256,640]{1,0:T(8,128)(2,1)} %pad_maximum_fusion.1.kv_ref, s32[1,256]{1,0:T(1,128)} %and_select_fusion.tag_ref), custom_call_target="tpu_custom_call" | custom-call | bytes 78643200 | tf_op jit(solution)/shard_map/pallas_call | solution.py:252
  81.0 0.8 slice.90
  82.1 0.7 pad_add_fusion.first_ref
  83.1 2.4 fusion.1
  85.6 0.9 maximum_multiply_fusion
  86.5 15.2 %shard_map.240 = (f32[960,256]{1,0:T(8,128)}, f32[16,256]{1,0:T(8,128)}) custom-call(s32[18]{0:T(128)} %pad_add_fusion.first_ref, bf16[960,256]{1,0:T(8,128)(2,1)} %bitcast.166, bf16[2048,640]{1,0:T(8,128)(2,1)} %bitcast.189, s32[1,256]{1,0:T(1,128)} %pos_ref.3, s32[16,1,128]{2,1,0:T(1,128)} %bitcast.194), custom_call_target="tpu_custom_call" | custom-call | flops 16106127360 | bytes 2621440 | tf_op jit(solution)/shard_map/pallas_call | solution.py:561
  101.7 7.4 %all-gather.4.cloned.1.call-done = bf16[1024,960]{0,1:T(8,128)(2,1)} async-done(((bf16[256,960]{0,1:T(8,128)(2,1)}), bf16[1024,960]{0,1:T(8,128)(2,1)}) %all-gather.4.cloned.1.call-update) | async-done | bytes 1966096 | tf_op jit(solution)/shard_map/all_gather | solution.py:711
  109.1 1.2 convert_element_type.166
  110.4 2.7 multiply_reduce_fusion.3
  113.1 1.0 multiply_convert_fusion.3
  114.3 42.2 %all-gather.8.cloned.1.call-done = bf16[1024,960]{0,1:T(8,128)(2,1)} async-done(((bf16[256,960]{0,1:T(8,128)(2,1)}), bf16[1024,960]{0,1:T(8,128)(2,1)}) %all-gather.8.cloned.1.call-update) | async-done | bytes 1966096 | tf_op jit(solution)/shard_map/all_gather | solution.py:735
  156.6 3.6 fusion.46
  160.2 1.6 fusion.47
  161.8 3.8 multiply_reduce_fusion
  165.6 1.7 fusion.48
  167.8 1.7 add_convert_fusion
  169.5 1.4 pad_maximum_fusion
  171.0 4.3 %convolution_convert_fusion.2 = bf16[1024,960]{0,1:T(8,128)(2,1)} fusion(bf16[640,960]{0,1:T(8,128)(2,1)S(1)} %copy-done, bf16[1024,640]{0,1:T(8,128)(2,1)} %get-tuple-element.83), kind=kOutput, calls=%fused_computation.14 | convolution fusion | flops 1259274240 | bytes 4505600 | tf_op jit(solution)/shard_map/dot_general | solution.py:742
  175.3 4.9 %convolution_convert_fusion.4 = bf16[640,960]{0,1:T(8,128)(2,1)} fusion(bf16[1024,640]{0,1:T(8,128)(2,1)} %get-tuple-element.83, bf16[1024,960]{0,1:T(8,128)(2,1)} %all-gather.4.cloned.1.call-done), kind=kOutput, calls=%fused_computation.16 | convolution fusion | flops 1258905600 | bytes 4505600 | tf_op jit(solution)/shard_map/dot_general | solution.py:749
  180.2 2.8 convolution_convert_fusion.5
  183.0 2.8 convolution_convert_fusion.6
  185.7 25.6 %reduce-scatter.3.cloned.1.call-done = bf16[256,961]{0,1:T(8,128)(2,1)} async-done(((bf16[1024,961]{0,1:T(8,128)(2,1)}), bf16[256,961]{0,1:T(8,128)(2,1)}) %reduce-scatter.3.cloned.1.call-update) | async-done | bytes 492048 | tf_op jit(solution)/shard_map/reduce_scatter | solution.py:739
  211.3 1.1 convert_element_type.172
  213.3 1.9 pad.41
  215.2 1.1 multiply_reduce_fusion.1
  216.7 0.7 copy-done.10
  218.1 1.8 convert_multiply_fusion.1
  219.9 1.3 reduce_sum.104
  221.9 28.8 %shard_map.241 = (bf16[256,1024]{1,0:T(8,128)(2,1)}, bf16[2048,640]{1,0:T(8,128)(2,1)}) custom-call(s32[18]{0:T(128)} %pad_add_fusion.first_ref, bf16[960,256]{1,0:T(8,128)(2,1)} %bitcast.167, bf16[2048,640]{1,0:T(8,128)(2,1)} %bitcast.190, s32[1,256]{1,0:T(1,128)} %pos_ref.3, s32[16,1,128]{2,1,0:T(1,128)} %bitcast.195, ...), custom_call_target="tpu_custom_call" | custom-call | flops 30198988800 | bytes 5242880 | tf_op jit(solution)/shard_map/pallas_call | solution.py:649
  250.7 27.4 %shard_map.242 = f32[8,32,640]{2,1,0:T(8,128)} custom-call(bf16[8,8,32,640]{3,2,1,0:T(8,128)(2,1)} %bitcast.149), custom_call_target="tpu_custom_call" | custom-call | bytes 78643200 | tf_op jit(solution)/shard_map/pallas_call | solution.py:354
  278.1 1.8 slice.117
  279.9 1.1 slice.118
  281.0 1.2 copy.40
  282.2 0.8 copy.41
  283.1 0.8 add_multiply_fusion
  283.9 2.5 fusion.3
  286.5 1.6 fusion.30
  288.5 0.7 pad.44.refs_3_
  289.2 1.7 convolution_convert_fusion.3
  290.9 3.2 convolution_convert_fusion
  294.1 2.0 convolution_convert_fusion.1
  296.1 62.9 %shard_map.243 = (bf16[8,32,1024]{2,1,0:T(8,128)(2,1)}, bf16[8,32,640]{2,1,0:T(8,128)(2,1)}, bf16[8,32,1024]{2,1,0:T(8,128)(2,1)}, f32[8,8,128]{2,1,0:T(8,128)}) custom-call(bf16[4,8,32,1024]{3,2,1,0:T(8,128)(2,1)} %bitcast.143, bf16[4,8,32,640]{3,2,1,0:T(8,128)(2,1)} %bitcast.144, bf16[4,8,32,1024]{3,2,1,0:T(8,128)(2,1)} %bitcast.142, ...), custom_call_target="tpu_custom_call" | custom-call | bytes 167116800 | tf_op jit(solution)/shard_map/pallas_call | solution.py:432
  359.1 3.0 convert_element_type.187
  362.1 1.6 convert_element_type.188
  363.9 1.6 convert_element_type.189
  365.8 0.9 fusion.42
  366.7 1.1 slice_convert_fusion
  367.8 1.1 slice_convert_fusion.1
  368.8 0.8 slice.123
  370.3 1.9 fusion.37
  (171 shorter events, 8.3 us)
Async XLA Ops:
  7.2 154.6 %copy-start = (bf16[640,960]{0,1:T(8,128)(2,1)S(1)}, bf16[640,960]{0,1:T(8,128)(2,1)}, u32[]{:S(2)}) copy-start(bf16[640,960]{0,1:T(8,128)(2,1)} %param.22) | copy-start | bytes 3686404
  7.2 5.6 %copy-start.20 = (bf16[240,960]{1,0:T(8,128)(2,1)S(1)}, bf16[240,960]{1,0:T(8,128)(2,1)}, u32[]{:S(2)}) copy-start(bf16[240,960]{1,0:T(8,128)(2,1)} %param.16) | copy-start | bytes 1382404
  7.2 94.5 %all-gather.6.cloned.1.call-start = ((), (), s32[]{:S(2)}) async-start(), calls=%async_computation.3 | async-start | bytes 2457600 | tf_op jit(solution)/shard_map/all_gather | solution.py:698
  7.9 101.2 %all-gather.4.cloned.1.call-start = ((), (), s32[]{:S(2)}) async-start(), calls=%async_computation.2 | async-start | bytes 2457600 | tf_op jit(solution)/shard_map/all_gather | solution.py:711
  48.4 3.6 copy-start.48
  48.4 3.7 copy-start.2
  48.4 3.9 %copy-start.44 = (s32[1,256]{1,0:T(1,128)S(1)}, s32[1,256]{1,0:T(1,128)}, u32[]{:S(2)}) copy-start(s32[1,256]{1,0:T(1,128)} %pos_ref.3) | copy-start | bytes 3076
  48.4 4.5 %copy-start.5 = (bf16[1,256,960]{1,2,0:T(8,128)(2,1)S(1)}, bf16[1,256,960]{1,2,0:T(8,128)(2,1)}, u32[]{:S(2)}) copy-start(bf16[1,256,960]{1,2,0:T(8,128)(2,1)} %param.26) | copy-start | bytes 1474564
  50.0 1.1 copy-start.11
  52.0 1.9 copy-start.30
  52.1 1.9 copy-start.36
  52.1 164.2 %copy-start.28 = (f32[1,960]{1,0:T(1,128)}, f32[1,960]{1,0:T(1,128)S(1)}, u32[]{:S(2)}) copy-start(f32[1,960]{1,0:T(1,128)S(1)} %get-tuple-element.96) | copy-start | bytes 11524
  52.9 29.0 %copy-start.38 = (f32[256]{0:T(256)}, f32[256]{0:T(256)S(1)}, u32[]{:S(2)}) copy-start(f32[256]{0:T(256)S(1)} %get-tuple-element.109) | copy-start | bytes 3076
  52.9 163.4 %copy-start.34 = (f32[256]{0:T(256)}, f32[256]{0:T(256)S(1)}, u32[]{:S(2)}) copy-start(f32[256]{0:T(256)S(1)} %get-tuple-element.112) | copy-start | bytes 3076
  53.9 102.7 %all-gather.8.cloned.1.call-start = ((), (), s32[]{:S(2)}) async-start(), calls=%async_computation.4 | async-start | bytes 2457600 | tf_op jit(solution)/shard_map/all_gather | solution.py:735
  82.1 3.3 copy-start.6
  83.1 2.4 copy-start.26
  83.1 2.4 copy-start.27
  110.4 2.7 copy-start.13
  113.1 103.2 %copy-start.32 = (f32[256]{0:T(256)}, f32[256]{0:T(256)S(1)}, u32[]{:S(2)}) copy-start(f32[256]{0:T(256)S(1)} %get-tuple-element.111) | copy-start | bytes 3076
  113.1 103.2 %copy-start.40 = (f32[256]{0:T(256)}, f32[256]{0:T(256)S(1)}, u32[]{:S(2)}) copy-start(f32[256]{0:T(256)S(1)} %get-tuple-element.110) | copy-start | bytes 3076
  114.1 97.2 %reduce-scatter.3.cloned.1.call-start = ((), (), s32[]{:S(2)}) async-start(), calls=%async_computation.5 | async-start | bytes 2478080 | tf_op jit(solution)/shard_map/reduce_scatter | solution.py:739
  156.6 3.6 copy-start.50
  156.6 3.6 copy-start.52
  160.2 1.6 copy-start.49
  165.6 1.7 copy-start.54
  165.6 1.7 copy-start.56
  165.6 2.2 copy-start.53
  171.0 188.1 %all-reduce.12.cloned.1.call-start = ((), (), s32[]{:S(2)}) async-start(), calls=%async_computation.7 | async-start | bytes 7372800 | tf_op jit(solution)/shard_map/psum | solution.py:757
  175.3 4.9 %copy-start.51 = (bf16[1024,960]{0,1:T(8,128)(2,1)S(1)}, bf16[1024,960]{0,1:T(8,128)(2,1)}, u32[]{:S(2)}) copy-start(bf16[1024,960]{0,1:T(8,128)(2,1)} %all-gather.8.cloned.1.call-done) | copy-start | bytes 5898244
  175.3 4.9 %copy-start.57 = (bf16[1024,640]{0,1:T(8,128)(2,1)S(1)}, bf16[1024,640]{0,1:T(8,128)(2,1)}, u32[]{:S(2)}) copy-start(bf16[1024,640]{0,1:T(8,128)(2,1)} %copy-done.56) | copy-start | bytes 3932164
  180.2 2.8 copy-start.55
  212.4 70.7 %copy-start.3 = (f32[256,961]{0,1:T(8,128)}, f32[256,961]{0,1:T(8,128)S(1)}, u32[]{:S(2)}) copy-start(f32[256,961]{0,1:T(8,128)S(1)} %convert_element_type.172) | copy-start | bytes 2952196
  212.5 146.6 %reduce-scatter.5.cloned.1.call-start = ((), (), s32[]{:S(2)}) async-start(), calls=%async_computation.6 | async-start | bytes 2457600 | tf_op jit(solution)/shard_map/reduce_scatter | solution.py:799
  216.3 1.2 copy-start.10
  216.3 1.9 copy-start.14
  216.3 3.6 copy-start.42
  218.1 1.8 copy-start.8
  250.7 32.3 %copy-start.25 = (f32[256,32]{0,1:T(8,128)S(1)}, f32[256,32]{0,1:T(8,128)}, u32[]{:S(2)}) copy-start(f32[256,32]{0,1:T(8,128)} %get-tuple-element.103) | copy-start | bytes 98308
  278.1 5.0 %copy-start.45 = (f32[256]{0:T(256)S(1)}, f32[256]{0:T(256)}, u32[]{:S(2)}) copy-start(f32[256]{0:T(256)} %get-tuple-element.72) | copy-start | bytes 3076
  283.1 3.4 copy-start.12
  283.1 3.4 copy-start.18
  283.1 3.4 copy-start.37
  283.1 3.4 copy-start.39
  286.5 2.7 copy-start.7
  288.1 2.8 copy-start.9
  290.9 3.2 copy-start.19
  359.1 3.0 copy-start.16
  362.1 1.8 copy-start.15
  363.9 1.6 copy-start.24
  365.6 1.1 copy-start.23
  365.7 2.1 copy-start.22
  365.7 4.5 %copy-start.4 = (f32[256,961]{0,1:T(8,128)S(1)}, f32[256,961]{0,1:T(8,128)}, u32[]{:S(2)}) copy-start(f32[256,961]{0,1:T(8,128)} %copy-done.3) | copy-start | bytes 2952196
  365.7 4.5 %copy-start.17 = (f32[256,960]{0,1:T(8,128)S(1)}, f32[256,960]{0,1:T(8,128)}, u32[]{:S(2)}) copy-start(f32[256,960]{0,1:T(8,128)} %get-tuple-element.118) | copy-start | bytes 2949124
  365.7 4.5 %copy-start.21 = (bf16[256,960]{0,1:T(8,128)(2,1)S(1)}, bf16[256,960]{0,1:T(8,128)(2,1)}, u32[]{:S(2)}) copy-start(bf16[256,960]{0,1:T(8,128)(2,1)} %reduce-scatter.5.cloned.1.call-done) | copy-start | bytes 1474564
  365.7 4.5 %copy-start.29 = (f32[1,960]{1,0:T(1,128)S(1)}, f32[1,960]{1,0:T(1,128)}, u32[]{:S(2)}) copy-start(f32[1,960]{1,0:T(1,128)} %copy-done.28) | copy-start | bytes 11524
  365.8 4.5 %copy-start.31 = (f32[1,960]{1,0:T(1,128)S(1)}, f32[1,960]{1,0:T(1,128)}, u32[]{:S(2)}) copy-start(f32[1,960]{1,0:T(1,128)} %copy-done.30) | copy-start | bytes 11524
  365.8 4.5 %copy-start.33 = (f32[256]{0:T(256)S(1)}, f32[256]{0:T(256)}, u32[]{:S(2)}) copy-start(f32[256]{0:T(256)} %copy-done.32) | copy-start | bytes 3076
  365.8 4.5 %copy-start.35 = (f32[256]{0:T(256)S(1)}, f32[256]{0:T(256)}, u32[]{:S(2)}) copy-start(f32[256]{0:T(256)} %copy-done.34) | copy-start | bytes 3076
  365.8 4.5 %copy-start.41 = (f32[256]{0:T(256)S(1)}, f32[256]{0:T(256)}, u32[]{:S(2)}) copy-start(f32[256]{0:T(256)} %copy-done.40) | copy-start | bytes 3076
  365.8 4.5 %copy-start.43 = (f32[256]{0:T(256)S(1)}, f32[256]{0:T(256)}, u32[]{:S(2)}) copy-start(f32[256]{0:T(256)} %copy-done.42) | copy-start | bytes 3076
  365.8 4.5 %copy-start.46 = (f32[256]{0:T(256)S(1)}, f32[256]{0:T(256)}, u32[]{:S(2)}) copy-start(f32[256]{0:T(256)} %get-tuple-element.108) | copy-start | bytes 3076
  365.8 4.5 %copy-start.47 = (f32[256]{0:T(256)S(1)}, f32[256]{0:T(256)}, u32[]{:S(2)}) copy-start(f32[256]{0:T(256)} %get-tuple-element.119) | copy-start | bytes 3076
  370.2 2.0 copy-start.1
Sparse Core Ops, SparseCore 0:
  9.6 54.0 all-gather.5
  65.8 43.2 all-gather.3
  114.2 42.2 all-gather.7
  171.1 40.1 reduce-scatter.2
  214.9 84.7 all-reduce.11
  302.4 53.0 reduce-scatter.4

commit v6 on v5

--- a/solution.py
+++ b/solution.py
@@ -326,7 +326,16 @@
     ]
 
 
-def scatter_plane_kernel(x_ref, out_ref, halves, sums, arrived, h_sems, p_sems):
+def turned_back(values, cos_tab, sin_tab):
+    half_dim, parts = HEAD // 2, []
+    for start in range(0, values.shape[1], HEAD):
+        low = values[:, start : start + half_dim]
+        high = values[:, start + half_dim : start + HEAD]
+        parts += [low * cos_tab + high * sin_tab, high * cos_tab - low * sin_tab]
+    return jnp.concatenate(parts, 1)
+
+
+def scatter_plane_kernel(x_ref, cos_ref, sin_ref, out_ref, halves, sums, arrived, h_sems, p_sems):
     me, core, chip, partner = plane_of()
     layer = lax.axis_index("fsdp")
     greet([(chip_at(chip, core, j), layer) for j in range(1, CHIPS)] + [(partner, layer)])
@@ -336,7 +345,10 @@
         copy.wait_recv()
 
     def add_slab(slab, carry):
-        out_ref[slab] = plane_total(sums, arrived, slab)
+        total = plane_total(sums, arrived, slab)
+        kdim = KV_HEADS * HEAD
+        keys = turned_back(total[:, :kdim], cos_ref[slab], sin_ref[slab])
+        out_ref[slab] = jnp.concatenate([keys, total[:, kdim:]], 1).astype(out_ref.dtype)
         return carry
 
     lax.fori_loop(0, x_ref.shape[1], add_slab, 0)
@@ -344,23 +356,29 @@
         copy.wait_send()
 
 
-def scatter_plane(values):
+def scatter_plane(values, cos_tab, sin_tab):
     if lax.axis_size("ctx") != SPAN:
         own = lax.psum_scatter(values, "ctx", scatter_dimension=0, tiled=True)
-        return own.astype(jnp.float32)
+        own, kdim = own.astype(jnp.float32), KV_HEADS * HEAD
+        keys = turned_back(own[:, :kdim], cos_tab, sin_tab)
+        return jnp.concatenate([keys, own[:, kdim:]], 1).astype(values.dtype)
     rows, columns = values.shape
     slabs = 8
     block = (slabs, rows // SPAN // slabs, columns)
     return pl.pallas_call(
         scatter_plane_kernel,
-        out_shape=jax.ShapeDtypeStruct(block, jnp.float32),
-        in_specs=in_vmem(1),
+        out_shape=jax.ShapeDtypeStruct(block, values.dtype),
+        in_specs=in_vmem(3),
         out_specs=in_vmem(1)[0],
         scratch_shapes=plane_scratch(block, values.dtype)
         + [pltpu.SemaphoreType.DMA((2, 1, CHIPS)), pltpu.SemaphoreType.DMA((2, 1, CHIPS - 1))],
         compiler_params=comm_params(3),
         cost_estimate=comm_cost(values.size * 2),
-    )(values.reshape(SPAN, *block)).reshape(rows // SPAN, columns)
+    )(
+        values.reshape(SPAN, *block),
+        cos_tab.reshape(*block[:2], -1),
+        sin_tab.reshape(*block[:2], -1),
+    ).reshape(rows // SPAN, columns)
 
 
 def reduce_rows_kernel(depth, count, *refs):
@@ -724,14 +742,13 @@
         [jnp.where(first_tags >= 0, first_tags, -first_tags - 1), query_pos[BLOCK - 1 :: BLOCK]]
     )
     attended, log_total = attend(firsts, queries, kv_all, query_pos, tags_all)
-    attended, grad_ffn_all, w_out_full = lax.optimization_barrier(
-        (attended, grad_ffn_all, w_out_full)
-    )
+    attended, w_out_full = lax.optimization_barrier((attended, w_out_full))
     outcome = attended.astype(jnp.bfloat16)
     branch = dot(outcome, w_out_full, (0, 0))
     middle = hidden + branch
     normed_two, inv_two = norm_forward(middle, gain_two)
     normed_two = normed_two.astype(jnp.bfloat16)
+    normed_two, grad_ffn_all = lax.optimization_barrier((normed_two, grad_ffn_all))
     normed_all = lax.all_gather(normed_two, "fsdp", axis=0, tiled=True)
     inner_act, grad_gate_act, grad_up_act, grad_normed_part = ffn_both(
         normed_all, grad_ffn_all, w_gate, w_up, w_down
@@ -750,15 +767,16 @@
         inner_act, grad_ffn_all, across_rows, preferred_element_type=jnp.float32
     )
     low = jnp.bfloat16
-    grad_normed_two, ffn_part, *grads = lax.optimization_barrier(
-        (grad_normed_two, ffn_part, *(g.astype(low) for g in (grad_wgate, grad_wup, grad_wdown)))
+    spread_out = padded_to(outcome.reshape(depth, own_rows, row_count), 1)
+    grads = [grad.astype(low) for grad in (grad_wgate, grad_wup, grad_wdown)]
+    grad_normed_two, ffn_part, spread_out, *grads = lax.optimization_barrier(
+        (grad_normed_two, ffn_part, spread_out, *grads)
     )
     grad_normed_two, row_dot = grad_normed_two[:, :width], grad_normed_two[:, width:]
     totals = tuple(lax.psum(grad, "ctx") for grad in grads)
     grad_middle, grad_gain_two = norm_backward(middle, inv_two, gain_two, grad_normed_two)
     grad_branch = (grad_inc + grad_middle).astype(jnp.bfloat16)
     grad_attended = dot(w_out_full, grad_branch, (1, 1)).astype(jnp.bfloat16)
-    spread_out = padded_to(outcome.reshape(depth, own_rows, row_count), 1)
     grad_wout = dot(spread_out.reshape(-1, row_count), padded_to(grad_branch, 1)).astype(low)
     row_delta = jnp.sum(
         (grad_attended.astype(jnp.float32) * attended).reshape(HEADS, HEAD, row_count), 1
@@ -775,12 +793,9 @@
         row_delta,
         (cos_tab.T, sin_tab.T),
     )
-    grad_kv = scatter_plane(grad_kv_all)
+    grad_kv_raw = scatter_plane(grad_kv_all, cos_tab, sin_tab)
     grad_logit = (jnp.sum(grad_inc * branch, -1, keepdims=True) + row_dot) * (1.0 - gating)
     grad_router = jnp.sum(hidden * grad_logit, 0)
-    grad_kv_raw = jnp.concatenate(
-        [rotate(grad_kv[:, :kdim], cos_tab, -sin_tab), grad_kv[:, kdim:]], 1
-    ).astype(jnp.bfloat16)
     grad_normed_one = dot(grad_query_raw, w_query, (1, 1)).reshape(row_count, depth, -1)
     grad_normed_one = grad_normed_one[..., :own_rows].reshape(row_count, width)
     grad_normed_one = grad_normed_one + dot(grad_kv_raw, w_kv, (1, 1))
@@ -793,14 +808,14 @@
     vectors = jnp.stack([grad_gain_one, grad_gain_two, grad_router]).reshape(3, depth, own_rows)
     vectors = jnp.pad(vectors.transpose(1, 0, 2).reshape(depth, -1), ((0, 0), (0, -3 * own_rows % 1024)))
     vectors = jnp.pad(vectors.reshape(depth, -1, 1, 128), ((0, 0), (0, 0), (0, 7), (0, 0)))
-    layered = [grad.reshape(depth, padded_rows, -1) for grad in (grad_wq, grad_wkv, grad_wout)]
+    layered = [grad.reshape(depth, padded_rows, -1) for grad in (grad_wout, grad_wq, grad_wkv)]
     layered.append(vectors.reshape(depth, -1, 128))
     owned = reduce_rows(layered, 4)
     ffn_out = lax.psum_scatter(ffn_part, "fsdp", scatter_dimension=0, tiled=True)
     *owned, totals, ffn_out = lax.optimization_barrier((*owned, totals, ffn_out))
     increment = branch + ffn_out.astype(jnp.float32)
     block_out = live_mask * (hidden + chosen_mask * gating * increment)
-    total_q, total_kv, total_out = (own[:own_rows].astype(jnp.float32) for own in owned[:3])
+    total_out, total_q, total_kv = (own[:own_rows].astype(jnp.float32) for own in owned[:3])
     total_q, total_out = total_q[:, :qdim], total_out[:, :width]
     total_k, total_v = total_kv[:, :kdim], total_kv[:, kdim:]
     mine = owned[3].reshape(-1, 8, 128)[:, 0].reshape(-1)[: 3 * own_rows].reshape(3, own_rows)

time: 380 us -> 419 us (1.10)
  waiting for transfers between devices: 76.1 us -> 118 us
    all_gather x1, waiting for transfers between devices: 7.45 us -> 44.3 us  [on_device(): grad_ffn_all = lax.all_gather(grad_ffn, 'fsdp', axis=0, tiled=True)]
    reduce_scatter x1, waiting for transfers between devices: 0.02 us -> 4.97 us  [on_device(): lax.psum_scatter(ffn_part, 'fsdp', scatter_dimension=0, tiled=True)]
  transfers between devices with their start and end apart: 6 -> 6, of which waited for: 3 -> 4; matrix products, arithmetic and copies ran while one was open for 16% -> 13% of each run, Pallas kernels for 50% -> 46%
where the time goes in v6:
time: 419 us; the launch traced here: 417 us
  Pallas kernels  191 us (46%)
  waiting for transfers between devices  118 us (28%)
  matrix products  45.5 us (11%)
  other arithmetic  26.2 us (6%)
  local copies, waits for them, and re-layouts  19.9 us (5%)
  between operations  15.5 us (4%)
    pallas_call x1, Pallas kernels, reduce_rows(): pl.pallas_call(functools.partial(reduce_rows_kernel, depth, count), out_s...  61.9 us
    all_gather x1, waiting for transfers between devices, on_device(): grad_ffn_all = lax.all_gather(grad_ffn, 'fsdp', axis=0, tiled=True)  44.3 us
    all_gather x1, waiting for transfers between devices, on_device(): normed_all = lax.all_gather(normed_two, 'fsdp', axis=0, tiled=True)  44.2 us
    pallas_call x1, Pallas kernels, gather_rows(): pl.pallas_call(functools.partial(gather_rows_kernel, depth, count), out_s...  34.7 us
    pallas_call x1, Pallas kernels, attend_back(): pl.pallas_call(attend_back_kernel, out_shape=(jax.ShapeDtypeStruct((slots...  28.7 us
    pallas_call x1, Pallas kernels, scatter_plane(): pl.pallas_call(scatter_plane_kernel, out_shape=jax.ShapeDtypeStruct(block...  28.7 us
    reduce_scatter x1, waiting for transfers between devices, on_device(): lax.psum_scatter(grad_normed_part, 'fsdp', scatter_dimension=0, tiled=True)  23.8 us
    pallas_call x1, Pallas kernels, gather_plane(): pl.pallas_call(gather_plane_kernel, out_shape=(jax.ShapeDtypeStruct((SPAN...  22.1 us
  transfers between devices with their start and end apart: 6, of which 4 were waited for; matrix products, arithmetic and copies ran while one was open for 13% of the time, Pallas kernels for 46%

profile of v6, /device:TPU:0, one launch (start us, length us, event | category | flops | bytes accessed | tf_op | source)
XLA Modules:
  0.0 417.1 jit_solution(7481951405310899847)
XLA Ops:
  7.2 0.7 all-gather.4.cloned.1.call-update
  8.0 0.7 stack.21
  8.7 0.7 stack.22
  9.3 0.7 stack.23
  10.0 1.9 concatenate.23
  12.0 0.8 pad.38.clone
  12.8 0.8 pad.58
  13.7 34.7 %shard_map.238 = (bf16[4,8,32,1024]{3,2,1,0:T(8,128)(2,1)}, bf16[4,8,32,643]{3,2,1,0:T(8,128)(2,1)}) custom-call(bf16[8,32,1024]{2,1,0:T(8,128)(2,1)} %bitcast.150, bf16[8,32,643]{2,1,0:T(8,128)(2,1)} %bitcast.156), custom_call_target="tpu_custom_call" | custom-call | bytes 102420480 | tf_op jit(solution)/shard_map/pallas_call | solution.py:201
  48.4 1.5 slice.102
  50.0 0.9 slice_convert_fusion.4
  50.9 1.2 copy.38
  52.9 0.7 fusion.5
  53.7 0.8 slice.105
  54.7 1.1 copy.31
  56.9 0.8 pad_maximum_fusion.1.kv_ref
  58.3 22.1 %shard_map.239 = (bf16[8,256,640]{2,1,0:T(8,128)(2,1)}, s32[8,1,256]{2,1,0:T(1,128)}) custom-call(bf16[256,640]{1,0:T(8,128)(2,1)} %pad_maximum_fusion.1.kv_ref, s32[1,256]{1,0:T(1,128)} %and_select_fusion.tag_ref), custom_call_target="tpu_custom_call" | custom-call | bytes 78643200 | tf_op jit(solution)/shard_map/pallas_call | solution.py:252
  80.4 0.8 slice.83
  81.5 0.7 pad_add_fusion.first_ref
  82.5 2.3 fusion.1
  85.0 0.9 maximum_multiply_fusion
  85.8 15.3 %shard_map.240 = (f32[960,256]{1,0:T(8,128)}, f32[16,256]{1,0:T(8,128)}) custom-call(s32[18]{0:T(128)} %pad_add_fusion.first_ref, bf16[960,256]{1,0:T(8,128)(2,1)} %bitcast.163, bf16[2048,640]{1,0:T(8,128)(2,1)} %bitcast.186, s32[1,256]{1,0:T(1,128)} %pos_ref.3, s32[16,1,128]{2,1,0:T(1,128)} %bitcast.191), custom_call_target="tpu_custom_call" | custom-call | flops 16106127360 | bytes 2621440 | tf_op jit(solution)/shard_map/pallas_call | solution.py:579
  101.1 1.3 convert_element_type.167
  102.4 2.8 fusion.19
  105.8 0.9 fusion.13
  106.8 1.0 multiply_convert_fusion.3
  107.8 44.3 %all-gather.6.cloned.1.call-done = bf16[1024,960]{0,1:T(8,128)(2,1)} async-done(((bf16[256,960]{0,1:T(8,128)(2,1)}), bf16[1024,960]{0,1:T(8,128)(2,1)}) %all-gather.6.cloned.1.call-update) | async-done | bytes 1966096 | tf_op jit(solution)/shard_map/all_gather | solution.py:729
  152.3 44.2 %all-gather.8.cloned.1.call-done = bf16[1024,960]{0,1:T(8,128)(2,1)} async-done(((bf16[256,960]{0,1:T(8,128)(2,1)}), bf16[1024,960]{0,1:T(8,128)(2,1)}) %all-gather.8.cloned.1.call-update) | async-done | bytes 1966096 | tf_op jit(solution)/shard_map/all_gather | solution.py:752
  196.5 3.6 fusion.43
  200.1 1.6 fusion.44
  201.8 3.8 multiply_reduce_fusion
  205.5 1.7 fusion.45
  207.7 1.7 add_convert_fusion
  209.5 1.4 pad_maximum_fusion
  211.0 1.9 pad.40
  212.8 4.3 %convolution_convert_fusion.2 = bf16[1024,960]{0,1:T(8,128)(2,1)} fusion(bf16[640,960]{0,1:T(8,128)(2,1)S(1)} %copy-done, bf16[1024,640]{0,1:T(8,128)(2,1)} %get-tuple-element.87), kind=kOutput, calls=%fused_computation.14 | convolution fusion | flops 1259274240 | bytes 4505600 | tf_op jit(solution)/shard_map/dot_general | solution.py:759
  217.1 4.8 %convolution_convert_fusion.4 = bf16[640,960]{0,1:T(8,128)(2,1)} fusion(bf16[1024,640]{0,1:T(8,128)(2,1)} %get-tuple-element.87, bf16[1024,960]{0,1:T(8,128)(2,1)} %all-gather.6.cloned.1.call-done), kind=kOutput, calls=%fused_computation.16 | convolution fusion | flops 1258905600 | bytes 4505600 | tf_op jit(solution)/shard_map/dot_general | solution.py:766
  222.0 2.8 convolution_convert_fusion.5
  224.7 2.8 convolution_convert_fusion.6
  227.5 23.8 %reduce-scatter.3.cloned.1.call-done = bf16[256,961]{0,1:T(8,128)(2,1)} async-done(((bf16[1024,961]{0,1:T(8,128)(2,1)}), bf16[256,961]{0,1:T(8,128)(2,1)}) %reduce-scatter.3.cloned.1.call-update) | async-done | bytes 492048 | tf_op jit(solution)/shard_map/reduce_scatter | solution.py:756
  251.3 1.1 convert_element_type.177
  252.8 1.2 multiply_sine_fusion
  255.1 0.7 copy-done.10
  255.8 0.7 copy-done.14
  256.5 1.8 convert_multiply_fusion.1
  258.3 1.4 reduce_sum.104
  260.3 28.7 %shard_map.241 = (bf16[256,1024]{1,0:T(8,128)(2,1)}, bf16[2048,640]{1,0:T(8,128)(2,1)}) custom-call(s32[18]{0:T(128)} %pad_add_fusion.first_ref, bf16[960,256]{1,0:T(8,128)(2,1)} %bitcast.164, bf16[2048,640]{1,0:T(8,128)(2,1)} %bitcast.187, s32[1,256]{1,0:T(1,128)} %pos_ref.3, s32[16,1,128]{2,1,0:T(1,128)} %bitcast.192, ...), custom_call_target="tpu_custom_call" | custom-call | flops 30198988800 | bytes 5242880 | tf_op jit(solution)/shard_map/pallas_call | solution.py:667
  289.0 28.7 %shard_map.242 = bf16[8,32,640]{2,1,0:T(8,128)(2,1)} custom-call(bf16[8,8,32,640]{3,2,1,0:T(8,128)(2,1)} %bitcast.149, f32[8,32,32]{2,1,0:T(8,128)} %get-tuple-element.103.cos_ref, f32[8,32,32]{2,1,0:T(8,128)} %get-tuple-element.102.sin_ref), custom_call_target="tpu_custom_call" | custom-call | bytes 78643200 | tf_op jit(solution)/shard_map/pallas_call | solution.py:368
  317.7 2.4 fusion.3
  320.2 1.6 fusion.30
  322.2 0.7 pad.44.refs_3_
  322.9 1.7 convolution_convert_fusion.3
  324.5 3.2 convolution_convert_fusion.1
  327.7 2.0 convolution_convert_fusion
  329.7 61.9 %shard_map.243 = (bf16[8,32,1024]{2,1,0:T(8,128)(2,1)}, bf16[8,32,1024]{2,1,0:T(8,128)(2,1)}, bf16[8,32,640]{2,1,0:T(8,128)(2,1)}, f32[8,8,128]{2,1,0:T(8,128)}) custom-call(bf16[4,8,32,1024]{3,2,1,0:T(8,128)(2,1)} %bitcast.142, bf16[4,8,32,1024]{3,2,1,0:T(8,128)(2,1)} %bitcast.143, bf16[4,8,32,640]{3,2,1,0:T(8,128)(2,1)} %bitcast.144, ...), custom_call_target="tpu_custom_call" | custom-call | bytes 167116800 | tf_op jit(solution)/shard_map/pallas_call | solution.py:450
  392.2 5.0 %reduce-scatter.5.cloned.1.call-done = bf16[256,960]{0,1:T(8,128)(2,1)} async-done(((bf16[1024,960]{0,1:T(8,128)(2,1)}), bf16[256,960]{0,1:T(8,128)(2,1)}) %reduce-scatter.5.cloned.1.call-update) | async-done | bytes 491536 | tf_op jit(solution)/shard_map/reduce_scatter | solution.py:814
  397.2 3.0 convert_element_type.194
  400.2 1.6 convert_element_type.195
  401.9 1.6 convert_element_type.196
  403.9 0.9 fusion.39
  404.8 1.1 slice_convert_fusion
  405.8 1.1 slice_convert_fusion.1
  406.9 0.8 slice.112
  407.6 0.6 fusion.41
  408.3 1.9 fusion.37
  (142 shorter events, 7.9 us)
Async XLA Ops:
  7.2 194.6 %copy-start = (bf16[640,960]{0,1:T(8,128)(2,1)S(1)}, bf16[640,960]{0,1:T(8,128)(2,1)}, u32[]{:S(2)}) copy-start(bf16[640,960]{0,1:T(8,128)(2,1)} %param.22) | copy-start | bytes 3686404
  7.2 5.6 %copy-start.21 = (bf16[240,960]{1,0:T(8,128)(2,1)S(1)}, bf16[240,960]{1,0:T(8,128)(2,1)}, u32[]{:S(2)}) copy-start(bf16[240,960]{1,0:T(8,128)(2,1)} %param.16) | copy-start | bytes 1382404
  7.2 93.9 %all-gather.4.cloned.1.call-start = ((), (), s32[]{:S(2)}) async-start(), calls=%async_computation.2 | async-start | bytes 2457600 | tf_op jit(solution)/shard_map/all_gather | solution.py:716
  7.9 144.1 %all-gather.6.cloned.1.call-start = ((), (), s32[]{:S(2)}) async-start(), calls=%async_computation.3 | async-start | bytes 2457600 | tf_op jit(solution)/shard_map/all_gather | solution.py:729
  48.4 3.7 copy-start.2
  49.9 3.7 copy-start.11
  52.9 1.7 copy-start.28
  53.6 4.1 copy-start.35
  81.5 3.3 copy-start.6
  82.4 2.4 copy-start.26
  82.4 2.4 copy-start.27
  102.4 2.8 copy-start.13
  102.4 2.8 copy-start.29
  102.4 3.4 copy-start.5
  106.7 89.8 %all-gather.8.cloned.1.call-start = ((), (), s32[]{:S(2)}) async-start(), calls=%async_computation.4 | async-start | bytes 2457600 | tf_op jit(solution)/shard_map/all_gather | solution.py:752
  152.0 99.2 %reduce-scatter.3.cloned.1.call-start = ((), (), s32[]{:S(2)}) async-start(), calls=%async_computation.5 | async-start | bytes 2478080 | tf_op jit(solution)/shard_map/reduce_scatter | solution.py:756
  196.5 3.6 copy-start.37
  196.5 3.6 copy-start.39
  200.1 1.6 copy-start.36
  205.5 1.7 copy-start.41
  205.5 1.7 copy-start.43
  205.5 2.2 copy-start.40
  210.9 181.3 %all-reduce.12.cloned.1.call-start = ((), (), s32[]{:S(2)}) async-start(), calls=%async_computation.7 | async-start | bytes 7372800 | tf_op jit(solution)/shard_map/psum | solution.py:776
  217.1 4.9 %copy-start.38 = (bf16[1024,960]{0,1:T(8,128)(2,1)S(1)}, bf16[1024,960]{0,1:T(8,128)(2,1)}, u32[]{:S(2)}) copy-start(bf16[1024,960]{0,1:T(8,128)(2,1)} %all-gather.8.cloned.1.call-done) | copy-start | bytes 5898244
  217.1 4.9 %copy-start.44 = (bf16[1024,640]{0,1:T(8,128)(2,1)S(1)}, bf16[1024,640]{0,1:T(8,128)(2,1)}, u32[]{:S(2)}) copy-start(bf16[1024,640]{0,1:T(8,128)(2,1)} %copy-done.43) | copy-start | bytes 3932164
  222.0 2.8 copy-start.42
  252.4 65.3 %copy-start.3 = (f32[256,961]{0,1:T(8,128)}, f32[256,961]{0,1:T(8,128)S(1)}, u32[]{:S(2)}) copy-start(f32[256,961]{0,1:T(8,128)S(1)} %convert_element_type.177) | copy-start | bytes 2952196
  252.4 144.8 %reduce-scatter.5.cloned.1.call-start = ((), (), s32[]{:S(2)}) async-start(), calls=%async_computation.6 | async-start | bytes 2457600 | tf_op jit(solution)/shard_map/reduce_scatter | solution.py:814
  254.6 1.2 copy-start.10
  254.6 1.8 copy-start.14
  256.5 1.8 copy-start.8
  289.0 28.7 %copy-start.19 = (bf16[256,1024]{1,0:T(8,128)(2,1)S(1)}, bf16[256,1024]{1,0:T(8,128)(2,1)}, u32[]{:S(2)}) copy-start(bf16[256,1024]{1,0:T(8,128)(2,1)} %get-tuple-element.54) | copy-start | bytes 1572868
  317.7 2.5 copy-start.12
  317.7 2.5 copy-start.15
  317.7 2.4 copy-start.33
  320.1 2.7 copy-start.7
  321.8 2.7 copy-start.9
  324.5 3.2 copy-start.20
  397.2 3.0 copy-start.17
  400.2 1.8 copy-start.16
  401.9 1.6 copy-start.25
  403.7 1.0 copy-start.24
  403.7 2.1 copy-start.23
  403.8 4.5 %copy-start.4 = (f32[256,961]{0,1:T(8,128)S(1)}, f32[256,961]{0,1:T(8,128)}, u32[]{:S(2)}) copy-start(f32[256,961]{0,1:T(8,128)} %copy-done.3) | copy-start | bytes 2952196
  403.8 4.5 %copy-start.18 = (f32[256,960]{0,1:T(8,128)S(1)}, f32[256,960]{0,1:T(8,128)}, u32[]{:S(2)}) copy-start(f32[256,960]{0,1:T(8,128)} %get-tuple-element.120) | copy-start | bytes 2949124
  403.8 4.5 %copy-start.22 = (bf16[256,960]{0,1:T(8,128)(2,1)S(1)}, bf16[256,960]{0,1:T(8,128)(2,1)}, u32[]{:S(2)}) copy-start(bf16[256,960]{0,1:T(8,128)(2,1)} %reduce-scatter.5.cloned.1.call-done) | copy-start | bytes 1474564
  403.8 4.5 %copy-start.30 = (f32[256]{0:T(256)S(1)}, f32[256]{0:T(256)}, u32[]{:S(2)}) copy-start(f32[256]{0:T(256)} %get-tuple-element.111) | copy-start | bytes 3076
  403.8 4.5 %copy-start.31 = (f32[256]{0:T(256)S(1)}, f32[256]{0:T(256)}, u32[]{:S(2)}) copy-start(f32[256]{0:T(256)} %get-tuple-element.121) | copy-start | bytes 3076
  403.8 4.5 %copy-start.32 = (f32[256]{0:T(256)S(1)}, f32[256]{0:T(256)}, u32[]{:S(2)}) copy-start(f32[256]{0:T(256)} %broadcast_multiply_fusion) | copy-start | bytes 3076
  403.9 4.5 %copy-start.34 = (f32[256,1]{0,1:T(1,128)S(1)}, f32[256,1]{0,1:T(1,128)}, u32[]{:S(2)}) copy-start(f32[256,1]{0,1:T(1,128)} %copy-done.33) | copy-start | bytes 3076
  408.3 2.0 copy-start.1
Sparse Core Ops, SparseCore 0:
  9.6 54.0 all-gather.3
  106.8 45.1 all-gather.5
  154.2 42.2 all-gather.7
  211.0 40.1 reduce-scatter.2
  254.8 83.6 all-reduce.11
  341.3 55.8 reduce-scatter.4

commit v7 on v6

--- a/solution.py
+++ b/solution.py
@@ -745,10 +745,10 @@
     attended, w_out_full = lax.optimization_barrier((attended, w_out_full))
     outcome = attended.astype(jnp.bfloat16)
     branch = dot(outcome, w_out_full, (0, 0))
+    branch, grad_ffn_all = lax.optimization_barrier((branch, grad_ffn_all))
     middle = hidden + branch
     normed_two, inv_two = norm_forward(middle, gain_two)
     normed_two = normed_two.astype(jnp.bfloat16)
-    normed_two, grad_ffn_all = lax.optimization_barrier((normed_two, grad_ffn_all))
     normed_all = lax.all_gather(normed_two, "fsdp", axis=0, tiled=True)
     inner_act, grad_gate_act, grad_up_act, grad_normed_part = ffn_both(
         normed_all, grad_ffn_all, w_gate, w_up, w_down

time: 419 us -> 375 us (0.89)
  waiting for transfers between devices: 118 us -> 74.4 us
    all_gather x1, waiting for transfers between devices: 44.3 us -> 1.2 us  [on_device(): grad_ffn_all = lax.all_gather(grad_ffn, 'fsdp', axis=0, tiled=True)]
  transfers between devices with their start and end apart: 6 -> 6, of which waited for: 4 -> 4; matrix products, arithmetic and copies ran while one was open for 13% -> 16% of each run, Pallas kernels for 46% -> 51%
where the time goes in v7:
time: 375 us
  Pallas kernels  191 us (51%)
  waiting for transfers between devices  74.4 us (20%)
  matrix products  46.5 us (12%)
  other arithmetic  26 us (7%)
  local copies, waits for them, and re-layouts  20.7 us (6%)
  between operations  15.5 us (4%)
    pallas_call x1, Pallas kernels, reduce_rows(): pl.pallas_call(functools.partial(reduce_rows_kernel, depth, count), out_s...  62.5 us
    all_gather x1, waiting for transfers between devices, on_device(): normed_all = lax.all_gather(normed_two, 'fsdp', axis=0, tiled=True)  43.9 us
    pallas_call x1, Pallas kernels, gather_rows(): pl.pallas_call(functools.partial(gather_rows_kernel, depth, count), out_s...  34.7 us
    pallas_call x1, Pallas kernels, attend_back(): pl.pallas_call(attend_back_kernel, out_shape=(jax.ShapeDtypeStruct((slots...  28.7 us
    pallas_call x1, Pallas kernels, scatter_plane(): pl.pallas_call(scatter_plane_kernel, out_shape=jax.ShapeDtypeStruct(block...  28.1 us
    reduce_scatter x1, waiting for transfers between devices, on_device(): lax.psum_scatter(grad_normed_part, 'fsdp', scatter_dimension=0, tiled=True)  23.7 us
    pallas_call x1, Pallas kernels, gather_plane(): pl.pallas_call(gather_plane_kernel, out_shape=(jax.ShapeDtypeStruct((SPAN...  22.1 us
    dot_general x9, matrix products, dot(): lax.dot_general(left, right, (((dims[0],), (dims[1],)), ((), ())), prefer...  19.5 us
  transfers between devices with their start and end apart: 6, of which 4 were waited for; matrix products, arithmetic and copies ran while one was open for 16% of the time, Pallas kernels for 51%

profile of v7, /device:TPU:0, one launch (start us, length us, event | category | flops | bytes accessed | tf_op | source)
XLA Modules:
  0.0 375.2 jit_solution(12120616649254810373)
XLA Ops:
  7.2 0.7 all-gather.4.cloned.1.call-update
  8.0 0.7 stack.21
  8.6 0.7 stack.22
  9.3 0.7 stack.23
  10.0 1.9 concatenate.23
  12.0 0.8 pad.38.clone
  12.8 0.8 pad.58
  13.7 34.7 %shard_map.238 = (bf16[4,8,32,1024]{3,2,1,0:T(8,128)(2,1)}, bf16[4,8,32,643]{3,2,1,0:T(8,128)(2,1)}) custom-call(bf16[8,32,1024]{2,1,0:T(8,128)(2,1)} %bitcast.151, bf16[8,32,643]{2,1,0:T(8,128)(2,1)} %bitcast.156), custom_call_target="tpu_custom_call" | custom-call | bytes 102420480 | tf_op jit(solution)/shard_map/pallas_call | solution.py:201
  48.4 1.6 slice.102
  50.0 1.1 copy-done.13
  52.3 0.6 broadcast_select_fusion
  52.9 0.9 fusion.13
  54.5 2.0 fusion.5
  57.9 0.8 pad_maximum_fusion.1.kv_ref
  58.7 22.1 %shard_map.239 = (bf16[8,256,640]{2,1,0:T(8,128)(2,1)}, s32[8,1,256]{2,1,0:T(1,128)}) custom-call(bf16[256,640]{1,0:T(8,128)(2,1)} %pad_maximum_fusion.1.kv_ref, s32[1,256]{1,0:T(1,128)} %and_select_fusion.tag_ref), custom_call_target="tpu_custom_call" | custom-call | bytes 78643200 | tf_op jit(solution)/shard_map/pallas_call | solution.py:252
  80.8 0.8 slice.83
  81.7 1.0 multiply_convert_fusion.4
  82.8 1.1 pad.39
  83.8 0.7 pad_add_fusion.first_ref
  84.7 2.3 fusion.1
  87.3 0.9 maximum_multiply_fusion
  88.1 15.3 %shard_map.240 = (f32[960,256]{1,0:T(8,128)}, f32[16,256]{1,0:T(8,128)}) custom-call(s32[18]{0:T(128)} %pad_add_fusion.first_ref, bf16[960,256]{1,0:T(8,128)(2,1)} %bitcast.163, bf16[2048,640]{1,0:T(8,128)(2,1)} %bitcast.186, s32[1,256]{1,0:T(1,128)} %pos_ref.3, s32[16,1,128]{2,1,0:T(1,128)} %bitcast.191), custom_call_target="tpu_custom_call" | custom-call | flops 16106127360 | bytes 2621440 | tf_op jit(solution)/shard_map/pallas_call | solution.py:579
  103.4 1.3 convert_element_type.167
  104.7 0.8 copy-done.11
  105.5 2.5 fusion.43
  107.9 1.2 all-gather.6.cloned.1.call-done
  109.4 1.0 multiply_convert_fusion.3
  110.6 43.9 %all-gather.8.cloned.1.call-done = bf16[1024,960]{0,1:T(8,128)(2,1)} async-done(((bf16[256,960]{0,1:T(8,128)(2,1)}), bf16[1024,960]{0,1:T(8,128)(2,1)}) %all-gather.8.cloned.1.call-update) | async-done | bytes 1966096 | tf_op jit(solution)/shard_map/all_gather | solution.py:752
  154.4 3.6 fusion.44
  158.1 1.6 fusion.45
  159.7 3.8 %multiply_reduce_fusion = (bf16[1024]{0:T(1024)(128)(2,1)S(1)}, bf16[1024,640]{0,1:T(8,128)(2,1)}, bf16[1024,640]{0,1:T(8,128)(2,1)S(1)}, bf16[1024,640]{0,1:T(8,128)(2,1)S(1)}) fusion(f32[1024,640]{0,1:T(8,128)S(1)} %fusion.44, f32[1024,640]{0,1:T(8,128)S(1)} %fusion.45, bf16[1024,960]{0,1:T(8,128)(2,1)S(1)} %copy-done.36, bf16[640,960]{0,1:T(8,128)(2,1)S(1)} %copy-done), kind=kOutput, calls=%fused_computation.1 | convolution fusion | flops 1270086656 | bytes 12371968 | tf_op jit(solution)/shard_map/dot_general | solution.py:71
  163.5 1.7 fusion.46
  165.7 1.7 add_convert_fusion
  167.4 1.4 pad_maximum_fusion
  168.9 1.9 pad.40
  170.8 4.3 %convolution_convert_fusion.2 = bf16[1024,960]{0,1:T(8,128)(2,1)} fusion(bf16[640,960]{0,1:T(8,128)(2,1)S(1)} %copy-done, bf16[1024,640]{0,1:T(8,128)(2,1)} %get-tuple-element.87), kind=kOutput, calls=%fused_computation.14 | convolution fusion | flops 1259274240 | bytes 4505600 | tf_op jit(solution)/shard_map/dot_general | solution.py:759
  175.1 4.9 %convolution_convert_fusion.4 = bf16[640,960]{0,1:T(8,128)(2,1)} fusion(bf16[1024,640]{0,1:T(8,128)(2,1)} %get-tuple-element.87, bf16[1024,960]{0,1:T(8,128)(2,1)} %all-gather.6.cloned.1.call-done), kind=kOutput, calls=%fused_computation.16 | convolution fusion | flops 1258905600 | bytes 4505600 | tf_op jit(solution)/shard_map/dot_general | solution.py:766
  179.9 2.8 convolution_convert_fusion.5
  182.7 2.8 convolution_convert_fusion.6
  185.5 23.7 %reduce-scatter.3.cloned.1.call-done = bf16[256,961]{0,1:T(8,128)(2,1)} async-done(((bf16[1024,961]{0,1:T(8,128)(2,1)}), bf16[256,961]{0,1:T(8,128)(2,1)}) %reduce-scatter.3.cloned.1.call-update) | async-done | bytes 492048 | tf_op jit(solution)/shard_map/reduce_scatter | solution.py:756
  209.2 1.1 convert_element_type.177
  211.1 1.2 multiply_sine_fusion
  213.4 1.1 copy-done.6
  214.7 1.8 convert_multiply_fusion.1
  216.5 1.6 reduce_sum.104
  218.1 0.6 pad.42.delta_ref
  218.7 28.7 %shard_map.241 = (bf16[256,1024]{1,0:T(8,128)(2,1)}, bf16[2048,640]{1,0:T(8,128)(2,1)}) custom-call(s32[18]{0:T(128)} %pad_add_fusion.first_ref, bf16[960,256]{1,0:T(8,128)(2,1)} %bitcast.164, bf16[2048,640]{1,0:T(8,128)(2,1)} %bitcast.187, s32[1,256]{1,0:T(1,128)} %pos_ref.3, s32[16,1,128]{2,1,0:T(1,128)} %bitcast.192, ...), custom_call_target="tpu_custom_call" | custom-call | flops 30198988800 | bytes 5242880 | tf_op jit(solution)/shard_map/pallas_call | solution.py:667
  247.5 28.1 %shard_map.242 = bf16[8,32,640]{2,1,0:T(8,128)(2,1)} custom-call(bf16[8,8,32,640]{3,2,1,0:T(8,128)(2,1)} %bitcast.150, f32[8,32,32]{2,1,0:T(8,128)} %get-tuple-element.103.cos_ref, f32[8,32,32]{2,1,0:T(8,128)} %get-tuple-element.102.sin_ref), custom_call_target="tpu_custom_call" | custom-call | bytes 78643200 | tf_op jit(solution)/shard_map/pallas_call | solution.py:368
  275.7 2.4 fusion.3
  278.1 1.6 fusion.30
  280.2 0.7 pad.44.refs_3_
  280.8 1.6 convolution_convert_fusion.3
  282.5 3.2 convolution_convert_fusion.1
  285.7 2.0 convolution_convert_fusion
  287.7 62.5 %shard_map.243 = (bf16[8,32,1024]{2,1,0:T(8,128)(2,1)}, bf16[8,32,1024]{2,1,0:T(8,128)(2,1)}, bf16[8,32,640]{2,1,0:T(8,128)(2,1)}, f32[8,8,128]{2,1,0:T(8,128)}) custom-call(bf16[4,8,32,1024]{3,2,1,0:T(8,128)(2,1)} %bitcast.142, bf16[4,8,32,1024]{3,2,1,0:T(8,128)(2,1)} %bitcast.143, bf16[4,8,32,640]{3,2,1,0:T(8,128)(2,1)} %bitcast.144, ...), custom_call_target="tpu_custom_call" | custom-call | bytes 167116800 | tf_op jit(solution)/shard_map/pallas_call | solution.py:450
  350.8 4.8 %reduce-scatter.5.cloned.1.call-done = bf16[256,960]{0,1:T(8,128)(2,1)} async-done(((bf16[1024,960]{0,1:T(8,128)(2,1)}), bf16[256,960]{0,1:T(8,128)(2,1)}) %reduce-scatter.5.cloned.1.call-update) | async-done | bytes 491536 | tf_op jit(solution)/shard_map/reduce_scatter | solution.py:814
  355.6 3.0 convert_element_type.194
  358.6 1.6 convert_element_type.195
  360.3 1.6 convert_element_type.196
  362.3 0.9 fusion.39
  363.1 1.1 slice.112
  364.2 0.6 fusion.41
  364.8 1.5 slice_convert_fusion
  366.4 1.9 fusion.37
  (143 shorter events, 7.8 us)
Async XLA Ops:
  7.2 152.5 %copy-start = (bf16[640,960]{0,1:T(8,128)(2,1)S(1)}, bf16[640,960]{0,1:T(8,128)(2,1)}, u32[]{:S(2)}) copy-start(bf16[640,960]{0,1:T(8,128)(2,1)} %param.22) | copy-start | bytes 3686404
  7.2 5.6 %copy-start.21 = (bf16[240,960]{1,0:T(8,128)(2,1)S(1)}, bf16[240,960]{1,0:T(8,128)(2,1)}, u32[]{:S(2)}) copy-start(bf16[240,960]{1,0:T(8,128)(2,1)} %param.16) | copy-start | bytes 1382404
  7.2 96.2 %all-gather.4.cloned.1.call-start = ((), (), s32[]{:S(2)}) async-start(), calls=%async_computation.2 | async-start | bytes 2457600 | tf_op jit(solution)/shard_map/all_gather | solution.py:716
  7.9 101.2 %all-gather.6.cloned.1.call-start = ((), (), s32[]{:S(2)}) async-start(), calls=%async_computation.3 | async-start | bytes 2457600 | tf_op jit(solution)/shard_map/all_gather | solution.py:729
  48.4 3.6 copy-start.35
  48.4 3.7 copy-start.2
  48.4 3.9 %copy-start.28 = (s32[1,256]{1,0:T(1,128)S(1)}, s32[1,256]{1,0:T(1,128)}, u32[]{:S(2)}) copy-start(s32[1,256]{1,0:T(1,128)} %pos_ref.3) | copy-start | bytes 3076
  48.4 4.5 %copy-start.5 = (bf16[1,256,960]{1,2,0:T(8,128)(2,1)S(1)}, bf16[1,256,960]{1,2,0:T(8,128)(2,1)}, u32[]{:S(2)}) copy-start(bf16[1,256,960]{1,2,0:T(8,128)(2,1)} %param.26) | copy-start | bytes 1474564
  50.0 1.1 copy-start.13
  53.8 100.6 %all-gather.8.cloned.1.call-start = ((), (), s32[]{:S(2)}) async-start(), calls=%async_computation.4 | async-start | bytes 2457600 | tf_op jit(solution)/shard_map/all_gather | solution.py:752
  83.8 3.2 copy-start.7
  84.7 2.4 copy-start.26
  84.7 2.4 copy-start.27
  104.7 0.8 copy-start.11
  110.4 98.8 %reduce-scatter.3.cloned.1.call-start = ((), (), s32[]{:S(2)}) async-start(), calls=%async_computation.5 | async-start | bytes 2478080 | tf_op jit(solution)/shard_map/reduce_scatter | solution.py:756
  154.4 3.6 copy-start.37
  154.4 3.6 copy-start.39
  158.1 1.6 copy-start.36
  163.5 1.7 copy-start.41
  163.5 1.7 copy-start.43
  163.5 2.2 copy-start.40
  168.9 181.9 %all-reduce.12.cloned.1.call-start = ((), (), s32[]{:S(2)}) async-start(), calls=%async_computation.7 | async-start | bytes 7372800 | tf_op jit(solution)/shard_map/psum | solution.py:776
  175.1 4.9 %copy-start.38 = (bf16[1024,960]{0,1:T(8,128)(2,1)S(1)}, bf16[1024,960]{0,1:T(8,128)(2,1)}, u32[]{:S(2)}) copy-start(bf16[1024,960]{0,1:T(8,128)(2,1)} %all-gather.8.cloned.1.call-done) | copy-start | bytes 5898244
  175.1 4.9 %copy-start.44 = (bf16[1024,640]{0,1:T(8,128)(2,1)S(1)}, bf16[1024,640]{0,1:T(8,128)(2,1)}, u32[]{:S(2)}) copy-start(bf16[1024,640]{0,1:T(8,128)(2,1)} %copy-done.43) | copy-start | bytes 3932164
  179.9 2.8 copy-start.42
  210.3 65.3 %copy-start.3 = (f32[256,961]{0,1:T(8,128)}, f32[256,961]{0,1:T(8,128)S(1)}, u32[]{:S(2)}) copy-start(f32[256,961]{0,1:T(8,128)S(1)} %convert_element_type.177) | copy-start | bytes 2952196
  210.3 0.7 copy-start.29
  210.3 145.2 %reduce-scatter.5.cloned.1.call-start = ((), (), s32[]{:S(2)}) async-start(), calls=%async_computation.6 | async-start | bytes 2457600 | tf_op jit(solution)/shard_map/reduce_scatter | solution.py:814
  212.9 1.5 copy-start.6
  213.0 1.8 copy-start.12
  214.7 1.8 copy-start.9
  247.5 28.2 %copy-start.19 = (bf16[256,1024]{1,0:T(8,128)(2,1)S(1)}, bf16[256,1024]{1,0:T(8,128)(2,1)}, u32[]{:S(2)}) copy-start(bf16[256,1024]{1,0:T(8,128)(2,1)} %get-tuple-element.54) | copy-start | bytes 1572868
  275.6 2.5 copy-start.14
  275.6 2.5 copy-start.15
  275.7 2.4 copy-start.33
  278.1 2.7 copy-start.8
  279.8 2.7 copy-start.10
  282.5 3.2 copy-start.20
  355.6 3.0 copy-start.17
  358.6 1.8 copy-start.16
  360.3 1.6 copy-start.25
  362.1 2.7 copy-start.23
  362.1 2.7 copy-start.24
  362.2 4.2 %copy-start.4 = (f32[256,961]{0,1:T(8,128)S(1)}, f32[256,961]{0,1:T(8,128)}, u32[]{:S(2)}) copy-start(f32[256,961]{0,1:T(8,128)} %copy-done.3) | copy-start | bytes 2952196
  362.2 4.1 %copy-start.18 = (f32[256,960]{0,1:T(8,128)S(1)}, f32[256,960]{0,1:T(8,128)}, u32[]{:S(2)}) copy-start(f32[256,960]{0,1:T(8,128)} %get-tuple-element.119) | copy-start | bytes 2949124
  362.2 4.1 %copy-start.22 = (bf16[256,960]{0,1:T(8,128)(2,1)S(1)}, bf16[256,960]{0,1:T(8,128)(2,1)}, u32[]{:S(2)}) copy-start(bf16[256,960]{0,1:T(8,128)(2,1)} %reduce-scatter.5.cloned.1.call-done) | copy-start | bytes 1474564
  362.2 4.1 %copy-start.30 = (f32[256]{0:T(256)S(1)}, f32[256]{0:T(256)}, u32[]{:S(2)}) copy-start(f32[256]{0:T(256)} %get-tuple-element.111) | copy-start | bytes 3076
  362.2 4.1 %copy-start.31 = (f32[256]{0:T(256)S(1)}, f32[256]{0:T(256)}, u32[]{:S(2)}) copy-start(f32[256]{0:T(256)} %broadcast_multiply_fusion) | copy-start | bytes 3076
  362.2 4.1 %copy-start.32 = (f32[256]{0:T(256)S(1)}, f32[256]{0:T(256)}, u32[]{:S(2)}) copy-start(f32[256]{0:T(256)} %get-tuple-element.83) | copy-start | bytes 3076
  362.3 4.1 %copy-start.34 = (f32[256,1]{0,1:T(1,128)S(1)}, f32[256,1]{0,1:T(1,128)}, u32[]{:S(2)}) copy-start(f32[256,1]{0,1:T(1,128)} %copy-done.33) | copy-start | bytes 3076
  366.3 2.0 copy-start.1
Sparse Core Ops, SparseCore 0:
  9.6 54.0 all-gather.3
  65.8 43.2 all-gather.5
  111.3 43.1 all-gather.7
  169.0 40.1 reduce-scatter.2
  212.7 84.1 all-reduce.11
  299.6 55.8 reduce-scatter.4

commit v8 on v7

--- a/solution.py
+++ b/solution.py
@@ -274,48 +274,80 @@
     return total
 
 
+def across_of(chip, core, way):
+    along_x, along_y = lax.rem(chip, 2), chip // 2
+    along_x = 1 - along_x if way % 2 else along_x
+    along_y = 1 - along_y if way // 2 else along_y
+    return 2 * (2 * along_y + along_x) + core
+
+
 def reduce_plane(arrays, h_sems, p_sems):
     me, core, chip, partner = plane_of()
     layer = lax.axis_index("fsdp")
-    handed, spread = [], []
+    ways = (3, 1, 2, 0)
+    near = (across_of(chip, core, 1), across_of(chip, core, 2))
+    handed, started, last = [], [], []
     for a, (piece_of, halves, sums, arrived) in enumerate(arrays):
-        for j in range(CHIPS):
-            slot = (j + 1) % CHIPS
+        for way in ways:
             handed.append(
                 send(
-                    piece_of(chip_at(chip, 1 - core, slot)),
-                    halves.at[slot],
-                    h_sems.at[0, a, slot],
-                    h_sems.at[1, a, slot],
+                    piece_of(across_of(chip, 1 - core, way)),
+                    halves.at[way],
+                    h_sems.at[0, a, way],
+                    h_sems.at[1, a, way],
                     (partner, layer),
                 )
             )
     for a, (piece_of, halves, sums, arrived) in enumerate(arrays):
-        for j in range(CHIPS):
-            slot = (j + 1) % CHIPS
+        middle = sums.shape[1] // 2
+        sides = (pl.ds(0, middle), pl.ds(middle, middle))
+        copies = {}
+
+        def pass_on(way, side, slot, hop, a=a, sums=sums, arrived=arrived, sides=sides):
+            number = 2 * slot + side
+            return send(
+                sums.at[way, sides[side]],
+                arrived.at[slot, sides[side]],
+                p_sems.at[0, a, number],
+                p_sems.at[1, a, number],
+                (near[hop], layer),
+            )
+
+        for j, way in enumerate(ways):
             handed[a * CHIPS + j].wait_recv()
-            mine = chip_at(chip, core, slot)
-
-            def add_half(slab, carry, piece=piece_of(mine), halves=halves, sums=sums, slot=slot):
-                sums[slot, slab] = added(piece[slab], halves[slot, slab]).astype(sums.dtype)
+            mine = piece_of(across_of(chip, core, way))
+
+            def add_half(slab, carry, mine=mine, halves=halves, sums=sums, way=way):
+                sums[way, slab] = added(mine[slab], halves[way, slab]).astype(sums.dtype)
                 return carry
 
             lax.fori_loop(0, sums.shape[1], add_half, 0)
-            if slot:
-                spread.append(
-                    send(
-                        sums.at[slot],
-                        arrived.at[slot - 1],
-                        p_sems.at[0, a, slot - 1],
-                        p_sems.at[1, a, slot - 1],
-                        (mine, layer),
-                    )
-                )
-    return handed, spread
+            if way == 3:
+                for side in range(2):
+                    copies[0, side] = pass_on(3, side, 0, side)
+            elif way:
+                copies[1, way - 1] = pass_on(way, way - 1, 1, way - 1)
+        started.append((copies, pass_on))
+    for (copies, pass_on), (_, _, sums, arrived) in zip(started, arrays):
+        middle = sums.shape[1] // 2
+        for side in range(2):
+            copies[0, side].wait_recv()
+            way = 2 - side
+
+            def add_opposite(slab, carry, way=way, sums=sums, arrived=arrived):
+                total = added(sums[way, slab], arrived[0, slab])
+                sums[way, slab] = total.astype(sums.dtype)
+                return carry
+
+            lax.fori_loop(side * middle, (side + 1) * middle, add_opposite, 0)
+            copies[2, side] = pass_on(way, side, 2, 1 - side)
+        last.append([copies[slot, side] for slot in (1, 2) for side in range(2)])
+    everything = handed + [copy for copies, _ in started for copy in copies.values()]
+    return everything, last
 
 
 def plane_total(sums, arrived, slab):
-    return added(sums[0, slab], *(arrived[j, slab] for j in range(CHIPS - 1)))
+    return added(sums[0, slab], arrived[1, slab], arrived[2, slab])
 
 
 def plane_scratch(block, dtype):
@@ -338,10 +370,11 @@
 def scatter_plane_kernel(x_ref, cos_ref, sin_ref, out_ref, halves, sums, arrived, h_sems, p_sems):
     me, core, chip, partner = plane_of()
     layer = lax.axis_index("fsdp")
-    greet([(chip_at(chip, core, j), layer) for j in range(1, CHIPS)] + [(partner, layer)])
+    near = [across_of(chip, core, way) for way in (1, 2)]
+    greet([(peer, layer) for peer in near + [partner]])
     arrays = [(lambda piece: x_ref.at[piece], halves, sums, arrived)]
-    handed, spread = reduce_plane(arrays, h_sems, p_sems)
-    for copy in spread:
+    started, last = reduce_plane(arrays, h_sems, p_sems)
+    for copy in last[0]:
         copy.wait_recv()
 
     def add_slab(slab, carry):
@@ -352,7 +385,7 @@
         return carry
 
     lax.fori_loop(0, x_ref.shape[1], add_slab, 0)
-    for copy in handed + spread:
+    for copy in started:
         copy.wait_send()
 
 
@@ -371,7 +404,7 @@
         in_specs=in_vmem(3),
         out_specs=in_vmem(1)[0],
         scratch_shapes=plane_scratch(block, values.dtype)
-        + [pltpu.SemaphoreType.DMA((2, 1, CHIPS)), pltpu.SemaphoreType.DMA((2, 1, CHIPS - 1))],
+        + [pltpu.SemaphoreType.DMA((2, 1, CHIPS)), pltpu.SemaphoreType.DMA((2, 1, 6))],
         compiler_params=comm_params(3),
         cost_estimate=comm_cost(values.size * 2),
     )(
@@ -394,10 +427,10 @@
         halves, sums, arrived, layers_ref = scratch[4 * a : 4 * a + 4]
         arrays.append((lambda piece, x_ref=x_ref: x_ref.at[:, piece], halves, sums, arrived))
         across.append(layers_ref)
-    handed, spread = reduce_plane(arrays, h_sems, p_sems)
+    started, last = reduce_plane(arrays, h_sems, p_sems)
     moved = []
     for a, (_, _, sums, arrived) in enumerate(arrays):
-        for copy in spread[a * (CHIPS - 1) : (a + 1) * (CHIPS - 1)]:
+        for copy in last[a]:
             copy.wait_recv()
         for d in list(range(1, depth)) + [0]:
             target = lax.rem(layer + d, depth)
@@ -429,7 +462,7 @@
             passed.append(
                 send(block, block, f_sems.at[0, a, j], f_sems.at[1, a, j], (partner, layer))
             )
-    for copy in handed + spread + moved + given:
+    for copy in started + moved + given:
         copy.wait_send()
     for copy in passed:
         copy.wait()
@@ -455,7 +488,7 @@
         scratch_shapes=scratch
         + [
             pltpu.SemaphoreType.DMA((2, count, CHIPS)),
-            pltpu.SemaphoreType.DMA((2, count, CHIPS - 1)),
+            pltpu.SemaphoreType.DMA((2, count, 6)),
             pltpu.SemaphoreType.DMA((2, count, depth - 1)),
             pltpu.SemaphoreType.DMA((2, count, CHIPS - 1)),
             pltpu.SemaphoreType.DMA((2, count, CHIPS)),
@@ -812,14 +845,16 @@
     layered.append(vectors.reshape(depth, -1, 128))
     owned = reduce_rows(layered, 4)
     ffn_out = lax.psum_scatter(ffn_part, "fsdp", scatter_dimension=0, tiled=True)
-    *owned, totals, ffn_out = lax.optimization_barrier((*owned, totals, ffn_out))
-    increment = branch + ffn_out.astype(jnp.float32)
-    block_out = live_mask * (hidden + chosen_mask * gating * increment)
+    *owned, totals = lax.optimization_barrier((*owned, totals))
     total_out, total_q, total_kv = (own[:own_rows].astype(jnp.float32) for own in owned[:3])
     total_q, total_out = total_q[:, :qdim], total_out[:, :width]
     total_k, total_v = total_kv[:, :kdim], total_kv[:, kdim:]
     mine = owned[3].reshape(-1, 8, 128)[:, 0].reshape(-1)[: 3 * own_rows].reshape(3, own_rows)
-    total_gate, total_up, total_down = (total.astype(jnp.float32) for total in totals)
+    totals = [total.astype(jnp.float32) for total in totals]
+    ffn_out, *totals = lax.optimization_barrier((ffn_out, *totals))
+    total_gate, total_up, total_down = totals
+    increment = branch + ffn_out.astype(jnp.float32)
+    block_out = live_mask * (hidden + chosen_mask * gating * increment)
     return (
         block_out.astype(jnp.bfloat16)[None],
         grad_tokens[None],

time: 375 us -> 377 us (level)
  Pallas kernels: 191 us -> 196 us
  waiting for transfers between devices: 74.4 us -> 69.5 us
    pallas_call x1, Pallas kernels: 62.5 us -> 71 us  [reduce_rows(): pl.pallas_call(functools.partial(reduce_rows_kernel, depth, count), out_s...]
    reduce_scatter x1, waiting for transfers between devices: 4.81 us -> 0.01 us  [on_device(): lax.psum_scatter(ffn_part, 'fsdp', scatter_dimension=0, tiled=True)]
    pallas_call x1, Pallas kernels: 28.1 us -> 23.9 us  [scatter_plane(): pl.pallas_call(scatter_plane_kernel, out_shape=jax.ShapeDtypeStruct(block...]
  transfers between devices with their start and end apart: 6 -> 6, of which waited for: 4 -> 3; matrix products, arithmetic and copies ran while one was open for 16% -> 19% of each run, Pallas kernels for 51% -> 52%
where the time goes in v8:
time: 377 us; the launch traced here: 376 us
  Pallas kernels  196 us (52%)
  waiting for transfers between devices  69.5 us (18%)
  matrix products  46.6 us (12%)
  other arithmetic  27.2 us (7%)
  local copies, waits for them, and re-layouts  20.5 us (5%)
  between operations  15.4 us (4%)
    pallas_call x1, Pallas kernels, reduce_rows(): pl.pallas_call(functools.partial(reduce_rows_kernel, depth, count), out_s...  71 us
    all_gather x1, waiting for transfers between devices, on_device(): normed_all = lax.all_gather(normed_two, 'fsdp', axis=0, tiled=True)  43.8 us
    pallas_call x1, Pallas kernels, gather_rows(): pl.pallas_call(functools.partial(gather_rows_kernel, depth, count), out_s...  34.7 us
    pallas_call x1, Pallas kernels, attend_back(): pl.pallas_call(attend_back_kernel, out_shape=(jax.ShapeDtypeStruct((slots...  28.8 us
    pallas_call x1, Pallas kernels, scatter_plane(): pl.pallas_call(scatter_plane_kernel, out_shape=jax.ShapeDtypeStruct(block...  23.9 us
    reduce_scatter x1, waiting for transfers between devices, on_device(): lax.psum_scatter(grad_normed_part, 'fsdp', scatter_dimension=0, tiled=True)  23.6 us
    pallas_call x1, Pallas kernels, gather_plane(): pl.pallas_call(gather_plane_kernel, out_shape=(jax.ShapeDtypeStruct((SPAN...  22.1 us
    dot_general x9, matrix products, dot(): lax.dot_general(left, right, (((dims[0],), (dims[1],)), ((), ())), prefer...  19.5 us
  transfers between devices with their start and end apart: 6, of which 3 were waited for; matrix products, arithmetic and copies ran while one was open for 19% of the time, Pallas kernels for 52%

profile of v8, /device:TPU:0, one launch (start us, length us, event | category | flops | bytes accessed | tf_op | source)
XLA Modules:
  0.0 375.6 jit_solution(12038291980112107653)
XLA Ops:
  7.2 0.7 all-gather.4.cloned.1.call-update
  8.0 0.7 stack.21
  8.6 0.7 stack.22
  9.3 0.7 stack.23
  10.0 1.9 concatenate.23
  12.0 0.8 pad.38.clone
  12.8 0.8 pad.58
  13.7 34.7 %shard_map.238 = (bf16[4,8,32,1024]{3,2,1,0:T(8,128)(2,1)}, bf16[4,8,32,643]{3,2,1,0:T(8,128)(2,1)}) custom-call(bf16[8,32,1024]{2,1,0:T(8,128)(2,1)} %bitcast.151, bf16[8,32,643]{2,1,0:T(8,128)(2,1)} %bitcast.156), custom_call_target="tpu_custom_call" | custom-call | bytes 102420480 | tf_op jit(solution)/shard_map/pallas_call | solution.py:201
  48.4 1.6 slice.102
  50.0 1.1 copy-done.12
  52.8 0.9 fusion.13
  54.4 2.0 fusion.5
  57.2 0.6 and_select_fusion.tag_ref
  57.8 0.8 pad_maximum_fusion.1.kv_ref
  58.6 22.1 %shard_map.239 = (bf16[8,256,640]{2,1,0:T(8,128)(2,1)}, s32[8,1,256]{2,1,0:T(1,128)}) custom-call(bf16[256,640]{1,0:T(8,128)(2,1)} %pad_maximum_fusion.1.kv_ref, s32[1,256]{1,0:T(1,128)} %and_select_fusion.tag_ref), custom_call_target="tpu_custom_call" | custom-call | bytes 78643200 | tf_op jit(solution)/shard_map/pallas_call | solution.py:252
  80.7 0.8 slice.83
  81.6 1.0 multiply_convert_fusion.4
  82.7 1.1 pad.39
  83.8 0.7 pad_add_fusion.first_ref
  84.7 2.3 fusion.1
  87.2 0.9 maximum_multiply_fusion
  88.1 15.2 %shard_map.240 = (f32[960,256]{1,0:T(8,128)}, f32[16,256]{1,0:T(8,128)}) custom-call(s32[18]{0:T(128)} %pad_add_fusion.first_ref, bf16[960,256]{1,0:T(8,128)(2,1)} %bitcast.163, bf16[2048,640]{1,0:T(8,128)(2,1)} %bitcast.186, s32[1,256]{1,0:T(1,128)} %pos_ref.3, s32[16,1,128]{2,1,0:T(1,128)} %bitcast.191), custom_call_target="tpu_custom_call" | custom-call | flops 16106127360 | bytes 2621440 | tf_op jit(solution)/shard_map/pallas_call | solution.py:612
  103.3 1.3 convert_element_type.167
  104.6 0.8 copy-done.10
  105.4 2.5 fusion.43
  107.9 1.3 all-gather.6.cloned.1.call-done
  109.4 1.0 multiply_convert_fusion.3
  110.6 43.8 %all-gather.8.cloned.1.call-done = bf16[1024,960]{0,1:T(8,128)(2,1)} async-done(((bf16[256,960]{0,1:T(8,128)(2,1)}), bf16[1024,960]{0,1:T(8,128)(2,1)}) %all-gather.8.cloned.1.call-update) | async-done | bytes 1966096 | tf_op jit(solution)/shard_map/all_gather | solution.py:785
  154.4 3.6 fusion.44
  158.0 1.6 fusion.45
  159.7 3.7 multiply_reduce_fusion
  163.4 1.7 fusion.46
  165.6 1.7 add_convert_fusion
  167.3 1.4 pad_maximum_fusion
  168.8 1.9 pad.40
  170.7 4.4 %convolution_convert_fusion.2 = bf16[1024,960]{0,1:T(8,128)(2,1)} fusion(bf16[640,960]{0,1:T(8,128)(2,1)S(1)} %copy-done, bf16[1024,640]{0,1:T(8,128)(2,1)} %get-tuple-element.93), kind=kOutput, calls=%fused_computation.14 | convolution fusion | flops 1259274240 | bytes 4505600 | tf_op jit(solution)/shard_map/dot_general | solution.py:792
  175.1 4.9 %convolution_convert_fusion.4 = bf16[640,960]{0,1:T(8,128)(2,1)} fusion(bf16[1024,640]{0,1:T(8,128)(2,1)} %get-tuple-element.93, bf16[1024,960]{0,1:T(8,128)(2,1)} %all-gather.6.cloned.1.call-done), kind=kOutput, calls=%fused_computation.16 | convolution fusion | flops 1258905600 | bytes 4505600 | tf_op jit(solution)/shard_map/dot_general | solution.py:799
  180.0 2.8 convolution_convert_fusion.5
  182.8 2.8 convolution_convert_fusion.6
  185.5 23.6 %reduce-scatter.3.cloned.1.call-done = bf16[256,961]{0,1:T(8,128)(2,1)} async-done(((bf16[1024,961]{0,1:T(8,128)(2,1)}), bf16[256,961]{0,1:T(8,128)(2,1)}) %reduce-scatter.3.cloned.1.call-update) | async-done | bytes 492048 | tf_op jit(solution)/shard_map/reduce_scatter | solution.py:789
  209.1 1.1 convert_element_type.177
  211.1 1.2 multiply_sine_fusion
  212.3 0.6 multiply_reduce_fusion.1
  213.3 1.1 copy-done.5
  214.7 1.8 convert_multiply_fusion.1
  216.5 1.6 reduce_sum.104
  218.1 0.6 pad.42.delta_ref
  218.7 28.8 %shard_map.241 = (bf16[256,1024]{1,0:T(8,128)(2,1)}, bf16[2048,640]{1,0:T(8,128)(2,1)}) custom-call(s32[18]{0:T(128)} %pad_add_fusion.first_ref, bf16[960,256]{1,0:T(8,128)(2,1)} %bitcast.164, bf16[2048,640]{1,0:T(8,128)(2,1)} %bitcast.187, s32[1,256]{1,0:T(1,128)} %pos_ref.3, s32[16,1,128]{2,1,0:T(1,128)} %bitcast.192, ...), custom_call_target="tpu_custom_call" | custom-call | flops 30198988800 | bytes 5242880 | tf_op jit(solution)/shard_map/pallas_call | solution.py:700
  247.5 23.9 %shard_map.242 = bf16[8,32,640]{2,1,0:T(8,128)(2,1)} custom-call(bf16[8,8,32,640]{3,2,1,0:T(8,128)(2,1)} %bitcast.150, f32[8,32,32]{2,1,0:T(8,128)} %get-tuple-element.109.cos_ref, f32[8,32,32]{2,1,0:T(8,128)} %get-tuple-element.108.sin_ref), custom_call_target="tpu_custom_call" | custom-call | bytes 78643200 | tf_op jit(solution)/shard_map/pallas_call | solution.py:401
  271.4 2.4 fusion.3
  273.9 1.6 fusion.30
  275.9 0.7 pad.44.refs_3_
  276.6 1.6 convolution_convert_fusion.3
  278.2 3.2 convolution_convert_fusion.1
  281.4 2.0 convolution_convert_fusion
  283.4 71.0 %shard_map.243 = (bf16[8,32,1024]{2,1,0:T(8,128)(2,1)}, bf16[8,32,1024]{2,1,0:T(8,128)(2,1)}, bf16[8,32,640]{2,1,0:T(8,128)(2,1)}, f32[8,8,128]{2,1,0:T(8,128)}) custom-call(bf16[4,8,32,1024]{3,2,1,0:T(8,128)(2,1)} %bitcast.142, bf16[4,8,32,1024]{3,2,1,0:T(8,128)(2,1)} %bitcast.143, bf16[4,8,32,640]{3,2,1,0:T(8,128)(2,1)} %bitcast.144, ...), custom_call_target="tpu_custom_call" | custom-call | bytes 167116800 | tf_op jit(solution)/shard_map/pallas_call | solution.py:483
  355.0 3.0 convert_element_type.190
  358.0 1.6 convert_element_type.191
  359.8 1.6 convert_element_type.192
  361.6 0.8 slice.112
  362.4 0.6 fusion.41
  363.1 0.9 fusion.39
  364.0 1.5 slice_convert_fusion
  365.6 3.2 fusion.37
  (137 shorter events, 7.1 us)
Async XLA Ops:
  7.2 152.5 %copy-start = (bf16[640,960]{0,1:T(8,128)(2,1)S(1)}, bf16[640,960]{0,1:T(8,128)(2,1)}, u32[]{:S(2)}) copy-start(bf16[640,960]{0,1:T(8,128)(2,1)} %param.22) | copy-start | bytes 3686404
  7.2 5.6 %copy-start.19 = (bf16[240,960]{1,0:T(8,128)(2,1)S(1)}, bf16[240,960]{1,0:T(8,128)(2,1)}, u32[]{:S(2)}) copy-start(bf16[240,960]{1,0:T(8,128)(2,1)} %param.16) | copy-start | bytes 1382404
  7.2 96.1 %all-gather.4.cloned.1.call-start = ((), (), s32[]{:S(2)}) async-start(), calls=%async_computation.2 | async-start | bytes 2457600 | tf_op jit(solution)/shard_map/all_gather | solution.py:749
  7.9 101.2 %all-gather.6.cloned.1.call-start = ((), (), s32[]{:S(2)}) async-start(), calls=%async_computation.3 | async-start | bytes 2457600 | tf_op jit(solution)/shard_map/all_gather | solution.py:762
  48.4 3.6 copy-start.32
  48.4 3.7 copy-start.2
  48.4 3.9 %copy-start.25 = (s32[1,256]{1,0:T(1,128)S(1)}, s32[1,256]{1,0:T(1,128)}, u32[]{:S(2)}) copy-start(s32[1,256]{1,0:T(1,128)} %pos_ref.3) | copy-start | bytes 3076
  48.4 4.4 %copy-start.4 = (bf16[1,256,960]{1,2,0:T(8,128)(2,1)S(1)}, bf16[1,256,960]{1,2,0:T(8,128)(2,1)}, u32[]{:S(2)}) copy-start(bf16[1,256,960]{1,2,0:T(8,128)(2,1)} %param.26) | copy-start | bytes 1474564
  50.0 1.1 copy-start.12
  53.8 100.6 %all-gather.8.cloned.1.call-start = ((), (), s32[]{:S(2)}) async-start(), calls=%async_computation.4 | async-start | bytes 2457600 | tf_op jit(solution)/shard_map/all_gather | solution.py:785
  83.8 3.3 copy-start.6
  84.6 2.4 copy-start.23
  84.7 2.4 copy-start.24
  104.6 0.8 copy-start.10
  110.4 98.8 %reduce-scatter.3.cloned.1.call-start = ((), (), s32[]{:S(2)}) async-start(), calls=%async_computation.5 | async-start | bytes 2478080 | tf_op jit(solution)/shard_map/reduce_scatter | solution.py:789
  154.4 3.6 copy-start.34
  154.4 3.6 copy-start.36
  158.0 1.6 copy-start.33
  163.4 1.7 copy-start.38
  163.4 1.7 copy-start.40
  163.4 2.2 copy-start.37
  168.8 186.2 %all-reduce.12.cloned.1.call-start = ((), (), s32[]{:S(2)}) async-start(), calls=%async_computation.7 | async-start | bytes 7372800 | tf_op jit(solution)/shard_map/psum | solution.py:809
  175.1 4.9 %copy-start.35 = (bf16[1024,960]{0,1:T(8,128)(2,1)S(1)}, bf16[1024,960]{0,1:T(8,128)(2,1)}, u32[]{:S(2)}) copy-start(bf16[1024,960]{0,1:T(8,128)(2,1)} %all-gather.8.cloned.1.call-done) | copy-start | bytes 5898244
  175.1 4.9 %copy-start.41 = (bf16[1024,640]{0,1:T(8,128)(2,1)S(1)}, bf16[1024,640]{0,1:T(8,128)(2,1)}, u32[]{:S(2)}) copy-start(bf16[1024,640]{0,1:T(8,128)(2,1)} %copy-done.40) | copy-start | bytes 3932164
  180.0 2.8 copy-start.39
  210.2 61.2 %copy-start.3 = (f32[256,961]{0,1:T(8,128)}, f32[256,961]{0,1:T(8,128)S(1)}, u32[]{:S(2)}) copy-start(f32[256,961]{0,1:T(8,128)S(1)} %convert_element_type.177) | copy-start | bytes 2952196
  210.2 0.7 copy-start.26
  210.3 155.2 %reduce-scatter.5.cloned.1.call-start = ((), (), s32[]{:S(2)}) async-start(), calls=%async_computation.6 | async-start | bytes 2457600 | tf_op jit(solution)/shard_map/reduce_scatter | solution.py:847
  212.9 1.5 copy-start.5
  212.9 1.8 copy-start.11
  214.7 1.8 copy-start.8
  247.5 23.9 %copy-start.17 = (bf16[256,1024]{1,0:T(8,128)(2,1)S(1)}, bf16[256,1024]{1,0:T(8,128)(2,1)}, u32[]{:S(2)}) copy-start(bf16[256,1024]{1,0:T(8,128)(2,1)} %get-tuple-element.58) | copy-start | bytes 1572868
  271.4 2.5 copy-start.13
  271.4 2.5 copy-start.14
  271.4 2.4 copy-start.30
  273.9 2.7 copy-start.7
  275.5 2.7 copy-start.9
  278.2 3.2 copy-start.18
  355.0 3.0 copy-start.16
  358.0 1.8 copy-start.15
  359.8 1.6 copy-start.22
  361.5 2.5 copy-start.20
  361.5 2.5 copy-start.21
  363.1 2.4 copy-start.27
  363.1 2.4 copy-start.28
  363.1 2.4 copy-start.29
  363.1 2.4 copy-start.31
  365.5 3.2 copy-start.1
Sparse Core Ops, SparseCore 0:
  9.6 54.0 all-gather.3
  65.8 43.2 all-gather.5
  111.3 43.0 all-gather.7
  168.9 40.1 reduce-scatter.2
  212.7 80.2 all-reduce.11
  295.1 55.4 reduce-scatter.4

commit v9 on v8

--- a/solution.py
+++ b/solution.py
@@ -286,7 +286,7 @@
     layer = lax.axis_index("fsdp")
     ways = (3, 1, 2, 0)
     near = (across_of(chip, core, 1), across_of(chip, core, 2))
-    handed, started, last = [], [], []
+    handed, started = [], []
     for a, (piece_of, halves, sums, arrived) in enumerate(arrays):
         for way in ways:
             handed.append(
@@ -328,7 +328,9 @@
             elif way:
                 copies[1, way - 1] = pass_on(way, way - 1, 1, way - 1)
         started.append((copies, pass_on))
-    for (copies, pass_on), (_, _, sums, arrived) in zip(started, arrays):
+
+    def second_hop(a):
+        (copies, pass_on), (_, _, sums, arrived) = started[a], arrays[a]
         middle = sums.shape[1] // 2
         for side in range(2):
             copies[0, side].wait_recv()
@@ -341,9 +343,10 @@
 
             lax.fori_loop(side * middle, (side + 1) * middle, add_opposite, 0)
             copies[2, side] = pass_on(way, side, 2, 1 - side)
-        last.append([copies[slot, side] for slot in (1, 2) for side in range(2)])
-    everything = handed + [copy for copies, _ in started for copy in copies.values()]
-    return everything, last
+        handed.extend(copies.values())
+        return [copies[slot, side] for slot in (1, 2) for side in range(2)]
+
+    return handed, second_hop
 
 
 def plane_total(sums, arrived, slab):
@@ -373,8 +376,8 @@
     near = [across_of(chip, core, way) for way in (1, 2)]
     greet([(peer, layer) for peer in near + [partner]])
     arrays = [(lambda piece: x_ref.at[piece], halves, sums, arrived)]
-    started, last = reduce_plane(arrays, h_sems, p_sems)
-    for copy in last[0]:
+    started, second_hop = reduce_plane(arrays, h_sems, p_sems)
+    for copy in second_hop(0):
         copy.wait_recv()
 
     def add_slab(slab, carry):
@@ -427,9 +430,11 @@
         halves, sums, arrived, layers_ref = scratch[4 * a : 4 * a + 4]
         arrays.append((lambda piece, x_ref=x_ref: x_ref.at[:, piece], halves, sums, arrived))
         across.append(layers_ref)
-    started, last = reduce_plane(arrays, h_sems, p_sems)
-    moved = []
-    for a, (_, _, sums, arrived) in enumerate(arrays):
+    started, second_hop = reduce_plane(arrays, h_sems, p_sems)
+    last, moved, given, passed = [], [], [], []
+
+    def over_layers(a):
+        _, _, sums, arrived = arrays[a]
         for copy in last[a]:
             copy.wait_recv()
         for d in list(range(1, depth)) + [0]:
@@ -445,8 +450,9 @@
                         (me, target),
                     )
                 )
-    given, passed = [], []
-    for a, out_ref in enumerate(outs):
+
+    def hand_out(a):
+        out_ref = outs[a]
         for copy in moved[a * (depth - 1) : (a + 1) * (depth - 1)]:
             copy.wait_recv()
         parts = [across[a][0, 0]] + [across[a][1, d] for d in range(1, depth)]
@@ -455,6 +461,14 @@
         for j, peer in enumerate(peers):
             given.append(send(mine, mine, g_sems.at[0, a, j], g_sems.at[1, a, j], (peer, layer)))
         passed.append(send(mine, mine, f_sems.at[0, a, 3], f_sems.at[1, a, 3], (partner, layer)))
+
+    for step in range(count + 2):
+        if step < count:
+            last.append(second_hop(step))
+        if 0 < step <= count:
+            over_layers(step - 1)
+        if step > 1:
+            hand_out(step - 2)
     for a, out_ref in enumerate(outs):
         for j in range(CHIPS - 1):
             given[a * (CHIPS - 1) + j].wait_recv()
@@ -842,14 +856,14 @@
     vectors = jnp.pad(vectors.transpose(1, 0, 2).reshape(depth, -1), ((0, 0), (0, -3 * own_rows % 1024)))
     vectors = jnp.pad(vectors.reshape(depth, -1, 1, 128), ((0, 0), (0, 0), (0, 7), (0, 0)))
     layered = [grad.reshape(depth, padded_rows, -1) for grad in (grad_wout, grad_wq, grad_wkv)]
-    layered.append(vectors.reshape(depth, -1, 128))
+    layered.insert(0, vectors.reshape(depth, -1, 128))
     owned = reduce_rows(layered, 4)
     ffn_out = lax.psum_scatter(ffn_part, "fsdp", scatter_dimension=0, tiled=True)
     *owned, totals = lax.optimization_barrier((*owned, totals))
-    total_out, total_q, total_kv = (own[:own_rows].astype(jnp.float32) for own in owned[:3])
+    total_out, total_q, total_kv = (own[:own_rows].astype(jnp.float32) for own in owned[1:])
     total_q, total_out = total_q[:, :qdim], total_out[:, :width]
     total_k, total_v = total_kv[:, :kdim], total_kv[:, kdim:]
-    mine = owned[3].reshape(-1, 8, 128)[:, 0].reshape(-1)[: 3 * own_rows].reshape(3, own_rows)
+    mine = owned[0].reshape(-1, 8, 128)[:, 0].reshape(-1)[: 3 * own_rows].reshape(3, own_rows)
     totals = [total.astype(jnp.float32) for total in totals]
     ffn_out, *totals = lax.optimization_barrier((ffn_out, *totals))
     total_gate, total_up, total_down = totals

time: 377 us -> 376 us (level)
  no operation moved by 1% of the time
where the time goes in v9:
time: 376 us; the launch traced here: 373 us
  Pallas kernels  193 us (51%)
  waiting for transfers between devices  69.5 us (18%)
  matrix products  46.6 us (12%)
  other arithmetic  27.2 us (7%)
  local copies, waits for them, and re-layouts  20.5 us (5%)
  between operations  15.4 us (4%)
    pallas_call x1, Pallas kernels, reduce_rows(): pl.pallas_call(functools.partial(reduce_rows_kernel, depth, count), out_s...  68.8 us
    all_gather x1, waiting for transfers between devices, on_device(): normed_all = lax.all_gather(normed_two, 'fsdp', axis=0, tiled=True)  43.8 us
    pallas_call x1, Pallas kernels, gather_rows(): pl.pallas_call(functools.partial(gather_rows_kernel, depth, count), out_s...  34.7 us
    pallas_call x1, Pallas kernels, attend_back(): pl.pallas_call(attend_back_kernel, out_shape=(jax.ShapeDtypeStruct((slots...  28.8 us
    pallas_call x1, Pallas kernels, scatter_plane(): pl.pallas_call(scatter_plane_kernel, out_shape=jax.ShapeDtypeStruct(block...  23.7 us
    reduce_scatter x1, waiting for transfers between devices, on_device(): lax.psum_scatter(grad_normed_part, 'fsdp', scatter_dimension=0, tiled=True)  23.6 us
    pallas_call x1, Pallas kernels, gather_plane(): pl.pallas_call(gather_plane_kernel, out_shape=(jax.ShapeDtypeStruct((SPAN...  22.1 us
    dot_general x9, matrix products, dot(): lax.dot_general(left, right, (((dims[0],), (dims[1],)), ((), ())), prefer...  19.5 us
  transfers between devices with their start and end apart: 6, of which 3 were waited for; matrix products, arithmetic and copies ran while one was open for 19% of the time, Pallas kernels for 52%

profile of v9, /device:TPU:0, one launch (start us, length us, event | category | flops | bytes accessed | tf_op | source)
XLA Modules:
  0.0 373.2 jit_solution(14296665298662511280)
XLA Ops:
  7.2 0.7 all-gather.4.cloned.1.call-update
  8.0 0.7 stack.21
  8.6 0.7 stack.22
  9.3 0.7 stack.23
  10.0 1.9 concatenate.23
  12.0 0.8 pad.38.clone
  12.8 0.8 pad.58
  13.7 34.7 %shard_map.238 = (bf16[4,8,32,1024]{3,2,1,0:T(8,128)(2,1)}, bf16[4,8,32,643]{3,2,1,0:T(8,128)(2,1)}) custom-call(bf16[8,32,1024]{2,1,0:T(8,128)(2,1)} %bitcast.151, bf16[8,32,643]{2,1,0:T(8,128)(2,1)} %bitcast.156), custom_call_target="tpu_custom_call" | custom-call | bytes 102420480 | tf_op jit(solution)/shard_map/pallas_call | solution.py:201
  48.4 1.6 slice.102
  50.0 1.1 copy-done.12
  52.8 0.9 fusion.13
  54.4 2.0 fusion.5
  57.2 0.6 and_select_fusion.tag_ref
  57.8 0.8 pad_maximum_fusion.1.kv_ref
  58.6 22.1 %shard_map.239 = (bf16[8,256,640]{2,1,0:T(8,128)(2,1)}, s32[8,1,256]{2,1,0:T(1,128)}) custom-call(bf16[256,640]{1,0:T(8,128)(2,1)} %pad_maximum_fusion.1.kv_ref, s32[1,256]{1,0:T(1,128)} %and_select_fusion.tag_ref), custom_call_target="tpu_custom_call" | custom-call | bytes 78643200 | tf_op jit(solution)/shard_map/pallas_call | solution.py:252
  80.7 0.8 slice.83
  81.6 1.0 multiply_convert_fusion.4
  82.7 1.1 pad.39
  83.8 0.7 pad_add_fusion.first_ref
  84.7 2.3 fusion.1
  87.2 0.9 maximum_multiply_fusion
  88.1 15.3 %shard_map.240 = (f32[960,256]{1,0:T(8,128)}, f32[16,256]{1,0:T(8,128)}) custom-call(s32[18]{0:T(128)} %pad_add_fusion.first_ref, bf16[960,256]{1,0:T(8,128)(2,1)} %bitcast.163, bf16[2048,640]{1,0:T(8,128)(2,1)} %bitcast.186, s32[1,256]{1,0:T(1,128)} %pos_ref.3, s32[16,1,128]{2,1,0:T(1,128)} %bitcast.191), custom_call_target="tpu_custom_call" | custom-call | flops 16106127360 | bytes 2621440 | tf_op jit(solution)/shard_map/pallas_call | solution.py:626
  103.3 1.3 convert_element_type.167
  104.6 0.8 copy-done.10
  105.4 2.5 fusion.43
  107.9 1.3 all-gather.6.cloned.1.call-done
  109.4 1.0 multiply_convert_fusion.3
  110.6 43.8 %all-gather.8.cloned.1.call-done = bf16[1024,960]{0,1:T(8,128)(2,1)} async-done(((bf16[256,960]{0,1:T(8,128)(2,1)}), bf16[1024,960]{0,1:T(8,128)(2,1)}) %all-gather.8.cloned.1.call-update) | async-done | bytes 1966096 | tf_op jit(solution)/shard_map/all_gather | solution.py:799
  154.4 3.6 fusion.44
  158.0 1.6 fusion.45
  159.7 3.7 %multiply_reduce_fusion = (bf16[1024]{0:T(1024)(128)(2,1)S(1)}, bf16[1024,640]{0,1:T(8,128)(2,1)}, bf16[1024,640]{0,1:T(8,128)(2,1)S(1)}, bf16[1024,640]{0,1:T(8,128)(2,1)S(1)}) fusion(f32[1024,640]{0,1:T(8,128)S(1)} %fusion.44, f32[1024,640]{0,1:T(8,128)S(1)} %fusion.45, bf16[1024,960]{0,1:T(8,128)(2,1)S(1)} %copy-done.33, bf16[640,960]{0,1:T(8,128)(2,1)S(1)} %copy-done), kind=kOutput, calls=%fused_computation.1 | convolution fusion | flops 1270086656 | bytes 12371968 | tf_op jit(solution)/shard_map/dot_general | solution.py:71
  163.4 1.7 fusion.46
  165.6 1.7 add_convert_fusion
  167.3 1.4 pad_maximum_fusion
  168.9 1.9 pad.40
  170.7 4.4 %convolution_convert_fusion.2 = bf16[1024,960]{0,1:T(8,128)(2,1)} fusion(bf16[640,960]{0,1:T(8,128)(2,1)S(1)} %copy-done, bf16[1024,640]{0,1:T(8,128)(2,1)} %get-tuple-element.93), kind=kOutput, calls=%fused_computation.14 | convolution fusion | flops 1259274240 | bytes 4505600 | tf_op jit(solution)/shard_map/dot_general | solution.py:806
  175.1 4.9 %convolution_convert_fusion.4 = bf16[640,960]{0,1:T(8,128)(2,1)} fusion(bf16[1024,640]{0,1:T(8,128)(2,1)} %get-tuple-element.93, bf16[1024,960]{0,1:T(8,128)(2,1)} %all-gather.6.cloned.1.call-done), kind=kOutput, calls=%fused_computation.16 | convolution fusion | flops 1258905600 | bytes 4505600 | tf_op jit(solution)/shard_map/dot_general | solution.py:813
  180.0 2.8 convolution_convert_fusion.5
  182.8 2.8 convolution_convert_fusion.6
  185.5 23.6 %reduce-scatter.3.cloned.1.call-done = bf16[256,961]{0,1:T(8,128)(2,1)} async-done(((bf16[1024,961]{0,1:T(8,128)(2,1)}), bf16[256,961]{0,1:T(8,128)(2,1)}) %reduce-scatter.3.cloned.1.call-update) | async-done | bytes 492048 | tf_op jit(solution)/shard_map/reduce_scatter | solution.py:803
  209.1 1.1 convert_element_type.177
  211.1 1.2 multiply_sine_fusion
  212.3 0.6 multiply_reduce_fusion.2
  213.3 1.1 copy-done.5
  214.7 1.8 convert_multiply_fusion.1
  216.5 1.6 reduce_sum.104
  218.1 0.6 pad.41.delta_ref
  218.7 28.8 %shard_map.241 = (bf16[256,1024]{1,0:T(8,128)(2,1)}, bf16[2048,640]{1,0:T(8,128)(2,1)}) custom-call(s32[18]{0:T(128)} %pad_add_fusion.first_ref, bf16[960,256]{1,0:T(8,128)(2,1)} %bitcast.164, bf16[2048,640]{1,0:T(8,128)(2,1)} %bitcast.187, s32[1,256]{1,0:T(1,128)} %pos_ref.3, s32[16,1,128]{2,1,0:T(1,128)} %bitcast.192, ...), custom_call_target="tpu_custom_call" | custom-call | flops 30198988800 | bytes 5242880 | tf_op jit(solution)/shard_map/pallas_call | solution.py:714
  247.5 23.7 %shard_map.242 = bf16[8,32,640]{2,1,0:T(8,128)(2,1)} custom-call(bf16[8,8,32,640]{3,2,1,0:T(8,128)(2,1)} %bitcast.150, f32[8,32,32]{2,1,0:T(8,128)} %get-tuple-element.109.cos_ref, f32[8,32,32]{2,1,0:T(8,128)} %get-tuple-element.108.sin_ref), custom_call_target="tpu_custom_call" | custom-call | bytes 78643200 | tf_op jit(solution)/shard_map/pallas_call | solution.py:404
  271.3 2.4 fusion.3
  273.7 1.6 fusion.30
  275.8 0.7 pad.43.refs_0_
  276.4 1.6 convolution_convert_fusion.3
  278.1 3.2 convolution_convert_fusion.1
  281.2 2.0 convolution_convert_fusion
  283.3 68.8 %shard_map.243 = (f32[8,8,128]{2,1,0:T(8,128)}, bf16[8,32,1024]{2,1,0:T(8,128)(2,1)}, bf16[8,32,1024]{2,1,0:T(8,128)(2,1)}, bf16[8,32,640]{2,1,0:T(8,128)(2,1)}) custom-call(f32[4,8,8,128]{3,2,1,0:T(8,128)} %pad.43.refs_0_, bf16[4,8,32,1024]{3,2,1,0:T(8,128)(2,1)} %bitcast.142, bf16[4,8,32,1024]{3,2,1,0:T(8,128)(2,1)} %bitcast.143, ...), custom_call_target="tpu_custom_call" | custom-call | bytes 167116800 | tf_op jit(solution)/shard_map/pallas_call | solution.py:497
  352.7 3.0 convert_element_type.190
  355.7 1.6 convert_element_type.191
  357.4 1.6 convert_element_type.192
  359.2 0.8 slice.112
  360.1 0.6 fusion.41
  360.8 0.9 fusion.39
  361.7 1.5 slice_convert_fusion
  363.2 3.2 fusion.37
  (137 shorter events, 7.1 us)
Async XLA Ops:
  7.2 152.5 %copy-start = (bf16[640,960]{0,1:T(8,128)(2,1)S(1)}, bf16[640,960]{0,1:T(8,128)(2,1)}, u32[]{:S(2)}) copy-start(bf16[640,960]{0,1:T(8,128)(2,1)} %param.22) | copy-start | bytes 3686404
  7.2 5.6 %copy-start.19 = (bf16[240,960]{1,0:T(8,128)(2,1)S(1)}, bf16[240,960]{1,0:T(8,128)(2,1)}, u32[]{:S(2)}) copy-start(bf16[240,960]{1,0:T(8,128)(2,1)} %param.16) | copy-start | bytes 1382404
  7.2 96.1 %all-gather.4.cloned.1.call-start = ((), (), s32[]{:S(2)}) async-start(), calls=%async_computation.2 | async-start | bytes 2457600 | tf_op jit(solution)/shard_map/all_gather | solution.py:763
  7.9 101.2 %all-gather.6.cloned.1.call-start = ((), (), s32[]{:S(2)}) async-start(), calls=%async_computation.3 | async-start | bytes 2457600 | tf_op jit(solution)/shard_map/all_gather | solution.py:776
  48.4 3.6 copy-start.32
  48.4 3.7 copy-start.2
  48.4 3.9 %copy-start.25 = (s32[1,256]{1,0:T(1,128)S(1)}, s32[1,256]{1,0:T(1,128)}, u32[]{:S(2)}) copy-start(s32[1,256]{1,0:T(1,128)} %pos_ref.3) | copy-start | bytes 3076
  48.4 4.4 %copy-start.4 = (bf16[1,256,960]{1,2,0:T(8,128)(2,1)S(1)}, bf16[1,256,960]{1,2,0:T(8,128)(2,1)}, u32[]{:S(2)}) copy-start(bf16[1,256,960]{1,2,0:T(8,128)(2,1)} %param.26) | copy-start | bytes 1474564
  50.0 1.1 copy-start.12
  53.8 100.6 %all-gather.8.cloned.1.call-start = ((), (), s32[]{:S(2)}) async-start(), calls=%async_computation.4 | async-start | bytes 2457600 | tf_op jit(solution)/shard_map/all_gather | solution.py:799
  83.8 3.3 copy-start.6
  84.6 2.4 copy-start.23
  84.7 2.4 copy-start.24
  104.6 0.8 copy-start.10
  110.4 98.8 %reduce-scatter.3.cloned.1.call-start = ((), (), s32[]{:S(2)}) async-start(), calls=%async_computation.5 | async-start | bytes 2478080 | tf_op jit(solution)/shard_map/reduce_scatter | solution.py:803
  154.4 3.6 copy-start.34
  154.4 3.6 copy-start.36
  158.0 1.6 copy-start.33
  163.4 1.7 copy-start.38
  163.4 1.7 copy-start.40
  163.4 2.2 copy-start.37
  168.8 183.9 %all-reduce.12.cloned.1.call-start = ((), (), s32[]{:S(2)}) async-start(), calls=%async_computation.7 | async-start | bytes 7372800 | tf_op jit(solution)/shard_map/psum | solution.py:823
  175.1 4.9 %copy-start.35 = (bf16[1024,960]{0,1:T(8,128)(2,1)S(1)}, bf16[1024,960]{0,1:T(8,128)(2,1)}, u32[]{:S(2)}) copy-start(bf16[1024,960]{0,1:T(8,128)(2,1)} %all-gather.8.cloned.1.call-done) | copy-start | bytes 5898244
  175.1 4.9 %copy-start.41 = (bf16[1024,640]{0,1:T(8,128)(2,1)S(1)}, bf16[1024,640]{0,1:T(8,128)(2,1)}, u32[]{:S(2)}) copy-start(bf16[1024,640]{0,1:T(8,128)(2,1)} %copy-done.40) | copy-start | bytes 3932164
  180.0 2.8 copy-start.39
  210.3 61.0 %copy-start.3 = (f32[256,961]{0,1:T(8,128)}, f32[256,961]{0,1:T(8,128)S(1)}, u32[]{:S(2)}) copy-start(f32[256,961]{0,1:T(8,128)S(1)} %convert_element_type.177) | copy-start | bytes 2952196
  210.3 0.7 copy-start.26
  210.3 152.9 %reduce-scatter.5.cloned.1.call-start = ((), (), s32[]{:S(2)}) async-start(), calls=%async_computation.6 | async-start | bytes 2457600 | tf_op jit(solution)/shard_map/reduce_scatter | solution.py:861
  212.9 1.5 copy-start.5
  212.9 1.8 copy-start.11
  214.7 1.8 copy-start.8
  247.5 23.8 %copy-start.17 = (bf16[256,1024]{1,0:T(8,128)(2,1)S(1)}, bf16[256,1024]{1,0:T(8,128)(2,1)}, u32[]{:S(2)}) copy-start(bf16[256,1024]{1,0:T(8,128)(2,1)} %get-tuple-element.57) | copy-start | bytes 1572868
  271.2 2.5 copy-start.13
  271.2 2.5 copy-start.14
  271.3 2.4 copy-start.30
  273.7 2.7 copy-start.7
  275.3 2.7 copy-start.9
  278.1 3.2 copy-start.18
  352.7 3.0 copy-start.16
  355.6 1.8 copy-start.15
  357.4 1.6 copy-start.22
  359.2 2.5 copy-start.20
  359.2 2.5 copy-start.21
  360.8 2.4 copy-start.27
  360.8 2.4 copy-start.28
  360.8 2.4 copy-start.29
  360.8 2.4 copy-start.31
  363.2 3.2 copy-start.1
Sparse Core Ops, SparseCore 0:
  9.6 54.0 all-gather.3
  65.8 43.2 all-gather.5
  111.3 43.0 all-gather.7
  168.9 40.1 reduce-scatter.2
  212.7 80.6 all-reduce.11
  295.6 55.9 reduce-scatter.4

commit v10 on v9

--- a/solution.py
+++ b/solution.py
@@ -370,62 +370,21 @@
     return jnp.concatenate(parts, 1)
 
 
-def scatter_plane_kernel(x_ref, cos_ref, sin_ref, out_ref, halves, sums, arrived, h_sems, p_sems):
-    me, core, chip, partner = plane_of()
-    layer = lax.axis_index("fsdp")
-    near = [across_of(chip, core, way) for way in (1, 2)]
-    greet([(peer, layer) for peer in near + [partner]])
-    arrays = [(lambda piece: x_ref.at[piece], halves, sums, arrived)]
-    started, second_hop = reduce_plane(arrays, h_sems, p_sems)
-    for copy in second_hop(0):
-        copy.wait_recv()
-
-    def add_slab(slab, carry):
-        total = plane_total(sums, arrived, slab)
-        kdim = KV_HEADS * HEAD
-        keys = turned_back(total[:, :kdim], cos_ref[slab], sin_ref[slab])
-        out_ref[slab] = jnp.concatenate([keys, total[:, kdim:]], 1).astype(out_ref.dtype)
-        return carry
-
-    lax.fori_loop(0, x_ref.shape[1], add_slab, 0)
-    for copy in started:
-        copy.wait_send()
-
-
-def scatter_plane(values, cos_tab, sin_tab):
-    if lax.axis_size("ctx") != SPAN:
-        own = lax.psum_scatter(values, "ctx", scatter_dimension=0, tiled=True)
-        own, kdim = own.astype(jnp.float32), KV_HEADS * HEAD
-        keys = turned_back(own[:, :kdim], cos_tab, sin_tab)
-        return jnp.concatenate([keys, own[:, kdim:]], 1).astype(values.dtype)
-    rows, columns = values.shape
-    slabs = 8
-    block = (slabs, rows // SPAN // slabs, columns)
-    return pl.pallas_call(
-        scatter_plane_kernel,
-        out_shape=jax.ShapeDtypeStruct(block, values.dtype),
-        in_specs=in_vmem(3),
-        out_specs=in_vmem(1)[0],
-        scratch_shapes=plane_scratch(block, values.dtype)
-        + [pltpu.SemaphoreType.DMA((2, 1, CHIPS)), pltpu.SemaphoreType.DMA((2, 1, 6))],
-        compiler_params=comm_params(3),
-        cost_estimate=comm_cost(values.size * 2),
-    )(
-        values.reshape(SPAN, *block),
-        cos_tab.reshape(*block[:2], -1),
-        sin_tab.reshape(*block[:2], -1),
-    ).reshape(rows // SPAN, columns)
-
-
-def reduce_rows_kernel(depth, count, *refs):
-    inputs, outs, scratch = refs[:count], refs[count : 2 * count], refs[2 * count : 6 * count]
-    h_sems, p_sems, z_sems, g_sems, f_sems = refs[6 * count :]
+def reduce_rows_kernel(depth, count, extra, *refs):
+    sizes = (count, 3 * extra, count, extra, 4 * count, 3 * extra, 5)
+    ends = [sum(sizes[: index + 1]) for index in range(len(sizes))]
+    inputs, kv_in, outs, kv_out, scratch, kv_scratch, sems = (
+        refs[end - size : end] for size, end in zip(sizes, ends)
+    )
+    h_sems, p_sems, z_sems, g_sems, f_sems = sems
     me, core, chip, partner = plane_of()
     layer = lax.axis_index("fsdp")
     layers = [lax.rem(layer + d, depth) for d in range(1, depth)]
     peers = [chip_at(chip, core, j) for j in range(1, CHIPS)]
     greet([(me, other) for other in layers] + [(peer, layer) for peer in peers + [partner]])
     arrays, across = [], []
+    if extra:
+        arrays.append((lambda piece: kv_in[0].at[piece], *kv_scratch))
     for a, x_ref in enumerate(inputs):
         halves, sums, arrived, layers_ref = scratch[4 * a : 4 * a + 4]
         arrays.append((lambda piece, x_ref=x_ref: x_ref.at[:, piece], halves, sums, arrived))
@@ -433,9 +392,24 @@
     started, second_hop = reduce_plane(arrays, h_sems, p_sems)
     last, moved, given, passed = [], [], [], []
 
+    def finish_kv():
+        _, _, sums, arrived = arrays[0]
+        for copy in last[0]:
+            copy.wait_recv()
+
+        def add_slab(slab, carry):
+            total = plane_total(sums, arrived, slab)
+            kdim = KV_HEADS * HEAD
+            keys = turned_back(total[:, :kdim], kv_in[1][slab], kv_in[2][slab])
+            both = jnp.concatenate([keys, total[:, kdim:]], 1)
+            kv_out[0][slab] = both.astype(kv_out[0].dtype)
+            return carry
+
+        lax.fori_loop(0, sums.shape[1], add_slab, 0)
+
     def over_layers(a):
-        _, _, sums, arrived = arrays[a]
-        for copy in last[a]:
+        _, _, sums, arrived = arrays[a + extra]
+        for copy in last[a + extra]:
             copy.wait_recv()
         for d in list(range(1, depth)) + [0]:
             target = lax.rem(layer + d, depth)
@@ -462,13 +436,15 @@
             given.append(send(mine, mine, g_sems.at[0, a, j], g_sems.at[1, a, j], (peer, layer)))
         passed.append(send(mine, mine, f_sems.at[0, a, 3], f_sems.at[1, a, 3], (partner, layer)))
 
-    for step in range(count + 2):
-        if step < count:
+    for step in range(count + extra + 2):
+        if step < count + extra:
             last.append(second_hop(step))
-        if 0 < step <= count:
-            over_layers(step - 1)
-        if step > 1:
-            hand_out(step - 2)
+        if 0 <= step - 1 - extra < count:
+            over_layers(step - 1 - extra)
+        if extra and step == 1:
+            finish_kv()
+        if 0 <= step - 2 - extra:
+            hand_out(step - 2 - extra)
     for a, out_ref in enumerate(outs):
         for j in range(CHIPS - 1):
             given[a * (CHIPS - 1) + j].wait_recv()
@@ -482,11 +458,17 @@
         copy.wait()
 
 
-def reduce_rows(arrays, number):
+def reduce_rows(arrays, number, kv=None):
     if lax.axis_size("ctx") != SPAN:
-        return [lax.psum(lax.psum_scatter(v, "fsdp", scatter_dimension=0), "ctx") for v in arrays]
-    depth, count = arrays[0].shape[0], len(arrays)
-    pieces, outs, scratch = [], [], []
+        own = [lax.psum(lax.psum_scatter(v, "fsdp", scatter_dimension=0), "ctx") for v in arrays]
+        if kv is None:
+            return own
+        total = lax.psum_scatter(kv[0], "ctx", scatter_dimension=0, tiled=True)
+        total, kdim = total.astype(jnp.float32), KV_HEADS * HEAD
+        keys = turned_back(total[:, :kdim], *kv[1:])
+        return own + [jnp.concatenate([keys, total[:, kdim:]], 1).astype(kv[0].dtype)]
+    depth, count, extra = arrays[0].shape[0], len(arrays), int(kv is not None)
+    pieces, outs, scratch, shapes = [], [], [], []
     for values in arrays:
         _, rows, columns = values.shape
         piece = (rows // SPAN, columns)
@@ -494,23 +476,35 @@
         outs.append(jax.ShapeDtypeStruct((SPAN, *piece), values.dtype))
         scratch += plane_scratch((depth, *piece), values.dtype)
         scratch.append(pltpu.VMEM((2, depth, *piece), values.dtype))
+        shapes.append(values.shape[1:])
+    moved = sum(values.size for values in arrays) * 2
+    if extra:
+        rows, columns = kv[0].shape
+        slabs = 8
+        block = (slabs, rows // SPAN // slabs, columns)
+        pieces.append(kv[0].reshape(SPAN, *block))
+        pieces += [table.reshape(*block[:2], -1) for table in kv[1:]]
+        outs.append(jax.ShapeDtypeStruct(block, kv[0].dtype))
+        scratch += plane_scratch(block, kv[0].dtype)
+        shapes.append((rows // SPAN, columns))
+        moved += kv[0].size * 2
     owned = pl.pallas_call(
-        functools.partial(reduce_rows_kernel, depth, count),
+        functools.partial(reduce_rows_kernel, depth, count, extra),
         out_shape=tuple(outs),
-        in_specs=in_vmem(count),
-        out_specs=tuple(in_vmem(count)),
+        in_specs=in_vmem(len(pieces)),
+        out_specs=tuple(in_vmem(len(outs))),
         scratch_shapes=scratch
         + [
-            pltpu.SemaphoreType.DMA((2, count, CHIPS)),
-            pltpu.SemaphoreType.DMA((2, count, 6)),
+            pltpu.SemaphoreType.DMA((2, count + extra, CHIPS)),
+            pltpu.SemaphoreType.DMA((2, count + extra, 6)),
             pltpu.SemaphoreType.DMA((2, count, depth - 1)),
             pltpu.SemaphoreType.DMA((2, count, CHIPS - 1)),
             pltpu.SemaphoreType.DMA((2, count, CHIPS)),
         ],
         compiler_params=comm_params(number),
-        cost_estimate=comm_cost(sum(values.size for values in arrays) * 2),
+        cost_estimate=comm_cost(moved),
     )(*pieces)
-    return [own.reshape(values.shape[1:]) for own, values in zip(owned, arrays)]
+    return [own.reshape(shape) for own, shape in zip(owned, shapes)]
 
 
 BLOCK = 128
@@ -840,7 +834,9 @@
         row_delta,
         (cos_tab.T, sin_tab.T),
     )
-    grad_kv_raw = scatter_plane(grad_kv_all, cos_tab, sin_tab)
+    own_out, grad_kv_raw = reduce_rows(
+        [grad_wout.reshape(depth, padded_rows, -1)], 3, (grad_kv_all, cos_tab, sin_tab)
+    )
     grad_logit = (jnp.sum(grad_inc * branch, -1, keepdims=True) + row_dot) * (1.0 - gating)
     grad_router = jnp.sum(hidden * grad_logit, 0)
     grad_normed_one = dot(grad_query_raw, w_query, (1, 1)).reshape(row_count, depth, -1)
@@ -855,12 +851,13 @@
     vectors = jnp.stack([grad_gain_one, grad_gain_two, grad_router]).reshape(3, depth, own_rows)
     vectors = jnp.pad(vectors.transpose(1, 0, 2).reshape(depth, -1), ((0, 0), (0, -3 * own_rows % 1024)))
     vectors = jnp.pad(vectors.reshape(depth, -1, 1, 128), ((0, 0), (0, 0), (0, 7), (0, 0)))
-    layered = [grad.reshape(depth, padded_rows, -1) for grad in (grad_wout, grad_wq, grad_wkv)]
+    layered = [grad.reshape(depth, padded_rows, -1) for grad in (grad_wq, grad_wkv)]
     layered.insert(0, vectors.reshape(depth, -1, 128))
     owned = reduce_rows(layered, 4)
     ffn_out = lax.psum_scatter(ffn_part, "fsdp", scatter_dimension=0, tiled=True)
     *owned, totals = lax.optimization_barrier((*owned, totals))
-    total_out, total_q, total_kv = (own[:own_rows].astype(jnp.float32) for own in owned[1:])
+    owned.append(own_out)
+    total_q, total_kv, total_out = (own[:own_rows].astype(jnp.float32) for own in owned[1:])
     total_q, total_out = total_q[:, :qdim], total_out[:, :width]
     total_k, total_v = total_kv[:, :kdim], total_kv[:, kdim:]
     mine = owned[0].reshape(-1, 8, 128)[:, 0].reshape(-1)[: 3 * own_rows].reshape(3, own_rows)

time: 376 us -> 379 us (level)
  Pallas kernels: 193 us -> 199 us
    pallas_call x2, Pallas kernels: 92.5 us -> 98 us  [reduce_rows(): pl.pallas_call(functools.partial(reduce_rows_kernel, depth, count, extra)...]
  transfers between devices with their start and end apart: 6 -> 6, of which waited for: 3 -> 3; matrix products, arithmetic and copies ran while one was open for 19% -> 19% of each run, Pallas kernels for 52% -> 53%
where the time goes in v10:
time: 379 us; the launch traced here: 378 us
  Pallas kernels  199 us (53%)
  waiting for transfers between devices  69.5 us (18%)
  matrix products  46.5 us (12%)
  other arithmetic  27 us (7%)
  local copies, waits for them, and re-layouts  20.5 us (5%)
  between operations  15.4 us (4%)
    pallas_call x2, Pallas kernels, reduce_rows(): pl.pallas_call(functools.partial(reduce_rows_kernel, depth, count, extra)...  98 us
    all_gather x1, waiting for transfers between devices, on_device(): normed_all = lax.all_gather(normed_two, 'fsdp', axis=0, tiled=True)  43.9 us
    pallas_call x1, Pallas kernels, gather_rows(): pl.pallas_call(functools.partial(gather_rows_kernel, depth, count), out_s...  34.7 us
    pallas_call x1, Pallas kernels, attend_back(): pl.pallas_call(attend_back_kernel, out_shape=(jax.ShapeDtypeStruct((slots...  28.8 us
    reduce_scatter x1, waiting for transfers between devices, on_device(): lax.psum_scatter(grad_normed_part, 'fsdp', scatter_dimension=0, tiled=True)  23.7 us
    pallas_call x1, Pallas kernels, gather_plane(): pl.pallas_call(gather_plane_kernel, out_shape=(jax.ShapeDtypeStruct((SPAN...  22.1 us
    dot_general x9, matrix products, dot(): lax.dot_general(left, right, (((dims[0],), (dims[1],)), ((), ())), prefer...  19.4 us
    pallas_call x1, Pallas kernels, attend(): pl.pallas_call(attend_kernel, out_shape=(jax.ShapeDtypeStruct(queries.sha...  15.3 us
  transfers between devices with their start and end apart: 6, of which 3 were waited for; matrix products, arithmetic and copies ran while one was open for 19% of the time, Pallas kernels for 53%

profile of v10, /device:TPU:0, one launch (start us, length us, event | category | flops | bytes accessed | tf_op | source)
XLA Modules:
  0.0 378.4 jit_solution(13931829490320330942)
XLA Ops:
  7.2 0.7 all-gather.4.cloned.1.call-update
  8.0 0.7 stack.21
  8.6 0.7 stack.22
  9.3 0.7 stack.23
  10.0 1.9 concatenate.23
  12.0 0.8 pad.38.clone
  12.8 0.8 pad.58
  13.7 34.7 %shard_map.238 = (bf16[4,8,32,1024]{3,2,1,0:T(8,128)(2,1)}, bf16[4,8,32,643]{3,2,1,0:T(8,128)(2,1)}) custom-call(bf16[8,32,1024]{2,1,0:T(8,128)(2,1)} %bitcast.151, bf16[8,32,643]{2,1,0:T(8,128)(2,1)} %bitcast.156), custom_call_target="tpu_custom_call" | custom-call | bytes 102420480 | tf_op jit(solution)/shard_map/pallas_call | solution.py:201
  48.4 1.6 slice.102
  50.0 1.1 copy-done.12
  52.3 0.6 broadcast_select_fusion
  52.9 0.9 fusion.13
  53.9 0.6 multiply_multiply_fusion
  54.5 2.0 fusion.5
  57.9 0.8 pad_maximum_fusion.1.kv_ref
  58.7 22.1 %shard_map.239 = (bf16[8,256,640]{2,1,0:T(8,128)(2,1)}, s32[8,1,256]{2,1,0:T(1,128)}) custom-call(bf16[256,640]{1,0:T(8,128)(2,1)} %pad_maximum_fusion.1.kv_ref, s32[1,256]{1,0:T(1,128)} %and_select_fusion.tag_ref), custom_call_target="tpu_custom_call" | custom-call | bytes 78643200 | tf_op jit(solution)/shard_map/pallas_call | solution.py:252
  80.8 0.8 slice.83
  81.7 1.0 multiply_convert_fusion.4
  82.8 1.1 pad.39
  83.8 0.7 pad_add_fusion.first_ref
  84.7 2.3 fusion.1
  87.3 0.9 maximum_multiply_fusion
  88.1 15.3 %shard_map.240 = (f32[960,256]{1,0:T(8,128)}, f32[16,256]{1,0:T(8,128)}) custom-call(s32[18]{0:T(128)} %pad_add_fusion.first_ref, bf16[960,256]{1,0:T(8,128)(2,1)} %bitcast.161, bf16[2048,640]{1,0:T(8,128)(2,1)} %bitcast.186, s32[1,256]{1,0:T(1,128)} %pos_ref.3, s32[16,1,128]{2,1,0:T(1,128)} %bitcast.191), custom_call_target="tpu_custom_call" | custom-call | flops 16106127360 | bytes 2621440 | tf_op jit(solution)/shard_map/pallas_call | solution.py:620
  103.4 1.3 convert_element_type.167
  104.7 0.8 copy-done.8
  105.5 2.5 fusion.43
  108.0 1.2 all-gather.6.cloned.1.call-done
  109.4 1.0 multiply_convert_fusion.3
  110.6 43.9 %all-gather.8.cloned.1.call-done = bf16[1024,960]{0,1:T(8,128)(2,1)} async-done(((bf16[256,960]{0,1:T(8,128)(2,1)}), bf16[1024,960]{0,1:T(8,128)(2,1)}) %all-gather.8.cloned.1.call-update) | async-done | bytes 1966096 | tf_op jit(solution)/shard_map/all_gather | solution.py:793
  154.5 3.6 fusion.44
  158.1 1.6 fusion.45
  159.7 3.7 multiply_reduce_fusion
  163.5 1.7 fusion.46
  165.6 1.7 add_convert_fusion
  167.4 1.4 pad_maximum_fusion
  168.9 1.9 pad.40
  170.8 4.4 %convolution_convert_fusion.2 = bf16[1024,960]{0,1:T(8,128)(2,1)} fusion(bf16[640,960]{0,1:T(8,128)(2,1)S(1)} %copy-done, bf16[1024,640]{0,1:T(8,128)(2,1)} %get-tuple-element.93), kind=kOutput, calls=%fused_computation.14 | convolution fusion | flops 1259274240 | bytes 4505600 | tf_op jit(solution)/shard_map/dot_general | solution.py:800
  175.1 4.9 %convolution_convert_fusion.4 = bf16[640,960]{0,1:T(8,128)(2,1)} fusion(bf16[1024,640]{0,1:T(8,128)(2,1)} %get-tuple-element.93, bf16[1024,960]{0,1:T(8,128)(2,1)} %all-gather.6.cloned.1.call-done), kind=kOutput, calls=%fused_computation.16 | convolution fusion | flops 1258905600 | bytes 4505600 | tf_op jit(solution)/shard_map/dot_general | solution.py:807
  180.0 2.8 convolution_convert_fusion.5
  182.8 2.8 convolution_convert_fusion.6
  185.6 23.7 %reduce-scatter.3.cloned.1.call-done = bf16[256,961]{0,1:T(8,128)(2,1)} async-done(((bf16[1024,961]{0,1:T(8,128)(2,1)}), bf16[256,961]{0,1:T(8,128)(2,1)}) %reduce-scatter.3.cloned.1.call-update) | async-done | bytes 492048 | tf_op jit(solution)/shard_map/reduce_scatter | solution.py:797
  209.2 1.1 convert_element_type.177
  211.1 1.2 multiply_sine_fusion
  213.4 1.1 copy-done.5
  214.8 1.8 convert_multiply_fusion.1
  216.5 1.3 reduce_sum.104
  217.8 0.6 pad.41.delta_ref
  218.5 28.8 %shard_map.241 = (bf16[256,1024]{1,0:T(8,128)(2,1)}, bf16[2048,640]{1,0:T(8,128)(2,1)}) custom-call(s32[18]{0:T(128)} %pad_add_fusion.first_ref, bf16[960,256]{1,0:T(8,128)(2,1)} %bitcast.162, bf16[2048,640]{1,0:T(8,128)(2,1)} %bitcast.187, s32[1,256]{1,0:T(1,128)} %pos_ref.3, s32[16,1,128]{2,1,0:T(1,128)} %bitcast.192, ...), custom_call_target="tpu_custom_call" | custom-call | flops 30198988800 | bytes 5242880 | tf_op jit(solution)/shard_map/pallas_call | solution.py:708
  247.3 3.1 convolution_convert_fusion.1
  250.4 52.2 %shard_map.242 = (bf16[8,32,1024]{2,1,0:T(8,128)(2,1)}, bf16[8,32,640]{2,1,0:T(8,128)(2,1)}) custom-call(bf16[4,8,32,1024]{3,2,1,0:T(8,128)(2,1)} %bitcast.143, bf16[8,8,32,640]{3,2,1,0:T(8,128)(2,1)} %bitcast.150, f32[8,32,32]{2,1,0:T(8,128)} %get-tuple-element.109.refs_2_, f32[8,32,32]{2,1,0:T(8,128)} %get-tuple-element.108.refs_3_), custom_call_target="tpu_custom_call" | custom-call | bytes 141557760 | tf_op jit(solution)/shard_map/pallas_call | solution.py:491
  302.7 2.4 fusion.3
  305.1 1.6 fusion.30
  307.1 0.7 pad.44.refs_0_
  307.8 1.6 convolution_convert_fusion.3
  309.4 2.0 convolution_convert_fusion
  311.5 45.8 %shard_map.243 = (f32[8,8,128]{2,1,0:T(8,128)}, bf16[8,32,1024]{2,1,0:T(8,128)(2,1)}, bf16[8,32,640]{2,1,0:T(8,128)(2,1)}) custom-call(f32[4,8,8,128]{3,2,1,0:T(8,128)} %pad.44.refs_0_, bf16[4,8,32,1024]{3,2,1,0:T(8,128)(2,1)} %bitcast.142, bf16[4,8,32,640]{3,2,1,0:T(8,128)(2,1)} %bitcast.144), custom_call_target="tpu_custom_call" | custom-call | bytes 104202240 | tf_op jit(solution)/shard_map/pallas_call | solution.py:491
  357.9 3.0 convert_element_type.190
  360.9 1.6 convert_element_type.191
  362.6 1.6 convert_element_type.192
  364.4 0.8 slice.113
  365.3 0.6 fusion.41
  366.0 0.9 fusion.39
  366.9 1.5 slice_convert_fusion
  368.4 3.2 fusion.37
  (137 shorter events, 7.1 us)
Async XLA Ops:
  7.2 152.5 %copy-start = (bf16[640,960]{0,1:T(8,128)(2,1)S(1)}, bf16[640,960]{0,1:T(8,128)(2,1)}, u32[]{:S(2)}) copy-start(bf16[640,960]{0,1:T(8,128)(2,1)} %param.22) | copy-start | bytes 3686404
  7.2 5.6 %copy-start.18 = (bf16[240,960]{1,0:T(8,128)(2,1)S(1)}, bf16[240,960]{1,0:T(8,128)(2,1)}, u32[]{:S(2)}) copy-start(bf16[240,960]{1,0:T(8,128)(2,1)} %param.16) | copy-start | bytes 1382404
  7.2 96.2 %all-gather.4.cloned.1.call-start = ((), (), s32[]{:S(2)}) async-start(), calls=%async_computation.2 | async-start | bytes 2457600 | tf_op jit(solution)/shard_map/all_gather | solution.py:757
  7.9 101.2 %all-gather.6.cloned.1.call-start = ((), (), s32[]{:S(2)}) async-start(), calls=%async_computation.3 | async-start | bytes 2457600 | tf_op jit(solution)/shard_map/all_gather | solution.py:770
  48.4 3.6 copy-start.32
  48.4 3.7 copy-start.2
  48.4 3.9 %copy-start.25 = (s32[1,256]{1,0:T(1,128)S(1)}, s32[1,256]{1,0:T(1,128)}, u32[]{:S(2)}) copy-start(s32[1,256]{1,0:T(1,128)} %pos_ref.3) | copy-start | bytes 3076
  48.4 4.5 %copy-start.4 = (bf16[1,256,960]{1,2,0:T(8,128)(2,1)S(1)}, bf16[1,256,960]{1,2,0:T(8,128)(2,1)}, u32[]{:S(2)}) copy-start(bf16[1,256,960]{1,2,0:T(8,128)(2,1)} %param.26) | copy-start | bytes 1474564
  50.0 1.1 copy-start.12
  53.9 100.6 %all-gather.8.cloned.1.call-start = ((), (), s32[]{:S(2)}) async-start(), calls=%async_computation.4 | async-start | bytes 2457600 | tf_op jit(solution)/shard_map/all_gather | solution.py:793
  83.8 3.2 copy-start.6
  84.7 2.4 copy-start.23
  84.7 2.4 copy-start.24
  104.7 0.8 copy-start.8
  110.4 98.9 %reduce-scatter.3.cloned.1.call-start = ((), (), s32[]{:S(2)}) async-start(), calls=%async_computation.5 | async-start | bytes 2478080 | tf_op jit(solution)/shard_map/reduce_scatter | solution.py:797
  154.5 3.6 copy-start.34
  154.5 3.6 copy-start.36
  158.1 1.6 copy-start.33
  163.5 1.7 copy-start.38
  163.5 1.7 copy-start.40
  163.5 2.2 copy-start.37
  168.9 189.0 %all-reduce.12.cloned.1.call-start = ((), (), s32[]{:S(2)}) async-start(), calls=%async_computation.7 | async-start | bytes 7372800 | tf_op jit(solution)/shard_map/psum | solution.py:817
  175.1 4.9 %copy-start.35 = (bf16[1024,960]{0,1:T(8,128)(2,1)S(1)}, bf16[1024,960]{0,1:T(8,128)(2,1)}, u32[]{:S(2)}) copy-start(bf16[1024,960]{0,1:T(8,128)(2,1)} %all-gather.8.cloned.1.call-done) | copy-start | bytes 5898244
  175.1 4.9 %copy-start.41 = (bf16[1024,640]{0,1:T(8,128)(2,1)S(1)}, bf16[1024,640]{0,1:T(8,128)(2,1)}, u32[]{:S(2)}) copy-start(bf16[1024,640]{0,1:T(8,128)(2,1)} %copy-done.40) | copy-start | bytes 3932164
  180.0 2.8 copy-start.39
  210.3 92.3 %copy-start.3 = (f32[256,961]{0,1:T(8,128)}, f32[256,961]{0,1:T(8,128)S(1)}, u32[]{:S(2)}) copy-start(f32[256,961]{0,1:T(8,128)S(1)} %convert_element_type.177) | copy-start | bytes 2952196
  210.3 0.7 copy-start.26
  210.4 158.0 %reduce-scatter.5.cloned.1.call-start = ((), (), s32[]{:S(2)}) async-start(), calls=%async_computation.6 | async-start | bytes 2457600 | tf_op jit(solution)/shard_map/reduce_scatter | solution.py:857
  213.0 1.5 copy-start.5
  213.0 1.8 copy-start.11
  214.8 1.8 copy-start.9
  218.5 28.8 %copy-start.10 = (bf16[256,960]{0,1:T(8,128)(2,1)S(1)}, bf16[256,960]{0,1:T(8,128)(2,1)}, u32[]{:S(2)}) copy-start(bf16[256,960]{0,1:T(8,128)(2,1)} %copy-done.9) | copy-start | bytes 1474564
  250.4 52.3 %copy-start.16 = (bf16[256,1024]{1,0:T(8,128)(2,1)S(1)}, bf16[256,1024]{1,0:T(8,128)(2,1)}, u32[]{:S(2)}) copy-start(bf16[256,1024]{1,0:T(8,128)(2,1)} %get-tuple-element.57) | copy-start | bytes 1572868
  302.6 2.5 copy-start.13
  302.6 2.5 copy-start.22
  302.7 2.4 copy-start.30
  305.1 2.7 copy-start.7
  306.7 2.7 copy-start.17
  357.9 3.0 copy-start.15
  360.9 1.8 copy-start.14
  362.6 1.6 copy-start.21
  364.4 2.5 copy-start.19
  364.4 2.5 copy-start.20
  366.0 2.4 copy-start.27
  366.0 2.4 copy-start.28
  366.0 2.4 copy-start.29
  366.0 2.4 copy-start.31
  368.4 3.2 copy-start.1
Sparse Core Ops, SparseCore 0:
  9.6 54.0 all-gather.3
  65.8 43.2 all-gather.5
  111.3 43.1 all-gather.7
  169.0 40.2 reduce-scatter.2
  213.3 87.2 all-reduce.11
  302.8 47.0 reduce-scatter.4

commit v11 on v8

--- a/solution.py
+++ b/solution.py
@@ -414,6 +414,50 @@
     ).reshape(rows // SPAN, columns)
 
 
+def reduce_direct(arrays, h_sems, p_sems):
+    me, core, chip, partner = plane_of()
+    layer = lax.axis_index("fsdp")
+    handed, spread = [], []
+    for a, (piece_of, halves, sums, arrived) in enumerate(arrays):
+        for j in range(CHIPS):
+            slot = (j + 1) % CHIPS
+            handed.append(
+                send(
+                    piece_of(chip_at(chip, 1 - core, slot)),
+                    halves.at[slot],
+                    h_sems.at[0, a, slot],
+                    h_sems.at[1, a, slot],
+                    (partner, layer),
+                )
+            )
+    for a, (piece_of, halves, sums, arrived) in enumerate(arrays):
+        for j in range(CHIPS):
+            slot = (j + 1) % CHIPS
+            handed[a * CHIPS + j].wait_recv()
+            mine = chip_at(chip, core, slot)
+
+            def add_half(slab, carry, piece=piece_of(mine), halves=halves, sums=sums, slot=slot):
+                sums[slot, slab] = added(piece[slab], halves[slot, slab]).astype(sums.dtype)
+                return carry
+
+            lax.fori_loop(0, sums.shape[1], add_half, 0)
+            if slot:
+                spread.append(
+                    send(
+                        sums.at[slot],
+                        arrived.at[slot - 1],
+                        p_sems.at[0, a, slot - 1],
+                        p_sems.at[1, a, slot - 1],
+                        (mine, layer),
+                    )
+                )
+    return handed, spread
+
+
+def direct_total(sums, arrived, slab):
+    return added(sums[0, slab], *(arrived[j, slab] for j in range(CHIPS - 1)))
+
+
 def reduce_rows_kernel(depth, count, *refs):
     inputs, outs, scratch = refs[:count], refs[count : 2 * count], refs[2 * count : 6 * count]
     h_sems, p_sems, z_sems, g_sems, f_sems = refs[6 * count :]
@@ -427,14 +471,14 @@
         halves, sums, arrived, layers_ref = scratch[4 * a : 4 * a + 4]
         arrays.append((lambda piece, x_ref=x_ref: x_ref.at[:, piece], halves, sums, arrived))
         across.append(layers_ref)
-    started, last = reduce_plane(arrays, h_sems, p_sems)
+    handed, spread = reduce_direct(arrays, h_sems, p_sems)
     moved = []
     for a, (_, _, sums, arrived) in enumerate(arrays):
-        for copy in last[a]:
+        for copy in spread[a * (CHIPS - 1) : (a + 1) * (CHIPS - 1)]:
             copy.wait_recv()
         for d in list(range(1, depth)) + [0]:
             target = lax.rem(layer + d, depth)
-            across[a][0, d] = plane_total(sums, arrived, target).astype(across[a].dtype)
+            across[a][0, d] = direct_total(sums, arrived, target).astype(across[a].dtype)
             if d:
                 moved.append(
                     send(
@@ -462,7 +506,7 @@
             passed.append(
                 send(block, block, f_sems.at[0, a, j], f_sems.at[1, a, j], (partner, layer))
             )
-    for copy in started + moved + given:
+    for copy in handed + spread + moved + given:
         copy.wait_send()
     for copy in passed:
         copy.wait()
@@ -488,7 +532,7 @@
         scratch_shapes=scratch
         + [
             pltpu.SemaphoreType.DMA((2, count, CHIPS)),
-            pltpu.SemaphoreType.DMA((2, count, 6)),
+            pltpu.SemaphoreType.DMA((2, count, CHIPS - 1)),
             pltpu.SemaphoreType.DMA((2, count, depth - 1)),
             pltpu.SemaphoreType.DMA((2, count, CHIPS - 1)),
             pltpu.SemaphoreType.DMA((2, count, CHIPS)),

time: 377 us -> 368 us (0.976)
  Pallas kernels: 196 us -> 187 us
    pallas_call x1, Pallas kernels: 71 us -> 62.7 us  [reduce_rows(): pl.pallas_call(functools.partial(reduce_rows_kernel, depth, count), out_s...]
  transfers between devices with their start and end apart: 6 -> 6, of which waited for: 3 -> 3; matrix products, arithmetic and copies ran while one was open for 19% -> 19% of each run, Pallas kernels for 52% -> 51%
where the time goes in v11:
time: 368 us; the launch traced here: 367 us
  Pallas kernels  187 us (51%)
  waiting for transfers between devices  69.5 us (19%)
  matrix products  46.6 us (13%)
  other arithmetic  27.2 us (7%)
  local copies, waits for them, and re-layouts  20.5 us (6%)
  between operations  15.4 us (4%)
    pallas_call x1, Pallas kernels, reduce_rows(): pl.pallas_call(functools.partial(reduce_rows_kernel, depth, count), out_s...  62.7 us
    all_gather x1, waiting for transfers between devices, on_device(): normed_all = lax.all_gather(normed_two, 'fsdp', axis=0, tiled=True)  43.8 us
    pallas_call x1, Pallas kernels, gather_rows(): pl.pallas_call(functools.partial(gather_rows_kernel, depth, count), out_s...  34.7 us
    pallas_call x1, Pallas kernels, attend_back(): pl.pallas_call(attend_back_kernel, out_shape=(jax.ShapeDtypeStruct((slots...  28.8 us
    pallas_call x1, Pallas kernels, scatter_plane(): pl.pallas_call(scatter_plane_kernel, out_shape=jax.ShapeDtypeStruct(block...  23.8 us
    reduce_scatter x1, waiting for transfers between devices, on_device(): lax.psum_scatter(grad_normed_part, 'fsdp', scatter_dimension=0, tiled=True)  23.6 us
    pallas_call x1, Pallas kernels, gather_plane(): pl.pallas_call(gather_plane_kernel, out_shape=(jax.ShapeDtypeStruct((SPAN...  22.1 us
    dot_general x9, matrix products, dot(): lax.dot_general(left, right, (((dims[0],), (dims[1],)), ((), ())), prefer...  19.5 us
  transfers between devices with their start and end apart: 6, of which 3 were waited for; matrix products, arithmetic and copies ran while one was open for 19% of the time, Pallas kernels for 51%

profile of v11, /device:TPU:0, one launch (start us, length us, event | category | flops | bytes accessed | tf_op | source)
XLA Modules:
  0.0 367.2 jit_solution(17426636988146296300)
XLA Ops:
  7.2 0.7 all-gather.4.cloned.1.call-update
  8.0 0.7 stack.21
  8.6 0.7 stack.22
  9.3 0.7 stack.23
  10.0 1.9 concatenate.23
  12.0 0.8 pad.38.clone
  12.8 0.8 pad.58
  13.7 34.7 %shard_map.238 = (bf16[4,8,32,1024]{3,2,1,0:T(8,128)(2,1)}, bf16[4,8,32,643]{3,2,1,0:T(8,128)(2,1)}) custom-call(bf16[8,32,1024]{2,1,0:T(8,128)(2,1)} %bitcast.151, bf16[8,32,643]{2,1,0:T(8,128)(2,1)} %bitcast.156), custom_call_target="tpu_custom_call" | custom-call | bytes 102420480 | tf_op jit(solution)/shard_map/pallas_call | solution.py:201
  48.4 1.6 slice.102
  50.0 1.1 copy-done.12
  52.8 0.9 fusion.13
  54.4 2.0 fusion.5
  57.2 0.6 and_select_fusion.tag_ref
  57.8 0.8 pad_maximum_fusion.1.kv_ref
  58.6 22.1 %shard_map.239 = (bf16[8,256,640]{2,1,0:T(8,128)(2,1)}, s32[8,1,256]{2,1,0:T(1,128)}) custom-call(bf16[256,640]{1,0:T(8,128)(2,1)} %pad_maximum_fusion.1.kv_ref, s32[1,256]{1,0:T(1,128)} %and_select_fusion.tag_ref), custom_call_target="tpu_custom_call" | custom-call | bytes 78643200 | tf_op jit(solution)/shard_map/pallas_call | solution.py:252
  80.7 0.8 slice.83
  81.6 1.0 multiply_convert_fusion.4
  82.7 1.1 pad.39
  83.8 0.7 pad_add_fusion.first_ref
  84.7 2.3 fusion.1
  87.2 0.9 maximum_multiply_fusion
  88.1 15.3 %shard_map.240 = (f32[960,256]{1,0:T(8,128)}, f32[16,256]{1,0:T(8,128)}) custom-call(s32[18]{0:T(128)} %pad_add_fusion.first_ref, bf16[960,256]{1,0:T(8,128)(2,1)} %bitcast.163, bf16[2048,640]{1,0:T(8,128)(2,1)} %bitcast.186, s32[1,256]{1,0:T(1,128)} %pos_ref.3, s32[16,1,128]{2,1,0:T(1,128)} %bitcast.191), custom_call_target="tpu_custom_call" | custom-call | flops 16106127360 | bytes 2621440 | tf_op jit(solution)/shard_map/pallas_call | solution.py:656
  103.3 1.3 convert_element_type.167
  104.6 0.8 copy-done.10
  105.4 2.5 fusion.43
  107.9 1.3 all-gather.6.cloned.1.call-done
  109.4 1.0 multiply_convert_fusion.3
  110.6 43.8 %all-gather.8.cloned.1.call-done = bf16[1024,960]{0,1:T(8,128)(2,1)} async-done(((bf16[256,960]{0,1:T(8,128)(2,1)}), bf16[1024,960]{0,1:T(8,128)(2,1)}) %all-gather.8.cloned.1.call-update) | async-done | bytes 1966096 | tf_op jit(solution)/shard_map/all_gather | solution.py:829
  154.4 3.6 fusion.44
  158.1 1.6 fusion.45
  159.7 3.7 %multiply_reduce_fusion = (bf16[1024]{0:T(1024)(128)(2,1)S(1)}, bf16[1024,640]{0,1:T(8,128)(2,1)}, bf16[1024,640]{0,1:T(8,128)(2,1)S(1)}, bf16[1024,640]{0,1:T(8,128)(2,1)S(1)}) fusion(f32[1024,640]{0,1:T(8,128)S(1)} %fusion.44, f32[1024,640]{0,1:T(8,128)S(1)} %fusion.45, bf16[1024,960]{0,1:T(8,128)(2,1)S(1)} %copy-done.33, bf16[640,960]{0,1:T(8,128)(2,1)S(1)} %copy-done), kind=kOutput, calls=%fused_computation.1 | convolution fusion | flops 1270086656 | bytes 12371968 | tf_op jit(solution)/shard_map/dot_general | solution.py:71
  163.4 1.7 fusion.46
  165.6 1.7 add_convert_fusion
  167.4 1.4 pad_maximum_fusion
  168.9 1.9 pad.40
  170.7 4.4 %convolution_convert_fusion.2 = bf16[1024,960]{0,1:T(8,128)(2,1)} fusion(bf16[640,960]{0,1:T(8,128)(2,1)S(1)} %copy-done, bf16[1024,640]{0,1:T(8,128)(2,1)} %get-tuple-element.93), kind=kOutput, calls=%fused_computation.14 | convolution fusion | flops 1259274240 | bytes 4505600 | tf_op jit(solution)/shard_map/dot_general | solution.py:836
  175.1 4.9 %convolution_convert_fusion.4 = bf16[640,960]{0,1:T(8,128)(2,1)} fusion(bf16[1024,640]{0,1:T(8,128)(2,1)} %get-tuple-element.93, bf16[1024,960]{0,1:T(8,128)(2,1)} %all-gather.6.cloned.1.call-done), kind=kOutput, calls=%fused_computation.16 | convolution fusion | flops 1258905600 | bytes 4505600 | tf_op jit(solution)/shard_map/dot_general | solution.py:843
  180.0 2.8 convolution_convert_fusion.5
  182.8 2.8 convolution_convert_fusion.6
  185.6 23.6 %reduce-scatter.3.cloned.1.call-done = bf16[256,961]{0,1:T(8,128)(2,1)} async-done(((bf16[1024,961]{0,1:T(8,128)(2,1)}), bf16[256,961]{0,1:T(8,128)(2,1)}) %reduce-scatter.3.cloned.1.call-update) | async-done | bytes 492048 | tf_op jit(solution)/shard_map/reduce_scatter | solution.py:833
  209.2 1.1 convert_element_type.177
  211.1 1.2 multiply_sine_fusion
  212.3 0.6 multiply_reduce_fusion.1
  213.4 1.1 copy-done.5
  214.7 1.8 convert_multiply_fusion.1
  216.5 1.6 reduce_sum.104
  218.1 0.6 pad.42.delta_ref
  218.7 28.8 %shard_map.241 = (bf16[256,1024]{1,0:T(8,128)(2,1)}, bf16[2048,640]{1,0:T(8,128)(2,1)}) custom-call(s32[18]{0:T(128)} %pad_add_fusion.first_ref, bf16[960,256]{1,0:T(8,128)(2,1)} %bitcast.164, bf16[2048,640]{1,0:T(8,128)(2,1)} %bitcast.187, s32[1,256]{1,0:T(1,128)} %pos_ref.3, s32[16,1,128]{2,1,0:T(1,128)} %bitcast.192, ...), custom_call_target="tpu_custom_call" | custom-call | flops 30198988800 | bytes 5242880 | tf_op jit(solution)/shard_map/pallas_call | solution.py:744
  247.5 23.8 %shard_map.242 = bf16[8,32,640]{2,1,0:T(8,128)(2,1)} custom-call(bf16[8,8,32,640]{3,2,1,0:T(8,128)(2,1)} %bitcast.150, f32[8,32,32]{2,1,0:T(8,128)} %get-tuple-element.109.cos_ref, f32[8,32,32]{2,1,0:T(8,128)} %get-tuple-element.108.sin_ref), custom_call_target="tpu_custom_call" | custom-call | bytes 78643200 | tf_op jit(solution)/shard_map/pallas_call | solution.py:401
  271.4 2.4 fusion.3
  273.8 1.6 fusion.30
  275.8 0.7 pad.44.refs_3_
  276.5 1.6 convolution_convert_fusion.3
  278.1 3.2 convolution_convert_fusion.1
  281.3 2.0 convolution_convert_fusion
  283.3 62.7 %shard_map.243 = (bf16[8,32,1024]{2,1,0:T(8,128)(2,1)}, bf16[8,32,1024]{2,1,0:T(8,128)(2,1)}, bf16[8,32,640]{2,1,0:T(8,128)(2,1)}, f32[8,8,128]{2,1,0:T(8,128)}) custom-call(bf16[4,8,32,1024]{3,2,1,0:T(8,128)(2,1)} %bitcast.142, bf16[4,8,32,1024]{3,2,1,0:T(8,128)(2,1)} %bitcast.143, bf16[4,8,32,640]{3,2,1,0:T(8,128)(2,1)} %bitcast.144, ...), custom_call_target="tpu_custom_call" | custom-call | bytes 167116800 | tf_op jit(solution)/shard_map/pallas_call | solution.py:527
  346.6 3.0 convert_element_type.190
  349.6 1.6 convert_element_type.191
  351.4 1.6 convert_element_type.192
  353.2 0.8 slice.112
  354.0 0.6 fusion.41
  354.8 0.9 fusion.39
  355.7 1.5 slice_convert_fusion
  357.2 3.2 fusion.37
  (137 shorter events, 7.1 us)
Async XLA Ops:
  7.2 152.5 %copy-start = (bf16[640,960]{0,1:T(8,128)(2,1)S(1)}, bf16[640,960]{0,1:T(8,128)(2,1)}, u32[]{:S(2)}) copy-start(bf16[640,960]{0,1:T(8,128)(2,1)} %param.22) | copy-start | bytes 3686404
  7.2 5.6 %copy-start.19 = (bf16[240,960]{1,0:T(8,128)(2,1)S(1)}, bf16[240,960]{1,0:T(8,128)(2,1)}, u32[]{:S(2)}) copy-start(bf16[240,960]{1,0:T(8,128)(2,1)} %param.16) | copy-start | bytes 1382404
  7.2 96.1 %all-gather.4.cloned.1.call-start = ((), (), s32[]{:S(2)}) async-start(), calls=%async_computation.2 | async-start | bytes 2457600 | tf_op jit(solution)/shard_map/all_gather | solution.py:793
  7.9 101.2 %all-gather.6.cloned.1.call-start = ((), (), s32[]{:S(2)}) async-start(), calls=%async_computation.3 | async-start | bytes 2457600 | tf_op jit(solution)/shard_map/all_gather | solution.py:806
  48.4 3.6 copy-start.32
  48.4 3.7 copy-start.2
  48.4 3.9 %copy-start.25 = (s32[1,256]{1,0:T(1,128)S(1)}, s32[1,256]{1,0:T(1,128)}, u32[]{:S(2)}) copy-start(s32[1,256]{1,0:T(1,128)} %pos_ref.3) | copy-start | bytes 3076
  48.4 4.4 %copy-start.4 = (bf16[1,256,960]{1,2,0:T(8,128)(2,1)S(1)}, bf16[1,256,960]{1,2,0:T(8,128)(2,1)}, u32[]{:S(2)}) copy-start(bf16[1,256,960]{1,2,0:T(8,128)(2,1)} %param.26) | copy-start | bytes 1474564
  50.0 1.1 copy-start.12
  53.8 100.6 %all-gather.8.cloned.1.call-start = ((), (), s32[]{:S(2)}) async-start(), calls=%async_computation.4 | async-start | bytes 2457600 | tf_op jit(solution)/shard_map/all_gather | solution.py:829
  83.8 3.3 copy-start.6
  84.6 2.4 copy-start.23
  84.7 2.4 copy-start.24
  104.6 0.8 copy-start.10
  110.4 98.8 %reduce-scatter.3.cloned.1.call-start = ((), (), s32[]{:S(2)}) async-start(), calls=%async_computation.5 | async-start | bytes 2478080 | tf_op jit(solution)/shard_map/reduce_scatter | solution.py:833
  154.4 3.6 copy-start.34
  154.4 3.6 copy-start.36
  158.0 1.6 copy-start.33
  163.4 1.7 copy-start.38
  163.4 1.7 copy-start.40
  163.4 2.2 copy-start.37
  168.8 177.8 %all-reduce.12.cloned.1.call-start = ((), (), s32[]{:S(2)}) async-start(), calls=%async_computation.7 | async-start | bytes 7372800 | tf_op jit(solution)/shard_map/psum | solution.py:853
  175.1 4.9 %copy-start.35 = (bf16[1024,960]{0,1:T(8,128)(2,1)S(1)}, bf16[1024,960]{0,1:T(8,128)(2,1)}, u32[]{:S(2)}) copy-start(bf16[1024,960]{0,1:T(8,128)(2,1)} %all-gather.8.cloned.1.call-done) | copy-start | bytes 5898244
  175.1 4.9 %copy-start.41 = (bf16[1024,640]{0,1:T(8,128)(2,1)S(1)}, bf16[1024,640]{0,1:T(8,128)(2,1)}, u32[]{:S(2)}) copy-start(bf16[1024,640]{0,1:T(8,128)(2,1)} %copy-done.40) | copy-start | bytes 3932164
  180.0 2.8 copy-start.39
  210.3 61.1 %copy-start.3 = (f32[256,961]{0,1:T(8,128)}, f32[256,961]{0,1:T(8,128)S(1)}, u32[]{:S(2)}) copy-start(f32[256,961]{0,1:T(8,128)S(1)} %convert_element_type.177) | copy-start | bytes 2952196
  210.3 0.7 copy-start.26
  210.3 146.8 %reduce-scatter.5.cloned.1.call-start = ((), (), s32[]{:S(2)}) async-start(), calls=%async_computation.6 | async-start | bytes 2457600 | tf_op jit(solution)/shard_map/reduce_scatter | solution.py:891
  212.9 1.5 copy-start.5
  212.9 1.8 copy-start.11
  214.7 1.8 copy-start.8
  247.5 23.8 %copy-start.17 = (bf16[256,1024]{1,0:T(8,128)(2,1)S(1)}, bf16[256,1024]{1,0:T(8,128)(2,1)}, u32[]{:S(2)}) copy-start(bf16[256,1024]{1,0:T(8,128)(2,1)} %get-tuple-element.58) | copy-start | bytes 1572868
  271.3 2.5 copy-start.13
  271.3 2.5 copy-start.14
  271.4 2.4 copy-start.30
  273.8 2.7 copy-start.7
  275.4 2.7 copy-start.9
  278.1 3.2 copy-start.18
  346.6 3.0 copy-start.16
  349.6 1.8 copy-start.15
  351.4 1.6 copy-start.22
  353.2 2.5 copy-start.20
  353.2 2.5 copy-start.21
  354.7 2.4 copy-start.27
  354.7 2.4 copy-start.28
  354.8 2.4 copy-start.29
  354.8 2.4 copy-start.31
  357.2 3.2 copy-start.1
Sparse Core Ops, SparseCore 0:
  9.6 54.0 all-gather.3
  65.8 43.2 all-gather.5
  111.3 43.0 all-gather.7
  168.9 40.1 reduce-scatter.2
  212.7 80.1 all-reduce.11
  295.1 56.4 reduce-scatter.4

commit v12 on v11

--- a/solution.py
+++ b/solution.py
@@ -886,14 +886,14 @@
     vectors = jnp.pad(vectors.transpose(1, 0, 2).reshape(depth, -1), ((0, 0), (0, -3 * own_rows % 1024)))
     vectors = jnp.pad(vectors.reshape(depth, -1, 1, 128), ((0, 0), (0, 0), (0, 7), (0, 0)))
     layered = [grad.reshape(depth, padded_rows, -1) for grad in (grad_wout, grad_wq, grad_wkv)]
-    layered.append(vectors.reshape(depth, -1, 128))
+    layered.insert(0, vectors.reshape(depth, -1, 128))
     owned = reduce_rows(layered, 4)
     ffn_out = lax.psum_scatter(ffn_part, "fsdp", scatter_dimension=0, tiled=True)
     *owned, totals = lax.optimization_barrier((*owned, totals))
-    total_out, total_q, total_kv = (own[:own_rows].astype(jnp.float32) for own in owned[:3])
+    total_out, total_q, total_kv = (own[:own_rows].astype(jnp.float32) for own in owned[1:])
     total_q, total_out = total_q[:, :qdim], total_out[:, :width]
     total_k, total_v = total_kv[:, :kdim], total_kv[:, kdim:]
-    mine = owned[3].reshape(-1, 8, 128)[:, 0].reshape(-1)[: 3 * own_rows].reshape(3, own_rows)
+    mine = owned[0].reshape(-1, 8, 128)[:, 0].reshape(-1)[: 3 * own_rows].reshape(3, own_rows)
     totals = [total.astype(jnp.float32) for total in totals]
     ffn_out, *totals = lax.optimization_barrier((ffn_out, *totals))
     total_gate, total_up, total_down = totals

time: 368 us -> 368 us (level)
  no operation moved by 1% of the time
where the time goes in v12:
time: 368 us; the launch traced here: 364 us
  Pallas kernels  184 us (50%)
  waiting for transfers between devices  69.4 us (19%)
  matrix products  46.6 us (13%)
  other arithmetic  27.2 us (7%)
  local copies, waits for them, and re-layouts  20.5 us (6%)
  between operations  15.4 us (4%)
    pallas_call x1, Pallas kernels, reduce_rows(): pl.pallas_call(functools.partial(reduce_rows_kernel, depth, count), out_s...  59.8 us
    all_gather x1, waiting for transfers between devices, on_device(): normed_all = lax.all_gather(normed_two, 'fsdp', axis=0, tiled=True)  43.8 us
    pallas_call x1, Pallas kernels, gather_rows(): pl.pallas_call(functools.partial(gather_rows_kernel, depth, count), out_s...  34.7 us
    pallas_call x1, Pallas kernels, attend_back(): pl.pallas_call(attend_back_kernel, out_shape=(jax.ShapeDtypeStruct((slots...  28.8 us
    pallas_call x1, Pallas kernels, scatter_plane(): pl.pallas_call(scatter_plane_kernel, out_shape=jax.ShapeDtypeStruct(block...  23.8 us
    reduce_scatter x1, waiting for transfers between devices, on_device(): lax.psum_scatter(grad_normed_part, 'fsdp', scatter_dimension=0, tiled=True)  23.6 us
    pallas_call x1, Pallas kernels, gather_plane(): pl.pallas_call(gather_plane_kernel, out_shape=(jax.ShapeDtypeStruct((SPAN...  22.1 us
    dot_general x9, matrix products, dot(): lax.dot_general(left, right, (((dims[0],), (dims[1],)), ((), ())), prefer...  19.5 us
  transfers between devices with their start and end apart: 6, of which 3 were waited for; matrix products, arithmetic and copies ran while one was open for 19% of the time, Pallas kernels for 51%

profile of v12, /device:TPU:0, one launch (start us, length us, event | category | flops | bytes accessed | tf_op | source)
XLA Modules:
  0.0 364.3 jit_solution(13338738944636526258)
XLA Ops:
  7.2 0.7 all-gather.4.cloned.1.call-update
  8.0 0.7 stack.21
  8.6 0.7 stack.22
  9.3 0.7 stack.23
  10.0 1.9 concatenate.23
  12.0 0.8 pad.38.clone
  12.8 0.8 pad.58
  13.7 34.7 %shard_map.238 = (bf16[4,8,32,1024]{3,2,1,0:T(8,128)(2,1)}, bf16[4,8,32,643]{3,2,1,0:T(8,128)(2,1)}) custom-call(bf16[8,32,1024]{2,1,0:T(8,128)(2,1)} %bitcast.151, bf16[8,32,643]{2,1,0:T(8,128)(2,1)} %bitcast.156), custom_call_target="tpu_custom_call" | custom-call | bytes 102420480 | tf_op jit(solution)/shard_map/pallas_call | solution.py:201
  48.4 1.6 slice.102
  50.0 1.1 copy-done.12
  52.8 0.9 fusion.13
  54.4 2.0 fusion.5
  57.2 0.6 and_select_fusion.tag_ref
  57.8 0.8 pad_maximum_fusion.1.kv_ref
  58.6 22.1 %shard_map.239 = (bf16[8,256,640]{2,1,0:T(8,128)(2,1)}, s32[8,1,256]{2,1,0:T(1,128)}) custom-call(bf16[256,640]{1,0:T(8,128)(2,1)} %pad_maximum_fusion.1.kv_ref, s32[1,256]{1,0:T(1,128)} %and_select_fusion.tag_ref), custom_call_target="tpu_custom_call" | custom-call | bytes 78643200 | tf_op jit(solution)/shard_map/pallas_call | solution.py:252
  80.7 0.8 slice.83
  81.6 1.0 multiply_convert_fusion.4
  82.7 1.1 pad.39
  83.8 0.7 pad_add_fusion.first_ref
  84.7 2.3 fusion.1
  87.2 0.9 maximum_multiply_fusion
  88.1 15.3 %shard_map.240 = (f32[960,256]{1,0:T(8,128)}, f32[16,256]{1,0:T(8,128)}) custom-call(s32[18]{0:T(128)} %pad_add_fusion.first_ref, bf16[960,256]{1,0:T(8,128)(2,1)} %bitcast.163, bf16[2048,640]{1,0:T(8,128)(2,1)} %bitcast.186, s32[1,256]{1,0:T(1,128)} %pos_ref.3, s32[16,1,128]{2,1,0:T(1,128)} %bitcast.191), custom_call_target="tpu_custom_call" | custom-call | flops 16106127360 | bytes 2621440 | tf_op jit(solution)/shard_map/pallas_call | solution.py:656
  103.3 1.3 convert_element_type.167
  104.6 0.8 copy-done.10
  105.4 2.5 fusion.43
  107.9 1.3 all-gather.6.cloned.1.call-done
  109.4 1.0 multiply_convert_fusion.3
  110.6 43.8 %all-gather.8.cloned.1.call-done = bf16[1024,960]{0,1:T(8,128)(2,1)} async-done(((bf16[256,960]{0,1:T(8,128)(2,1)}), bf16[1024,960]{0,1:T(8,128)(2,1)}) %all-gather.8.cloned.1.call-update) | async-done | bytes 1966096 | tf_op jit(solution)/shard_map/all_gather | solution.py:829
  154.4 3.6 fusion.44
  158.0 1.6 fusion.45
  159.7 3.7 %multiply_reduce_fusion = (bf16[1024]{0:T(1024)(128)(2,1)S(1)}, bf16[1024,640]{0,1:T(8,128)(2,1)}, bf16[1024,640]{0,1:T(8,128)(2,1)S(1)}, bf16[1024,640]{0,1:T(8,128)(2,1)S(1)}) fusion(f32[1024,640]{0,1:T(8,128)S(1)} %fusion.44, f32[1024,640]{0,1:T(8,128)S(1)} %fusion.45, bf16[1024,960]{0,1:T(8,128)(2,1)S(1)} %copy-done.33, bf16[640,960]{0,1:T(8,128)(2,1)S(1)} %copy-done), kind=kOutput, calls=%fused_computation.1 | convolution fusion | flops 1270086656 | bytes 12371968 | tf_op jit(solution)/shard_map/dot_general | solution.py:71
  163.4 1.7 fusion.46
  165.6 1.7 add_convert_fusion
  167.3 1.4 pad_maximum_fusion
  168.8 1.9 pad.40
  170.7 4.4 %convolution_convert_fusion.2 = bf16[1024,960]{0,1:T(8,128)(2,1)} fusion(bf16[640,960]{0,1:T(8,128)(2,1)S(1)} %copy-done, bf16[1024,640]{0,1:T(8,128)(2,1)} %get-tuple-element.93), kind=kOutput, calls=%fused_computation.14 | convolution fusion | flops 1259274240 | bytes 4505600 | tf_op jit(solution)/shard_map/dot_general | solution.py:836
  175.1 4.9 %convolution_convert_fusion.4 = bf16[640,960]{0,1:T(8,128)(2,1)} fusion(bf16[1024,640]{0,1:T(8,128)(2,1)} %get-tuple-element.93, bf16[1024,960]{0,1:T(8,128)(2,1)} %all-gather.6.cloned.1.call-done), kind=kOutput, calls=%fused_computation.16 | convolution fusion | flops 1258905600 | bytes 4505600 | tf_op jit(solution)/shard_map/dot_general | solution.py:843
  180.0 2.8 convolution_convert_fusion.5
  182.8 2.8 convolution_convert_fusion.6
  185.5 23.6 %reduce-scatter.3.cloned.1.call-done = bf16[256,961]{0,1:T(8,128)(2,1)} async-done(((bf16[1024,961]{0,1:T(8,128)(2,1)}), bf16[256,961]{0,1:T(8,128)(2,1)}) %reduce-scatter.3.cloned.1.call-update) | async-done | bytes 492048 | tf_op jit(solution)/shard_map/reduce_scatter | solution.py:833
  209.1 1.1 convert_element_type.177
  211.1 1.2 multiply_sine_fusion
  212.3 0.6 multiply_reduce_fusion.2
  213.3 1.1 copy-done.5
  214.7 1.8 convert_multiply_fusion.1
  216.5 1.6 reduce_sum.104
  218.1 0.6 pad.41.delta_ref
  218.7 28.8 %shard_map.241 = (bf16[256,1024]{1,0:T(8,128)(2,1)}, bf16[2048,640]{1,0:T(8,128)(2,1)}) custom-call(s32[18]{0:T(128)} %pad_add_fusion.first_ref, bf16[960,256]{1,0:T(8,128)(2,1)} %bitcast.164, bf16[2048,640]{1,0:T(8,128)(2,1)} %bitcast.187, s32[1,256]{1,0:T(1,128)} %pos_ref.3, s32[16,1,128]{2,1,0:T(1,128)} %bitcast.192, ...), custom_call_target="tpu_custom_call" | custom-call | flops 30198988800 | bytes 5242880 | tf_op jit(solution)/shard_map/pallas_call | solution.py:744
  247.5 23.8 %shard_map.242 = bf16[8,32,640]{2,1,0:T(8,128)(2,1)} custom-call(bf16[8,8,32,640]{3,2,1,0:T(8,128)(2,1)} %bitcast.150, f32[8,32,32]{2,1,0:T(8,128)} %get-tuple-element.109.cos_ref, f32[8,32,32]{2,1,0:T(8,128)} %get-tuple-element.108.sin_ref), custom_call_target="tpu_custom_call" | custom-call | bytes 78643200 | tf_op jit(solution)/shard_map/pallas_call | solution.py:401
  271.3 2.4 fusion.3
  273.8 1.6 fusion.30
  275.8 0.7 pad.43.refs_0_
  276.5 1.6 convolution_convert_fusion.3
  278.1 3.2 convolution_convert_fusion.1
  281.3 2.0 convolution_convert_fusion
  283.3 59.8 %shard_map.243 = (f32[8,8,128]{2,1,0:T(8,128)}, bf16[8,32,1024]{2,1,0:T(8,128)(2,1)}, bf16[8,32,1024]{2,1,0:T(8,128)(2,1)}, bf16[8,32,640]{2,1,0:T(8,128)(2,1)}) custom-call(f32[4,8,8,128]{3,2,1,0:T(8,128)} %pad.43.refs_0_, bf16[4,8,32,1024]{3,2,1,0:T(8,128)(2,1)} %bitcast.142, bf16[4,8,32,1024]{3,2,1,0:T(8,128)(2,1)} %bitcast.143, ...), custom_call_target="tpu_custom_call" | custom-call | bytes 167116800 | tf_op jit(solution)/shard_map/pallas_call | solution.py:527
  343.7 3.0 convert_element_type.190
  346.7 1.6 convert_element_type.191
  348.5 1.6 convert_element_type.192
  350.3 0.8 slice.112
  351.1 0.6 fusion.41
  351.9 0.9 fusion.39
  352.7 1.5 slice_convert_fusion
  354.3 3.2 fusion.37
  (137 shorter events, 7.1 us)
Async XLA Ops:
  7.2 152.5 %copy-start = (bf16[640,960]{0,1:T(8,128)(2,1)S(1)}, bf16[640,960]{0,1:T(8,128)(2,1)}, u32[]{:S(2)}) copy-start(bf16[640,960]{0,1:T(8,128)(2,1)} %param.22) | copy-start | bytes 3686404
  7.2 5.6 %copy-start.19 = (bf16[240,960]{1,0:T(8,128)(2,1)S(1)}, bf16[240,960]{1,0:T(8,128)(2,1)}, u32[]{:S(2)}) copy-start(bf16[240,960]{1,0:T(8,128)(2,1)} %param.16) | copy-start | bytes 1382404
  7.2 96.1 %all-gather.4.cloned.1.call-start = ((), (), s32[]{:S(2)}) async-start(), calls=%async_computation.2 | async-start | bytes 2457600 | tf_op jit(solution)/shard_map/all_gather | solution.py:793
  7.9 101.2 %all-gather.6.cloned.1.call-start = ((), (), s32[]{:S(2)}) async-start(), calls=%async_computation.3 | async-start | bytes 2457600 | tf_op jit(solution)/shard_map/all_gather | solution.py:806
  48.4 3.6 copy-start.32
  48.4 3.7 %copy-start.2 = (bf16[1,256,960]{1,2,0:T(8,128)(2,1)S(1)}, bf16[1,256,960]{1,2,0:T(8,128)(2,1)}, u32[]{:S(2)}) copy-start(bf16[1,256,960]{1,2,0:T(8,128)(2,1)} %param.15) | copy-start | bytes 1474564
  48.4 3.9 %copy-start.25 = (s32[1,256]{1,0:T(1,128)S(1)}, s32[1,256]{1,0:T(1,128)}, u32[]{:S(2)}) copy-start(s32[1,256]{1,0:T(1,128)} %pos_ref.3) | copy-start | bytes 3076
  48.4 4.4 %copy-start.4 = (bf16[1,256,960]{1,2,0:T(8,128)(2,1)S(1)}, bf16[1,256,960]{1,2,0:T(8,128)(2,1)}, u32[]{:S(2)}) copy-start(bf16[1,256,960]{1,2,0:T(8,128)(2,1)} %param.26) | copy-start | bytes 1474564
  50.0 1.1 copy-start.12
  53.8 100.6 %all-gather.8.cloned.1.call-start = ((), (), s32[]{:S(2)}) async-start(), calls=%async_computation.4 | async-start | bytes 2457600 | tf_op jit(solution)/shard_map/all_gather | solution.py:829
  83.8 3.3 copy-start.6
  84.6 2.4 copy-start.23
  84.7 2.4 copy-start.24
  104.6 0.8 copy-start.10
  110.4 98.8 %reduce-scatter.3.cloned.1.call-start = ((), (), s32[]{:S(2)}) async-start(), calls=%async_computation.5 | async-start | bytes 2478080 | tf_op jit(solution)/shard_map/reduce_scatter | solution.py:833
  154.4 3.6 copy-start.34
  154.4 3.6 copy-start.36
  158.0 1.6 copy-start.33
  163.4 1.7 copy-start.38
  163.4 1.7 copy-start.40
  163.4 2.2 copy-start.37
  168.8 174.9 %all-reduce.12.cloned.1.call-start = ((), (), s32[]{:S(2)}) async-start(), calls=%async_computation.7 | async-start | bytes 7372800 | tf_op jit(solution)/shard_map/psum | solution.py:853
  175.1 4.9 %copy-start.35 = (bf16[1024,960]{0,1:T(8,128)(2,1)S(1)}, bf16[1024,960]{0,1:T(8,128)(2,1)}, u32[]{:S(2)}) copy-start(bf16[1024,960]{0,1:T(8,128)(2,1)} %all-gather.8.cloned.1.call-done) | copy-start | bytes 5898244
  175.1 4.9 %copy-start.41 = (bf16[1024,640]{0,1:T(8,128)(2,1)S(1)}, bf16[1024,640]{0,1:T(8,128)(2,1)}, u32[]{:S(2)}) copy-start(bf16[1024,640]{0,1:T(8,128)(2,1)} %copy-done.40) | copy-start | bytes 3932164
  180.0 2.8 copy-start.39
  210.2 61.0 %copy-start.3 = (f32[256,961]{0,1:T(8,128)}, f32[256,961]{0,1:T(8,128)S(1)}, u32[]{:S(2)}) copy-start(f32[256,961]{0,1:T(8,128)S(1)} %convert_element_type.177) | copy-start | bytes 2952196
  210.3 0.7 copy-start.26
  210.3 144.0 %reduce-scatter.5.cloned.1.call-start = ((), (), s32[]{:S(2)}) async-start(), calls=%async_computation.6 | async-start | bytes 2457600 | tf_op jit(solution)/shard_map/reduce_scatter | solution.py:891
  212.9 1.5 copy-start.5
  212.9 1.8 copy-start.11
  214.7 1.8 copy-start.8
  247.5 23.8 %copy-start.17 = (bf16[256,1024]{1,0:T(8,128)(2,1)S(1)}, bf16[256,1024]{1,0:T(8,128)(2,1)}, u32[]{:S(2)}) copy-start(bf16[256,1024]{1,0:T(8,128)(2,1)} %get-tuple-element.57) | copy-start | bytes 1572868
  271.3 2.5 copy-start.13
  271.3 2.5 copy-start.14
  271.3 2.4 copy-start.30
  273.8 2.7 copy-start.7
  275.4 2.7 copy-start.9
  278.1 3.2 copy-start.18
  343.7 3.0 copy-start.16
  346.7 1.8 copy-start.15
  348.5 1.6 copy-start.22
  350.3 2.5 copy-start.20
  350.3 2.5 copy-start.21
  351.8 2.4 copy-start.27
  351.8 2.4 copy-start.28
  351.8 2.4 copy-start.29
  351.9 2.4 copy-start.31
  354.2 3.2 copy-start.1
Sparse Core Ops, SparseCore 0:
  9.6 54.0 all-gather.3
  65.8 43.2 all-gather.5
  111.3 43.0 all-gather.7
  168.9 40.1 reduce-scatter.2
  212.7 80.6 all-reduce.11
  295.5 56.2 reduce-scatter.4
